TPU v7x, 32 devices: a whole 2x2x4 slice. The times are simulated.
32 devices in a mesh: parts: 2 (over y), row: 4 (over x, core), col: 4 (over z).
Axes of the slice: x: 2, y: 2, z: 4, core: 2. Of those that a mesh axis runs over, the one named last changes fastest.
Arguments:
- alignment_tensor: bfloat16 [256, 256, 256], P(('parts', 'col'), 'row'), parts along dimension 0, may hold values from -6 to 6
- standardizer_scaling: float32 [256], replicated, may hold values from 0.25 to 1.75
- standardizer_offset: float32 [256], replicated, may hold values from -3 to 3
- first_projector: bfloat16 [256, 32], replicated, may hold values from -0.375 to 0.375
- second_projector: bfloat16 [256, 32], replicated, may hold values from -0.375 to 0.375
- final_projector: bfloat16 [1024, 128], replicated, may hold values from -1 to 1
- final_offset: float32 [128], replicated, may hold values from -3 to 3
- amino_strand_label: int32 [512], P('parts'), parts along dimension 0, may hold values from 0 to 7, never falling along the last dimension, each value on 1 to 128 neighbouring positions
- matched_strand_count: int32 [16, 8], P('parts'), parts along dimension 0, may hold values from 32 to 128, as said below
- couple_delta_adjoint: bfloat16 [512, 256, 128], P(('parts', 'row'), 'col'), parts along dimension 0, may hold values from -6 to 6
Outputs:
- pair_update: bfloat16 [512, 256, 128], P(('parts', 'row'), 'col'), parts along dimension 0
- adjoint_first_factor: bfloat16 [256, 8192], P(('parts', 'col'), 'row'), parts along dimension 0
- grad_right: bfloat16 [256, 8192], P(('parts', 'col'), 'row'), parts along dimension 0
- grad_w_out: float32 [2048, 128], P('parts'), parts along dimension 0
There are 2 independent parts, one for each index of `parts`. A program takes and returns all parts, laid end to end along the dimension named above; an argument that names none is the same for every part. Nothing has to cross between parts.
Inputs may be any that keep to these rules, and one draw needn't show every extreme that they name: `amino_strand_label`: chain numbers never fall along the residues; a chain has 1 to 128 residues. `matched_strand_count`: every entry is a multiple of 32.
All inputs are finite; a program needn't handle non-finite values.
Results may differ from a plain program's by a relative error of at most 0.018.
Values may be sent and summed in bfloat16 or wider, within the bound.
No kernel may reach another device: no remote copies, remote signals or barrier semaphores. Data moves between devices by JAX's collectives and lax.ppermute only.
A program may use at most 256 MiB of HBM per device.

v0:
```python
import jax
import jax.numpy as jnp
from jax import lax
from jax.sharding import PartitionSpec as P

PROJECTED_SIZE = 32
CZ = 128
WINDOW_AMINOS = 256
DEPTH_STEP = 32
CHAINS = 8
LEVELS = 4


def standardize_entries(alignment_tensor, standard_multiplier, additive_offset):
    incoming_entries = alignment_tensor.astype(jnp.float32)
    center = incoming_entries - jnp.mean(incoming_entries, axis=-1, keepdims=True)
    spread = jnp.mean(center * center, axis=-1, keepdims=True)
    return (center * lax.rsqrt(spread + 1e-05) * standard_multiplier + additive_offset).astype(
        jnp.bfloat16
    )


def shards(
    alignment_tensor,
    standardizer_scaling,
    standardizer_offset,
    first_projector,
    second_projector,
    final_projector,
    final_offset,
    amino_strand_label,
    matched_strand_count,
    couple_delta_adjoint,
):
    homolog_portion, incoming_matrix, embedding_extent = alignment_tensor.shape
    cols = couple_delta_adjoint.shape[1]
    standardized_entries = standardize_entries(
        alignment_tensor, standardizer_scaling, standardizer_offset
    ).reshape(-1, embedding_extent)
    first_factor = (
        jnp.dot(standardized_entries, first_projector, preferred_element_type=jnp.float32)
        .astype(jnp.bfloat16)
        .reshape(homolog_portion, incoming_matrix * PROJECTED_SIZE)
    )
    second_factor = (
        jnp.dot(standardized_entries, second_projector, preferred_element_type=jnp.float32)
        .astype(jnp.bfloat16)
        .reshape(homolog_portion, incoming_matrix * PROJECTED_SIZE)
    )
    left_panel = lax.all_gather(first_factor, "col", axis=0, tiled=True)
    right_rows = lax.all_gather(second_factor, "row", axis=1, tiled=True)
    right_panel = lax.all_to_all(right_rows, "col", split_axis=1, concat_axis=0, tiled=True)
    row_start = lax.axis_index("row") * incoming_matrix
    col_start = lax.axis_index("col") * cols
    chains = jnp.arange(CHAINS, dtype=jnp.int32)
    row_hot = (
        lax.dynamic_slice_in_dim(amino_strand_label, row_start, incoming_matrix, 0)[:, None]
        == chains[None, :]
    ).astype(jnp.float32)
    col_hot = (
        lax.dynamic_slice_in_dim(amino_strand_label, col_start, cols, 0)[:, None] == chains[None, :]
    ).astype(jnp.float32)
    table = matched_strand_count.astype(jnp.float32)
    depth = jnp.dot(
        jnp.dot(row_hot, table, precision=lax.Precision.HIGHEST),
        col_hot.T,
        precision=lax.Precision.HIGHEST,
    )
    count = LEVELS

    def forward_level(level, acc):
        low = level * DEPTH_STEP
        left_level = lax.dynamic_slice_in_dim(left_panel, low, DEPTH_STEP, 0)
        right_level = lax.dynamic_slice_in_dim(right_panel, low, DEPTH_STEP, 0)
        prod = lax.dot_general(
            left_level, right_level, (((0,), (0,)), ((), ())), preferred_element_type=jnp.float32
        )
        prod = (
            prod.reshape(incoming_matrix, PROJECTED_SIZE, cols, PROJECTED_SIZE)
            .transpose(0, 2, 1, 3)
            .reshape(incoming_matrix, cols, PROJECTED_SIZE * PROJECTED_SIZE)
        )
        keep = (depth > low.astype(jnp.float32)).astype(jnp.float32)
        return acc + keep[:, :, None] * prod

    acc = lax.fori_loop(
        0,
        count,
        forward_level,
        jnp.zeros((incoming_matrix, cols, PROJECTED_SIZE * PROJECTED_SIZE), jnp.float32),
    )
    outer = (acc / depth[:, :, None]).astype(jnp.bfloat16)
    flat_outer = outer.reshape(-1, PROJECTED_SIZE * PROJECTED_SIZE)
    pair = (
        jnp.dot(flat_outer, final_projector, preferred_element_type=jnp.float32) + final_offset
    ).astype(jnp.bfloat16)
    pair_update = pair.reshape(incoming_matrix, cols, CZ)
    flat_grad = couple_delta_adjoint.reshape(-1, CZ)
    back = lax.dot_general(
        flat_grad, final_projector, (((1,), (1,)), ((), ())), preferred_element_type=jnp.float32
    )
    scaled = (
        back.reshape(incoming_matrix, cols, PROJECTED_SIZE * PROJECTED_SIZE) / depth[:, :, None]
    ).astype(jnp.bfloat16)
    turned = (
        scaled.reshape(incoming_matrix, cols, PROJECTED_SIZE, PROJECTED_SIZE)
        .transpose(0, 2, 1, 3)
        .reshape(incoming_matrix * PROJECTED_SIZE, cols * PROJECTED_SIZE)
    )

    def backward_level(level, grads):
        left_grad, right_grad = grads
        low = level * DEPTH_STEP
        left_level = lax.dynamic_slice_in_dim(left_panel, low, DEPTH_STEP, 0)
        right_level = lax.dynamic_slice_in_dim(right_panel, low, DEPTH_STEP, 0)
        keep = (depth > low.astype(jnp.float32)).astype(jnp.bfloat16)
        keep_wide = jnp.broadcast_to(
            keep[:, None, :, None], (incoming_matrix, PROJECTED_SIZE, cols, PROJECTED_SIZE)
        ).reshape(incoming_matrix * PROJECTED_SIZE, cols * PROJECTED_SIZE)
        masked = turned * keep_wide
        left_piece = lax.dot_general(
            right_level, masked, (((1,), (1,)), ((), ())), preferred_element_type=jnp.float32
        )
        right_piece = jnp.dot(left_level, masked, preferred_element_type=jnp.float32)
        left_grad = lax.dynamic_update_slice_in_dim(left_grad, left_piece, low, 0)
        right_grad = lax.dynamic_update_slice_in_dim(right_grad, right_piece, low, 0)
        return (left_grad, right_grad)

    seqs = left_panel.shape[0]
    start_grads = (
        jnp.zeros((seqs, incoming_matrix * PROJECTED_SIZE), jnp.float32),
        jnp.zeros((seqs, cols * PROJECTED_SIZE), jnp.float32),
    )
    left_grad, right_grad = lax.fori_loop(0, count, backward_level, start_grads)
    weight_part = lax.dot_general(
        flat_outer, flat_grad, (((0,), (0,)), ((), ())), preferred_element_type=jnp.float32
    )
    adjoint_first_factor = lax.psum_scatter(
        left_grad.astype(jnp.bfloat16), "col", scatter_dimension=0, tiled=True
    )
    right_parts = lax.all_to_all(
        right_grad.astype(jnp.bfloat16), "col", split_axis=0, concat_axis=1, tiled=True
    ).astype(right_grad.dtype)
    grad_right = lax.psum_scatter(
        right_parts.astype(jnp.bfloat16), "row", scatter_dimension=1, tiled=True
    )
    weight_total = lax.psum(weight_part, ("row", "col"))
    grad_w_out = weight_total / WINDOW_AMINOS
    return (pair_update, adjoint_first_factor, grad_right, grad_w_out)


def solution(mesh):
    in_specs = (
        P(("parts", "col"), "row", None),
        P(),
        P(),
        P(),
        P(),
        P(),
        P(),
        P("parts"),
        P("parts", None),
        P(("parts", "row"), "col", None),
    )
    out_specs = (
        P(("parts", "row"), "col", None),
        P(("parts", "col"), "row"),
        P(("parts", "col"), "row"),
        P("parts", None),
    )
    return jax.shard_map(shards, mesh=mesh, in_specs=in_specs, out_specs=out_specs, check_vma=False)
```

profile of v0, /device:TPU:0, one launch (start us, length us, event | category | flops | bytes accessed | tf_op | source)
XLA Modules:
  0.0 1022.6 jit_solution(9267214551704113431)
XLA Ops:
  15.4 8.6 all_gather.7
  36.7 15.6 %copy.44 = bf16[64,64,1024]{1,2,0:T(8,128)(2,1)} copy(bf16[64,64,1024]{2,1,0:T(8,128)(2,1)} %divide_convert_fusion) | data formatting | bytes 16777216 | tf_op jit(solution)/shard_map/convert_element_type | solution.py:104
  52.3 30.2 %copy.45 = bf16[64,32,64,32]{3,2,1,0:T(8,128)(2,1)} copy(bf16[64,32,64,32]{2,3,1,0:T(8,128)(2,1)} %bitcast.45) | data formatting | bytes 16777216 | tf_op jit(solution)/shard_map/transpose | solution.py:107
  82.6 43.6 %reshape.96 = bf16[2048,2048]{1,0:T(8,128)(2,1)} reshape(bf16[64,32,64,32]{3,2,1,0:T(8,128)(2,1)} %copy.45) | data formatting | bytes 16777216 | tf_op jit(solution)/shard_map/reshape | solution.py:108
  126.1 16.3 %all_gather.6 = bf16[128,2048]{1,0:T(8,128)(2,1)S(1)} all-gather(bf16[32,2048]{1,0:T(8,128)(2,1)S(1)} %reshape.91), channel_id=1, replica_groups=mesh['parts'=2,'row'=4,'col'=4] {'col'}, dimensions={0}, use_global_device_ids=true | all-gather | bytes 655360 | tf_op jit(solution)/shard_map/all_gather | solution.py:50
  142.4 510.9 %while.30 = (s32[]{:T(128)}, f32[64,64,1024]{1,2,0:T(8,128)}, f32[64,64]{1,0:T(8,128)S(1)}, bf16[128,2048]{1,0:T(8,128)(2,1)S(1)}, bf16[128,2048]{1,0:T(8,128)(2...) while((s32[]{:T(128)}, f32[64,64,1024]{1,2,0:T(8,128)}, f32[64,64]{1,0:T(8,128)S(1)}, ...), condition=%wide.region_3.0_spmd.clone, body=%wide.region_2.0_spmd.clone.sunk | while | flops 281026560 | bytes 134530192 | solution.py:86
  150.5 40.6 %reshape.104 = f32[64,32,64,32]{3,2,1,0:T(8,128)} reshape(f32[2048,2048]{1,0:T(8,128)} %fusion.61) | data formatting | bytes 33554432 | tf_op jit(solution)/shard_map/while/body/eval_jaxpr/reshape | solution.py:79
  191.1 48.2 %copy.52 = f32[64,64,32,32]{1,3,2,0:T(8,128)} copy(f32[64,64,32,32]{3,1,2,0:T(8,128)} %bitcast.44) | data formatting | bytes 33554432 | tf_op jit(solution)/shard_map/while/body/eval_jaxpr/transpose | solution.py:80
  239.4 23.0 %fusion.62 = f32[64,64,1024]{1,2,0:T(8,128)} fusion(f32[64,64,32,32]{1,3,2,0:T(8,128)} %copy.52, f32[64,64,1024]{1,2,0:T(8,128)} %get-tuple-element.354, f32[64,64]{1,0:T(8,128)S(1)} %compare_convert_fusion.5, pred[]{:T(512)S(6)} %compare.3), kind=kLoop, calls=%fused_computation.12.clone.1 | loop fusion | flops 12582912 | bytes 50348032 | tf_op jit(solution)/shard_map/while/body/eval_jaxpr/add | solution.py:84
  270.5 40.6 %reshape.104 = f32[64,32,64,32]{3,2,1,0:T(8,128)} reshape(f32[2048,2048]{1,0:T(8,128)} %fusion.61) | data formatting | bytes 33554432 | tf_op jit(solution)/shard_map/while/body/eval_jaxpr/reshape | solution.py:79
  311.1 48.2 %copy.52 = f32[64,64,32,32]{1,3,2,0:T(8,128)} copy(f32[64,64,32,32]{3,1,2,0:T(8,128)} %bitcast.44) | data formatting | bytes 33554432 | tf_op jit(solution)/shard_map/while/body/eval_jaxpr/transpose | solution.py:80
  359.3 33.4 %fusion.62 = f32[64,64,1024]{1,2,0:T(8,128)} fusion(f32[64,64,32,32]{1,3,2,0:T(8,128)} %copy.52, f32[64,64,1024]{1,2,0:T(8,128)} %get-tuple-element.354, f32[64,64]{1,0:T(8,128)S(1)} %compare_convert_fusion.5, pred[]{:T(512)S(6)} %compare.3), kind=kLoop, calls=%fused_computation.12.clone.1 | loop fusion | flops 12582912 | bytes 50348032 | tf_op jit(solution)/shard_map/while/body/eval_jaxpr/add | solution.py:84
  400.8 40.6 %reshape.104 = f32[64,32,64,32]{3,2,1,0:T(8,128)} reshape(f32[2048,2048]{1,0:T(8,128)} %fusion.61) | data formatting | bytes 33554432 | tf_op jit(solution)/shard_map/while/body/eval_jaxpr/reshape | solution.py:79
  441.4 48.2 %copy.52 = f32[64,64,32,32]{1,3,2,0:T(8,128)} copy(f32[64,64,32,32]{3,1,2,0:T(8,128)} %bitcast.44) | data formatting | bytes 33554432 | tf_op jit(solution)/shard_map/while/body/eval_jaxpr/transpose | solution.py:80
  489.6 33.4 %fusion.62 = f32[64,64,1024]{1,2,0:T(8,128)} fusion(f32[64,64,32,32]{1,3,2,0:T(8,128)} %copy.52, f32[64,64,1024]{1,2,0:T(8,128)} %get-tuple-element.354, f32[64,64]{1,0:T(8,128)S(1)} %compare_convert_fusion.5, pred[]{:T(512)S(6)} %compare.3), kind=kLoop, calls=%fused_computation.12.clone.1 | loop fusion | flops 12582912 | bytes 50348032 | tf_op jit(solution)/shard_map/while/body/eval_jaxpr/add | solution.py:84
  531.1 40.6 %reshape.104 = f32[64,32,64,32]{3,2,1,0:T(8,128)} reshape(f32[2048,2048]{1,0:T(8,128)} %fusion.61) | data formatting | bytes 33554432 | tf_op jit(solution)/shard_map/while/body/eval_jaxpr/reshape | solution.py:79
  571.7 48.2 %copy.52 = f32[64,64,32,32]{1,3,2,0:T(8,128)} copy(f32[64,64,32,32]{3,1,2,0:T(8,128)} %bitcast.44) | data formatting | bytes 33554432 | tf_op jit(solution)/shard_map/while/body/eval_jaxpr/transpose | solution.py:80
  620.0 33.4 %fusion.62 = f32[64,64,1024]{1,2,0:T(8,128)} fusion(f32[64,64,32,32]{1,3,2,0:T(8,128)} %copy.52, f32[64,64,1024]{1,2,0:T(8,128)} %get-tuple-element.354, f32[64,64]{1,0:T(8,128)S(1)} %compare_convert_fusion.5, pred[]{:T(512)S(6)} %compare.3), kind=kLoop, calls=%fused_computation.12.clone.1 | loop fusion | flops 12582912 | bytes 50348032 | tf_op jit(solution)/shard_map/while/body/eval_jaxpr/add | solution.py:84
  653.4 24.5 %copy.43 = f32[64,64,1024]{2,1,0:T(8,128)} copy(f32[64,64,1024]{1,2,0:T(8,128)} %get-tuple-element.223) | data formatting | bytes 33554432 | tf_op jit(solution)/shard_map/while | solution.py:86
  692.5 272.7 %while.29 = (s32[]{:T(128)}, bf16[128,2048]{1,0:T(8,128)(2,1)S(1)}, bf16[128,2048]{1,0:T(8,128)(2,1)}, bf16[128,2048]{1,0:T(8,128)(2,1)S(1)}, f32[64,64]{1,0:T(8...) while((s32[]{:T(128)}, bf16[128,2048]{1,0:T(8,128)(2,1)S(1)}, ...), condition=%wide.region_5.0_spmd, body=%wide.region_4.0_spmd.sunk | while | flops 545267712 | bytes 126650592 | solution.py:134
  692.5 11.5 %broadcast_in_dim.37 = bf16[64,32,64,32]{3,2,1,0:T(8,128)(2,1)} broadcast(bf16[64,64]{1,0:T(8,128)(2,1)S(1)} %compare_convert_fusion.4), dimensions={0,2} | broadcast | bytes 8396800 | tf_op jit(solution)/shard_map/while/body/eval_jaxpr/broadcast_in_dim | solution.py:117
  703.9 43.7 %reshape.103 = bf16[2048,2048]{1,0:T(8,128)(2,1)} reshape(bf16[64,32,64,32]{3,2,1,0:T(8,128)(2,1)} %broadcast_in_dim.37) | data formatting | bytes 16777216 | tf_op jit(solution)/shard_map/while/body/eval_jaxpr/reshape | solution.py:119
  747.6 8.2 fusion.58
  760.7 11.4 %broadcast_in_dim.37 = bf16[64,32,64,32]{3,2,1,0:T(8,128)(2,1)} broadcast(bf16[64,64]{1,0:T(8,128)(2,1)S(1)} %compare_convert_fusion.4), dimensions={0,2} | broadcast | bytes 8396800 | tf_op jit(solution)/shard_map/while/body/eval_jaxpr/broadcast_in_dim | solution.py:117
  772.2 43.6 %reshape.103 = bf16[2048,2048]{1,0:T(8,128)(2,1)} reshape(bf16[64,32,64,32]{3,2,1,0:T(8,128)(2,1)} %broadcast_in_dim.37) | data formatting | bytes 16777216 | tf_op jit(solution)/shard_map/while/body/eval_jaxpr/reshape | solution.py:119
  815.8 8.2 fusion.58
  828.9 11.4 %broadcast_in_dim.37 = bf16[64,32,64,32]{3,2,1,0:T(8,128)(2,1)} broadcast(bf16[64,64]{1,0:T(8,128)(2,1)S(1)} %compare_convert_fusion.4), dimensions={0,2} | broadcast | bytes 8396800 | tf_op jit(solution)/shard_map/while/body/eval_jaxpr/broadcast_in_dim | solution.py:117
  840.4 43.6 %reshape.103 = bf16[2048,2048]{1,0:T(8,128)(2,1)} reshape(bf16[64,32,64,32]{3,2,1,0:T(8,128)(2,1)} %broadcast_in_dim.37) | data formatting | bytes 16777216 | tf_op jit(solution)/shard_map/while/body/eval_jaxpr/reshape | solution.py:119
  897.1 11.4 %broadcast_in_dim.37 = bf16[64,32,64,32]{3,2,1,0:T(8,128)(2,1)} broadcast(bf16[64,64]{1,0:T(8,128)(2,1)S(1)} %compare_convert_fusion.4), dimensions={0,2} | broadcast | bytes 8396800 | tf_op jit(solution)/shard_map/while/body/eval_jaxpr/broadcast_in_dim | solution.py:117
  908.5 43.6 %reshape.103 = bf16[2048,2048]{1,0:T(8,128)(2,1)} reshape(bf16[64,32,64,32]{3,2,1,0:T(8,128)(2,1)} %broadcast_in_dim.37) | data formatting | bytes 16777216 | tf_op jit(solution)/shard_map/while/body/eval_jaxpr/reshape | solution.py:119
  966.1 25.1 %all_to_all.38 = bf16[4,32,2048]{2,1,0:T(8,128)(2,1)S(1)} all-to-all(bf16[4,32,2048]{2,1,0:T(8,128)(2,1)} %bitcast.52), channel_id=1, replica_groups=mesh['parts'=2,'row'=4,'col'=4] {'col'}, dimensions={0} | all-to-all | bytes 1048576 | tf_op jit(solution)/shard_map/all_to_all | solution.py:141
  1000.7 14.5 %reduce-scatter.5.cloned.1.call-done = bf16[32,2048]{1,0:T(8,128)(2,1)} async-done(((bf16[32,8192]{1,0:T(8,128)(2,1)}), bf16[32,2048]{1,0:T(8,128)(2,1)}) %reduce-scatter.5.cloned.1.call-update) | async-done | bytes 131088 | tf_op jit(solution)/shard_map/reduce_scatter | solution.py:144
  (90 shorter events, 113.3 us)
Async XLA Ops:
  8.0 22.9 %copy-start = (bf16[64,64,128]{2,1,0:T(8,128)(2,1)S(1)}, bf16[64,64,128]{2,1,0:T(8,128)(2,1)}, u32[]{:S(2)}) copy-start(bf16[64,64,128]{2,1,0:T(8,128)(2,1)} %param.23) | copy-start | bytes 3145732
  8.0 21.7 %copy-start.8 = (s32[256]{0:T(256)S(1)}, s32[256]{0:T(256)}, u32[]{:S(2)}) copy-start(s32[256]{0:T(256)} %param.21) | copy-start | bytes 3076
  8.0 21.8 %copy-start.11 = (s32[8,8]{1,0:T(8,128)S(1)}, s32[8,8]{1,0:T(8,128)}, u32[]{:S(2)}) copy-start(s32[8,8]{1,0:T(8,128)} %param.22) | copy-start | bytes 772
  8.0 22.9 %copy-start.9 = (bf16[1024,128]{1,0:T(8,128)(2,1)S(1)}, bf16[1024,128]{1,0:T(8,128)(2,1)}, u32[]{:S(2)}) copy-start(bf16[1024,128]{1,0:T(8,128)(2,1)} %param.19) | copy-start | bytes 786436
  24.8 117.6 %all-to-all-start = ((bf16[32,4,2048]{2,0,1:T(8,128)(2,1)}), bf16[32,4,2048]{2,0,1:T(8,128)(2,1)S(1)}, u32[]{:S(2)}, u32[]{:S(2)}) async-start(bf16[32,4,2048]{2,0,1:T(8,128)(2,1)} %bitcast.40), calls=%async_computation | async-start | bytes 1048576 | tf_op jit(solution)/shard_map/all_to_all | solution.py:52
  29.7 969.1 %all-reduce.2.cloned.1.call-start = ((), (), s32[]{:S(2)}) async-start(), calls=%async_computation.6 | async-start | bytes 1048576 | tf_op jit(solution)/shard_map/psum | solution.py:147
  30.3 0.6 copy-start.4
  30.9 4.6 copy-start.7
  82.5 59.9 %copy-start.5 = (f32[64,64]{1,0:T(8,128)S(1)}, f32[64,64]{1,0:T(8,128)}, u32[]{:S(2)}) copy-start(f32[64,64]{1,0:T(8,128)} %copy-done.4) | copy-start | bytes 49156
  684.9 3.2 copy-start.3
  691.3 309.4 %reduce-scatter.3.cloned.1.call-start = ((), (), s32[]{:S(2)}) async-start(), calls=%async_computation.4 | async-start | bytes 655360 | tf_op jit(solution)/shard_map/reduce_scatter | solution.py:138
  692.5 299.6 %copy-start.10 = (bf16[1024,128]{1,0:T(8,128)(2,1)S(1)}, bf16[1024,128]{1,0:T(8,128)(2,1)}, u32[]{:S(2)}) copy-start(bf16[1024,128]{1,0:T(8,128)(2,1)} %param.19) | copy-start | bytes 786436
  692.5 299.6 %copy-start.12 = (f32[128]{0:T(128)S(1)}, f32[128]{0:T(128)}, u32[]{:S(2)}) copy-start(f32[128]{0:T(128)} %param.20) | copy-start | bytes 1540
  747.6 8.2 copy-start.1
  747.6 10.6 %copy-start.2 = (bf16[2048,2048]{1,0:T(8,128)(2,1)S(1)}, bf16[2048,2048]{1,0:T(8,128)(2,1)}, u32[]{:S(2)}) copy-start(bf16[2048,2048]{1,0:T(8,128)(2,1)} %get-tuple-element.398) | copy-start | bytes 25165828 | tf_op jit(solution)/shard_map/while
  815.8 8.2 copy-start.1
  815.8 10.6 %copy-start.2 = (bf16[2048,2048]{1,0:T(8,128)(2,1)S(1)}, bf16[2048,2048]{1,0:T(8,128)(2,1)}, u32[]{:S(2)}) copy-start(bf16[2048,2048]{1,0:T(8,128)(2,1)} %get-tuple-element.398) | copy-start | bytes 25165828 | tf_op jit(solution)/shard_map/while
  883.9 8.2 copy-start.1
  883.9 10.6 %copy-start.2 = (bf16[2048,2048]{1,0:T(8,128)(2,1)S(1)}, bf16[2048,2048]{1,0:T(8,128)(2,1)}, u32[]{:S(2)}) copy-start(bf16[2048,2048]{1,0:T(8,128)(2,1)} %get-tuple-element.398) | copy-start | bytes 25165828 | tf_op jit(solution)/shard_map/while
  952.1 8.2 copy-start.1
  952.1 10.6 %copy-start.2 = (bf16[2048,2048]{1,0:T(8,128)(2,1)S(1)}, bf16[2048,2048]{1,0:T(8,128)(2,1)}, u32[]{:S(2)}) copy-start(bf16[2048,2048]{1,0:T(8,128)(2,1)} %get-tuple-element.398) | copy-start | bytes 25165828 | tf_op jit(solution)/shard_map/while
  965.2 0.8 copy-start.6
  966.1 49.1 %reduce-scatter.5.cloned.1.call-start = ((), (), s32[]{:S(2)}) async-start(), calls=%async_computation.5 | async-start | bytes 655360 | tf_op jit(solution)/shard_map/reduce_scatter | solution.py:144
Sparse Core Ops, SparseCore 0:
  691.4 92.0 all-reduce.1
Sparse Core Ops, SparseCore 1:
  966.1 24.5 reduce-scatter.2
  993.6 21.6 reduce-scatter.4
where the time goes:
time: 1040 us; the launch traced here: 1020 us
  local copies, waits for them, and re-layouts  708 us (68%)
  other arithmetic  137 us (13%)
  matrix products  91.5 us (9%)
  blocking collectives  50 us (5%)
  between operations  15.7 us (2%)
  waiting for transfers between devices  14.6 us (1%)
    transpose x4, local copies, waits for them, and re-layouts, forward_level(): prod = prod.reshape(incoming_matrix, PROJECTED_SIZE, cols, PROJECTED_SIZE...  193 us
    reshape x4, local copies, waits for them, and re-layouts, backward_level(): keep_wide = jnp.broadcast_to(keep[:, None, :, None], (incoming_matrix, PR...  174 us
    reshape x4, local copies, waits for them, and re-layouts, forward_level(): prod.reshape(incoming_matrix, PROJECTED_SIZE, cols, PROJECTED_SIZE)  162 us
    add x4, other arithmetic, forward_level(): return acc + keep[:, :, None] * prod  123 us
    broadcast_in_dim x4, local copies, waits for them, and re-layouts, backward_level(): jnp.broadcast_to(keep[:, None, :, None], (incoming_matrix, PROJECTED_SIZE...  45.8 us
    reshape x1, local copies, waits for them, and re-layouts, shards(): turned = scaled.reshape(incoming_matrix, cols, PROJECTED_SIZE, PROJECTED_...  43.6 us
    dot_general x4, matrix products, backward_level(): jnp.dot(left_level, masked, preferred_element_type=jnp.float32)  32.6 us
    dot_general x4, matrix products, forward_level(): lax.dot_general(left_level, right_level, (((0,), (0,)), ((), ())), prefer...  32.4 us
  transfers between devices with their start and end apart: 4, of which 1 were waited for; matrix products, arithmetic and copies ran while one was open for 36% of the time, Pallas kernels for 0%

commit v1 on v0

v1 whole, which is shorter than its diff:
```python
import functools

import jax
import jax.numpy as jnp
from jax import lax
from jax.experimental import pallas as pl
from jax.experimental.pallas import tpu as pltpu
from jax.sharding import PartitionSpec as P

PROJ = 32
CHAINS = 8
LANES = 128
PER_TILE = LANES // PROJ
WIDE = 256
F32 = jnp.float32
BF16 = jnp.bfloat16


def standardize_entries(alignment_tensor, standard_multiplier, additive_offset):
    incoming_entries = alignment_tensor.astype(F32)
    center = incoming_entries - jnp.mean(incoming_entries, axis=-1, keepdims=True)
    spread = jnp.mean(center * center, axis=-1, keepdims=True)
    return (center * lax.rsqrt(spread + 1e-05) * standard_multiplier + additive_offset).astype(BF16)


def swap_blocks(parts):
    return [
        jnp.concatenate([part[:, q * PROJ : (q + 1) * PROJ] for part in parts], axis=1)
        for q in range(PER_TILE)
    ]


def nt_dot(a, b):
    return lax.dot_general(a, b, (((1,), (1,)), ((), ())), preferred_element_type=F32)


def nn_dot(a, b):
    return lax.dot_general(a, b, (((1,), (0,)), ((), ())), preferred_element_type=F32)


def back_body(grad_ref, wt_ref, out_ref):
    rows, cols, width = grad_ref.shape
    for half in range(rows // PER_TILE):
        block = grad_ref[half * PER_TILE : (half + 1) * PER_TILE].reshape(PER_TILE * cols, width)
        for t in range(PROJ // PER_TILE):
            prod = nn_dot(block, wt_ref[:, t * LANES : (t + 1) * LANES]).astype(BF16)
            turned = swap_blocks([prod[p * cols : (p + 1) * cols] for p in range(PER_TILE)])
            for q in range(PER_TILE):
                e = t * PER_TILE + q
                out_ref[e * cols : (e + 1) * cols, half * LANES : (half + 1) * LANES] = turned[q]


def back_call(grad, wt):
    rows, cols, width = grad.shape
    step = WIDE // PROJ
    return pl.pallas_call(
        back_body,
        grid=(rows // step,),
        in_specs=[
            pl.BlockSpec((step, cols, width), lambda g: (g, 0, 0)),
            pl.BlockSpec((width, PROJ * PROJ), lambda g: (0, 0)),
        ],
        out_specs=pl.BlockSpec((PROJ * cols, WIDE), lambda g: (0, g)),
        out_shape=jax.ShapeDtypeStruct((PROJ * cols, rows * PROJ), BF16),
        compiler_params=pltpu.CompilerParams(dimension_semantics=("arbitrary",)),
        name="back",
    )(grad, wt)


def masked_left(left_ref, lab_ref, lb_ref, pair):
    seqs = left_ref.shape[0]
    left = left_ref[...].astype(F32)
    for side in range(2):
        keep = (lab_ref[...] == 2 * pair + side).astype(F32)
        lb_ref[side * seqs : (side + 1) * seqs] = (left * keep).astype(BF16)


def grads_body(lo_ref, hi_ref, back_ref, left_ref, lab_ref, right_ref, wide_ref, tall_ref,
               left_out, right_out, rm_ref, q_ref, lb_ref, flip_ref, turn_ref):
    g = pl.program_id(0)
    seqs = left_ref.shape[0]
    span = back_ref.shape[0]
    cols = span // PROJ
    chunk = min(512, span)

    @pl.when(g == 0)
    def _():
        for a in range(CHAINS):
            weight = tall_ref[a * seqs : (a + 1) * seqs]
            row = (a % 2) * seqs
            for t in range(span // LANES):
                lanes = slice(t * LANES, (t + 1) * LANES)
                rm_ref[a // 2, row : row + seqs, lanes] = (
                    right_ref[:, lanes].astype(F32) * weight
                ).astype(BF16)
        q_ref[...] = jnp.zeros_like(q_ref)

    left_out[...] = jnp.zeros_like(left_out)

    def one_pair(pair, carry):
        masked_left(left_ref, lab_ref, lb_ref, pair)
        part = nn_dot(rm_ref[pair], back_ref[...])
        keep0 = lab_ref[...] == 2 * pair
        keep1 = lab_ref[...] == 2 * pair + 1
        left_out[...] += jnp.where(keep0, part[:seqs], 0.0) + jnp.where(keep1, part[seqs:], 0.0)

        def rows_of(m, c):
            rows = pl.ds(pl.multiple_of(m * chunk, chunk), chunk)
            q_ref[pair, rows] += nt_dot(back_ref[rows], lb_ref[...])
            return c

        lax.fori_loop(0, span // chunk, rows_of, 0)
        return carry

    lax.fori_loop(lo_ref[g], hi_ref[g] + 1, one_pair, 0)

    @pl.when(g == pl.num_programs(0) - 1)
    def _():
        for e in range(PROJ):
            rows = slice(e * cols, (e + 1) * cols)
            total = jnp.zeros((cols, seqs), F32)
            for a in range(CHAINS):
                lanes = slice((a % 2) * seqs, (a % 2 + 1) * seqs)
                total += q_ref[a // 2, rows, lanes] * wide_ref[:, a * seqs : (a + 1) * seqs]
            flip_ref[rows] = total
        for j in range(cols):
            turn_ref[j * PROJ : (j + 1) * PROJ] = flip_ref[pl.ds(j, PROJ, stride=cols)]
        for t in range(span // LANES):
            rows = slice(t * LANES, (t + 1) * LANES)
            right_out[:, rows] = turn_ref[rows].T.astype(BF16)


def grads_call(lo, hi, back, left, lab, right, wide, tall):
    span, total = back.shape
    seqs = left.shape[0]
    whole = lambda shape: pl.BlockSpec(shape, lambda g, lo, hi: (0, 0))
    return pl.pallas_call(
        grads_body,
        grid_spec=pltpu.PrefetchScalarGridSpec(
            num_scalar_prefetch=2,
            grid=(total // WIDE,),
            in_specs=[
                pl.BlockSpec((span, WIDE), lambda g, lo, hi: (0, g)),
                pl.BlockSpec((seqs, WIDE), lambda g, lo, hi: (0, g)),
                pl.BlockSpec((1, WIDE), lambda g, lo, hi: (0, g)),
                whole(right.shape),
                whole(wide.shape),
                whole(tall.shape),
            ],
            out_specs=[
                pl.BlockSpec((seqs, WIDE), lambda g, lo, hi: (0, g)),
                whole((seqs, span)),
            ],
            scratch_shapes=[
                pltpu.VMEM((CHAINS // 2, 2 * seqs, span), BF16),
                pltpu.VMEM((CHAINS // 2, span, 2 * seqs), F32),
                pltpu.VMEM((2 * seqs, WIDE), BF16),
                pltpu.VMEM((span, seqs), F32),
                pltpu.VMEM((span, seqs), F32),
            ],
        ),
        out_shape=[
            jax.ShapeDtypeStruct((seqs, total), F32),
            jax.ShapeDtypeStruct((seqs, span), BF16),
        ],
        compiler_params=pltpu.CompilerParams(dimension_semantics=("arbitrary",)),
        name="grads",
    )(lo, hi, back, left, lab, right, wide, tall)


def forward_body(lo_ref, hi_ref, left_ref, lab_ref, right_ref, wide_ref, w_ref, bias_ref, grad_ref,
                 pair_out, weight_out, rm_ref, lb_ref, acc_ref, x_ref, sum_ref, turn_ref):
    g = pl.program_id(0)
    seqs = left_ref.shape[0]
    span = right_ref.shape[0]
    cols = span // PROJ
    chunk = min(512, span)
    rows_here, _, width = grad_ref.shape

    @pl.when(g == 0)
    def _():
        for a in range(CHAINS):
            weight = wide_ref[:, a * seqs : (a + 1) * seqs]
            lanes = slice((a % 2) * seqs, (a % 2 + 1) * seqs)
            for e in range(PROJ):
                rows = slice(e * cols, (e + 1) * cols)
                rm_ref[a // 2, rows, lanes] = (right_ref[rows].astype(F32) * weight).astype(BF16)
        sum_ref[...] = jnp.zeros_like(sum_ref)

    def product(pair, add):
        masked_left(left_ref, lab_ref, lb_ref, pair)

        def rows_of(m, c):
            rows = pl.ds(pl.multiple_of(m * chunk, chunk), chunk)
            part = nn_dot(rm_ref[pair, rows], lb_ref[...])
            acc_ref[rows] = acc_ref[rows] + part if add else part
            return c

        lax.fori_loop(0, span // chunk, rows_of, 0)

    product(lo_ref[g], False)

    def more(pair, carry):
        product(pair, True)
        return carry

    lax.fori_loop(lo_ref[g] + 1, hi_ref[g] + 1, more, 0)

    for half in range(WIDE // LANES):
        lanes = slice(half * LANES, (half + 1) * LANES)
        for t in range(PROJ // PER_TILE):
            parts = []
            for q in range(PER_TILE):
                e = t * PER_TILE + q
                parts.append(acc_ref[e * cols : (e + 1) * cols, lanes].astype(BF16))
            turned = swap_blocks(parts)
            for p in range(PER_TILE):
                i = half * PER_TILE + p
                x_ref[i * cols : (i + 1) * cols, t * LANES : (t + 1) * LANES] = turned[p]

    pair = nn_dot(x_ref[...], w_ref[...]) + bias_ref[...]
    pair_out[...] = pair.astype(BF16).reshape(rows_here, cols, width)
    flat = grad_ref[...].reshape(rows_here * cols, width)
    sum_ref[...] += nn_dot(flat.T, x_ref[...])

    @pl.when(g == pl.num_programs(0) - 1)
    def _():
        for t in range(PROJ * PROJ // LANES):
            part = slice(t * LANES, (t + 1) * LANES)
            turn_ref[part] = sum_ref[:, part].T
        for c in range(PROJ):
            weight_out[c * PROJ : (c + 1) * PROJ] = turn_ref[pl.ds(c, PROJ, stride=PROJ)]


def forward_call(lo, hi, left, lab, right, wide, w, bias, grad):
    rows, cols, width = grad.shape
    seqs, total = left.shape
    span = right.shape[0]
    step = WIDE // PROJ
    whole = lambda shape: pl.BlockSpec(shape, lambda g, lo, hi: (0, 0))
    return pl.pallas_call(
        forward_body,
        grid_spec=pltpu.PrefetchScalarGridSpec(
            num_scalar_prefetch=2,
            grid=(total // WIDE,),
            in_specs=[
                pl.BlockSpec((seqs, WIDE), lambda g, lo, hi: (0, g)),
                pl.BlockSpec((1, WIDE), lambda g, lo, hi: (0, g)),
                whole(right.shape),
                whole(wide.shape),
                whole(w.shape),
                whole(bias.shape),
                pl.BlockSpec((step, cols, width), lambda g, lo, hi: (g, 0, 0)),
            ],
            out_specs=[
                pl.BlockSpec((step, cols, width), lambda g, lo, hi: (g, 0, 0)),
                whole((PROJ * PROJ, width)),
            ],
            scratch_shapes=[
                pltpu.VMEM((CHAINS // 2, span, 2 * seqs), BF16),
                pltpu.VMEM((2 * seqs, WIDE), BF16),
                pltpu.VMEM((span, WIDE), F32),
                pltpu.VMEM((step * cols, PROJ * PROJ), BF16),
                pltpu.VMEM((width, PROJ * PROJ), F32),
                pltpu.VMEM((PROJ * PROJ, width), F32),
            ],
        ),
        out_shape=[
            jax.ShapeDtypeStruct((rows, cols, width), BF16),
            jax.ShapeDtypeStruct((PROJ * PROJ, width), F32),
        ],
        compiler_params=pltpu.CompilerParams(dimension_semantics=("arbitrary",)),
        name="forward",
    )(lo, hi, left, lab, right, wide, w, bias, grad)


def shards(n_row, n_col, alignment_tensor, gain, shift, first_projector, second_projector,
           final_projector, final_offset, labels, counts, grad):
    here, rows, feats = alignment_tensor.shape
    cols, width = grad.shape[1:]
    seqs = here * n_col
    my_row, my_col = lax.axis_index("row"), lax.axis_index("col")
    normed = standardize_entries(alignment_tensor, gain, shift).reshape(-1, feats)
    left = jnp.dot(normed, first_projector, preferred_element_type=F32).astype(BF16)
    right = jnp.dot(normed, second_projector, preferred_element_type=F32).astype(BF16)
    left = left.reshape(here, rows * PROJ)
    right = right.reshape(here, rows * PROJ)

    left = lax.all_gather(left, "col", axis=0, tiled=True)
    right = lax.all_gather(right, "row", axis=1, tiled=True)
    right = lax.all_to_all(right, "col", split_axis=1, concat_axis=0, tiled=True)

    w = final_projector.reshape(PROJ, PROJ, width).transpose(1, 0, 2).reshape(PROJ * PROJ, width)
    back = back_call(grad, w.T)

    row_labels = lax.dynamic_slice_in_dim(labels, my_row * rows, rows, 0)
    col_labels = lax.dynamic_slice_in_dim(labels, my_col * cols, cols, 0)
    lab = jnp.repeat(row_labels, PROJ)[None, :]
    step = WIDE // PROJ
    lo = row_labels[::step] // 2
    hi = row_labels[step - 1 :: step] // 2
    chains = jnp.arange(CHAINS, dtype=jnp.int32)
    col_hot = col_labels[:, None, None] == chains[None, None, :]
    depth = jnp.sum(jnp.where(col_hot, counts[None, :, :], 0), axis=-1)
    seq = jnp.arange(seqs, dtype=jnp.int32)
    wide = jnp.where(seq[None, None, :] < depth[:, :, None], 1.0 / depth.astype(F32)[:, :, None], 0.0)
    tall = jnp.tile(wide.transpose(1, 2, 0).reshape(CHAINS * seqs, cols), (1, LANES // cols))
    wide = wide.reshape(cols, CHAINS * seqs)

    turned = right.reshape(seqs, cols, PROJ).transpose(0, 2, 1).reshape(seqs, PROJ * cols)
    left_grad, right_grad = grads_call(lo, hi, back, left, lab, turned, wide, tall)
    pair_update, weight = forward_call(
        lo, hi, left, lab, turned.T, wide, w, final_offset[None, :], grad
    )

    adjoint_first = lax.psum_scatter(left_grad.astype(BF16), "col", scatter_dimension=0, tiled=True)
    parts = lax.all_to_all(right_grad, "col", split_axis=0, concat_axis=1, tiled=True)
    grad_right = lax.psum_scatter(parts, "row", scatter_dimension=1, tiled=True)
    grad_w_out = lax.psum(weight, ("row", "col")) / (n_row * rows)
    return pair_update, adjoint_first, grad_right, grad_w_out


def solution(mesh):
    in_specs = (
        P(("parts", "col"), "row", None),
        P(),
        P(),
        P(),
        P(),
        P(),
        P(),
        P("parts"),
        P("parts", None),
        P(("parts", "row"), "col", None),
    )
    out_specs = (
        P(("parts", "row"), "col", None),
        P(("parts", "col"), "row"),
        P(("parts", "col"), "row"),
        P("parts", None),
    )
    body = functools.partial(shards, mesh.shape["row"], mesh.shape["col"])
    return jax.shard_map(body, mesh=mesh, in_specs=in_specs, out_specs=out_specs, check_vma=False)
```

time: 1040 us -> 188 us (0.18); the launches traced: 1020 us -> 186 us
  local copies, waits for them, and re-layouts: 708 us -> 13.9 us
  other arithmetic: 137 us -> 9.82 us
  matrix products: 91.5 us -> 0.8 us
  Pallas kernels: 0 us -> 50.5 us
  waiting for transfers between devices: 14.6 us -> 36.8 us
    reshape x11 -> x5, local copies, waits for them, and re-layouts: 382 us -> 4.56 us  [the longest x2 2.63 us: shards(): right.reshape(seqs, cols, PROJ).transpose(0, 2, 1)]
    transpose x5 -> x2, local copies, waits for them, and re-layouts: 223 us -> 4.14 us  [the longest x1 3.33 us: shards(): right.reshape(seqs, cols, PROJ).transpose(0, 2, 1)]
    add x4 -> x0, other arithmetic: 123 us -> none  [forward_level(): return acc + keep[:, :, None] * prod]
    dot_general x19 -> x2, matrix products: 91.5 us -> 0.8 us  [the longest x1 0.4 us: shards(): jnp.dot(normed, first_projector, preferred_element_type=F32).astype(BF16)]
    pallas_call x0 -> x3, Pallas kernels: none -> 50.5 us  [the longest x1 21.2 us: forward_call(): pl.pallas_call(forward_body, grid_spec=pltpu.PrefetchScalarGridSpec(num_s...]
    broadcast_in_dim x4 -> x3, local copies, waits for them, and re-layouts: 45.8 us -> 0.31 us  [the longest x2 0.24 us: shards(): jnp.where(seq[None, None, :] < depth[:, :, None], 1.0 / depth.astype(F32)...]
    psum x1, waiting for transfers between devices: 0.01 us -> 36.7 us  [shards(): grad_w_out = lax.psum(weight, ('row', 'col')) / (n_row * rows)]
    while x17 -> x0, local copies, waits for them, and re-layouts: 34.3 us -> none  [the longest x1 24.5 us: shards(): lax.fori_loop(0, count, forward_level, jnp.zeros((incoming_matrix, cols,...]
  transfers between devices with their start and end apart: 4 -> 4, of which waited for: 1 -> 1; matrix products, arithmetic and copies ran while one was open for 36% -> 7% of each run, Pallas kernels for 0% -> 16%
where the time goes in v1:
time: 188 us; the launch traced here: 186 us
  blocking collectives  53.4 us (28%)
  Pallas kernels  50.5 us (27%)
  waiting for transfers between devices  36.8 us (20%)
  between operations  15.8 us (8%)
  local copies, waits for them, and re-layouts  13.9 us (7%)
  other arithmetic  9.82 us (5%)
  starting transfers between devices  5.27 us (3%)
    psum x1, waiting for transfers between devices, shards(): grad_w_out = lax.psum(weight, ('row', 'col')) / (n_row * rows)  36.7 us
    all_to_all x1, blocking collectives, shards(): lax.all_to_all(right_grad, 'col', split_axis=0, concat_axis=1, tiled=True)  23 us
    all_gather x1, blocking collectives, shards(): left = lax.all_gather(left, 'col', axis=0, tiled=True)  21.7 us
    pallas_call x1, Pallas kernels, forward_call(): pl.pallas_call(forward_body, grid_spec=pltpu.PrefetchScalarGridSpec(num_s...  21.2 us
    pallas_call x1, Pallas kernels, grads_call(): pl.pallas_call(grads_body, grid_spec=pltpu.PrefetchScalarGridSpec(num_sca...  18.6 us
    pallas_call x1, Pallas kernels, back_call(): pl.pallas_call(back_body, grid=(rows // step,), in_specs=[pl.BlockSpec((s...  10.7 us
    all_gather x1, blocking collectives, shards(): right = lax.all_gather(right, 'row', axis=1, tiled=True)  8.65 us
    all_to_all x1, starting transfers between devices, shards(): lax.all_to_all(right, 'col', split_axis=1, concat_axis=0, tiled=True)  5 us
  transfers between devices with their start and end apart: 4, of which 1 were waited for; matrix products, arithmetic and copies ran while one was open for 7% of the time, Pallas kernels for 16%

profile of v1, /device:TPU:0, one launch (start us, length us, event | category | flops | bytes accessed | tf_op | source)
XLA Modules:
  0.0 186.2 jit_solution(9061105311194552951)
XLA Ops:
  8.0 1.7 convert_reduce_fusion
  9.7 1.9 %fusion.2 = f32[32,64]{1,0:T(8,128)S(1)} fusion(bf16[32,64,256]{2,1,0:T(8,128)(2,1)} %param.10, f32[32,64]{1,0:T(8,128)S(1)} %broadcast_multiply_fusion.1), kind=kLoop, calls=%fused_computation.6 | loop fusion | flops 2095104 | bytes 1064960 | tf_op jit(solution)/shard_map/reduce_sum | solution.py:22
  11.6 0.7 fusion.5
  12.4 0.4 convolution_convert_fusion
  12.8 0.3 copy.39
  13.1 0.5 reshape.108
  13.7 8.7 %all_gather.7 = bf16[32,8192]{1,0:T(8,128)(2,1)S(1)} all-gather(bf16[32,2048]{1,0:T(8,128)(2,1)S(1)} %reshape.108), channel_id=1, replica_groups=mesh['parts'=2,'row'=4,'col'=4] {'row'}, dimensions={1}, use_global_device_ids=true | all-gather | bytes 655360 | tf_op jit(solution)/shard_map/all_gather | solution.py:290
  22.3 0.8 copy.66
  23.1 5.0 %all-to-all-start = ((bf16[32,4,2048]{2,0,1:T(8,128)(2,1)}), bf16[32,4,2048]{2,0,1:T(8,128)(2,1)S(1)}, u32[]{:S(2)}, u32[]{:S(2)}) async-start(bf16[32,4,2048]{2,0,1:T(8,128)(2,1)} %bitcast.48), calls=%async_computation | async-start | bytes 1048576 | tf_op jit(solution)/shard_map/all_to_all | solution.py:291
  28.2 0.4 convolution_convert_fusion.1
  29.2 0.7 broadcast_in_dim_reshape.3.lab_ref
  29.9 0.3 copy.38
  30.2 0.5 reshape.107
  30.7 0.8 copy.44
  31.5 21.7 %all_gather.6.left_ref = bf16[128,2048]{1,0:T(8,128)(2,1)} all-gather(bf16[32,2048]{1,0:T(8,128)(2,1)S(1)} %reshape.107), channel_id=1, replica_groups=mesh['parts'=2,'row'=4,'col'=4] {'col'}, dimensions={0}, use_global_device_ids=true | all-gather | bytes 655360 | tf_op jit(solution)/shard_map/all_gather | solution.py:289
  53.2 0.5 and_select_fusion
  54.0 0.8 bitcast_select_fusion.1.wide_ref
  54.8 1.6 reshape.109
  56.4 3.3 %copy.41 = bf16[128,32,64]{0,2,1:T(8,128)(2,1)} copy(bf16[128,32,64]{1,2,0:T(8,128)(2,1)S(1)} %bitcast.51) | data formatting | bytes 1048576 | tf_op jit(solution)/shard_map/transpose | solution.py:310
  59.8 21.2 %forward.1 = (bf16[64,64,128]{2,1,0:T(8,128)(2,1)}, f32[1024,128]{1,0:T(8,128)}) custom-call(s32[8]{0:T(128)} %get-tuple-element.15.lo_ref, s32[8]{0:T(128)} %get-tuple-element.14.hi_ref, bf16[128,2048]{1,0:T(8,128)(2,1)} %all_gather.6.left_ref, s32[1,2048]{1,0:T(1,128)} %broadcast_in_dim_reshape.3.lab_ref, bf16[2048,128]{1,0:T(8,128)(2,1)} %bitcast.52, ...), custom_call_target="tpu_custom_call" | custom-call | tf_op jit(solution)/shard_map/forward/pallas_call | solution.py:241
  81.0 0.2 reduce-scatter.3.cloned.1.call-start
  81.3 0.9 copy.45
  82.4 0.1 lt.55
  82.7 1.0 copy.49.tall_ref
  83.7 10.7 %back.1.back_ref = bf16[2048,2048]{1,0:T(8,128)(2,1)} custom-call(bf16[64,64,128]{2,1,0:T(8,128)(2,1)} %grad_ref.3, bf16[128,1024]{1,0:T(8,128)(2,1)} %bitcast.61), custom_call_target="tpu_custom_call" | custom-call | tf_op jit(solution)/shard_map/back/pallas_call | solution.py:56
  94.4 1.0 copy.48.right_ref
  95.4 18.6 %grads.1 = (f32[128,2048]{1,0:T(8,128)}, bf16[128,2048]{1,0:T(8,128)(2,1)}) custom-call(s32[8]{0:T(128)} %get-tuple-element.15.lo_ref, s32[8]{0:T(128)} %get-tuple-element.14.hi_ref, bf16[2048,2048]{1,0:T(8,128)(2,1)} %back.1.back_ref, bf16[128,2048]{1,0:T(8,128)(2,1)} %all_gather.6.left_ref, s32[1,2048]{1,0:T(1,128)} %broadcast_in_dim_reshape.3.lab_ref, ...), custom_call_target="tpu_custom_call" | custom-call | tf_op jit(solution)/shard_map/grads/pallas_call | solution.py:137
  114.0 2.2 %convert_element_type.31 = bf16[128,2048]{1,0:T(8,128)(2,1)} convert(f32[128,2048]{1,0:T(8,128)} %get-tuple-element.9) | non-fusion elementwise | flops 262144 | bytes 1572864 | tf_op jit(solution)/shard_map/convert_element_type | solution.py:316
  116.3 23.0 %all_to_all.35 = bf16[4,32,2048]{2,1,0:T(8,128)(2,1)S(1)} all-to-all(bf16[4,32,2048]{2,1,0:T(8,128)(2,1)S(1)} %bitcast.66), channel_id=1, replica_groups=mesh['parts'=2,'row'=4,'col'=4] {'col'}, dimensions={0} | all-to-all | bytes 1048576 | tf_op jit(solution)/shard_map/all_to_all | solution.py:317
  139.3 0.8 copy.52
  140.2 36.7 %all-reduce.2.cloned.1.call-done = f32[1024,128]{1,0:T(8,128)} async-done(((f32[1024,128]{1,0:T(8,128)}), f32[1024,128]{1,0:T(8,128)}) %all-reduce.2.cloned.1.call-update) | async-done | bytes 524304 | tf_op jit(solution)/shard_map/psum | solution.py:319
  176.9 1.9 %broadcast_multiply_fusion = f32[1024,128]{1,0:T(8,128)} fusion(f32[1024,128]{1,0:T(8,128)} %all-reduce.2.cloned.1.call-done), kind=kLoop, calls=%fused_computation.15 | loop fusion | flops 131072 | bytes 1048576 | tf_op jit(solution)/shard_map/div | solution.py:319
  (50 shorter events, 1.5 us)
Async XLA Ops:
  8.0 4.4 %copy-start = (bf16[256,32]{0,1:T(8,128)(2,1)S(1)}, bf16[256,32]{0,1:T(8,128)(2,1)}, u32[]{:S(2)}) copy-start(bf16[256,32]{0,1:T(8,128)(2,1)} %param.14) | copy-start | bytes 49156
  8.0 3.6 %copy-start.1 = (bf16[32,64,256]{2,1,0:T(8,128)(2,1)S(1)}, bf16[32,64,256]{2,1,0:T(8,128)(2,1)}, u32[]{:S(2)}) copy-start(bf16[32,64,256]{2,1,0:T(8,128)(2,1)} %param.10) | copy-start | bytes 3145732
  8.0 3.6 %copy-start.9 = (f32[256]{0:T(256)S(1)}, f32[256]{0:T(256)}, u32[]{:S(2)}) copy-start(f32[256]{0:T(256)} %param.11) | copy-start | bytes 3076
  8.0 3.6 %copy-start.8 = (f32[256]{0:T(256)S(1)}, f32[256]{0:T(256)}, u32[]{:S(2)}) copy-start(f32[256]{0:T(256)} %param.12) | copy-start | bytes 3076
  12.8 15.4 %copy-start.10 = (s32[256]{0:T(256)S(1)}, s32[256]{0:T(256)}, u32[]{:S(2)}) copy-start(s32[256]{0:T(256)} %param.17) | copy-start | bytes 3076
  12.8 15.4 %copy-start.6 = (bf16[256,32]{0,1:T(8,128)(2,1)S(1)}, bf16[256,32]{0,1:T(8,128)(2,1)}, u32[]{:S(2)}) copy-start(bf16[256,32]{0,1:T(8,128)(2,1)} %param.13) | copy-start | bytes 49156
  13.6 15.0 %copy-start.7 = (s32[8,8]{1,0:T(8,128)S(1)}, s32[8,8]{1,0:T(8,128)}, u32[]{:S(2)}) copy-start(s32[8,8]{1,0:T(8,128)} %param.18) | copy-start | bytes 772
  23.1 7.6 %copy-start.5 = (bf16[1024,128]{1,0:T(8,128)(2,1)S(1)}, bf16[1024,128]{1,0:T(8,128)(2,1)}, u32[]{:S(2)}) copy-start(bf16[1024,128]{1,0:T(8,128)(2,1)} %param.15) | copy-start | bytes 786436
  23.1 31.7 %all-to-all-start = ((bf16[32,4,2048]{2,0,1:T(8,128)(2,1)}), bf16[32,4,2048]{2,0,1:T(8,128)(2,1)S(1)}, u32[]{:S(2)}, u32[]{:S(2)}) async-start(bf16[32,4,2048]{2,0,1:T(8,128)(2,1)} %bitcast.48), calls=%async_computation | async-start | bytes 1048576 | tf_op jit(solution)/shard_map/all_to_all | solution.py:291
  28.1 148.7 %all-reduce.2.cloned.1.call-start = ((), (), s32[]{:S(2)}) async-start(), calls=%async_computation.6 | async-start | bytes 1048576 | tf_op jit(solution)/shard_map/psum | solution.py:319
  59.8 21.5 %copy-start.3 = (bf16[32,32,128]{2,1,0:T(8,128)(2,1)S(1)}, bf16[32,32,128]{2,1,0:T(8,128)(2,1)}, u32[]{:S(2)}) copy-start(bf16[32,32,128]{2,1,0:T(8,128)(2,1)} %copy.44) | copy-start | bytes 786436
  81.0 97.7 %reduce-scatter.3.cloned.1.call-start = ((), (), s32[]{:S(2)}) async-start(), calls=%async_computation.4 | async-start | bytes 655360 | tf_op jit(solution)/shard_map/reduce_scatter | solution.py:316
  83.7 10.7 %copy-start.2 = (bf16[128,32,64]{0,2,1:T(8,128)(2,1)S(1)}, bf16[128,32,64]{0,2,1:T(8,128)(2,1)}, u32[]{:S(2)}) copy-start(bf16[128,32,64]{0,2,1:T(8,128)(2,1)} %copy.41) | copy-start | bytes 1572868
  114.0 2.3 %copy-start.4 = (bf16[128,2048]{1,0:T(8,128)(2,1)S(1)}, bf16[128,2048]{1,0:T(8,128)(2,1)}, u32[]{:S(2)}) copy-start(bf16[128,2048]{1,0:T(8,128)(2,1)} %get-tuple-element.10) | copy-start | bytes 1572868
  116.2 62.5 %reduce-scatter.5.cloned.1.call-start = ((), (), s32[]{:S(2)}) async-start(), calls=%async_computation.5 | async-start | bytes 655360 | tf_op jit(solution)/shard_map/reduce_scatter | solution.py:318
Sparse Core Ops, SparseCore 0:
  81.1 95.6 all-reduce.1
Sparse Core Ops, SparseCore 1:
  116.3 26.8 reduce-scatter.2
  146.1 21.7 reduce-scatter.4

commit v2 on v1

--- a/solution.py
+++ b/solution.py
@@ -36,6 +36,12 @@
 
 def nn_dot(a, b):
     return lax.dot_general(a, b, (((1,), (0,)), ((), ())), preferred_element_type=F32)
+
+
+def cost(passes, span, total, seqs):
+    return pl.CostEstimate(
+        flops=4 * passes * span * total * seqs, bytes_accessed=2 * span * total, transcendentals=0
+    )
 
 
 def back_body(grad_ref, wt_ref, out_ref):
@@ -63,6 +69,7 @@
         out_specs=pl.BlockSpec((PROJ * cols, WIDE), lambda g: (0, g)),
         out_shape=jax.ShapeDtypeStruct((PROJ * cols, rows * PROJ), BF16),
         compiler_params=pltpu.CompilerParams(dimension_semantics=("arbitrary",)),
+        cost_estimate=cost(10, PROJ * cols, rows * PROJ, width),
         name="back",
     )(grad, wt)
 
@@ -75,8 +82,8 @@
         lb_ref[side * seqs : (side + 1) * seqs] = (left * keep).astype(BF16)
 
 
-def grads_body(lo_ref, hi_ref, back_ref, left_ref, lab_ref, right_ref, wide_ref, tall_ref,
-               left_out, right_out, rm_ref, q_ref, lb_ref, flip_ref, turn_ref):
+def right_grad_body(lo_ref, hi_ref, back_ref, left_ref, lab_ref, wide_ref,
+                    right_out, q_ref, lb_ref, flip_ref, turn_ref):
     g = pl.program_id(0)
     seqs = left_ref.shape[0]
     span = back_ref.shape[0]
@@ -85,24 +92,10 @@
 
     @pl.when(g == 0)
     def _():
-        for a in range(CHAINS):
-            weight = tall_ref[a * seqs : (a + 1) * seqs]
-            row = (a % 2) * seqs
-            for t in range(span // LANES):
-                lanes = slice(t * LANES, (t + 1) * LANES)
-                rm_ref[a // 2, row : row + seqs, lanes] = (
-                    right_ref[:, lanes].astype(F32) * weight
-                ).astype(BF16)
         q_ref[...] = jnp.zeros_like(q_ref)
-
-    left_out[...] = jnp.zeros_like(left_out)
 
     def one_pair(pair, carry):
         masked_left(left_ref, lab_ref, lb_ref, pair)
-        part = nn_dot(rm_ref[pair], back_ref[...])
-        keep0 = lab_ref[...] == 2 * pair
-        keep1 = lab_ref[...] == 2 * pair + 1
-        left_out[...] += jnp.where(keep0, part[:seqs], 0.0) + jnp.where(keep1, part[seqs:], 0.0)
 
         def rows_of(m, c):
             rows = pl.ds(pl.multiple_of(m * chunk, chunk), chunk)
@@ -130,12 +123,12 @@
             right_out[:, rows] = turn_ref[rows].T.astype(BF16)
 
 
-def grads_call(lo, hi, back, left, lab, right, wide, tall):
+def right_grad_call(lo, hi, back, left, lab, wide):
     span, total = back.shape
     seqs = left.shape[0]
     whole = lambda shape: pl.BlockSpec(shape, lambda g, lo, hi: (0, 0))
     return pl.pallas_call(
-        grads_body,
+        right_grad_body,
         grid_spec=pltpu.PrefetchScalarGridSpec(
             num_scalar_prefetch=2,
             grid=(total // WIDE,),
@@ -143,29 +136,72 @@
                 pl.BlockSpec((span, WIDE), lambda g, lo, hi: (0, g)),
                 pl.BlockSpec((seqs, WIDE), lambda g, lo, hi: (0, g)),
                 pl.BlockSpec((1, WIDE), lambda g, lo, hi: (0, g)),
-                whole(right.shape),
                 whole(wide.shape),
-                whole(tall.shape),
-            ],
-            out_specs=[
-                pl.BlockSpec((seqs, WIDE), lambda g, lo, hi: (0, g)),
-                whole((seqs, span)),
-            ],
+            ],
+            out_specs=whole((seqs, span)),
             scratch_shapes=[
-                pltpu.VMEM((CHAINS // 2, 2 * seqs, span), BF16),
                 pltpu.VMEM((CHAINS // 2, span, 2 * seqs), F32),
                 pltpu.VMEM((2 * seqs, WIDE), BF16),
                 pltpu.VMEM((span, seqs), F32),
                 pltpu.VMEM((span, seqs), F32),
             ],
         ),
-        out_shape=[
-            jax.ShapeDtypeStruct((seqs, total), F32),
-            jax.ShapeDtypeStruct((seqs, span), BF16),
-        ],
+        out_shape=jax.ShapeDtypeStruct((seqs, span), BF16),
         compiler_params=pltpu.CompilerParams(dimension_semantics=("arbitrary",)),
-        name="grads",
-    )(lo, hi, back, left, lab, right, wide, tall)
+        cost_estimate=cost(10, span, total, seqs),
+        name="right_grad",
+    )(lo, hi, back, left, lab, wide)
+
+
+def left_grad_body(lo_ref, hi_ref, back_ref, lab_ref, right_ref, tall_ref, left_out, rm_ref):
+    g = pl.program_id(0)
+    seqs = right_ref.shape[0]
+    span = back_ref.shape[0]
+
+    @pl.when(g == 0)
+    def _():
+        for a in range(CHAINS):
+            weight = tall_ref[a * seqs : (a + 1) * seqs]
+            row = (a % 2) * seqs
+            for t in range(span // LANES):
+                lanes = slice(t * LANES, (t + 1) * LANES)
+                rm_ref[a // 2, row : row + seqs, lanes] = (
+                    right_ref[:, lanes].astype(F32) * weight
+                ).astype(BF16)
+
+    def one_pair(pair, total):
+        part = nn_dot(rm_ref[pair], back_ref[...])
+        keep0 = lab_ref[...] == 2 * pair
+        keep1 = lab_ref[...] == 2 * pair + 1
+        return total + jnp.where(keep0, part[:seqs], 0.0) + jnp.where(keep1, part[seqs:], 0.0)
+
+    total = lax.fori_loop(lo_ref[g], hi_ref[g] + 1, one_pair, jnp.zeros(left_out.shape, F32))
+    left_out[...] = total.astype(BF16)
+
+
+def left_grad_call(lo, hi, back, lab, right, tall):
+    span, total = back.shape
+    seqs = right.shape[0]
+    whole = lambda shape: pl.BlockSpec(shape, lambda g, lo, hi: (0, 0))
+    return pl.pallas_call(
+        left_grad_body,
+        grid_spec=pltpu.PrefetchScalarGridSpec(
+            num_scalar_prefetch=2,
+            grid=(total // WIDE,),
+            in_specs=[
+                pl.BlockSpec((span, WIDE), lambda g, lo, hi: (0, g)),
+                pl.BlockSpec((1, WIDE), lambda g, lo, hi: (0, g)),
+                whole(right.shape),
+                whole(tall.shape),
+            ],
+            out_specs=pl.BlockSpec((seqs, WIDE), lambda g, lo, hi: (0, g)),
+            scratch_shapes=[pltpu.VMEM((CHAINS // 2, 2 * seqs, span), BF16)],
+        ),
+        out_shape=jax.ShapeDtypeStruct((seqs, total), BF16),
+        compiler_params=pltpu.CompilerParams(dimension_semantics=("arbitrary",)),
+        cost_estimate=cost(10, span, total, seqs),
+        name="left_grad",
+    )(lo, hi, back, lab, right, tall)
 
 
 def forward_body(lo_ref, hi_ref, left_ref, lab_ref, right_ref, wide_ref, w_ref, bias_ref, grad_ref,
@@ -270,31 +306,118 @@
             jax.ShapeDtypeStruct((PROJ * PROJ, width), F32),
         ],
         compiler_params=pltpu.CompilerParams(dimension_semantics=("arbitrary",)),
+        cost_estimate=cost(20, span, total, seqs),
         name="forward",
     )(lo, hi, left, lab, right, wide, w, bias, grad)
 
 
+class Ring:
+    def __init__(self, n_row, n_col):
+        self.n_row, self.n_col = n_row, n_col
+        self.n_x = n_row // 2
+        self.per_row = n_col // n_row
+        self.row = lax.axis_index("row").astype(jnp.uint32)
+        self.col = lax.axis_index("col").astype(jnp.uint32)
+        self.x, self.core = self.row // 2, self.row % 2
+
+    def core_of(self, col):
+        return (col // self.per_row) % 2
+
+    def col_shift(self, value, k):
+        n = self.n_col
+        return lax.ppermute(value, "col", [((t + k) % n, t) for t in range(n)])
+
+    def row_shift(self, value, k):
+        n = self.n_row
+        return lax.ppermute(value, "row", [((t + k) % n, t) for t in range(n)])
+
+    def x_shift(self, value, k):
+        return self.row_shift(value, 2 * k)
+
+    def other_core(self, value):
+        return lax.ppermute(value, "row", [(t ^ 1, t) for t in range(self.n_row)])
+
+    def along_col(self, value, k, outward):
+        pairs = []
+        for r in range(self.n_row):
+            for t in range(self.n_col):
+                q = (t - k) % self.n_col
+                if self.core_of(q) == r % 2:
+                    far, near = r * self.n_col + t, r * self.n_col + q
+                    pairs.append((far, near) if outward else (near, far))
+        return lax.ppermute(value, ("row", "col"), pairs)
+
+    def right_to_cols(self, right):
+        here, lanes = right.shape
+        lanes //= self.per_row
+        by_x = jnp.stack([right] + [self.x_shift(right, k) for k in range(1, self.n_x)])
+        blocks = []
+        for k in range(self.n_col):
+            q = (self.col + (self.n_col - k)) % self.n_col
+            which = ((q // self.per_row) // 2 + self.n_x - self.x) % self.n_x
+            piece = lax.dynamic_slice(
+                by_x, (which, jnp.uint32(0), (q % self.per_row) * lanes), (1, here, lanes)
+            )
+            blocks.append(self.along_col(piece[0], k, True) if k else piece[0])
+        mine = jnp.concatenate(blocks, axis=0)
+        return jnp.where(self.core_of(self.col) == self.core, mine, self.other_core(mine))
+
+    def right_from_cols(self, grad):
+        lanes = grad.shape[1]
+        here = grad.shape[0] // self.n_col
+        both = (grad.astype(F32) + self.other_core(grad).astype(F32)).astype(BF16)
+        by_row = jnp.zeros((self.n_x, here, self.per_row * lanes), BF16)
+        for k in range(self.n_col):
+            block = both[k * here : (k + 1) * here]
+            q = (self.col + (self.n_col - k)) % self.n_col
+            fits = self.core_of(q) == self.core
+            got = self.along_col(block, k, False) if k else block
+            got = jnp.where(fits, got, 0)
+            which = ((q // self.per_row) // 2 + self.n_x - self.x) % self.n_x
+            at = (which, jnp.uint32(0), (q % self.per_row) * lanes)
+            old = lax.dynamic_slice(by_row, at, (1, here, lanes))
+            by_row = lax.dynamic_update_slice(by_row, old + got[None], at)
+        total = by_row[0].astype(F32)
+        for k in range(1, self.n_x):
+            total += self.x_shift(by_row[k], self.n_x - k).astype(F32)
+        return total.astype(BF16)
+
+    def weight_sum(self, weight):
+        n = self.n_row
+        size = weight.shape[0] // n
+        sent = weight.astype(BF16).reshape(n, size, -1)
+        pick = lambda k: lax.dynamic_index_in_dim(sent, (self.row + k) % n, 0, keepdims=False)
+        total = lax.dynamic_index_in_dim(weight.reshape(n, size, -1), self.row, 0, keepdims=False)
+        for k in range(1, n):
+            total += self.row_shift(pick(k), n - k).astype(F32)
+        mine = total.astype(BF16)
+        for k in range(1, self.n_col):
+            total += self.col_shift(mine, k).astype(F32)
+        mine = total.astype(BF16)
+        turns = jnp.stack([mine] + [self.row_shift(mine, k) for k in range(1, n)])
+        turns = jnp.concatenate([turns, turns])
+        return lax.dynamic_slice_in_dim(turns, (n - self.row) % n, n, 0).reshape(weight.shape)
+
+
 def shards(n_row, n_col, alignment_tensor, gain, shift, first_projector, second_projector,
            final_projector, final_offset, labels, counts, grad):
+    ring = Ring(n_row, n_col)
     here, rows, feats = alignment_tensor.shape
     cols, width = grad.shape[1:]
     seqs = here * n_col
-    my_row, my_col = lax.axis_index("row"), lax.axis_index("col")
     normed = standardize_entries(alignment_tensor, gain, shift).reshape(-1, feats)
     left = jnp.dot(normed, first_projector, preferred_element_type=F32).astype(BF16)
     right = jnp.dot(normed, second_projector, preferred_element_type=F32).astype(BF16)
     left = left.reshape(here, rows * PROJ)
-    right = right.reshape(here, rows * PROJ)
-
-    left = lax.all_gather(left, "col", axis=0, tiled=True)
-    right = lax.all_gather(right, "row", axis=1, tiled=True)
-    right = lax.all_to_all(right, "col", split_axis=1, concat_axis=0, tiled=True)
+    right = right.reshape(here, rows // cols, cols, PROJ).transpose(0, 1, 3, 2)
+    right = ring.right_to_cols(right.reshape(here, rows * PROJ))
+    left = jnp.concatenate([left] + [ring.col_shift(left, k) for k in range(1, n_col)])
 
     w = final_projector.reshape(PROJ, PROJ, width).transpose(1, 0, 2).reshape(PROJ * PROJ, width)
     back = back_call(grad, w.T)
 
-    row_labels = lax.dynamic_slice_in_dim(labels, my_row * rows, rows, 0)
-    col_labels = lax.dynamic_slice_in_dim(labels, my_col * cols, cols, 0)
+    row_labels = lax.dynamic_slice_in_dim(labels, ring.row * rows, rows, 0)
+    col_labels = lax.dynamic_slice_in_dim(labels, ring.col * cols, cols, 0)
     lab = jnp.repeat(row_labels, PROJ)[None, :]
     step = WIDE // PROJ
     lo = row_labels[::step] // 2
@@ -302,21 +425,24 @@
     chains = jnp.arange(CHAINS, dtype=jnp.int32)
     col_hot = col_labels[:, None, None] == chains[None, None, :]
     depth = jnp.sum(jnp.where(col_hot, counts[None, :, :], 0), axis=-1)
-    seq = jnp.arange(seqs, dtype=jnp.int32)
+    seq = (jnp.arange(seqs, dtype=jnp.uint32) + ring.col * here) % seqs
+    seq = seq.astype(jnp.int32)
     wide = jnp.where(seq[None, None, :] < depth[:, :, None], 1.0 / depth.astype(F32)[:, :, None], 0.0)
     tall = jnp.tile(wide.transpose(1, 2, 0).reshape(CHAINS * seqs, cols), (1, LANES // cols))
     wide = wide.reshape(cols, CHAINS * seqs)
 
-    turned = right.reshape(seqs, cols, PROJ).transpose(0, 2, 1).reshape(seqs, PROJ * cols)
-    left_grad, right_grad = grads_call(lo, hi, back, left, lab, turned, wide, tall)
+    right_grad = right_grad_call(lo, hi, back, left, lab, wide)
+    left_grad = left_grad_call(lo, hi, back, lab, right, tall)
     pair_update, weight = forward_call(
-        lo, hi, left, lab, turned.T, wide, w, final_offset[None, :], grad
+        lo, hi, left, lab, right.T, wide, w, final_offset[None, :], grad
     )
 
-    adjoint_first = lax.psum_scatter(left_grad.astype(BF16), "col", scatter_dimension=0, tiled=True)
-    parts = lax.all_to_all(right_grad, "col", split_axis=0, concat_axis=1, tiled=True)
-    grad_right = lax.psum_scatter(parts, "row", scatter_dimension=1, tiled=True)
-    grad_w_out = lax.psum(weight, ("row", "col")) / (n_row * rows)
+    grad_right = ring.right_from_cols(right_grad)
+    total = left_grad[:here].astype(F32)
+    for k in range(1, n_col):
+        total += ring.col_shift(left_grad[k * here : (k + 1) * here], n_col - k).astype(F32)
+    adjoint_first = total.astype(BF16)
+    grad_w_out = ring.weight_sum(weight).astype(F32) / (n_row * rows)
     return pair_update, adjoint_first, grad_right, grad_w_out
 
 

time: 188 us -> 134 us (0.71); the launches traced: 186 us -> 134 us
  blocking collectives: 53.4 us -> 0 us
  starting transfers between devices: 5.27 us -> 33.5 us
  waiting for transfers between devices: 36.8 us -> 18.3 us
  between operations: 15.8 us -> 1.27 us
  Pallas kernels: 50.5 us -> 60.7 us
  local copies, waits for them, and re-layouts: 13.9 us -> 8.78 us
    psum x1 -> x0, waiting for transfers between devices: 36.7 us -> none  [shards(): grad_w_out = lax.psum(weight, ('row', 'col')) / (n_row * rows)]
    ppermute x0 -> x25, starting transfers between devices: none -> 33.5 us  [the longest x9 13.5 us: col_shift(): return lax.ppermute(value, 'col', [((t + k) % n, t) for t in range(n)])]
    all_gather x2 -> x0, blocking collectives: 30.3 us -> none  [the longest x1 21.7 us: shards(): left = lax.all_gather(left, 'col', axis=0, tiled=True)]
    all_to_all x1 -> x0, blocking collectives: 23 us -> none  [shards(): lax.all_to_all(right_grad, 'col', split_axis=0, concat_axis=1, tiled=True)]
    ppermute x0 -> x25, waiting for transfers between devices: none -> 18.3 us  [the longest x9 8.92 us: col_shift(): return lax.ppermute(value, 'col', [((t + k) % n, t) for t in range(n)])]
    pallas_call x1 -> x2, Pallas kernels: 18.6 us -> 27.1 us  [the longest x1 16 us: right_grad_call(): pl.pallas_call(right_grad_body, grid_spec=pltpu.PrefetchScalarGridSpec(nu...]
    all_to_all x1 -> x0, starting transfers between devices: 5 us -> none  [shards(): lax.all_to_all(right, 'col', split_axis=1, concat_axis=0, tiled=True)]
    reshape x3 -> x2, local copies, waits for them, and re-layouts: 3.17 us -> 0.53 us  [the longest x1 0.27 us: shards(): right = ring.right_to_cols(right.reshape(here, rows * PROJ))]
  transfers between devices with their start and end apart: 4 -> 25, of which waited for: 1 -> 9; matrix products, arithmetic and copies ran while one was open for 7% -> 10% of each run, Pallas kernels for 16% -> 45%
where the time goes in v2:
time: 134 us
  Pallas kernels  60.7 us (45%)
  starting transfers between devices  33.5 us (25%)
  waiting for transfers between devices  18.3 us (14%)
  other arithmetic  10.8 us (8%)
  local copies, waits for them, and re-layouts  8.78 us (7%)
    pallas_call x1, Pallas kernels, forward_call(): pl.pallas_call(forward_body, grid_spec=pltpu.PrefetchScalarGridSpec(num_s...  23 us
    pallas_call x1, Pallas kernels, right_grad_call(): pl.pallas_call(right_grad_body, grid_spec=pltpu.PrefetchScalarGridSpec(nu...  16 us
    ppermute x9, starting transfers between devices, col_shift(): return lax.ppermute(value, 'col', [((t + k) % n, t) for t in range(n)])  13.5 us
    ppermute x6, starting transfers between devices, along_col(): return lax.ppermute(value, ('row', 'col'), pairs)  13.4 us
    pallas_call x1, Pallas kernels, left_grad_call(): pl.pallas_call(left_grad_body, grid_spec=pltpu.PrefetchScalarGridSpec(num...  11 us
    pallas_call x1, Pallas kernels, back_call(): pl.pallas_call(back_body, grid=(rows // step,), in_specs=[pl.BlockSpec((s...  10.6 us
    ppermute x9, waiting for transfers between devices, col_shift(): return lax.ppermute(value, 'col', [((t + k) % n, t) for t in range(n)])  8.92 us
    ppermute x8, starting transfers between devices, row_shift(): return lax.ppermute(value, 'row', [((t + k) % n, t) for t in range(n)])  6.55 us
  transfers between devices with their start and end apart: 25, of which 9 were waited for; matrix products, arithmetic and copies ran while one was open for 10% of the time, Pallas kernels for 45%

profile of v2, /device:TPU:0, one launch (start us, length us, event | category | flops | bytes accessed | tf_op | source)
XLA Modules:
  0.0 134.1 jit_solution(14761196573784748410)
XLA Ops:
  0.7 1.7 %convert_reduce_fusion = f32[32,64]{1,0:T(8,128)S(1)} fusion(bf16[32,64,256]{2,1,0:T(8,128)(2,1)} %param.10), kind=kLoop, calls=%fused_computation.1 | loop fusion | flops 1046528 | bytes 1056768 | tf_op jit(solution)/shard_map/reduce_sum | solution.py:21
  2.3 1.9 %fusion.2 = f32[32,64]{1,0:T(8,128)S(1)} fusion(bf16[32,64,256]{2,1,0:T(8,128)(2,1)} %param.10, f32[32,64]{1,0:T(8,128)S(1)} %broadcast_multiply_fusion), kind=kLoop, calls=%fused_computation.6 | loop fusion | flops 2095104 | bytes 1064960 | tf_op jit(solution)/shard_map/reduce_sum | solution.py:22
  6.3 5.1 %collective-permute-start = (bf16[32,2048]{1,0:T(8,128)(2,1)S(1)}, bf16[32,2048]{1,0:T(8,128)(2,1)S(1)}, u32[]{:S(2)}, u32[]{:S(2)}) collective-permute-start(bf16[32,2048]{1,0:T(8,128)(2,1)S(1)} %reshape.115), channel_id=1, source_target_pairs={{1,0},{2,1},{3,2},{0,3},{5,4},{6,5},{7,6},{4,7},{9,8},{10,9},{11,1... | collective-permute-start | bytes 393224 | tf_op jit(solution)/shard_map/ppermute | solution.py:328
  11.4 1.0 collective-permute-start.2
  13.5 1.6 %collective-permute-start.3 = (bf16[32,2048]{1,0:T(8,128)(2,1)S(1)}, bf16[32,2048]{1,0:T(8,128)(2,1)S(1)}, u32[]{:S(2)}, u32[]{:S(2)}) collective-permute-start(bf16[32,2048]{1,0:T(8,128)(2,1)S(1)} %reshape.117), channel_id=1, source_target_pairs={{8,0},{12,4},{0,8},{4,12},{9,1},{13,5},{1,9},{5,13},{10,2},{14,6},... | collective-permute-start | bytes 393224 | tf_op jit(solution)/shard_map/ppermute | solution.py:332
  17.9 10.6 %back.1.back_ref = bf16[2048,2048]{1,0:T(8,128)(2,1)} custom-call(bf16[64,64,128]{2,1,0:T(8,128)(2,1)} %grad_ref.3, bf16[128,1024]{1,0:T(8,128)(2,1)} %bitcast.128), custom_call_target="tpu_custom_call" | custom-call | flops 21474836480 | bytes 8388608 | tf_op jit(solution)/shard_map/back/pallas_call | solution.py:62
  31.0 16.0 %right_grad.1 = bf16[128,2048]{1,0:T(8,128)(2,1)} custom-call(s32[8]{0:T(128)} %get-tuple-element.26.lo_ref, s32[8]{0:T(128)} %get-tuple-element.25.hi_ref, bf16[2048,2048]{1,0:T(8,128)(2,1)} %back.1.back_ref, bf16[128,2048]{1,0:T(8,128)(2,1)} %copy-done.7, s32[1,2048]{1,0:T(1,128)} %broadcast_in_dim_reshape.3.lab_ref, f32[64,1024]{1,0:T(8,128)} %bitcast_select_fusion.1.wide_ref), custom_call_target="tpu_custom_call" | custom-call | flops 21474836480 | bytes 8388608 | tf_op jit(solution)/shard_map/right_grad/pallas_call | solution.py:130
  47.2 1.3 collective-permute-start.4
  48.5 3.9 %collective-permute-start.5 = (bf16[32,2048]{1,0:T(8,128)(2,1)S(1)}, bf16[32,2048]{1,0:T(8,128)(2,1)S(1)}, u32[]{:S(2)}, u32[]{:S(2)}) collective-permute-start(bf16[32,2048]{1,0:T(8,128)(2,1)S(1)} %get-tuple-element.21), channel_id=1, source_target_pairs={{0,2},{2,0},{5,7},{7,5},{8,10},{10,8},{13,15},{15,13},{16,18},{18,... | collective-permute-start | bytes 393224 | tf_op jit(solution)/shard_map/ppermute | solution.py:348
  52.4 1.4 %collective-permute-start.6 = (bf16[32,2048]{1,0:T(8,128)(2,1)S(1)}, bf16[32,2048]{1,0:T(8,128)(2,1)S(1)}, u32[]{:S(2)}, u32[]{:S(2)}) collective-permute-start(bf16[32,2048]{1,0:T(8,128)(2,1)S(1)} %get-tuple-element.22), channel_id=1, source_target_pairs={{1,2},{3,0},{4,5},{6,7},{9,10},{11,8},{12,13},{14,15},{17,18},{19,... | collective-permute-start | bytes 393224 | tf_op jit(solution)/shard_map/ppermute | solution.py:348
  54.3 1.0 copy.45.tall_ref
  55.3 3.1 %collective-permute-done.5 = bf16[32,2048]{1,0:T(8,128)(2,1)S(1)} collective-permute-done((bf16[32,2048]{1,0:T(8,128)(2,1)S(1)}, bf16[32,2048]{1,0:T(8,128)(2,1)S(1)}, u32[]{:S(2)}, u32[]{:S(2)}) %collective-permute-start.5) | collective-permute-done | bytes 131104 | tf_op jit(solution)/shard_map/ppermute | solution.py:348
  58.4 2.8 %collective-permute-done.6 = bf16[32,2048]{1,0:T(8,128)(2,1)S(1)} collective-permute-done((bf16[32,2048]{1,0:T(8,128)(2,1)S(1)}, bf16[32,2048]{1,0:T(8,128)(2,1)S(1)}, u32[]{:S(2)}, u32[]{:S(2)}) %collective-permute-start.6) | collective-permute-done | bytes 131104 | tf_op jit(solution)/shard_map/ppermute | solution.py:348
  61.5 1.3 collective-permute-start.12
  62.8 4.2 %collective-permute-start.13 = (bf16[32,2048]{1,0:T(8,128)(2,1)S(1)}, bf16[32,2048]{1,0:T(8,128)(2,1)S(1)}, u32[]{:S(2)}, u32[]{:S(2)}) collective-permute-start(bf16[32,2048]{1,0:T(8,128)(2,1)S(1)} %get-tuple-element.11), channel_id=1, source_target_pairs={{2,0},{0,2},{7,5},{5,7},{10,8},{8,10},{15,13},{13,15},{18,16},{16,... | collective-permute-start | bytes 393224 | tf_op jit(solution)/shard_map/ppermute | solution.py:348
  67.1 1.3 collective-permute-start.14
  68.6 1.0 copy.41.right_ref
  69.6 23.0 %forward.1 = (bf16[64,64,128]{2,1,0:T(8,128)(2,1)}, f32[1024,128]{1,0:T(8,128)}) custom-call(s32[8]{0:T(128)} %get-tuple-element.26.lo_ref, s32[8]{0:T(128)} %get-tuple-element.25.hi_ref, bf16[128,2048]{1,0:T(8,128)(2,1)} %copy-done.7, s32[1,2048]{1,0:T(1,128)} %broadcast_in_dim_reshape.3.lab_ref, bf16[2048,128]{1,0:T(8,128)(2,1)} %copy.41.right_ref, ...), custom_call_target="tpu_custom_call" | custom-call | flops 42949672960 | bytes 8388608 | tf_op jit(solution)/shard_map/forward/pallas_call | solution.py:277
  92.6 1.1 convert_element_type.188
  94.0 11.0 %left_grad.1 = bf16[128,2048]{1,0:T(8,128)(2,1)} custom-call(s32[8]{0:T(128)} %get-tuple-element.26.lo_ref, s32[8]{0:T(128)} %get-tuple-element.25.hi_ref, bf16[2048,2048]{1,0:T(8,128)(2,1)} %back.1.back_ref, s32[1,2048]{1,0:T(1,128)} %broadcast_in_dim_reshape.3.lab_ref, bf16[128,2048]{1,0:T(8,128)(2,1)} %copy-done.2, f32[1024,128]{1,0:T(8,128)} %copy.45.tall_ref), custom_call_target="tpu_custom_call" | custom-call | flops 21474836480 | bytes 8388608 | tf_op jit(solution)/shard_map/left_grad/pallas_call | solution.py:186
  105.1 1.1 fusion.24
  106.2 1.1 collective-permute-start.18
  107.4 1.1 collective-permute-start.10
  108.5 1.0 collective-permute-start.8
  110.4 1.9 %collective-permute-start.15 = (bf16[32,2048]{1,0:T(8,128)(2,1)S(1)}, bf16[32,2048]{1,0:T(8,128)(2,1)S(1)}, u32[]{:S(2)}, u32[]{:S(2)}) collective-permute-start(bf16[32,2048]{1,0:T(8,128)(2,1)S(1)} %slice_bitcast_fusion), channel_id=1, source_target_pairs={{8,0},{12,4},{0,8},{4,12},{9,1},{13,5},{1,9},{5,13},{10,2},{14,6},... | collective-permute-start | bytes 393224 | tf_op jit(solution)/shard_map/ppermute | solution.py:332
  112.4 1.9 %collective-permute-start.19 = (bf16[256,128]{1,0:T(8,128)(2,1)S(1)}, bf16[256,128]{1,0:T(8,128)(2,1)S(1)}, u32[]{:S(2)}, u32[]{:S(2)}) collective-permute-start(bf16[256,128]{1,0:T(8,128)(2,1)S(1)} %fusion.22), channel_id=1, source_target_pairs={{1,0},{2,1},{3,2},{0,3},{5,4},{6,5},{7,6},{4,7},{9,8},{10,9},{11,1... | collective-permute-start | bytes 196616 | tf_op jit(solution)/shard_map/ppermute | solution.py:328
  114.2 1.8 %collective-permute-done.10 = bf16[32,2048]{1,0:T(8,128)(2,1)S(1)} collective-permute-done((bf16[32,2048]{1,0:T(8,128)(2,1)S(1)}, bf16[32,2048]{1,0:T(8,128)(2,1)S(1)}, u32[]{:S(2)}, u32[]{:S(2)}) %collective-permute-start.10) | collective-permute-done | bytes 131104 | tf_op jit(solution)/shard_map/ppermute | solution.py:328
  116.8 2.5 %collective-permute-start.21 = (bf16[256,128]{1,0:T(8,128)(2,1)S(1)}, bf16[256,128]{1,0:T(8,128)(2,1)S(1)}, u32[]{:S(2)}, u32[]{:S(2)}) collective-permute-start(bf16[256,128]{1,0:T(8,128)(2,1)S(1)} %fusion.22), channel_id=1, source_target_pairs={{3,0},{0,1},{1,2},{2,3},{7,4},{4,5},{5,6},{6,7},{11,8},{8,9},{9,10... | collective-permute-start | bytes 196616 | tf_op jit(solution)/shard_map/ppermute | solution.py:328
  119.3 5.5 %collective-permute-done.9 = bf16[32,2048]{1,0:T(8,128)(2,1)S(1)} collective-permute-done((bf16[32,2048]{1,0:T(8,128)(2,1)S(1)}, bf16[32,2048]{1,0:T(8,128)(2,1)S(1)}, u32[]{:S(2)}, u32[]{:S(2)}) %collective-permute-start.9) | collective-permute-done | bytes 131104 | tf_op jit(solution)/shard_map/ppermute | solution.py:328
  124.8 1.6 %add_convert_fusion.1 = bf16[32,2048]{1,0:T(8,128)(2,1)} fusion(bf16[32,2048]{1,0:T(8,128)(2,1)S(1)} %collective-permute-done.10, bf16[32,2048]{1,0:T(8,128)(2,1)S(1)} %collective-permute-done.9, bf16[32,2048]{1,0:T(8,128)(2,1)S(1)} %collective-permute-done.8, bf16[128,2048]{1,0:T(8,128)(2,1)} %left_grad.1), kind=kLoop, calls=%fused_computation.28 | loop fusion | flops 524288 | bytes 655360 | tf_op jit(solution)/shard_map/convert_element_type | solution.py:444
  126.4 0.9 collective-permute-done.20
  130.2 2.8 %collective-permute-done.23 = bf16[256,128]{1,0:T(8,128)(2,1)S(1)} collective-permute-done((bf16[256,128]{1,0:T(8,128)(2,1)S(1)}, bf16[256,128]{1,0:T(8,128)(2,1)S(1)}, u32[]{:S(2)}, u32[]{:S(2)}) %collective-permute-start.23) | collective-permute-done | bytes 65568 | tf_op jit(solution)/shard_map/ppermute | solution.py:332
  (118 shorter events, 15.3 us)
Async XLA Ops:
  4.3 8.2 %copy-start.8 = (bf16[256,32]{0,1:T(8,128)(2,1)S(1)}, bf16[256,32]{0,1:T(8,128)(2,1)}, u32[]{:S(2)}) copy-start(bf16[256,32]{0,1:T(8,128)(2,1)} %param.14) | copy-start | bytes 49156
  5.4 9.9 %copy-start.12 = (s32[256]{0:T(256)S(1)}, s32[256]{0:T(256)}, u32[]{:S(2)}) copy-start(s32[256]{0:T(256)} %param.17) | copy-start | bytes 3076
  5.4 10.0 %copy-start.9 = (s32[8,8]{1,0:T(8,128)S(1)}, s32[8,8]{1,0:T(8,128)}, u32[]{:S(2)}) copy-start(s32[8,8]{1,0:T(8,128)} %param.18) | copy-start | bytes 772
  5.7 11.0 %copy-start.6 = (bf16[1024,128]{1,0:T(8,128)(2,1)S(1)}, bf16[1024,128]{1,0:T(8,128)(2,1)}, u32[]{:S(2)}) copy-start(bf16[1024,128]{1,0:T(8,128)(2,1)} %param.15) | copy-start | bytes 786436
  6.3 23.8 %collective-permute-start = (bf16[32,2048]{1,0:T(8,128)(2,1)S(1)}, bf16[32,2048]{1,0:T(8,128)(2,1)S(1)}, u32[]{:S(2)}, u32[]{:S(2)}) collective-permute-start(bf16[32,2048]{1,0:T(8,128)(2,1)S(1)} %reshape.115), channel_id=1, source_target_pairs={{1,0},{2,1},{3,2},{0,3},{5,4},{6,5},{7,6},{4,7},{9,8},{10,9},{11,1... | collective-permute-start | bytes 393224 | tf_op jit(solution)/shard_map/ppermute | solution.py:328
  11.4 18.7 %collective-permute-start.1 = (bf16[32,2048]{1,0:T(8,128)(2,1)S(1)}, bf16[32,2048]{1,0:T(8,128)(2,1)S(1)}, u32[]{:S(2)}, u32[]{:S(2)}) collective-permute-start(bf16[32,2048]{1,0:T(8,128)(2,1)S(1)} %reshape.115), channel_id=1, source_target_pairs={{2,0},{3,1},{0,2},{1,3},{6,4},{7,5},{4,6},{5,7},{10,8},{11,9},{8,1... | collective-permute-start | bytes 393224 | tf_op jit(solution)/shard_map/ppermute | solution.py:328
  11.4 18.7 %collective-permute-start.2 = (bf16[32,2048]{1,0:T(8,128)(2,1)S(1)}, bf16[32,2048]{1,0:T(8,128)(2,1)S(1)}, u32[]{:S(2)}, u32[]{:S(2)}) collective-permute-start(bf16[32,2048]{1,0:T(8,128)(2,1)S(1)} %reshape.115), channel_id=1, source_target_pairs={{3,0},{0,1},{1,2},{2,3},{7,4},{4,5},{5,6},{6,7},{11,8},{8,9},{9,10... | collective-permute-start | bytes 393224 | tf_op jit(solution)/shard_map/ppermute | solution.py:328
  13.5 33.5 %collective-permute-start.3 = (bf16[32,2048]{1,0:T(8,128)(2,1)S(1)}, bf16[32,2048]{1,0:T(8,128)(2,1)S(1)}, u32[]{:S(2)}, u32[]{:S(2)}) collective-permute-start(bf16[32,2048]{1,0:T(8,128)(2,1)S(1)} %reshape.117), channel_id=1, source_target_pairs={{8,0},{12,4},{0,8},{4,12},{9,1},{13,5},{1,9},{5,13},{10,2},{14,6},... | collective-permute-start | bytes 393224 | tf_op jit(solution)/shard_map/ppermute | solution.py:332
  16.8 11.7 %copy-start.4 = (bf16[32,32,128]{2,1,0:T(8,128)(2,1)}, bf16[32,32,128]{2,1,0:T(8,128)(2,1)S(1)}, u32[]{:S(2)}) copy-start(bf16[32,32,128]{2,1,0:T(8,128)(2,1)S(1)} %copy.40) | copy-start | bytes 786436
  47.0 14.3 %collective-permute-start.11 = (bf16[128,2048]{1,0:T(8,128)(2,1)}, bf16[128,2048]{1,0:T(8,128)(2,1)S(1)}, u32[]{:S(2)}, u32[]{:S(2)}) collective-permute-start(bf16[128,2048]{1,0:T(8,128)(2,1)} %right_grad.1), channel_id=1, source_target_pairs={{4,0},{0,4},{12,8},{8,12},{5,1},{1,5},{13,9},{9,13},{6,2},{2,6},{1... | collective-permute-start | bytes 1572872 | tf_op jit(solution)/shard_map/ppermute | solution.py:338
  47.2 8.0 %collective-permute-start.4 = (bf16[32,2048]{1,0:T(8,128)(2,1)S(1)}, bf16[32,2048]{1,0:T(8,128)(2,1)S(1)}, u32[]{:S(2)}, u32[]{:S(2)}) collective-permute-start(bf16[32,2048]{1,0:T(8,128)(2,1)S(1)} %get-tuple-element.20), channel_id=1, source_target_pairs={{1,0},{3,2},{4,7},{6,5},{9,8},{11,10},{12,15},{14,13},{17,16},{19,... | collective-permute-start | bytes 393224 | tf_op jit(solution)/shard_map/ppermute | solution.py:348
  48.5 9.8 %collective-permute-start.5 = (bf16[32,2048]{1,0:T(8,128)(2,1)S(1)}, bf16[32,2048]{1,0:T(8,128)(2,1)S(1)}, u32[]{:S(2)}, u32[]{:S(2)}) collective-permute-start(bf16[32,2048]{1,0:T(8,128)(2,1)S(1)} %get-tuple-element.21), channel_id=1, source_target_pairs={{0,2},{2,0},{5,7},{7,5},{8,10},{10,8},{13,15},{15,13},{16,18},{18,... | collective-permute-start | bytes 393224 | tf_op jit(solution)/shard_map/ppermute | solution.py:348
  52.4 8.9 %copy-start.5 = (bf16[128,2048]{1,0:T(8,128)(2,1)S(1)}, bf16[128,2048]{1,0:T(8,128)(2,1)}, u32[]{:S(2)}) copy-start(bf16[128,2048]{1,0:T(8,128)(2,1)} %right_grad.1) | copy-start | bytes 1572868
  52.4 8.8 %collective-permute-start.6 = (bf16[32,2048]{1,0:T(8,128)(2,1)S(1)}, bf16[32,2048]{1,0:T(8,128)(2,1)S(1)}, u32[]{:S(2)}, u32[]{:S(2)}) collective-permute-start(bf16[32,2048]{1,0:T(8,128)(2,1)S(1)} %get-tuple-element.22), channel_id=1, source_target_pairs={{1,2},{3,0},{4,5},{6,7},{9,10},{11,8},{12,13},{14,15},{17,18},{19,... | collective-permute-start | bytes 393224 | tf_op jit(solution)/shard_map/ppermute | solution.py:348
  61.3 7.2 %collective-permute-start.7 = (bf16[128,2048]{1,0:T(8,128)(2,1)S(1)}, bf16[128,2048]{1,0:T(8,128)(2,1)S(1)}, u32[]{:S(2)}, u32[]{:S(2)}) collective-permute-start(bf16[128,2048]{1,0:T(8,128)(2,1)S(1)} %pad_maximum_fusion), channel_id=1, source_target_pairs={{4,0},{0,4},{12,8},{8,12},{5,1},{1,5},{13,9},{9,13},{6,2},{2,6},{1... | collective-permute-start | bytes 1572872 | tf_op jit(solution)/shard_map/ppermute | solution.py:338
  61.5 44.7 %collective-permute-start.12 = (bf16[32,2048]{1,0:T(8,128)(2,1)S(1)}, bf16[32,2048]{1,0:T(8,128)(2,1)S(1)}, u32[]{:S(2)}, u32[]{:S(2)}) collective-permute-start(bf16[32,2048]{1,0:T(8,128)(2,1)S(1)} %get-tuple-element.12), channel_id=1, source_target_pairs={{0,1},{2,3},{7,4},{5,6},{8,9},{10,11},{15,12},{13,14},{16,17},{18,... | collective-permute-start | bytes 393224 | tf_op jit(solution)/shard_map/ppermute | solution.py:348
  62.8 44.5 %collective-permute-start.13 = (bf16[32,2048]{1,0:T(8,128)(2,1)S(1)}, bf16[32,2048]{1,0:T(8,128)(2,1)S(1)}, u32[]{:S(2)}, u32[]{:S(2)}) collective-permute-start(bf16[32,2048]{1,0:T(8,128)(2,1)S(1)} %get-tuple-element.11), channel_id=1, source_target_pairs={{2,0},{0,2},{7,5},{5,7},{10,8},{8,10},{15,13},{13,15},{18,16},{16,... | collective-permute-start | bytes 393224 | tf_op jit(solution)/shard_map/ppermute | solution.py:348
  67.1 41.4 %collective-permute-start.14 = (bf16[32,2048]{1,0:T(8,128)(2,1)S(1)}, bf16[32,2048]{1,0:T(8,128)(2,1)S(1)}, u32[]{:S(2)}, u32[]{:S(2)}) collective-permute-start(bf16[32,2048]{1,0:T(8,128)(2,1)S(1)} %get-tuple-element.10), channel_id=1, source_target_pairs={{2,1},{0,3},{5,4},{7,6},{10,9},{8,11},{13,12},{15,14},{18,17},{16,... | collective-permute-start | bytes 393224 | tf_op jit(solution)/shard_map/ppermute | solution.py:348
  68.6 24.0 %copy-start.2 = (bf16[128,2048]{1,0:T(8,128)(2,1)}, bf16[128,2048]{1,0:T(8,128)(2,1)S(1)}, u32[]{:S(2)}) copy-start(bf16[128,2048]{1,0:T(8,128)(2,1)S(1)} %broadcast_select_fusion.right_ref) | copy-start | bytes 1572868
  93.7 15.9 %collective-permute-start.16 = (bf16[256,128]{1,0:T(8,128)(2,1)S(1)}, bf16[256,128]{1,0:T(8,128)(2,1)S(1)}, u32[]{:S(2)}, u32[]{:S(2)}) collective-permute-start(bf16[256,128]{1,0:T(8,128)(2,1)S(1)} %get-tuple-element.16), channel_id=1, source_target_pairs={{12,0},{0,4},{4,8},{8,12},{13,1},{1,5},{5,9},{9,13},{14,2},{2,6},{... | collective-permute-start | bytes 196616 | tf_op jit(solution)/shard_map/ppermute | solution.py:332
  94.0 16.5 %collective-permute-start.17 = (bf16[256,128]{1,0:T(8,128)(2,1)S(1)}, bf16[256,128]{1,0:T(8,128)(2,1)S(1)}, u32[]{:S(2)}, u32[]{:S(2)}) collective-permute-start(bf16[256,128]{1,0:T(8,128)(2,1)S(1)} %get-tuple-element.18), channel_id=1, source_target_pairs={{8,0},{12,4},{0,8},{4,12},{9,1},{13,5},{1,9},{5,13},{10,2},{14,6},... | collective-permute-start | bytes 196616 | tf_op jit(solution)/shard_map/ppermute | solution.py:332
  106.2 6.1 %collective-permute-start.18 = (bf16[256,128]{1,0:T(8,128)(2,1)S(1)}, bf16[256,128]{1,0:T(8,128)(2,1)S(1)}, u32[]{:S(2)}, u32[]{:S(2)}) collective-permute-start(bf16[256,128]{1,0:T(8,128)(2,1)S(1)} %get-tuple-element.17), channel_id=1, source_target_pairs={{4,0},{8,4},{12,8},{0,12},{5,1},{9,5},{13,9},{1,13},{6,2},{10,6},{... | collective-permute-start | bytes 196616 | tf_op jit(solution)/shard_map/ppermute | solution.py:332
  107.4 8.7 %collective-permute-start.10 = (bf16[32,2048]{1,0:T(8,128)(2,1)S(1)}, bf16[32,2048]{1,0:T(8,128)(2,1)S(1)}, u32[]{:S(2)}, u32[]{:S(2)}) collective-permute-start(bf16[32,2048]{1,0:T(8,128)(2,1)S(1)} %get-tuple-element.14), channel_id=1, source_target_pairs={{1,0},{2,1},{3,2},{0,3},{5,4},{6,5},{7,6},{4,7},{9,8},{10,9},{11,1... | collective-permute-start | bytes 393224 | tf_op jit(solution)/shard_map/ppermute | solution.py:328
  108.5 8.3 %collective-permute-start.8 = (bf16[32,2048]{1,0:T(8,128)(2,1)S(1)}, bf16[32,2048]{1,0:T(8,128)(2,1)S(1)}, u32[]{:S(2)}, u32[]{:S(2)}) collective-permute-start(bf16[32,2048]{1,0:T(8,128)(2,1)S(1)} %get-tuple-element.13), channel_id=1, source_target_pairs={{3,0},{0,1},{1,2},{2,3},{7,4},{4,5},{5,6},{6,7},{11,8},{8,9},{9,10... | collective-permute-start | bytes 393224 | tf_op jit(solution)/shard_map/ppermute | solution.py:328
  109.6 15.2 %collective-permute-start.9 = (bf16[32,2048]{1,0:T(8,128)(2,1)S(1)}, bf16[32,2048]{1,0:T(8,128)(2,1)S(1)}, u32[]{:S(2)}, u32[]{:S(2)}) collective-permute-start(bf16[32,2048]{1,0:T(8,128)(2,1)S(1)} %get-tuple-element.15), channel_id=1, source_target_pairs={{2,0},{3,1},{0,2},{1,3},{6,4},{7,5},{4,6},{5,7},{10,8},{11,9},{8,1... | collective-permute-start | bytes 393224 | tf_op jit(solution)/shard_map/ppermute | solution.py:328
  110.4 18.6 %collective-permute-start.15 = (bf16[32,2048]{1,0:T(8,128)(2,1)S(1)}, bf16[32,2048]{1,0:T(8,128)(2,1)S(1)}, u32[]{:S(2)}, u32[]{:S(2)}) collective-permute-start(bf16[32,2048]{1,0:T(8,128)(2,1)S(1)} %slice_bitcast_fusion), channel_id=1, source_target_pairs={{8,0},{12,4},{0,8},{4,12},{9,1},{13,5},{1,9},{5,13},{10,2},{14,6},... | collective-permute-start | bytes 393224 | tf_op jit(solution)/shard_map/ppermute | solution.py:332
  112.4 14.0 %collective-permute-start.19 = (bf16[256,128]{1,0:T(8,128)(2,1)S(1)}, bf16[256,128]{1,0:T(8,128)(2,1)S(1)}, u32[]{:S(2)}, u32[]{:S(2)}) collective-permute-start(bf16[256,128]{1,0:T(8,128)(2,1)S(1)} %fusion.22), channel_id=1, source_target_pairs={{1,0},{2,1},{3,2},{0,3},{5,4},{6,5},{7,6},{4,7},{9,8},{10,9},{11,1... | collective-permute-start | bytes 196616 | tf_op jit(solution)/shard_map/ppermute | solution.py:328
  116.0 11.2 %collective-permute-start.20 = (bf16[256,128]{1,0:T(8,128)(2,1)S(1)}, bf16[256,128]{1,0:T(8,128)(2,1)S(1)}, u32[]{:S(2)}, u32[]{:S(2)}) collective-permute-start(bf16[256,128]{1,0:T(8,128)(2,1)S(1)} %fusion.22), channel_id=1, source_target_pairs={{2,0},{3,1},{0,2},{1,3},{6,4},{7,5},{4,6},{5,7},{10,8},{11,9},{8,1... | collective-permute-start | bytes 196616 | tf_op jit(solution)/shard_map/ppermute | solution.py:328
  116.8 10.5 %collective-permute-start.21 = (bf16[256,128]{1,0:T(8,128)(2,1)S(1)}, bf16[256,128]{1,0:T(8,128)(2,1)S(1)}, u32[]{:S(2)}, u32[]{:S(2)}) collective-permute-start(bf16[256,128]{1,0:T(8,128)(2,1)S(1)} %fusion.22), channel_id=1, source_target_pairs={{3,0},{0,1},{1,2},{2,3},{7,4},{4,5},{5,6},{6,7},{11,8},{8,9},{9,10... | collective-permute-start | bytes 196616 | tf_op jit(solution)/shard_map/ppermute | solution.py:328
  127.4 2.9 %collective-permute-start.22 = (bf16[256,128]{1,0:T(8,128)(2,1)S(1)}, bf16[256,128]{1,0:T(8,128)(2,1)S(1)}, u32[]{:S(2)}, u32[]{:S(2)}) collective-permute-start(bf16[256,128]{1,0:T(8,128)(2,1)S(1)} %get-tuple-element.9), channel_id=1, source_target_pairs={{4,0},{8,4},{12,8},{0,12},{5,1},{9,5},{13,9},{1,13},{6,2},{10,6},{... | collective-permute-start | bytes 196616 | tf_op jit(solution)/shard_map/ppermute | solution.py:332
  128.0 5.0 %collective-permute-start.23 = (bf16[256,128]{1,0:T(8,128)(2,1)S(1)}, bf16[256,128]{1,0:T(8,128)(2,1)S(1)}, u32[]{:S(2)}, u32[]{:S(2)}) collective-permute-start(bf16[256,128]{1,0:T(8,128)(2,1)S(1)} %get-tuple-element.9), channel_id=1, source_target_pairs={{8,0},{12,4},{0,8},{4,12},{9,1},{13,5},{1,9},{5,13},{10,2},{14,6},... | collective-permute-start | bytes 196616 | tf_op jit(solution)/shard_map/ppermute | solution.py:332
  128.9 4.3 %collective-permute-start.24 = (bf16[256,128]{1,0:T(8,128)(2,1)S(1)}, bf16[256,128]{1,0:T(8,128)(2,1)S(1)}, u32[]{:S(2)}, u32[]{:S(2)}) collective-permute-start(bf16[256,128]{1,0:T(8,128)(2,1)S(1)} %get-tuple-element.9), channel_id=1, source_target_pairs={{12,0},{0,4},{4,8},{8,12},{13,1},{1,5},{5,9},{9,13},{14,2},{2,6},{... | collective-permute-start | bytes 196616 | tf_op jit(solution)/shard_map/ppermute | solution.py:332
  (6 other events, 23.2 us)

commit v3 on v2

v3 whole, which is shorter than its diff:
```python
import jax
import jax.numpy as jnp
from jax import lax
from jax.experimental import pallas as pl
from jax.experimental.pallas import tpu as pltpu
from jax.sharding import PartitionSpec as P


PROJ = 32
CHAINS = 8
LANES = 128
PER_TILE = LANES // PROJ
WIDE = 256
F32 = jnp.float32
BF16 = jnp.bfloat16


def standardize_entries(alignment_tensor, standard_multiplier, additive_offset):
    incoming_entries = alignment_tensor.astype(F32)
    center = incoming_entries - jnp.mean(incoming_entries, axis=-1, keepdims=True)
    spread = jnp.mean(center * center, axis=-1, keepdims=True)
    return (center * lax.rsqrt(spread + 1e-05) * standard_multiplier + additive_offset).astype(BF16)


def swap_blocks(parts):
    lane = lax.broadcasted_iota(jnp.int32, parts[0].shape, 1)
    for bit in (2, 1):
        shift = bit * PROJ
        low = (lane & shift) == 0
        out = list(parts)
        for p in range(PER_TILE):
            if not p & bit:
                a, b = parts[p], parts[p | bit]
                out[p] = jnp.where(low, a, pltpu.roll(b, shift, 1))
                out[p | bit] = jnp.where(low, pltpu.roll(a, LANES - shift, 1), b)
        parts = out
    return parts


def nt_dot(a, b):
    return lax.dot_general(a, b, (((1,), (1,)), ((), ())), preferred_element_type=F32)


def nn_dot(a, b):
    return lax.dot_general(a, b, (((1,), (0,)), ((), ())), preferred_element_type=F32)


def cost(passes, span, total, seqs):
    return pl.CostEstimate(
        flops=4 * passes * span * total * seqs, bytes_accessed=2 * span * total, transcendentals=0
    )


def back_body(grad_ref, wt_ref, out_ref):
    rows, cols, width = grad_ref.shape
    block = grad_ref[...].reshape(rows * cols, width)
    for u in range(PROJ * PROJ // WIDE):
        prod = nn_dot(block, wt_ref[:, u * WIDE : (u + 1) * WIDE]).astype(BF16)
        for half in range(rows // PER_TILE):
            for t in range(WIDE // LANES):
                parts = [
                    prod[(half * PER_TILE + p) * cols : (half * PER_TILE + p + 1) * cols,
                         t * LANES : (t + 1) * LANES]
                    for p in range(PER_TILE)
                ]
                for q, part in enumerate(swap_blocks(parts)):
                    e = u * (WIDE // PROJ) + t * PER_TILE + q
                    out_ref[0, e * cols : (e + 1) * cols, half * LANES : (half + 1) * LANES] = part


def back_call(grad, wt):
    rows, cols, width = grad.shape
    step = WIDE // PROJ
    return pl.pallas_call(
        back_body,
        grid=(rows // step,),
        in_specs=[
            pl.BlockSpec((step, cols, width), lambda g: (g, 0, 0)),
            pl.BlockSpec((width, PROJ * PROJ), lambda g: (0, 0)),
        ],
        out_specs=pl.BlockSpec((1, PROJ * cols, WIDE), lambda g: (g, 0, 0)),
        out_shape=jax.ShapeDtypeStruct((rows // step, PROJ * cols, WIDE), BF16),
        compiler_params=pltpu.CompilerParams(dimension_semantics=("arbitrary",)),
        cost_estimate=cost(10, PROJ * cols, rows * PROJ, width),
        name="back",
    )(grad, wt)


def masked_left(left_ref, lab_ref, lb_ref, pair):
    seqs = left_ref.shape[0]
    for side in range(2):
        keep = (lab_ref[...] == 2 * pair + side).astype(F32).astype(BF16)
        lb_ref[side * seqs : (side + 1) * seqs] = left_ref[...] * keep


def right_grad_body(lo_ref, hi_ref, back_ref, left_ref, lab_ref, wide_ref,
                    right_out, q_ref, lb_ref, flip_ref, turn_ref):
    g = pl.program_id(0)
    seqs = left_ref.shape[0]
    span = back_ref.shape[1]
    cols = span // PROJ
    last = pl.num_programs(0) - 1

    def over_pairs(fn):
        def step(pair, carry):
            fn(pair)
            return carry

        return step

    @pl.when(g == 0)
    def _():
        def clear(pair):
            q_ref[pair] = jnp.zeros(q_ref.shape[1:], F32)

        lax.fori_loop(lo_ref[0], hi_ref[last] + 1, over_pairs(clear), 0)
        flip_ref[...] = jnp.zeros_like(flip_ref)

    def one_pair(pair):
        masked_left(left_ref, lab_ref, lb_ref, pair)
        q_ref[pair] += nt_dot(back_ref[0], lb_ref[...])

    lax.fori_loop(lo_ref[g], hi_ref[g] + 1, over_pairs(one_pair), 0)

    @pl.when(g == last)
    def _():
        def combine(pair):
            for e in range(PROJ):
                rows = slice(e * cols, (e + 1) * cols)
                both = q_ref[pair, rows] * wide_ref[pair]
                flip_ref[rows] += both[:, :seqs] + both[:, seqs:]

        lax.fori_loop(lo_ref[0], hi_ref[last] + 1, over_pairs(combine), 0)
        for j in range(cols):
            turn_ref[j * PROJ : (j + 1) * PROJ] = flip_ref[pl.ds(j, PROJ, stride=cols)]
        for t in range(span // LANES):
            rows = slice(t * LANES, (t + 1) * LANES)
            right_out[:, rows] = turn_ref[rows].T.astype(BF16)


def right_grad_call(lo, hi, back, left, lab, wide):
    groups, span, _ = back.shape
    total = groups * WIDE
    seqs = left.shape[0]
    whole = lambda shape: pl.BlockSpec(shape, lambda g, lo, hi: (0,) * len(shape))
    return pl.pallas_call(
        right_grad_body,
        grid_spec=pltpu.PrefetchScalarGridSpec(
            num_scalar_prefetch=2,
            grid=(total // WIDE,),
            in_specs=[
                pl.BlockSpec((1, span, WIDE), lambda g, lo, hi: (g, 0, 0)),
                pl.BlockSpec((seqs, WIDE), lambda g, lo, hi: (0, g)),
                pl.BlockSpec((1, WIDE), lambda g, lo, hi: (0, g)),
                whole(wide.shape),
            ],
            out_specs=whole((seqs, span)),
            scratch_shapes=[
                pltpu.VMEM((CHAINS // 2, span, 2 * seqs), F32),
                pltpu.VMEM((2 * seqs, WIDE), BF16),
                pltpu.VMEM((span, seqs), F32),
                pltpu.VMEM((span, seqs), F32),
            ],
        ),
        out_shape=jax.ShapeDtypeStruct((seqs, span), BF16),
        compiler_params=pltpu.CompilerParams(dimension_semantics=("arbitrary",)),
        cost_estimate=cost(10, span, total, seqs),
        name="right_grad",
    )(lo, hi, back, left, lab, wide)


def left_grad_body(lo_ref, hi_ref, back_ref, lab_ref, right_ref, tall_ref, left_out, rm_ref):
    g = pl.program_id(0)
    seqs = right_ref.shape[1]
    span = back_ref.shape[1]

    last = pl.num_programs(0) - 1

    @pl.when(g == 0)
    def _():
        def build(pair, carry):
            for side in range(2):
                row = side * seqs
                plain, third = tall_ref[pair, 0, row : row + seqs], tall_ref[pair, 1, row : row + seqs]
                for t in range(span // LANES):
                    lanes = slice(t * LANES, (t + 1) * LANES)
                    rm_ref[pair, row : row + seqs, lanes] = (
                        right_ref[0, :, lanes] * plain + right_ref[1, :, lanes] * third
                    )
            return carry

        lax.fori_loop(lo_ref[0], hi_ref[last] + 1, build, 0)

    def one_pair(pair, total):
        part = nn_dot(rm_ref[pair], back_ref[0])
        keep0 = lab_ref[...] == 2 * pair
        keep1 = lab_ref[...] == 2 * pair + 1
        return total + jnp.where(keep0, part[:seqs], 0.0) + jnp.where(keep1, part[seqs:], 0.0)

    total = lax.fori_loop(lo_ref[g], hi_ref[g] + 1, one_pair, jnp.zeros(left_out.shape, F32))
    left_out[...] = total.astype(BF16)


def left_grad_call(lo, hi, back, lab, right, tall):
    groups, span, _ = back.shape
    total = groups * WIDE
    seqs = right.shape[1]
    whole = lambda shape: pl.BlockSpec(shape, lambda g, lo, hi: (0,) * len(shape))
    return pl.pallas_call(
        left_grad_body,
        grid_spec=pltpu.PrefetchScalarGridSpec(
            num_scalar_prefetch=2,
            grid=(total // WIDE,),
            in_specs=[
                pl.BlockSpec((1, span, WIDE), lambda g, lo, hi: (g, 0, 0)),
                pl.BlockSpec((1, WIDE), lambda g, lo, hi: (0, g)),
                whole(right.shape),
                whole(tall.shape),
            ],
            out_specs=pl.BlockSpec((seqs, WIDE), lambda g, lo, hi: (0, g)),
            scratch_shapes=[pltpu.VMEM((CHAINS // 2, 2 * seqs, span), BF16)],
        ),
        out_shape=jax.ShapeDtypeStruct((seqs, total), BF16),
        compiler_params=pltpu.CompilerParams(dimension_semantics=("arbitrary",)),
        cost_estimate=cost(10, span, total, seqs),
        name="left_grad",
    )(lo, hi, back, lab, right, tall)


def outer_body(lo_ref, hi_ref, left_ref, lab_ref, right_ref, wide_ref, grad_ref,
               x_ref, weight_out, rm_ref, lb_ref, acc_ref, sum_ref, turn_ref):
    g = pl.program_id(0)
    seqs = left_ref.shape[0]
    span = right_ref.shape[1]
    cols = span // PROJ
    rows_here, _, width = grad_ref.shape

    last = pl.num_programs(0) - 1

    @pl.when(g == 0)
    def _():
        def build(pair, carry):
            plain, third = wide_ref[pair, 0], wide_ref[pair, 1]
            for e in range(PROJ):
                rows = slice(e * cols, (e + 1) * cols)
                for side in range(2):
                    lanes = slice(side * seqs, (side + 1) * seqs)
                    rm_ref[pair, rows, lanes] = (
                        right_ref[0, rows] * plain[:, lanes] + right_ref[1, rows] * third[:, lanes]
                    )
            return carry

        lax.fori_loop(lo_ref[0], hi_ref[last] + 1, build, 0)
        sum_ref[...] = jnp.zeros_like(sum_ref)

    def product(pair):
        masked_left(left_ref, lab_ref, lb_ref, pair)
        return nn_dot(rm_ref[pair], lb_ref[...])

    acc_ref[...] = product(lo_ref[g])

    def more(pair, carry):
        acc_ref[...] += product(pair)
        return carry

    lax.fori_loop(lo_ref[g] + 1, hi_ref[g] + 1, more, 0)

    for half in range(WIDE // LANES):
        lanes = slice(half * LANES, (half + 1) * LANES)
        for t in range(PROJ // PER_TILE):
            parts = []
            for q in range(PER_TILE):
                e = t * PER_TILE + q
                parts.append(acc_ref[e * cols : (e + 1) * cols, lanes].astype(BF16))
            turned = swap_blocks(parts)
            for p in range(PER_TILE):
                i = half * PER_TILE + p
                x_ref[i * cols : (i + 1) * cols, t * LANES : (t + 1) * LANES] = turned[p]

    flat = grad_ref[...].reshape(rows_here * cols, width)
    sum_ref[...] += nn_dot(flat.T, x_ref[...])

    @pl.when(g == last)
    def _():
        for t in range(PROJ * PROJ // LANES):
            part = slice(t * LANES, (t + 1) * LANES)
            turn_ref[part] = sum_ref[:, part].T
        for c in range(PROJ):
            weight_out[c * PROJ : (c + 1) * PROJ] = turn_ref[pl.ds(c, PROJ, stride=PROJ)]


def outer_call(lo, hi, left, lab, right, wide, grad):
    rows, cols, width = grad.shape
    seqs, total = left.shape
    span = right.shape[1]
    step = WIDE // PROJ
    whole = lambda shape: pl.BlockSpec(shape, lambda g, lo, hi: (0,) * len(shape))
    return pl.pallas_call(
        outer_body,
        grid_spec=pltpu.PrefetchScalarGridSpec(
            num_scalar_prefetch=2,
            grid=(total // WIDE,),
            in_specs=[
                pl.BlockSpec((seqs, WIDE), lambda g, lo, hi: (0, g)),
                pl.BlockSpec((1, WIDE), lambda g, lo, hi: (0, g)),
                whole(right.shape),
                whole(wide.shape),
                pl.BlockSpec((step, cols, width), lambda g, lo, hi: (g, 0, 0)),
            ],
            out_specs=[
                pl.BlockSpec((step * cols, PROJ * PROJ), lambda g, lo, hi: (g, 0)),
                whole((PROJ * PROJ, width)),
            ],
            scratch_shapes=[
                pltpu.VMEM((CHAINS // 2, span, 2 * seqs), BF16),
                pltpu.VMEM((2 * seqs, WIDE), BF16),
                pltpu.VMEM((span, WIDE), F32),
                pltpu.VMEM((width, PROJ * PROJ), F32),
                pltpu.VMEM((PROJ * PROJ, width), F32),
            ],
        ),
        out_shape=[
            jax.ShapeDtypeStruct((rows * cols, PROJ * PROJ), BF16),
            jax.ShapeDtypeStruct((PROJ * PROJ, width), F32),
        ],
        compiler_params=pltpu.CompilerParams(dimension_semantics=("arbitrary",)),
        cost_estimate=cost(20, span, total, seqs),
        name="outer",
    )(lo, hi, left, lab, right, wide, grad)


class Ring:
    def __init__(self, n_row, n_col):
        self.n_row, self.n_col = n_row, n_col
        self.n_x = n_row // 2
        self.per_row = n_col // n_row
        self.row = lax.axis_index("row").astype(jnp.uint32)
        self.col = lax.axis_index("col").astype(jnp.uint32)
        self.x, self.core = self.row // 2, self.row % 2

    def core_of(self, col):
        return (col // self.per_row) % 2

    def col_shift(self, value, k):
        n = self.n_col
        return lax.ppermute(value, "col", [((t + k) % n, t) for t in range(n)])

    def row_shift(self, value, k):
        n = self.n_row
        return lax.ppermute(value, "row", [((t + k) % n, t) for t in range(n)])

    def x_shift(self, value, k):
        return self.row_shift(value, 2 * k)

    def other_core(self, value):
        return lax.ppermute(value, "row", [(t ^ 1, t) for t in range(self.n_row)])

    def along_col(self, value, k, outward):
        pairs = []
        for r in range(self.n_row):
            for t in range(self.n_col):
                q = (t - k) % self.n_col
                if self.core_of(q) == r % 2:
                    far, near = r * self.n_col + t, r * self.n_col + q
                    pairs.append((far, near) if outward else (near, far))
        return lax.ppermute(value, ("row", "col"), pairs)

    def right_along_x(self, right):
        here, lanes = right.shape
        lanes //= self.per_row
        by_x = jnp.stack([right] + [self.x_shift(right, k) for k in range(1, self.n_x)])
        pieces = []
        for k in range(self.n_col):
            q = (self.col + (self.n_col - k)) % self.n_col
            which = ((q // self.per_row) // 2 + self.n_x - self.x) % self.n_x
            at = (which, jnp.uint32(0), (q % self.per_row) * lanes)
            pieces.append(lax.dynamic_slice(by_x, at, (1, here, lanes))[0])
        return pieces

    def right_along_col(self, pieces):
        blocks = [self.along_col(p, k, True) if k else p for k, p in enumerate(pieces)]
        return jnp.concatenate(blocks, axis=0)

    def right_to_both(self, mine):
        return jnp.where(self.core_of(self.col) == self.core, mine, self.other_core(mine))

    def grad_of_chip(self, grad):
        return (grad.astype(F32) + self.other_core(grad).astype(F32)).astype(BF16)

    def grad_along_col(self, both):
        lanes = both.shape[1]
        here = both.shape[0] // self.n_col
        by_row = jnp.zeros((self.n_x, here, self.per_row * lanes), BF16)
        for k in range(self.n_col):
            block = both[k * here : (k + 1) * here]
            q = (self.col + (self.n_col - k)) % self.n_col
            fits = self.core_of(q) == self.core
            got = self.along_col(block, k, False) if k else block
            got = jnp.where(fits, got, 0)
            which = ((q // self.per_row) // 2 + self.n_x - self.x) % self.n_x
            at = (which, jnp.uint32(0), (q % self.per_row) * lanes)
            old = lax.dynamic_slice(by_row, at, (1, here, lanes))
            by_row = lax.dynamic_update_slice(by_row, old + got[None], at)
        return by_row

    def grad_along_x(self, by_row):
        total = by_row[0].astype(F32)
        for k in range(1, self.n_x):
            total += self.x_shift(by_row[k], self.n_x - k).astype(F32)
        return total.astype(BF16)

    def weight_over_row(self, weight):
        n = self.n_row
        size = weight.shape[0] // n
        sent = weight.astype(BF16).reshape(n, size, -1)
        total = lax.dynamic_index_in_dim(weight.reshape(n, size, -1), self.row, 0, keepdims=False)
        for k in range(1, n):
            piece = lax.dynamic_index_in_dim(sent, (self.row + k) % n, 0, keepdims=False)
            total += self.row_shift(piece, n - k).astype(F32)
        return total

    def weight_over_col(self, total):
        mine = total.astype(BF16)
        for k in range(1, self.n_col):
            total += self.col_shift(mine, k).astype(F32)
        return total.astype(BF16)

    def weight_to_all(self, mine):
        n = self.n_row
        which = (lax.broadcasted_iota(jnp.uint32, (n, 1, 1), 0) + (n - self.row)) % n
        shares = mine[None]
        for k in range(1, n):
            shares = jnp.where(which == k, self.row_shift(mine, k)[None], shares)
        return shares.reshape(n * mine.shape[0], mine.shape[1])


def after(value, *others):
    return lax.optimization_barrier((value,) + others)[0]


def shards(n_row, n_col, alignment_tensor, gain, shift, first_projector, second_projector,
           final_projector, final_offset, labels, counts, grad):
    ring = Ring(n_row, n_col)
    here, rows, feats = alignment_tensor.shape
    cols, width = grad.shape[1:]
    seqs = here * n_col
    normed = standardize_entries(alignment_tensor, gain, shift).reshape(-1, feats)
    left = jnp.dot(normed, first_projector, preferred_element_type=F32).astype(BF16)
    right = jnp.dot(normed, second_projector, preferred_element_type=F32).astype(BF16)
    left = left.reshape(here, rows * PROJ)
    right = right.reshape(here, rows // cols, cols, PROJ).transpose(0, 1, 3, 2)
    pieces = ring.right_along_x(right.reshape(here, rows * PROJ))
    left = jnp.concatenate([left] + [ring.col_shift(left, k) for k in range(1, n_col)])

    row_labels = lax.dynamic_slice_in_dim(labels, ring.row * rows, rows, 0)
    col_labels = lax.dynamic_slice_in_dim(labels, ring.col * cols, cols, 0)
    lab = jnp.repeat(row_labels, PROJ)[None, :]
    step = WIDE // PROJ
    lo = row_labels[::step] // 2
    hi = row_labels[step - 1 :: step] // 2
    chains = jnp.arange(CHAINS, dtype=jnp.int32)
    col_hot = col_labels[:, None, None] == chains[None, None, :]
    depth = jnp.sum(jnp.where(col_hot, counts[None, :, :], 0), axis=-1)
    seq = (jnp.arange(seqs, dtype=jnp.uint32) + ring.col * here) % seqs
    seq = seq.astype(jnp.int32)
    keep = seq[None, None, :] < depth[:, :, None]
    weight = jnp.where(keep, 1.0 / depth.astype(F32)[:, :, None], 0.0)
    third = (depth % 3 == 0)[:, :, None]
    weights = jnp.stack([jnp.where(third, 0.0, weight), jnp.where(third, 3.0 * weight, 0.0)])
    weights = weights.astype(BF16)
    pairs = CHAINS // 2
    tall = weights.transpose(2, 0, 3, 1).reshape(pairs, 2, 2, seqs, cols).swapaxes(1, 2)
    tall = jnp.tile(tall.reshape(pairs, 2, 2 * seqs, cols), (1, 1, 1, LANES // cols))
    wide = weights.reshape(2, cols, pairs, 2 * seqs).transpose(2, 0, 1, 3)
    plain = weight.reshape(cols, pairs, 2 * seqs).transpose(1, 0, 2)

    w = final_projector.reshape(PROJ, PROJ, width).transpose(1, 0, 2).reshape(PROJ * PROJ, width)
    back = back_call(after(grad, *pieces), w.T)
    mine = ring.right_along_col(pieces)
    right_grad = right_grad_call(lo, hi, back, left, lab, plain)

    mine = after(mine, right_grad)
    right = ring.right_to_both(mine)
    right = jnp.stack([right, (right.astype(F32) / 3).astype(BF16)])
    both = ring.grad_of_chip(right_grad)
    by_row = ring.grad_along_col(both)
    outer, weight = outer_call(
        lo, hi, after(left, both), lab, right.swapaxes(1, 2), wide, grad
    )
    by_row = after(by_row, weight)
    share = ring.weight_over_row(weight)
    left_grad = left_grad_call(lo, hi, after(back, weight), lab, right, tall)
    share = after(share, left_grad)
    by_row = after(by_row, left_grad)
    grad_right = ring.grad_along_x(by_row)

    total = left_grad[:here].astype(F32)
    for k in range(1, n_col):
        total += ring.col_shift(left_grad[k * here : (k + 1) * here], n_col - k).astype(F32)
    adjoint_first = total.astype(BF16)
    pair = jnp.dot(after(outer, left_grad, share), w, preferred_element_type=F32) + final_offset
    pair_update = pair.astype(BF16).reshape(rows, cols, width)
    mine = after(ring.weight_over_col(share), pair_update)
    grad_w_out = ring.weight_to_all(mine).astype(F32) / (n_row * rows)
    return pair_update, adjoint_first, grad_right, grad_w_out


def solution(mesh):
    in_specs = (
        P(("parts", "col"), "row", None),
        P(),
        P(),
        P(),
        P(),
        P(),
        P(),
        P("parts"),
        P("parts", None),
        P(("parts", "row"), "col", None),
    )
    out_specs = (
        P(("parts", "row"), "col", None),
        P(("parts", "col"), "row"),
        P(("parts", "col"), "row"),
        P("parts", None),
    )

    def body(*args):
        return shards(mesh.shape["row"], mesh.shape["col"], *args)

    return jax.shard_map(body, mesh=mesh, in_specs=in_specs, out_specs=out_specs, check_vma=False)
```

time: 134 us -> 133 us (level); the launches traced: 134 us -> 132 us
  Pallas kernels: 60.7 us -> 51.5 us
  matrix products: 0.8 us -> 7.51 us
  waiting for transfers between devices: 18.3 us -> 12.5 us
  other arithmetic: 10.8 us -> 14.8 us
  local copies, waits for them, and re-layouts: 8.78 us -> 10.3 us
    dot_general x0 -> x1, matrix products: none -> 6.71 us  [shards(): jnp.dot(after(outer, left_grad, share), w, preferred_element_type=F32)]
    pallas_call x1, Pallas kernels: 16 us -> 11.1 us  [right_grad_call(): pl.pallas_call(right_grad_body, grid_spec=pltpu.PrefetchScalarGridSpec(nu...]
    ppermute x9, waiting for transfers between devices: 8.92 us -> 4.62 us  [col_shift(): return lax.ppermute(value, 'col', [((t + k) % n, t) for t in range(n)])]
    pallas_call x1, Pallas kernels: 23 us -> 19.9 us  [outer_call(): pl.pallas_call(outer_body, grid_spec=pltpu.PrefetchScalarGridSpec(num_sca...]
    ppermute x9, starting transfers between devices: 13.5 us -> 15.9 us  [col_shift(): return lax.ppermute(value, 'col', [((t + k) % n, t) for t in range(n)])]
    ppermute x8, starting transfers between devices: 6.55 us -> 4.19 us  [row_shift(): return lax.ppermute(value, 'row', [((t + k) % n, t) for t in range(n)])]
    another operation x0 -> x8, other arithmetic: none -> 2.12 us  [the longest x3 1.32 us: shards(): right = jnp.stack([right, (right.astype(F32) / 3).astype(BF16)])]
    transpose x0 -> x2, other arithmetic: none -> 1.57 us  [the longest x1 0.83 us: shards(): plain = weight.reshape(cols, pairs, 2 * seqs).transpose(1, 0, 2)]
  transfers between devices with their start and end apart: 25 -> 25, of which waited for: 9 -> 5; matrix products, arithmetic and copies ran while one was open for 10% -> 19% of each run, Pallas kernels for 45% -> 31%
where the time goes in v3:
time: 133 us; the launch traced here: 132 us
  Pallas kernels  51.5 us (39%)
  starting transfers between devices  33.7 us (25%)
  other arithmetic  14.8 us (11%)
  waiting for transfers between devices  12.5 us (9%)
  local copies, waits for them, and re-layouts  10.3 us (8%)
  matrix products  7.51 us (6%)
    pallas_call x1, Pallas kernels, outer_call(): pl.pallas_call(outer_body, grid_spec=pltpu.PrefetchScalarGridSpec(num_sca...  19.9 us
    ppermute x9, starting transfers between devices, col_shift(): return lax.ppermute(value, 'col', [((t + k) % n, t) for t in range(n)])  15.9 us
    ppermute x6, starting transfers between devices, along_col(): return lax.ppermute(value, ('row', 'col'), pairs)  13.5 us
    pallas_call x1, Pallas kernels, right_grad_call(): pl.pallas_call(right_grad_body, grid_spec=pltpu.PrefetchScalarGridSpec(nu...  11.1 us
    pallas_call x1, Pallas kernels, left_grad_call(): pl.pallas_call(left_grad_body, grid_spec=pltpu.PrefetchScalarGridSpec(num...  10.7 us
    pallas_call x1, Pallas kernels, back_call(): pl.pallas_call(back_body, grid=(rows // step,), in_specs=[pl.BlockSpec((s...  9.81 us
    dot_general x1, matrix products, shards(): jnp.dot(after(outer, left_grad, share), w, preferred_element_type=F32)  6.71 us
    ppermute x6, waiting for transfers between devices, along_col(): return lax.ppermute(value, ('row', 'col'), pairs)  5.24 us
  transfers between devices with their start and end apart: 25, of which 5 were waited for; matrix products, arithmetic and copies ran while one was open for 19% of the time, Pallas kernels for 31%

profile of v3, /device:TPU:0, one launch (start us, length us, event | category | flops | bytes accessed | tf_op | source)
XLA Modules:
  0.0 131.6 jit_solution(16819545384689700846)
XLA Ops:
  0.7 1.7 %convert_reduce_fusion = f32[32,64]{1,0:T(8,128)S(1)} fusion(bf16[32,64,256]{2,1,0:T(8,128)(2,1)} %param.10), kind=kLoop, calls=%fused_computation.3 | loop fusion | flops 1046528 | bytes 1056768 | tf_op jit(solution)/shard_map/reduce_sum | solution.py:20
  2.3 1.9 %fusion.3 = f32[32,64]{1,0:T(8,128)S(1)} fusion(bf16[32,64,256]{2,1,0:T(8,128)(2,1)} %param.10, f32[32,64]{1,0:T(8,128)S(1)} %broadcast_multiply_fusion), kind=kLoop, calls=%fused_computation.8 | loop fusion | flops 2095104 | bytes 1064960 | tf_op jit(solution)/shard_map/reduce_sum | solution.py:21
  6.3 5.1 %collective-permute-start = (bf16[32,2048]{1,0:T(8,128)(2,1)S(1)}, bf16[32,2048]{1,0:T(8,128)(2,1)S(1)}, u32[]{:S(2)}, u32[]{:S(2)}) collective-permute-start(bf16[32,2048]{1,0:T(8,128)(2,1)S(1)} %reshape.209), channel_id=1, source_target_pairs={{1,0},{2,1},{3,2},{0,3},{5,4},{6,5},{7,6},{4,7},{9,8},{10,9},{11,1... | collective-permute-start | bytes 393224 | tf_op jit(solution)/shard_map/ppermute | solution.py:346
  11.4 1.0 collective-permute-start.2
  13.5 1.6 %collective-permute-start.3 = (bf16[32,2048]{1,0:T(8,128)(2,1)S(1)}, bf16[32,2048]{1,0:T(8,128)(2,1)S(1)}, u32[]{:S(2)}, u32[]{:S(2)}) collective-permute-start(bf16[32,2048]{1,0:T(8,128)(2,1)S(1)} %reshape.211), channel_id=1, source_target_pairs={{8,0},{12,4},{0,8},{4,12},{9,1},{13,5},{1,9},{5,13},{10,2},{14,6},... | collective-permute-start | bytes 393224 | tf_op jit(solution)/shard_map/ppermute | solution.py:350
  21.9 9.8 %back.1.back_ref = bf16[8,2048,256]{2,1,0:T(8,128)(2,1)} custom-call(bf16[64,64,128]{2,1,0:T(8,128)(2,1)} %grad_ref.2, bf16[128,1024]{1,0:T(8,128)(2,1)} %bitcast.115), custom_call_target="tpu_custom_call" | custom-call | flops 21474836480 | bytes 8388608 | tf_op jit(solution)/shard_map/back/pallas_call | solution.py:74
  32.6 11.1 %right_grad.1 = bf16[128,2048]{1,0:T(8,128)(2,1)} custom-call(s32[8]{0:T(128)} %get-tuple-element.44.lo_ref, s32[8]{0:T(128)} %get-tuple-element.43.hi_ref, bf16[8,2048,256]{2,1,0:T(8,128)(2,1)} %back.1.back_ref, bf16[128,2048]{1,0:T(8,128)(2,1)} %copy-done.5, s32[1,2048]{1,0:T(1,128)} %broadcast_in_dim_reshape.3.lab_ref, f32[4,64,256]{2,1,0:T(8,128)} %fusion.14.wide_ref), custom_call_target="tpu_custom_call" | custom-call | flops 21474836480 | bytes 8388608 | tf_op jit(solution)/shard_map/right_grad/pallas_call | solution.py:146
  43.7 1.4 %collective-permute-start.5 = (bf16[32,2048]{1,0:T(8,128)(2,1)S(1)}, bf16[32,2048]{1,0:T(8,128)(2,1)S(1)}, u32[]{:S(2)}, u32[]{:S(2)}) collective-permute-start(bf16[32,2048]{1,0:T(8,128)(2,1)S(1)} %get-tuple-element.39), channel_id=1, source_target_pairs={{1,0},{3,2},{4,7},{6,5},{9,8},{11,10},{12,15},{14,13},{17,16},{19,... | collective-permute-start | bytes 393224 | tf_op jit(solution)/shard_map/ppermute | solution.py:366
  45.2 3.8 %collective-permute-start.6 = (bf16[32,2048]{1,0:T(8,128)(2,1)S(1)}, bf16[32,2048]{1,0:T(8,128)(2,1)S(1)}, u32[]{:S(2)}, u32[]{:S(2)}) collective-permute-start(bf16[32,2048]{1,0:T(8,128)(2,1)S(1)} %get-tuple-element.40), channel_id=1, source_target_pairs={{0,2},{2,0},{5,7},{7,5},{8,10},{10,8},{13,15},{15,13},{16,18},{18,... | collective-permute-start | bytes 393224 | tf_op jit(solution)/shard_map/ppermute | solution.py:366
  49.0 1.3 collective-permute-start.7
  52.4 2.4 %collective-permute-done.6 = bf16[32,2048]{1,0:T(8,128)(2,1)S(1)} collective-permute-done((bf16[32,2048]{1,0:T(8,128)(2,1)S(1)}, bf16[32,2048]{1,0:T(8,128)(2,1)S(1)}, u32[]{:S(2)}, u32[]{:S(2)}) %collective-permute-start.6) | collective-permute-done | bytes 131104 | tf_op jit(solution)/shard_map/ppermute | solution.py:366
  54.8 2.8 %collective-permute-done.7 = bf16[32,2048]{1,0:T(8,128)(2,1)S(1)} collective-permute-done((bf16[32,2048]{1,0:T(8,128)(2,1)S(1)}, bf16[32,2048]{1,0:T(8,128)(2,1)S(1)}, u32[]{:S(2)}, u32[]{:S(2)}) %collective-permute-start.7) | collective-permute-done | bytes 131104 | tf_op jit(solution)/shard_map/ppermute | solution.py:366
  58.0 1.3 collective-permute-start.15
  59.3 4.2 %collective-permute-start.16 = (bf16[32,2048]{1,0:T(8,128)(2,1)S(1)}, bf16[32,2048]{1,0:T(8,128)(2,1)S(1)}, u32[]{:S(2)}, u32[]{:S(2)}) collective-permute-start(bf16[32,2048]{1,0:T(8,128)(2,1)S(1)} %get-tuple-element.29), channel_id=1, source_target_pairs={{2,0},{0,2},{7,5},{5,7},{10,8},{8,10},{15,13},{13,15},{18,16},{16,... | collective-permute-start | bytes 393224 | tf_op jit(solution)/shard_map/ppermute | solution.py:366
  63.5 1.5 %collective-permute-start.17 = (bf16[32,2048]{1,0:T(8,128)(2,1)S(1)}, bf16[32,2048]{1,0:T(8,128)(2,1)S(1)}, u32[]{:S(2)}, u32[]{:S(2)}) collective-permute-start(bf16[32,2048]{1,0:T(8,128)(2,1)S(1)} %get-tuple-element.28), channel_id=1, source_target_pairs={{2,1},{0,3},{5,4},{7,6},{10,9},{8,11},{13,12},{15,14},{18,17},{16,... | collective-permute-start | bytes 393224 | tf_op jit(solution)/shard_map/ppermute | solution.py:366
  65.3 1.1 pad_maximum_fusion
  66.4 1.3 copy.65.right_ref
  67.7 19.9 %outer.1 = (bf16[4096,1024]{1,0:T(8,128)(2,1)}, f32[1024,128]{1,0:T(8,128)}) custom-call(s32[8]{0:T(128)} %get-tuple-element.44.lo_ref, s32[8]{0:T(128)} %get-tuple-element.43.hi_ref, bf16[128,2048]{1,0:T(8,128)(2,1)} %copy-done.5, s32[1,2048]{1,0:T(1,128)} %broadcast_in_dim_reshape.3.lab_ref, bf16[2,2048,128]{2,1,0:T(8,128)(2,1)} %copy.65.right_ref, ...), custom_call_target="tpu_custom_call" | custom-call | flops 42949672960 | bytes 8388608 | tf_op jit(solution)/shard_map/outer/pallas_call | solution.py:298
  87.6 1.1 convert_element_type.188
  88.8 10.7 %left_grad.1 = bf16[128,2048]{1,0:T(8,128)(2,1)} custom-call(s32[8]{0:T(128)} %get-tuple-element.44.lo_ref, s32[8]{0:T(128)} %get-tuple-element.43.hi_ref, bf16[8,2048,256]{2,1,0:T(8,128)(2,1)} %back.1.back_ref, s32[1,2048]{1,0:T(1,128)} %broadcast_in_dim_reshape.3.lab_ref, bf16[2,128,2048]{2,1,0:T(8,128)(2,1)} %get-tuple-element.26.right_ref, ...), custom_call_target="tpu_custom_call" | custom-call | flops 21474836480 | bytes 8388608 | tf_op jit(solution)/shard_map/left_grad/pallas_call | solution.py:209
  99.5 1.1 fusion.34
  101.1 3.6 %collective-permute-start.12 = (bf16[32,2048]{1,0:T(8,128)(2,1)S(1)}, bf16[32,2048]{1,0:T(8,128)(2,1)S(1)}, u32[]{:S(2)}, u32[]{:S(2)}) collective-permute-start(bf16[32,2048]{1,0:T(8,128)(2,1)S(1)} %get-tuple-element.31), channel_id=1, source_target_pairs={{3,0},{0,1},{1,2},{2,3},{7,4},{4,5},{5,6},{6,7},{11,8},{8,9},{9,10... | collective-permute-start | bytes 393224 | tf_op jit(solution)/shard_map/ppermute | solution.py:346
  105.2 2.1 %collective-permute-start.14 = (bf16[32,2048]{1,0:T(8,128)(2,1)S(1)}, bf16[32,2048]{1,0:T(8,128)(2,1)S(1)}, u32[]{:S(2)}, u32[]{:S(2)}) collective-permute-start(bf16[32,2048]{1,0:T(8,128)(2,1)S(1)} %get-tuple-element.32), channel_id=1, source_target_pairs={{1,0},{2,1},{3,2},{0,3},{5,4},{6,5},{7,6},{4,7},{9,8},{10,9},{11,1... | collective-permute-start | bytes 393224 | tf_op jit(solution)/shard_map/ppermute | solution.py:346
  108.5 2.1 %collective-permute-start.19 = (bf16[256,128]{1,0:T(8,128)(2,1)S(1)}, bf16[256,128]{1,0:T(8,128)(2,1)S(1)}, u32[]{:S(2)}, u32[]{:S(2)}) collective-permute-start(bf16[256,128]{1,0:T(8,128)(2,1)S(1)} %convert_element_type.202), channel_id=1, source_target_pairs={{1,0},{2,1},{3,2},{0,3},{5,4},{6,5},{7,6},{4,7},{9,8},{10,9},{11,1... | collective-permute-start | bytes 196616 | tf_op jit(solution)/shard_map/ppermute | solution.py:346
  110.6 6.7 %fusion = bf16[4096,128]{1,0:T(8,128)(2,1)} fusion(bf16[4096,1024]{1,0:T(8,128)(2,1)} %get-tuple-element.22, bf16[1024,128]{1,0:T(8,128)(2,1)S(1)} %bitcast.109, f32[128]{0:T(128)S(1)} %copy-done.11), kind=kOutput, calls=%fused_computation.1 | convolution fusion | flops 1074790400 | bytes 9699840 | tf_op jit(solution)/shard_map/dot_general | solution.py:501
  117.4 1.5 %collective-permute-start.21 = (bf16[256,128]{1,0:T(8,128)(2,1)S(1)}, bf16[256,128]{1,0:T(8,128)(2,1)S(1)}, u32[]{:S(2)}, u32[]{:S(2)}) collective-permute-start(bf16[256,128]{1,0:T(8,128)(2,1)S(1)} %convert_element_type.202), channel_id=1, source_target_pairs={{3,0},{0,1},{1,2},{2,3},{7,4},{4,5},{5,6},{6,7},{11,8},{8,9},{9,10... | collective-permute-start | bytes 196616 | tf_op jit(solution)/shard_map/ppermute | solution.py:346
  119.0 1.6 %add_convert_fusion.1 = bf16[32,2048]{1,0:T(8,128)(2,1)} fusion(bf16[32,2048]{1,0:T(8,128)(2,1)S(1)} %collective-permute-done.14, bf16[32,2048]{1,0:T(8,128)(2,1)S(1)} %collective-permute-done.13, bf16[32,2048]{1,0:T(8,128)(2,1)S(1)} %collective-permute-done.12, bf16[128,2048]{1,0:T(8,128)(2,1)} %left_grad.1), kind=kLoop, calls=%fused_computation.45 | loop fusion | flops 524288 | bytes 655360 | tf_op jit(solution)/shard_map/convert_element_type | solution.py:500
  120.6 4.6 %collective-permute-done.20 = bf16[256,128]{1,0:T(8,128)(2,1)S(1)} collective-permute-done((bf16[256,128]{1,0:T(8,128)(2,1)S(1)}, bf16[256,128]{1,0:T(8,128)(2,1)S(1)}, u32[]{:S(2)}, u32[]{:S(2)}) %collective-permute-start.20) | collective-permute-done | bytes 65568 | tf_op jit(solution)/shard_map/ppermute | solution.py:346
  125.7 1.4 %collective-permute-start.24 = (bf16[256,128]{1,0:T(8,128)(2,1)S(1)}, bf16[256,128]{1,0:T(8,128)(2,1)S(1)}, u32[]{:S(2)}, u32[]{:S(2)}) collective-permute-start(bf16[256,128]{1,0:T(8,128)(2,1)S(1)} %add_convert_fusion.2), channel_id=1, source_target_pairs={{4,0},{8,4},{12,8},{0,12},{5,1},{9,5},{13,9},{1,13},{6,2},{10,6},{... | collective-permute-start | bytes 196616 | tf_op jit(solution)/shard_map/ppermute | solution.py:350
  127.7 1.3 collective-permute-done.22
  129.0 1.3 collective-permute-done.23
  130.3 1.3 convert_multiply_fusion
  (130 shorter events, 16.8 us)
Async XLA Ops:
  0.6 4.4 %copy-start = (bf16[256,32]{0,1:T(8,128)(2,1)S(1)}, bf16[256,32]{0,1:T(8,128)(2,1)}, u32[]{:S(2)}) copy-start(bf16[256,32]{0,1:T(8,128)(2,1)} %param.13) | copy-start | bytes 49156
  4.3 8.2 %copy-start.6 = (bf16[256,32]{0,1:T(8,128)(2,1)S(1)}, bf16[256,32]{0,1:T(8,128)(2,1)}, u32[]{:S(2)}) copy-start(bf16[256,32]{0,1:T(8,128)(2,1)} %param.14) | copy-start | bytes 49156
  5.4 9.6 %copy-start.10 = (s32[256]{0:T(256)S(1)}, s32[256]{0:T(256)}, u32[]{:S(2)}) copy-start(s32[256]{0:T(256)} %param.17) | copy-start | bytes 3076
  5.4 9.7 %copy-start.7 = (s32[8,8]{1,0:T(8,128)S(1)}, s32[8,8]{1,0:T(8,128)}, u32[]{:S(2)}) copy-start(s32[8,8]{1,0:T(8,128)} %param.18) | copy-start | bytes 772
  6.3 25.4 %collective-permute-start = (bf16[32,2048]{1,0:T(8,128)(2,1)S(1)}, bf16[32,2048]{1,0:T(8,128)(2,1)S(1)}, u32[]{:S(2)}, u32[]{:S(2)}) collective-permute-start(bf16[32,2048]{1,0:T(8,128)(2,1)S(1)} %reshape.209), channel_id=1, source_target_pairs={{1,0},{2,1},{3,2},{0,3},{5,4},{6,5},{7,6},{4,7},{9,8},{10,9},{11,1... | collective-permute-start | bytes 393224 | tf_op jit(solution)/shard_map/ppermute | solution.py:346
  11.4 20.3 %collective-permute-start.1 = (bf16[32,2048]{1,0:T(8,128)(2,1)S(1)}, bf16[32,2048]{1,0:T(8,128)(2,1)S(1)}, u32[]{:S(2)}, u32[]{:S(2)}) collective-permute-start(bf16[32,2048]{1,0:T(8,128)(2,1)S(1)} %reshape.209), channel_id=1, source_target_pairs={{2,0},{3,1},{0,2},{1,3},{6,4},{7,5},{4,6},{5,7},{10,8},{11,9},{8,1... | collective-permute-start | bytes 393224 | tf_op jit(solution)/shard_map/ppermute | solution.py:346
  11.4 20.3 %collective-permute-start.2 = (bf16[32,2048]{1,0:T(8,128)(2,1)S(1)}, bf16[32,2048]{1,0:T(8,128)(2,1)S(1)}, u32[]{:S(2)}, u32[]{:S(2)}) collective-permute-start(bf16[32,2048]{1,0:T(8,128)(2,1)S(1)} %reshape.209), channel_id=1, source_target_pairs={{3,0},{0,1},{1,2},{2,3},{7,4},{4,5},{5,6},{6,7},{11,8},{8,9},{9,10... | collective-permute-start | bytes 393224 | tf_op jit(solution)/shard_map/ppermute | solution.py:346
  13.5 8.2 %collective-permute-start.3 = (bf16[32,2048]{1,0:T(8,128)(2,1)S(1)}, bf16[32,2048]{1,0:T(8,128)(2,1)S(1)}, u32[]{:S(2)}, u32[]{:S(2)}) collective-permute-start(bf16[32,2048]{1,0:T(8,128)(2,1)S(1)} %reshape.211), channel_id=1, source_target_pairs={{8,0},{12,4},{0,8},{4,12},{9,1},{13,5},{1,9},{5,13},{10,2},{14,6},... | collective-permute-start | bytes 393224 | tf_op jit(solution)/shard_map/ppermute | solution.py:350
  21.9 9.8 %copy-start.4 = (bf16[128,2048]{1,0:T(8,128)(2,1)S(1)}, bf16[128,2048]{1,0:T(8,128)(2,1)}, u32[]{:S(2)}) copy-start(bf16[128,2048]{1,0:T(8,128)(2,1)} %constant_dynamic-update-slice_fusion.3) | copy-start | bytes 1572868
  43.7 14.1 %copy-start.2 = (bf16[128,2048]{1,0:T(8,128)(2,1)S(1)}, bf16[128,2048]{1,0:T(8,128)(2,1)}, u32[]{:S(2)}) copy-start(bf16[128,2048]{1,0:T(8,128)(2,1)} %right_grad.1) | copy-start | bytes 1572868
  43.7 14.1 %collective-permute-start.4 = (bf16[128,2048]{1,0:T(8,128)(2,1)}, bf16[128,2048]{1,0:T(8,128)(2,1)S(1)}, u32[]{:S(2)}, u32[]{:S(2)}) collective-permute-start(bf16[128,2048]{1,0:T(8,128)(2,1)} %right_grad.1), channel_id=1, source_target_pairs={{4,0},{0,4},{12,8},{8,12},{5,1},{1,5},{13,9},{9,13},{6,2},{2,6},{1... | collective-permute-start | bytes 1572872 | tf_op jit(solution)/shard_map/ppermute | solution.py:356
  43.7 8.7 %collective-permute-start.5 = (bf16[32,2048]{1,0:T(8,128)(2,1)S(1)}, bf16[32,2048]{1,0:T(8,128)(2,1)S(1)}, u32[]{:S(2)}, u32[]{:S(2)}) collective-permute-start(bf16[32,2048]{1,0:T(8,128)(2,1)S(1)} %get-tuple-element.39), channel_id=1, source_target_pairs={{1,0},{3,2},{4,7},{6,5},{9,8},{11,10},{12,15},{14,13},{17,16},{19,... | collective-permute-start | bytes 393224 | tf_op jit(solution)/shard_map/ppermute | solution.py:366
  45.2 9.7 %collective-permute-start.6 = (bf16[32,2048]{1,0:T(8,128)(2,1)S(1)}, bf16[32,2048]{1,0:T(8,128)(2,1)S(1)}, u32[]{:S(2)}, u32[]{:S(2)}) collective-permute-start(bf16[32,2048]{1,0:T(8,128)(2,1)S(1)} %get-tuple-element.40), channel_id=1, source_target_pairs={{0,2},{2,0},{5,7},{7,5},{8,10},{10,8},{13,15},{15,13},{16,18},{18,... | collective-permute-start | bytes 393224 | tf_op jit(solution)/shard_map/ppermute | solution.py:366
  49.0 8.7 %collective-permute-start.7 = (bf16[32,2048]{1,0:T(8,128)(2,1)S(1)}, bf16[32,2048]{1,0:T(8,128)(2,1)S(1)}, u32[]{:S(2)}, u32[]{:S(2)}) collective-permute-start(bf16[32,2048]{1,0:T(8,128)(2,1)S(1)} %get-tuple-element.37), channel_id=1, source_target_pairs={{1,2},{3,0},{4,5},{6,7},{9,10},{11,8},{12,13},{14,15},{17,18},{19,... | collective-permute-start | bytes 393224 | tf_op jit(solution)/shard_map/ppermute | solution.py:366
  57.7 7.4 %collective-permute-start.8 = (bf16[128,2048]{1,0:T(8,128)(2,1)S(1)}, bf16[128,2048]{1,0:T(8,128)(2,1)S(1)}, u32[]{:S(2)}, u32[]{:S(2)}) collective-permute-start(bf16[128,2048]{1,0:T(8,128)(2,1)S(1)} %pad_maximum_fusion.1), channel_id=1, source_target_pairs={{4,0},{0,4},{12,8},{8,12},{5,1},{1,5},{13,9},{9,13},{6,2},{2,6},{1... | collective-permute-start | bytes 1572872 | tf_op jit(solution)/shard_map/ppermute | solution.py:356
  58.0 42.6 %collective-permute-start.15 = (bf16[32,2048]{1,0:T(8,128)(2,1)S(1)}, bf16[32,2048]{1,0:T(8,128)(2,1)S(1)}, u32[]{:S(2)}, u32[]{:S(2)}) collective-permute-start(bf16[32,2048]{1,0:T(8,128)(2,1)S(1)} %get-tuple-element.30), channel_id=1, source_target_pairs={{0,1},{2,3},{7,4},{5,6},{8,9},{10,11},{15,12},{13,14},{16,17},{18,... | collective-permute-start | bytes 393224 | tf_op jit(solution)/shard_map/ppermute | solution.py:366
  59.3 41.8 %collective-permute-start.16 = (bf16[32,2048]{1,0:T(8,128)(2,1)S(1)}, bf16[32,2048]{1,0:T(8,128)(2,1)S(1)}, u32[]{:S(2)}, u32[]{:S(2)}) collective-permute-start(bf16[32,2048]{1,0:T(8,128)(2,1)S(1)} %get-tuple-element.29), channel_id=1, source_target_pairs={{2,0},{0,2},{7,5},{5,7},{10,8},{8,10},{15,13},{13,15},{18,16},{16,... | collective-permute-start | bytes 393224 | tf_op jit(solution)/shard_map/ppermute | solution.py:366
  63.5 41.2 %collective-permute-start.17 = (bf16[32,2048]{1,0:T(8,128)(2,1)S(1)}, bf16[32,2048]{1,0:T(8,128)(2,1)S(1)}, u32[]{:S(2)}, u32[]{:S(2)}) collective-permute-start(bf16[32,2048]{1,0:T(8,128)(2,1)S(1)} %get-tuple-element.28), channel_id=1, source_target_pairs={{2,1},{0,3},{5,4},{7,6},{10,9},{8,11},{13,12},{15,14},{18,17},{16,... | collective-permute-start | bytes 393224 | tf_op jit(solution)/shard_map/ppermute | solution.py:366
  88.7 16.5 %collective-permute-start.10 = (bf16[256,128]{1,0:T(8,128)(2,1)S(1)}, bf16[256,128]{1,0:T(8,128)(2,1)S(1)}, u32[]{:S(2)}, u32[]{:S(2)}) collective-permute-start(bf16[256,128]{1,0:T(8,128)(2,1)S(1)} %get-tuple-element.36), channel_id=1, source_target_pairs={{8,0},{12,4},{0,8},{4,12},{9,1},{13,5},{1,9},{5,13},{10,2},{14,6},... | collective-permute-start | bytes 196616 | tf_op jit(solution)/shard_map/ppermute | solution.py:350
  88.8 18.5 %collective-permute-start.11 = (bf16[256,128]{1,0:T(8,128)(2,1)S(1)}, bf16[256,128]{1,0:T(8,128)(2,1)S(1)}, u32[]{:S(2)}, u32[]{:S(2)}) collective-permute-start(bf16[256,128]{1,0:T(8,128)(2,1)S(1)} %get-tuple-element.35), channel_id=1, source_target_pairs={{4,0},{8,4},{12,8},{0,12},{5,1},{9,5},{13,9},{1,13},{6,2},{10,6},{... | collective-permute-start | bytes 196616 | tf_op jit(solution)/shard_map/ppermute | solution.py:350
  99.5 11.1 %copy-start.11 = (f32[128]{0:T(128)S(1)}, f32[128]{0:T(128)}, u32[]{:S(2)}) copy-start(f32[128]{0:T(128)} %param.16) | copy-start | bytes 1540
  100.6 7.0 %collective-permute-start.9 = (bf16[256,128]{1,0:T(8,128)(2,1)S(1)}, bf16[256,128]{1,0:T(8,128)(2,1)S(1)}, u32[]{:S(2)}, u32[]{:S(2)}) collective-permute-start(bf16[256,128]{1,0:T(8,128)(2,1)S(1)} %get-tuple-element.34), channel_id=1, source_target_pairs={{12,0},{0,4},{4,8},{8,12},{13,1},{1,5},{5,9},{9,13},{14,2},{2,6},{... | collective-permute-start | bytes 196616 | tf_op jit(solution)/shard_map/ppermute | solution.py:350
  101.1 16.2 %collective-permute-start.12 = (bf16[32,2048]{1,0:T(8,128)(2,1)S(1)}, bf16[32,2048]{1,0:T(8,128)(2,1)S(1)}, u32[]{:S(2)}, u32[]{:S(2)}) collective-permute-start(bf16[32,2048]{1,0:T(8,128)(2,1)S(1)} %get-tuple-element.31), channel_id=1, source_target_pairs={{3,0},{0,1},{1,2},{2,3},{7,4},{4,5},{5,6},{6,7},{11,8},{8,9},{9,10... | collective-permute-start | bytes 393224 | tf_op jit(solution)/shard_map/ppermute | solution.py:346
  104.7 12.7 %collective-permute-start.13 = (bf16[32,2048]{1,0:T(8,128)(2,1)S(1)}, bf16[32,2048]{1,0:T(8,128)(2,1)S(1)}, u32[]{:S(2)}, u32[]{:S(2)}) collective-permute-start(bf16[32,2048]{1,0:T(8,128)(2,1)S(1)} %get-tuple-element.33), channel_id=1, source_target_pairs={{2,0},{3,1},{0,2},{1,3},{6,4},{7,5},{4,6},{5,7},{10,8},{11,9},{8,1... | collective-permute-start | bytes 393224 | tf_op jit(solution)/shard_map/ppermute | solution.py:346
  105.2 13.8 %collective-permute-start.14 = (bf16[32,2048]{1,0:T(8,128)(2,1)S(1)}, bf16[32,2048]{1,0:T(8,128)(2,1)S(1)}, u32[]{:S(2)}, u32[]{:S(2)}) collective-permute-start(bf16[32,2048]{1,0:T(8,128)(2,1)S(1)} %get-tuple-element.32), channel_id=1, source_target_pairs={{1,0},{2,1},{3,2},{0,3},{5,4},{6,5},{7,6},{4,7},{9,8},{10,9},{11,1... | collective-permute-start | bytes 393224 | tf_op jit(solution)/shard_map/ppermute | solution.py:346
  107.3 19.7 %collective-permute-start.18 = (bf16[32,2048]{1,0:T(8,128)(2,1)S(1)}, bf16[32,2048]{1,0:T(8,128)(2,1)S(1)}, u32[]{:S(2)}, u32[]{:S(2)}) collective-permute-start(bf16[32,2048]{1,0:T(8,128)(2,1)S(1)} %slice_bitcast_fusion), channel_id=1, source_target_pairs={{8,0},{12,4},{0,8},{4,12},{9,1},{13,5},{1,9},{5,13},{10,2},{14,6},... | collective-permute-start | bytes 393224 | tf_op jit(solution)/shard_map/ppermute | solution.py:350
  108.5 12.1 %collective-permute-start.19 = (bf16[256,128]{1,0:T(8,128)(2,1)S(1)}, bf16[256,128]{1,0:T(8,128)(2,1)S(1)}, u32[]{:S(2)}, u32[]{:S(2)}) collective-permute-start(bf16[256,128]{1,0:T(8,128)(2,1)S(1)} %convert_element_type.202), channel_id=1, source_target_pairs={{1,0},{2,1},{3,2},{0,3},{5,4},{6,5},{7,6},{4,7},{9,8},{10,9},{11,1... | collective-permute-start | bytes 196616 | tf_op jit(solution)/shard_map/ppermute | solution.py:346
  117.3 7.9 %collective-permute-start.20 = (bf16[256,128]{1,0:T(8,128)(2,1)S(1)}, bf16[256,128]{1,0:T(8,128)(2,1)S(1)}, u32[]{:S(2)}, u32[]{:S(2)}) collective-permute-start(bf16[256,128]{1,0:T(8,128)(2,1)S(1)} %convert_element_type.202), channel_id=1, source_target_pairs={{2,0},{3,1},{0,2},{1,3},{6,4},{7,5},{4,6},{5,7},{10,8},{11,9},{8,1... | collective-permute-start | bytes 196616 | tf_op jit(solution)/shard_map/ppermute | solution.py:346
  117.4 7.8 %collective-permute-start.21 = (bf16[256,128]{1,0:T(8,128)(2,1)S(1)}, bf16[256,128]{1,0:T(8,128)(2,1)S(1)}, u32[]{:S(2)}, u32[]{:S(2)}) collective-permute-start(bf16[256,128]{1,0:T(8,128)(2,1)S(1)} %convert_element_type.202), channel_id=1, source_target_pairs={{3,0},{0,1},{1,2},{2,3},{7,4},{4,5},{5,6},{6,7},{11,8},{8,9},{9,10... | collective-permute-start | bytes 196616 | tf_op jit(solution)/shard_map/ppermute | solution.py:346
  125.2 3.8 %collective-permute-start.22 = (bf16[256,128]{1,0:T(8,128)(2,1)S(1)}, bf16[256,128]{1,0:T(8,128)(2,1)S(1)}, u32[]{:S(2)}, u32[]{:S(2)}) collective-permute-start(bf16[256,128]{1,0:T(8,128)(2,1)S(1)} %add_convert_fusion.2), channel_id=1, source_target_pairs={{12,0},{0,4},{4,8},{8,12},{13,1},{1,5},{5,9},{9,13},{14,2},{2,6},{... | collective-permute-start | bytes 196616 | tf_op jit(solution)/shard_map/ppermute | solution.py:350
  125.4 5.0 %collective-permute-start.23 = (bf16[256,128]{1,0:T(8,128)(2,1)S(1)}, bf16[256,128]{1,0:T(8,128)(2,1)S(1)}, u32[]{:S(2)}, u32[]{:S(2)}) collective-permute-start(bf16[256,128]{1,0:T(8,128)(2,1)S(1)} %add_convert_fusion.2), channel_id=1, source_target_pairs={{8,0},{12,4},{0,8},{4,12},{9,1},{13,5},{1,9},{5,13},{10,2},{14,6},... | collective-permute-start | bytes 196616 | tf_op jit(solution)/shard_map/ppermute | solution.py:350
  125.7 4.7 %collective-permute-start.24 = (bf16[256,128]{1,0:T(8,128)(2,1)S(1)}, bf16[256,128]{1,0:T(8,128)(2,1)S(1)}, u32[]{:S(2)}, u32[]{:S(2)}) collective-permute-start(bf16[256,128]{1,0:T(8,128)(2,1)S(1)} %add_convert_fusion.2), channel_id=1, source_target_pairs={{4,0},{8,4},{12,8},{0,12},{5,1},{9,5},{13,9},{1,13},{6,2},{10,6},{... | collective-permute-start | bytes 196616 | tf_op jit(solution)/shard_map/ppermute | solution.py:350
  (5 other events, 14.7 us)

commit v4 on v3

v4 whole, which is shorter than its diff:
```python
import jax
import jax.numpy as jnp
from jax import lax
from jax.experimental import pallas as pl
from jax.experimental.pallas import tpu as pltpu
from jax.sharding import PartitionSpec as P


PROJ = 32
CHAINS = 8
LANES = 128
PER_TILE = LANES // PROJ
WIDE = 256
F32 = jnp.float32
BF16 = jnp.bfloat16


def swap_blocks(parts):
    lane = lax.broadcasted_iota(jnp.int32, parts[0].shape, 1)
    for bit in (2, 1):
        shift = bit * PROJ
        low = (lane & shift) == 0
        out = list(parts)
        for p in range(PER_TILE):
            if not p & bit:
                a, b = parts[p], parts[p | bit]
                out[p] = jnp.where(low, a, pltpu.roll(b, shift, 1))
                out[p | bit] = jnp.where(low, pltpu.roll(a, LANES - shift, 1), b)
        parts = out
    return parts


def nt_dot(a, b):
    return lax.dot_general(a, b, (((1,), (1,)), ((), ())), preferred_element_type=F32)


def nn_dot(a, b):
    return lax.dot_general(a, b, (((1,), (0,)), ((), ())), preferred_element_type=F32)


def project_body(x_ref, gain_ref, shift_ref, w_ref, left_ref, right_ref, proj_ref, turn_ref, out_ref,
                 *, cols):
    here, rows, feats = x_ref.shape
    chunk = max(1, WIDE // rows)

    def norm(step, carry):
        x = x_ref[pl.ds(step * chunk, chunk)].astype(F32).reshape(chunk * rows, feats)
        center = x - jnp.mean(x, axis=-1, keepdims=True)
        spread = jnp.mean(center * center, axis=-1, keepdims=True)
        normed = center * lax.rsqrt(spread + 1e-05) * gain_ref[...] + shift_ref[...]
        at = pl.multiple_of(step * (chunk * rows), chunk * rows)
        proj_ref[pl.ds(at, chunk * rows)] = nn_dot(normed.astype(BF16), w_ref[...])
        return carry

    lax.fori_loop(0, here // chunk, norm, 0)

    lane = lax.broadcasted_iota(jnp.int32, (here, LANES), 1)
    for t in range(rows // PER_TILE):
        tile = proj_ref[pl.ds(t * PER_TILE, here, stride=rows)]
        for p in range(1, PER_TILE):
            part = proj_ref[pl.ds(t * PER_TILE + p, here, stride=rows)]
            tile = jnp.where(lane < p * PROJ, tile, pltpu.roll(part, p * PROJ, 1))
        left_ref[:, t * LANES : (t + 1) * LANES] = tile.astype(BF16)

    tiles = here * rows // LANES
    for t in range(tiles):
        flipped = proj_ref[t * LANES : (t + 1) * LANES].T
        turn_ref[t * PROJ : (t + 1) * PROJ] = flipped[PROJ : 2 * PROJ]
    seqs = LANES // rows
    per = LANES // cols
    lane = lax.broadcasted_iota(jnp.int32, (tiles, LANES), 1)
    for block in range(rows // cols):
        for t in range(PROJ // per):
            at = (block * (PROJ // per) + t) * LANES
            parts = [turn_ref[pl.ds(t * per + p, tiles, stride=PROJ)] for p in range(per)]
            for u in range(seqs):
                start = u * rows + block * cols
                tile = None
                for p, part in enumerate(parts):
                    amount = (p * cols - start) % LANES
                    part = pltpu.roll(part, amount, 1) if amount else part
                    tile = part if tile is None else jnp.where(lane < p * cols, tile, part)
                out_ref[pl.ds(u, tiles, stride=seqs), :] = tile
            right_ref[:, at : at + LANES] = out_ref[...].astype(BF16)


def project_call(x, gain, shift, w, cols):
    here, rows, _ = x.shape
    return pl.pallas_call(
        lambda *refs: project_body(*refs, cols=cols),
        out_shape=[jax.ShapeDtypeStruct((here, rows * PROJ), BF16)] * 2,
        scratch_shapes=[
            pltpu.VMEM((here * rows, LANES), F32),
            pltpu.VMEM((here * rows // LANES * PROJ, LANES), F32),
            pltpu.VMEM((here, LANES), F32),
        ],
        name="project",
    )(x, gain, shift, w)


def prep_body(at_ref, labels_ref, counts_ref, w_ref, lab_ref, tall_ref, wide_ref, plain_ref,
              w_out, wt_out, wide_w_ref, *, rows, cols, seqs):
    res = labels_ref.shape[1]
    labels = jnp.broadcast_to(labels_ref[...], (8, res))
    own = pltpu.roll(labels, (res - at_ref[0]) % res, 1)[:, :rows]
    spread = (
        lax.broadcasted_iota(jnp.int32, (rows, rows * PROJ), 1) // PROJ
        == lax.broadcasted_iota(jnp.int32, (rows, rows * PROJ), 0)
    )
    lab = nn_dot(own.astype(F32).astype(BF16), spread.astype(F32).astype(BF16))
    lab_ref[...] = lab[:1].astype(jnp.int32)

    there = pltpu.roll(labels, (res - at_ref[1]) % res, 1)[:, :LANES]
    there = jnp.where(lax.broadcasted_iota(jnp.int32, (8, LANES), 1) < cols, there, 0)
    reach = cols
    while reach < LANES:
        there = there + pltpu.roll(there, reach, 1)
        reach *= 2
    depth = jnp.zeros((CHAINS, LANES), jnp.int32)
    for b in range(CHAINS):
        depth += jnp.where(there == b, counts_ref[:, b : b + 1], 0)
    seq = (lax.broadcasted_iota(jnp.int32, (seqs, LANES), 0) + at_ref[2]) % seqs
    for a in range(CHAINS):
        deep = jnp.broadcast_to(depth[a : a + 1], (seqs, LANES))
        weight = jnp.where(seq < deep, 1.0 / deep.astype(F32), 0.0)
        three = deep % 3 == 0
        side = slice((a % 2) * seqs, (a % 2 + 1) * seqs)
        for x, part in enumerate((jnp.where(three, 0.0, weight), jnp.where(three, 3.0 * weight, 0.0))):
            tall_ref[a // 2, x, side] = part.astype(BF16)
            wide_ref[a // 2, x, :, side] = part.T[:cols].astype(BF16)
        plain_ref[a // 2, :, side] = weight.T[:cols]

    wide_w_ref[...] = w_ref[...].astype(F32)
    for t in range(PROJ // PER_TILE):
        for q in range(PER_TILE):
            e = t * PER_TILE + q
            w_out[e * PROJ : (e + 1) * PROJ] = wide_w_ref[pl.ds(e, PROJ, stride=PROJ)].astype(BF16)
        block = w_out[t * LANES : (t + 1) * LANES].astype(F32)
        wt_out[:, t * LANES : (t + 1) * LANES] = block.T.astype(BF16)


def prep_call(at, labels, counts, w, rows, cols, seqs):
    pairs = CHAINS // 2
    width = w.shape[1]
    vmem = pl.BlockSpec(memory_space=pltpu.VMEM)
    return pl.pallas_call(
        lambda *refs: prep_body(*refs, rows=rows, cols=cols, seqs=seqs),
        in_specs=[pl.BlockSpec(memory_space=pltpu.SMEM), vmem, vmem, vmem],
        out_specs=[vmem] * 6,
        out_shape=[
            jax.ShapeDtypeStruct((1, rows * PROJ), jnp.int32),
            jax.ShapeDtypeStruct((pairs, 2, 2 * seqs, LANES), BF16),
            jax.ShapeDtypeStruct((pairs, 2, cols, 2 * seqs), BF16),
            jax.ShapeDtypeStruct((pairs, cols, 2 * seqs), F32),
            jax.ShapeDtypeStruct(w.shape, BF16),
            jax.ShapeDtypeStruct((width, PROJ * PROJ), BF16),
        ],
        scratch_shapes=[pltpu.VMEM(w.shape, F32)],
        name="prep",
    )(at, labels[None, :], counts, w)


def cost(passes, span, total, seqs):
    return pl.CostEstimate(
        flops=4 * passes * span * total * seqs, bytes_accessed=2 * span * total, transcendentals=0
    )


def back_body(grad_ref, wt_ref, out_ref):
    rows, cols, width = grad_ref.shape
    block = grad_ref[...].reshape(rows * cols, width)
    for u in range(PROJ * PROJ // WIDE):
        prod = nn_dot(block, wt_ref[:, u * WIDE : (u + 1) * WIDE]).astype(BF16)
        for half in range(rows // PER_TILE):
            for t in range(WIDE // LANES):
                parts = [
                    prod[(half * PER_TILE + p) * cols : (half * PER_TILE + p + 1) * cols,
                         t * LANES : (t + 1) * LANES]
                    for p in range(PER_TILE)
                ]
                for q, part in enumerate(swap_blocks(parts)):
                    e = u * (WIDE // PROJ) + t * PER_TILE + q
                    out_ref[0, e * cols : (e + 1) * cols, half * LANES : (half + 1) * LANES] = part


def back_call(grad, wt):
    rows, cols, width = grad.shape
    step = WIDE // PROJ
    return pl.pallas_call(
        back_body,
        grid=(rows // step,),
        in_specs=[
            pl.BlockSpec((step, cols, width), lambda g: (g, 0, 0)),
            pl.BlockSpec((width, PROJ * PROJ), lambda g: (0, 0)),
        ],
        out_specs=pl.BlockSpec((1, PROJ * cols, WIDE), lambda g: (g, 0, 0)),
        out_shape=jax.ShapeDtypeStruct((rows // step, PROJ * cols, WIDE), BF16),
        compiler_params=pltpu.CompilerParams(dimension_semantics=("arbitrary",)),
        cost_estimate=cost(10, PROJ * cols, rows * PROJ, width),
        name="back",
    )(grad, wt)


def first_pair(at_ref, labels_ref, group):
    return labels_ref[at_ref[0] + group * (WIDE // PROJ)] // 2


def last_pair(at_ref, labels_ref, group):
    return labels_ref[at_ref[0] + (group + 1) * (WIDE // PROJ) - 1] // 2


def masked_left(left_ref, lab_ref, lb_ref, pair):
    seqs = left_ref.shape[0]
    for side in range(2):
        keep = (lab_ref[...] == 2 * pair + side).astype(F32).astype(BF16)
        lb_ref[side * seqs : (side + 1) * seqs] = left_ref[...] * keep


def right_grad_body(at_ref, labels_ref, back_ref, left_ref, lab_ref, wide_ref,
                    right_out, q_ref, lb_ref, flip_ref, turn_ref):
    g = pl.program_id(0)
    seqs = left_ref.shape[0]
    span = back_ref.shape[1]
    cols = span // PROJ
    last = pl.num_programs(0) - 1

    def over_pairs(fn):
        def step(pair, carry):
            fn(pair)
            return carry

        return step

    @pl.when(g == 0)
    def _():
        def clear(pair):
            q_ref[pair] = jnp.zeros(q_ref.shape[1:], F32)

        lax.fori_loop(first_pair(at_ref, labels_ref, 0), last_pair(at_ref, labels_ref, last) + 1, over_pairs(clear), 0)
        flip_ref[...] = jnp.zeros_like(flip_ref)

    def one_pair(pair):
        masked_left(left_ref, lab_ref, lb_ref, pair)
        q_ref[pair] += nt_dot(back_ref[0], lb_ref[...])

    lax.fori_loop(first_pair(at_ref, labels_ref, g), last_pair(at_ref, labels_ref, g) + 1, over_pairs(one_pair), 0)

    @pl.when(g == last)
    def _():
        def combine(pair):
            for e in range(PROJ):
                rows = slice(e * cols, (e + 1) * cols)
                both = q_ref[pair, rows] * wide_ref[pair]
                flip_ref[rows] += both[:, :seqs] + both[:, seqs:]

        lax.fori_loop(first_pair(at_ref, labels_ref, 0), last_pair(at_ref, labels_ref, last) + 1, over_pairs(combine), 0)
        for j in range(cols):
            turn_ref[j * PROJ : (j + 1) * PROJ] = flip_ref[pl.ds(j, PROJ, stride=cols)]
        for t in range(span // LANES):
            rows = slice(t * LANES, (t + 1) * LANES)
            right_out[:, rows] = turn_ref[rows].T.astype(BF16)


def right_grad_call(at, labels, back, left, lab, wide):
    groups, span, _ = back.shape
    total = groups * WIDE
    seqs = left.shape[0]
    whole = lambda shape: pl.BlockSpec(shape, lambda g, *_: (0,) * len(shape))
    return pl.pallas_call(
        right_grad_body,
        grid_spec=pltpu.PrefetchScalarGridSpec(
            num_scalar_prefetch=2,
            grid=(total // WIDE,),
            in_specs=[
                pl.BlockSpec((1, span, WIDE), lambda g, *_: (g, 0, 0)),
                pl.BlockSpec((seqs, WIDE), lambda g, *_: (0, g)),
                pl.BlockSpec((1, WIDE), lambda g, *_: (0, g)),
                whole(wide.shape),
            ],
            out_specs=whole((seqs, span)),
            scratch_shapes=[
                pltpu.VMEM((CHAINS // 2, span, 2 * seqs), F32),
                pltpu.VMEM((2 * seqs, WIDE), BF16),
                pltpu.VMEM((span, seqs), F32),
                pltpu.VMEM((span, seqs), F32),
            ],
        ),
        out_shape=jax.ShapeDtypeStruct((seqs, span), BF16),
        compiler_params=pltpu.CompilerParams(dimension_semantics=("arbitrary",)),
        cost_estimate=cost(10, span, total, seqs),
        name="right_grad",
    )(at, labels, back, left, lab, wide)


def left_grad_body(at_ref, labels_ref, back_ref, lab_ref, right_ref, tall_ref, left_out, rm_ref, part_ref):
    g = pl.program_id(0)
    seqs = right_ref.shape[0]
    span = back_ref.shape[1]

    last = pl.num_programs(0) - 1

    @pl.when(g == 0)
    def _():
        part_ref[...] = (right_ref[...].astype(F32) / 3).astype(BF16)

        def build(pair, carry):
            for side in range(2):
                row = side * seqs
                plain, third = tall_ref[pair, 0, row : row + seqs], tall_ref[pair, 1, row : row + seqs]
                for t in range(span // LANES):
                    lanes = slice(t * LANES, (t + 1) * LANES)
                    rm_ref[pair, row : row + seqs, lanes] = (
                        right_ref[:, lanes] * plain + part_ref[:, lanes] * third
                    )
            return carry

        lax.fori_loop(first_pair(at_ref, labels_ref, 0), last_pair(at_ref, labels_ref, last) + 1, build, 0)

    def one_pair(pair, total):
        part = nn_dot(rm_ref[pair], back_ref[0])
        keep0 = lab_ref[...] == 2 * pair
        keep1 = lab_ref[...] == 2 * pair + 1
        return total + jnp.where(keep0, part[:seqs], 0.0) + jnp.where(keep1, part[seqs:], 0.0)

    total = lax.fori_loop(first_pair(at_ref, labels_ref, g), last_pair(at_ref, labels_ref, g) + 1, one_pair, jnp.zeros(left_out.shape, F32))
    left_out[...] = total.astype(BF16)


def left_grad_call(at, labels, back, lab, right, tall):
    groups, span, _ = back.shape
    total = groups * WIDE
    seqs = right.shape[0]
    whole = lambda shape: pl.BlockSpec(shape, lambda g, *_: (0,) * len(shape))
    return pl.pallas_call(
        left_grad_body,
        grid_spec=pltpu.PrefetchScalarGridSpec(
            num_scalar_prefetch=2,
            grid=(total // WIDE,),
            in_specs=[
                pl.BlockSpec((1, span, WIDE), lambda g, *_: (g, 0, 0)),
                pl.BlockSpec((1, WIDE), lambda g, *_: (0, g)),
                whole(right.shape),
                whole(tall.shape),
            ],
            out_specs=pl.BlockSpec((seqs, WIDE), lambda g, *_: (0, g)),
            scratch_shapes=[
                pltpu.VMEM((CHAINS // 2, 2 * seqs, span), BF16),
                pltpu.VMEM((seqs, span), BF16),
            ],
        ),
        out_shape=jax.ShapeDtypeStruct((seqs, total), BF16),
        compiler_params=pltpu.CompilerParams(dimension_semantics=("arbitrary",)),
        cost_estimate=cost(10, span, total, seqs),
        name="left_grad",
    )(at, labels, back, lab, right, tall)


def outer_body(at_ref, labels_ref, left_ref, lab_ref, right_ref, wide_ref, grad_ref,
               x_ref, weight_out, rm_ref, lb_ref, acc_ref, sum_ref, turn_ref, flip_ref, part_ref):
    g = pl.program_id(0)
    seqs = left_ref.shape[0]
    span = right_ref.shape[1]
    cols = span // PROJ
    rows_here, _, width = grad_ref.shape

    last = pl.num_programs(0) - 1

    @pl.when(g == 0)
    def _():
        for t in range(span // LANES):
            lanes = slice(t * LANES, (t + 1) * LANES)
            flipped = right_ref[:, lanes].astype(F32).T
            flip_ref[lanes] = flipped.astype(BF16)
            part_ref[lanes] = (flipped / 3).astype(BF16)

        def build(pair, carry):
            plain, third = wide_ref[pair, 0], wide_ref[pair, 1]
            for e in range(PROJ):
                rows = slice(e * cols, (e + 1) * cols)
                for side in range(2):
                    lanes = slice(side * seqs, (side + 1) * seqs)
                    rm_ref[pair, rows, lanes] = (
                        flip_ref[rows] * plain[:, lanes] + part_ref[rows] * third[:, lanes]
                    )
            return carry

        lax.fori_loop(first_pair(at_ref, labels_ref, 0), last_pair(at_ref, labels_ref, last) + 1, build, 0)
        sum_ref[...] = jnp.zeros_like(sum_ref)

    def product(pair):
        masked_left(left_ref, lab_ref, lb_ref, pair)
        return nn_dot(rm_ref[pair], lb_ref[...])

    acc_ref[...] = product(first_pair(at_ref, labels_ref, g))

    def more(pair, carry):
        acc_ref[...] += product(pair)
        return carry

    lax.fori_loop(first_pair(at_ref, labels_ref, g) + 1, last_pair(at_ref, labels_ref, g) + 1, more, 0)

    for half in range(WIDE // LANES):
        lanes = slice(half * LANES, (half + 1) * LANES)
        for t in range(PROJ // PER_TILE):
            parts = []
            for q in range(PER_TILE):
                e = t * PER_TILE + q
                parts.append(acc_ref[e * cols : (e + 1) * cols, lanes].astype(BF16))
            turned = swap_blocks(parts)
            for p in range(PER_TILE):
                i = half * PER_TILE + p
                x_ref[i * cols : (i + 1) * cols, t * LANES : (t + 1) * LANES] = turned[p]

    flat = grad_ref[...].reshape(rows_here * cols, width)
    sum_ref[...] += nn_dot(flat.T, x_ref[...])

    @pl.when(g == last)
    def _():
        for t in range(PROJ * PROJ // LANES):
            part = slice(t * LANES, (t + 1) * LANES)
            turn_ref[part] = sum_ref[:, part].T
        for c in range(PROJ):
            weight_out[c * PROJ : (c + 1) * PROJ] = turn_ref[pl.ds(c, PROJ, stride=PROJ)]


def outer_call(at, labels, left, lab, right, wide, grad):
    rows, cols, width = grad.shape
    seqs, total = left.shape
    span = right.shape[1]
    step = WIDE // PROJ
    whole = lambda shape: pl.BlockSpec(shape, lambda g, *_: (0,) * len(shape))
    return pl.pallas_call(
        outer_body,
        grid_spec=pltpu.PrefetchScalarGridSpec(
            num_scalar_prefetch=2,
            grid=(total // WIDE,),
            in_specs=[
                pl.BlockSpec((seqs, WIDE), lambda g, *_: (0, g)),
                pl.BlockSpec((1, WIDE), lambda g, *_: (0, g)),
                whole(right.shape),
                whole(wide.shape),
                pl.BlockSpec((step, cols, width), lambda g, *_: (g, 0, 0)),
            ],
            out_specs=[
                pl.BlockSpec((step * cols, PROJ * PROJ), lambda g, *_: (g, 0)),
                whole((PROJ * PROJ, width)),
            ],
            scratch_shapes=[
                pltpu.VMEM((CHAINS // 2, span, 2 * seqs), BF16),
                pltpu.VMEM((2 * seqs, WIDE), BF16),
                pltpu.VMEM((span, WIDE), F32),
                pltpu.VMEM((width, PROJ * PROJ), F32),
                pltpu.VMEM((PROJ * PROJ, width), F32),
                pltpu.VMEM((span, seqs), BF16),
                pltpu.VMEM((span, seqs), BF16),
            ],
        ),
        out_shape=[
            jax.ShapeDtypeStruct((rows * cols, PROJ * PROJ), BF16),
            jax.ShapeDtypeStruct((PROJ * PROJ, width), F32),
        ],
        compiler_params=pltpu.CompilerParams(dimension_semantics=("arbitrary",)),
        cost_estimate=cost(20, span, total, seqs),
        name="outer",
    )(at, labels, left, lab, right, wide, grad)


class Ring:
    def __init__(self, n_row, n_col):
        self.n_row, self.n_col = n_row, n_col
        self.per_row = n_col // n_row
        self.row = lax.axis_index("row").astype(jnp.uint32)
        self.col = lax.axis_index("col").astype(jnp.uint32)

    def col_shift(self, value, k):
        n = self.n_col
        return lax.ppermute(value, "col", [((t + k) % n, t) for t in range(n)])

    def row_shift(self, value, k):
        n = self.n_row
        return lax.ppermute(value, "row", [((t + k) % n, t) for t in range(n)])

    def right_along_row(self, right):
        n, m = self.n_row, self.per_row
        here, lanes = right.shape
        lanes //= m
        by_row = jnp.stack([right] + [self.row_shift(right, k) for k in range(1, n)])
        pieces = []
        for k in range(self.n_col):
            q = (self.col + (self.n_col - k)) % self.n_col
            at = ((q // m + (n - self.row)) % n, jnp.uint32(0), (q % m) * lanes)
            pieces.append(lax.dynamic_slice(by_row, at, (1, here, lanes))[0])
        return pieces

    def right_along_col(self, pieces):
        return jnp.concatenate([self.col_shift(p, k) if k else p for k, p in enumerate(pieces)])

    def right_grad_home(self, grad):
        n, m = self.n_col, self.per_row
        here, lanes = grad.shape[0] // n, grad.shape[1]
        total = jnp.zeros((m, here, lanes), F32)
        slot = lax.broadcasted_iota(jnp.uint32, (m, 1, 1), 0)
        for k in range(n):
            t = (self.row * m + self.col % m + k) % n
            block = lax.dynamic_slice_in_dim(grad, ((t + n - self.col) % n) * here, here, 0)
            pairs = []
            for r in range(self.n_row):
                for q in range(n):
                    pairs.append((r * n + q, (q // m) * n + (r * m + q % m + k) % n))
            got = lax.ppermute(block, ("row", "col"), pairs).astype(F32)[None]
            total += got if m == 1 else jnp.where(slot == (self.col + (n - k)) % n % m, got, 0)
        return total.swapaxes(0, 1).reshape(here, m * lanes).astype(BF16)

    def weight_over_row(self, weight):
        n = self.n_row
        size = weight.shape[0] // n
        sent = weight.astype(BF16).reshape(n, size, -1)
        total = lax.dynamic_index_in_dim(weight.reshape(n, size, -1), self.row, 0, keepdims=False)
        for k in range(1, n):
            piece = lax.dynamic_index_in_dim(sent, (self.row + k) % n, 0, keepdims=False)
            total += self.row_shift(piece, n - k).astype(F32)
        return total

    def weight_over_col(self, total):
        mine = total.astype(BF16)
        for k in range(1, self.n_col):
            total += self.col_shift(mine, k).astype(F32)
        return total.astype(BF16)

    def weight_to_all(self, mine):
        n = self.n_row
        which = (lax.broadcasted_iota(jnp.uint32, (n, 1, 1), 0) + (n - self.row)) % n
        shares = mine[None]
        for k in range(1, n):
            shares = jnp.where(which == k, self.row_shift(mine, k)[None], shares)
        return shares.reshape(n * mine.shape[0], mine.shape[1])


def after(value, *others):
    return lax.optimization_barrier((value,) + others)[0]


def shards(n_row, n_col, alignment_tensor, gain, shift, first_projector, second_projector,
           final_projector, final_offset, labels, counts, grad):
    ring = Ring(n_row, n_col)
    here, rows, _ = alignment_tensor.shape
    cols, width = grad.shape[1:]
    seqs = here * n_col
    both = jnp.concatenate([first_projector, second_projector], axis=1)
    both = jnp.pad(both, ((0, 0), (0, LANES - 2 * PROJ)))
    left, right = project_call(alignment_tensor, gain[None, :], shift[None, :], both, cols)
    pieces = ring.right_along_row(right)
    left = jnp.concatenate([left] + [ring.col_shift(left, k) for k in range(1, n_col)])

    at = jnp.stack([ring.row * rows, ring.col * cols, ring.col * here]).astype(jnp.int32)
    lab, tall, wide, plain, w, wt = prep_call(
        at, labels, counts, after(final_projector, right), rows, cols, seqs
    )
    back = back_call(after(grad, *pieces), wt)
    mine = ring.right_along_col(pieces)
    right_grad = right_grad_call(at, labels, back, left, lab, plain)

    right = after(mine, right_grad)
    grad_right = ring.right_grad_home(right_grad)
    outer, weight = outer_call(
        at, labels, left, lab, right, wide, grad
    )
    share = ring.weight_over_row(weight)
    left_grad = left_grad_call(at, labels, after(back, weight), lab, right, tall)
    share = after(share, left_grad)

    total = left_grad[:here].astype(F32)
    for k in range(1, n_col):
        total += ring.col_shift(left_grad[k * here : (k + 1) * here], n_col - k).astype(F32)
    adjoint_first = total.astype(BF16)
    pair = jnp.dot(after(outer, left_grad, share), w, preferred_element_type=F32) + final_offset
    pair_update = pair.astype(BF16).reshape(rows, cols, width)
    mine = after(ring.weight_over_col(share), pair_update)
    grad_w_out = ring.weight_to_all(mine).astype(F32) / (n_row * rows)
    return pair_update, adjoint_first, grad_right, grad_w_out


def solution(mesh):
    in_specs = (
        P(("parts", "col"), "row", None),
        P(),
        P(),
        P(),
        P(),
        P(),
        P(),
        P("parts"),
        P("parts", None),
        P(("parts", "row"), "col", None),
    )
    out_specs = (
        P(("parts", "row"), "col", None),
        P(("parts", "col"), "row"),
        P(("parts", "col"), "row"),
        P("parts", None),
    )

    def body(*args):
        return shards(mesh.shape["row"], mesh.shape["col"], *args)

    return jax.shard_map(body, mesh=mesh, in_specs=in_specs, out_specs=out_specs, check_vma=False)
```

time: 133 us -> 123 us (0.925)
  Pallas kernels: 51.5 us -> 60.3 us
  waiting for transfers between devices: 12.5 us -> 3.86 us
  other arithmetic: 14.8 us -> 8.85 us
  local copies, waits for them, and re-layouts: 10.3 us -> 5.93 us
  starting transfers between devices: 33.7 us -> 35.7 us
    pallas_call x0 -> x2, Pallas kernels: none -> 8.3 us  [the longest x1 5.64 us: project_call(): pl.pallas_call(lambda *refs: project_body(*refs, cols=cols), out_shape=[j...]
    ppermute x8 -> x4, starting transfers between devices: 13.6 us -> 8.1 us  [right_grad_home(): got = lax.ppermute(block, ('row', 'col'), pairs).astype(F32)[None]]
    ppermute x8 -> x4, waiting for transfers between devices: 5.24 us -> 0.01 us  [right_grad_home(): got = lax.ppermute(block, ('row', 'col'), pairs).astype(F32)[None]]
    ppermute x9 -> x12, starting transfers between devices: 15.9 us -> 20.7 us  [col_shift(): return lax.ppermute(value, 'col', [((t + k) % n, t) for t in range(n)])]
    reduce_sum x3 -> x0, other arithmetic: 3.61 us -> none  [the longest x1 1.87 us: standardize_entries(): spread = jnp.mean(center * center, axis=-1, keepdims=True)]
    ppermute x8 -> x9, starting transfers between devices: 4.19 us -> 6.91 us  [row_shift(): return lax.ppermute(value, 'row', [((t + k) % n, t) for t in range(n)])]
    ppermute x8 -> x9, waiting for transfers between devices: 2.62 us -> 0.02 us  [row_shift(): return lax.ppermute(value, 'row', [((t + k) % n, t) for t in range(n)])]
    another operation x5 -> x0, local copies, waits for them, and re-layouts: 2.04 us -> none  [the longest x3 1.08 us: shards(): jnp.tile(tall.reshape(pairs, 2, 2 * seqs, cols), (1, 1, 1, LANES // cols))]
  transfers between devices with their start and end apart: 25 -> 25, of which waited for: 5 -> 1; matrix products, arithmetic and copies ran while one was open for 19% -> 14% of each run, Pallas kernels for 31% -> 45%
where the time goes in v4:
time: 123 us; the launch traced here: 122 us
  Pallas kernels  60.3 us (49%)
  starting transfers between devices  35.7 us (29%)
  other arithmetic  8.85 us (7%)
  matrix products  6.7 us (5%)
  local copies, waits for them, and re-layouts  5.93 us (5%)
  waiting for transfers between devices  3.86 us (3%)
    ppermute x12, starting transfers between devices, col_shift(): return lax.ppermute(value, 'col', [((t + k) % n, t) for t in range(n)])  20.7 us
    pallas_call x1, Pallas kernels, outer_call(): pl.pallas_call(outer_body, grid_spec=pltpu.PrefetchScalarGridSpec(num_sca...  20 us
    pallas_call x1, Pallas kernels, right_grad_call(): pl.pallas_call(right_grad_body, grid_spec=pltpu.PrefetchScalarGridSpec(nu...  11.5 us
    pallas_call x1, Pallas kernels, left_grad_call(): pl.pallas_call(left_grad_body, grid_spec=pltpu.PrefetchScalarGridSpec(num...  10.7 us
    pallas_call x1, Pallas kernels, back_call(): pl.pallas_call(back_body, grid=(rows // step,), in_specs=[pl.BlockSpec((s...  9.73 us
    ppermute x4, starting transfers between devices, right_grad_home(): got = lax.ppermute(block, ('row', 'col'), pairs).astype(F32)[None]  8.1 us
    ppermute x9, starting transfers between devices, row_shift(): return lax.ppermute(value, 'row', [((t + k) % n, t) for t in range(n)])  6.91 us
    dot_general x1, matrix products, shards(): jnp.dot(after(outer, left_grad, share), w, preferred_element_type=F32)  6.7 us
  transfers between devices with their start and end apart: 25, of which 1 were waited for; matrix products, arithmetic and copies ran while one was open for 14% of the time, Pallas kernels for 45%

profile of v4, /device:TPU:0, one launch (start us, length us, event | category | flops | bytes accessed | tf_op | source)
XLA Modules:
  0.0 122.2 jit_solution(4098676565303814498)
XLA Ops:
  0.6 0.8 copy.14
  1.5 0.8 copy.15
  3.0 5.6 %project.1 = (bf16[32,2048]{1,0:T(8,128)(2,1)}, bf16[32,2048]{1,0:T(8,128)(2,1)}) custom-call(bf16[32,64,256]{2,1,0:T(8,128)(2,1)} %refs_0_.1, f32[1,256]{1,0:T(1,128)} %bitcast.56, f32[1,256]{1,0:T(1,128)} %bitcast.57, bf16[256,128]{1,0:T(8,128)(2,1)} %fusion.7.refs_3_), custom_call_target="tpu_custom_call" | custom-call | tf_op jit(solution)/shard_map/project/pallas_call | solution.py:89
  8.7 3.1 %collective-permute-start.2 = (bf16[32,2048]{1,0:T(8,128)(2,1)}, bf16[32,2048]{1,0:T(8,128)(2,1)S(1)}, u32[]{:S(2)}, u32[]{:S(2)}) collective-permute-start(bf16[32,2048]{1,0:T(8,128)(2,1)} %get-tuple-element.21), channel_id=1, source_target_pairs={{3,0},{0,1},{1,2},{2,3},{7,4},{4,5},{5,6},{6,7},{11,8},{8,9},{9,10... | collective-permute-start | bytes 393224 | tf_op jit(solution)/shard_map/ppermute | solution.py:477
  11.7 2.6 %collective-permute-start.1 = (bf16[32,2048]{1,0:T(8,128)(2,1)}, bf16[32,2048]{1,0:T(8,128)(2,1)S(1)}, u32[]{:S(2)}, u32[]{:S(2)}) collective-permute-start(bf16[32,2048]{1,0:T(8,128)(2,1)} %get-tuple-element.21), channel_id=1, source_target_pairs={{2,0},{3,1},{0,2},{1,3},{6,4},{7,5},{4,6},{5,7},{10,8},{11,9},{8,1... | collective-permute-start | bytes 393224 | tf_op jit(solution)/shard_map/ppermute | solution.py:477
  14.3 1.5 %collective-permute-start.4 = (bf16[32,2048]{1,0:T(8,128)(2,1)}, bf16[32,2048]{1,0:T(8,128)(2,1)S(1)}, u32[]{:S(2)}, u32[]{:S(2)}) collective-permute-start(bf16[32,2048]{1,0:T(8,128)(2,1)} %get-tuple-element.22), channel_id=1, source_target_pairs={{8,0},{12,4},{0,8},{4,12},{9,1},{13,5},{1,9},{5,13},{10,2},{14,6},... | collective-permute-start | bytes 393224 | tf_op jit(solution)/shard_map/ppermute | solution.py:481
  15.8 1.5 %collective-permute-start.3 = (bf16[32,2048]{1,0:T(8,128)(2,1)}, bf16[32,2048]{1,0:T(8,128)(2,1)S(1)}, u32[]{:S(2)}, u32[]{:S(2)}) collective-permute-start(bf16[32,2048]{1,0:T(8,128)(2,1)} %get-tuple-element.22), channel_id=1, source_target_pairs={{4,0},{8,4},{12,8},{0,12},{5,1},{9,5},{13,9},{1,13},{6,2},{10,6},{... | collective-permute-start | bytes 393224 | tf_op jit(solution)/shard_map/ppermute | solution.py:481
  18.2 2.7 %prep.1 = (s32[1,2048]{1,0:T(1,128)}, bf16[4,2,256,128]{3,2,1,0:T(8,128)(2,1)}, bf16[4,2,64,256]{3,2,1,0:T(8,128)(2,1)}, f32[4,64,256]{2,1,0:T(8,128)}, bf16[102...) custom-call(s32[3]{0:T(128)} %add_convert_fusion.3.refs_0_.at_ref, s32[1,256]{1,0:T(1,128)} %bitcast.55, s32[8,8]{1,0:T(8,128)} %refs_2_.1, ...), custom_call_target="tpu_custom_call" | custom-call | tf_op jit(solution)/shard_map/prep/pallas_call | solution.py:146
  20.9 0.9 constant_dynamic-update-slice_fusion.3
  21.8 1.4 %collective-permute-start = (bf16[32,2048]{1,0:T(8,128)(2,1)}, bf16[32,2048]{1,0:T(8,128)(2,1)S(1)}, u32[]{:S(2)}, u32[]{:S(2)}) collective-permute-start(bf16[32,2048]{1,0:T(8,128)(2,1)} %get-tuple-element.21), channel_id=1, source_target_pairs={{1,0},{2,1},{3,2},{0,3},{5,4},{6,5},{7,6},{4,7},{9,8},{10,9},{11,1... | collective-permute-start | bytes 393224 | tf_op jit(solution)/shard_map/ppermute | solution.py:477
  23.2 1.0 pad_maximum_fusion
  25.3 9.7 %back.1.back_ref = bf16[8,2048,256]{2,1,0:T(8,128)(2,1)} custom-call(bf16[64,64,128]{2,1,0:T(8,128)(2,1)} %grad_ref.2, bf16[128,1024]{1,0:T(8,128)(2,1)} %get-tuple-element.26.wt_ref), custom_call_target="tpu_custom_call" | custom-call | flops 21474836480 | bytes 8388608 | tf_op jit(solution)/shard_map/back/pallas_call | solution.py:189
  35.1 2.8 %collective-permute-start.6 = (bf16[32,2048]{1,0:T(8,128)(2,1)S(1)}, bf16[32,2048]{1,0:T(8,128)(2,1)S(1)}, u32[]{:S(2)}, u32[]{:S(2)}) collective-permute-start(bf16[32,2048]{1,0:T(8,128)(2,1)S(1)} %get-tuple-element.48), channel_id=1, source_target_pairs={{1,0},{2,1},{3,2},{0,3},{5,4},{6,5},{7,6},{4,7},{9,8},{10,9},{11,1... | collective-permute-start | bytes 393224 | tf_op jit(solution)/shard_map/ppermute | solution.py:477
  38.7 11.5 %right_grad.1 = bf16[128,2048]{1,0:T(8,128)(2,1)} custom-call(s32[3]{0:T(128)} %add_convert_fusion.3.refs_0_.at_ref, s32[256]{0:T(256)} %labels_ref.5, bf16[8,2048,256]{2,1,0:T(8,128)(2,1)} %back.1.back_ref, bf16[128,2048]{1,0:T(8,128)(2,1)} %copy-done, s32[1,2048]{1,0:T(1,128)} %get-tuple-element.24.lab_ref, f32[4,64,256]{2,1,0:T(8,128)} %get-tuple-element.27.wide_ref), custom_call_target="tpu_custom_call" | custom-call | flops 21474836480 | bytes 8388608 | tf_op jit(solution)/shard_map/right_grad/pallas_call | solution.py:269
  50.2 1.1 constant_dynamic-slice_fusion.3
  52.0 5.0 %collective-permute-start.18 = (bf16[32,2048]{1,0:T(8,128)(2,1)S(1)}, bf16[32,2048]{1,0:T(8,128)(2,1)S(1)}, u32[]{:S(2)}, u32[]{:S(2)}) collective-permute-start(bf16[32,2048]{1,0:T(8,128)(2,1)S(1)} %get-tuple-element.39), channel_id=1, source_target_pairs={{0,3},{1,7},{2,11},{3,15},{4,0},{5,4},{6,8},{7,12},{8,1},{9,5},{10... | collective-permute-start | bytes 393224 | tf_op jit(solution)/shard_map/ppermute | solution.py:510
  57.0 2.5 %collective-permute-start.16 = (bf16[32,2048]{1,0:T(8,128)(2,1)S(1)}, bf16[32,2048]{1,0:T(8,128)(2,1)S(1)}, u32[]{:S(2)}, u32[]{:S(2)}) collective-permute-start(bf16[32,2048]{1,0:T(8,128)(2,1)S(1)} %get-tuple-element.41), channel_id=1, source_target_pairs={{0,1},{1,5},{2,9},{3,13},{4,2},{5,6},{6,10},{7,14},{8,3},{9,7},{10... | collective-permute-start | bytes 393224 | tf_op jit(solution)/shard_map/ppermute | solution.py:510
  59.5 0.8 pad_maximum_fusion.1.right_ref
  60.3 20.0 %outer.1 = (bf16[4096,1024]{1,0:T(8,128)(2,1)}, f32[1024,128]{1,0:T(8,128)}) custom-call(s32[3]{0:T(128)} %add_convert_fusion.3.refs_0_.at_ref, s32[256]{0:T(256)} %labels_ref.5, bf16[128,2048]{1,0:T(8,128)(2,1)} %copy-done, s32[1,2048]{1,0:T(1,128)} %get-tuple-element.24.lab_ref, bf16[128,2048]{1,0:T(8,128)(2,1)} %pad_maximum_fusion.1.right_ref, ...), custom_call_target="tpu_custom_call" | custom-call | flops 42949672960 | bytes 8388608 | tf_op jit(solution)/shard_map/outer/pallas_call | solution.py:432
  80.3 1.1 convert_element_type.112
  81.5 10.7 %left_grad.1 = bf16[128,2048]{1,0:T(8,128)(2,1)} custom-call(s32[3]{0:T(128)} %add_convert_fusion.3.refs_0_.at_ref, s32[256]{0:T(256)} %labels_ref.5, bf16[8,2048,256]{2,1,0:T(8,128)(2,1)} %back.1.back_ref, s32[1,2048]{1,0:T(1,128)} %get-tuple-element.24.lab_ref, bf16[128,2048]{1,0:T(8,128)(2,1)} %pad_maximum_fusion.1.right_ref, ...), custom_call_target="tpu_custom_call" | custom-call | flops 21474836480 | bytes 8388608 | tf_op jit(solution)/shard_map/left_grad/pallas_call | solution.py:334
  92.2 1.1 fusion.8
  93.3 1.6 %collective-permute-start.11 = (bf16[256,128]{1,0:T(8,128)(2,1)S(1)}, bf16[256,128]{1,0:T(8,128)(2,1)S(1)}, u32[]{:S(2)}, u32[]{:S(2)}) collective-permute-start(bf16[256,128]{1,0:T(8,128)(2,1)S(1)} %get-tuple-element.50), channel_id=1, source_target_pairs={{4,0},{8,4},{12,8},{0,12},{5,1},{9,5},{13,9},{1,13},{6,2},{10,6},{... | collective-permute-start | bytes 196616 | tf_op jit(solution)/shard_map/ppermute | solution.py:481
  95.6 3.2 %collective-permute-start.14 = (bf16[32,2048]{1,0:T(8,128)(2,1)S(1)}, bf16[32,2048]{1,0:T(8,128)(2,1)S(1)}, u32[]{:S(2)}, u32[]{:S(2)}) collective-permute-start(bf16[32,2048]{1,0:T(8,128)(2,1)S(1)} %get-tuple-element.43), channel_id=1, source_target_pairs={{1,0},{2,1},{3,2},{0,3},{5,4},{6,5},{7,6},{4,7},{9,8},{10,9},{11,1... | collective-permute-start | bytes 393224 | tf_op jit(solution)/shard_map/ppermute | solution.py:477
  99.6 0.9 fusion.6
  101.2 3.3 %collective-permute-start.19 = (bf16[256,128]{1,0:T(8,128)(2,1)S(1)}, bf16[256,128]{1,0:T(8,128)(2,1)S(1)}, u32[]{:S(2)}, u32[]{:S(2)}) collective-permute-start(bf16[256,128]{1,0:T(8,128)(2,1)S(1)} %convert_element_type.127), channel_id=1, source_target_pairs={{1,0},{2,1},{3,2},{0,3},{5,4},{6,5},{7,6},{4,7},{9,8},{10,9},{11,1... | collective-permute-start | bytes 196616 | tf_op jit(solution)/shard_map/ppermute | solution.py:477
  104.4 6.7 %fusion = bf16[4096,128]{1,0:T(8,128)(2,1)} fusion(bf16[4096,1024]{1,0:T(8,128)(2,1)} %get-tuple-element.35, bf16[1024,128]{1,0:T(8,128)(2,1)S(1)} %copy-done.1, f32[128]{0:T(128)S(1)} %copy-done.2), kind=kOutput, calls=%fused_computation.1 | convolution fusion | flops 1074790400 | bytes 9699840 | tf_op jit(solution)/shard_map/dot_general | solution.py:576
  111.1 2.0 %collective-permute-start.13 = (bf16[32,2048]{1,0:T(8,128)(2,1)S(1)}, bf16[32,2048]{1,0:T(8,128)(2,1)S(1)}, u32[]{:S(2)}, u32[]{:S(2)}) collective-permute-start(bf16[32,2048]{1,0:T(8,128)(2,1)S(1)} %get-tuple-element.44), channel_id=1, source_target_pairs={{2,0},{3,1},{0,2},{1,3},{6,4},{7,5},{4,6},{5,7},{10,8},{11,9},{8,1... | collective-permute-start | bytes 393224 | tf_op jit(solution)/shard_map/ppermute | solution.py:477
  113.3 2.0 %collective-permute-start.23 = (bf16[256,128]{1,0:T(8,128)(2,1)S(1)}, bf16[256,128]{1,0:T(8,128)(2,1)S(1)}, u32[]{:S(2)}, u32[]{:S(2)}) collective-permute-start(bf16[256,128]{1,0:T(8,128)(2,1)S(1)} %add_convert_fusion.2), channel_id=1, source_target_pairs={{8,0},{12,4},{0,8},{4,12},{9,1},{13,5},{1,9},{5,13},{10,2},{14,6},... | collective-permute-start | bytes 196616 | tf_op jit(solution)/shard_map/ppermute | solution.py:481
  115.5 3.8 %collective-permute-done.13 = bf16[32,2048]{1,0:T(8,128)(2,1)S(1)} collective-permute-done((bf16[32,2048]{1,0:T(8,128)(2,1)S(1)}, bf16[32,2048]{1,0:T(8,128)(2,1)S(1)}, u32[]{:S(2)}, u32[]{:S(2)}) %collective-permute-start.13) | collective-permute-done | bytes 131104 | tf_op jit(solution)/shard_map/ppermute | solution.py:477
  119.3 1.6 %add_convert_fusion.1 = bf16[32,2048]{1,0:T(8,128)(2,1)} fusion(bf16[32,2048]{1,0:T(8,128)(2,1)S(1)} %collective-permute-done.14, bf16[32,2048]{1,0:T(8,128)(2,1)S(1)} %collective-permute-done.13, bf16[32,2048]{1,0:T(8,128)(2,1)S(1)} %collective-permute-done.12, bf16[128,2048]{1,0:T(8,128)(2,1)} %left_grad.1), kind=kLoop, calls=%fused_computation.9 | loop fusion | flops 524288 | bytes 655360 | tf_op jit(solution)/shard_map/convert_element_type | solution.py:575
  120.9 1.3 %convert_multiply_fusion = f32[1024,128]{1,0:T(8,128)} fusion(pred[1024]{0:T(1024)(128)(4,1)S(1)} %broadcast_in_dim.102, pred[1024]{0:T(1024)(128)(4,1)S(1)} %broadcast_in_dim.97, pred[1024]{0:T(1024)(128)(4,1)S(1)} %broadcast_in_dim.92, bf16[256,128]{1,0:T(8,128)(2,1)S(1)} %add_convert_fusion.2, bf16[256,128]{1,0:T(8,128)(2,1)S(1)} %collective-permute-done.24, ...), kind=kLoop, calls=%fused_computation.4 | loop fusion | flops 655360 | bytes 789504 | tf_op jit(solution)/shard_map/div | solution.py:579
  (60 shorter events, 6.6 us)
Async XLA Ops:
  8.7 29.2 %collective-permute-start.2 = (bf16[32,2048]{1,0:T(8,128)(2,1)}, bf16[32,2048]{1,0:T(8,128)(2,1)S(1)}, u32[]{:S(2)}, u32[]{:S(2)}) collective-permute-start(bf16[32,2048]{1,0:T(8,128)(2,1)} %get-tuple-element.21), channel_id=1, source_target_pairs={{3,0},{0,1},{1,2},{2,3},{7,4},{4,5},{5,6},{6,7},{11,8},{8,9},{9,10... | collective-permute-start | bytes 393224 | tf_op jit(solution)/shard_map/ppermute | solution.py:477
  11.7 26.2 %collective-permute-start.1 = (bf16[32,2048]{1,0:T(8,128)(2,1)}, bf16[32,2048]{1,0:T(8,128)(2,1)S(1)}, u32[]{:S(2)}, u32[]{:S(2)}) collective-permute-start(bf16[32,2048]{1,0:T(8,128)(2,1)} %get-tuple-element.21), channel_id=1, source_target_pairs={{2,0},{3,1},{0,2},{1,3},{6,4},{7,5},{4,6},{5,7},{10,8},{11,9},{8,1... | collective-permute-start | bytes 393224 | tf_op jit(solution)/shard_map/ppermute | solution.py:477
  14.3 7.5 %collective-permute-start.5 = (bf16[32,2048]{1,0:T(8,128)(2,1)}, bf16[32,2048]{1,0:T(8,128)(2,1)S(1)}, u32[]{:S(2)}, u32[]{:S(2)}) collective-permute-start(bf16[32,2048]{1,0:T(8,128)(2,1)} %get-tuple-element.22), channel_id=1, source_target_pairs={{12,0},{0,4},{4,8},{8,12},{13,1},{1,5},{5,9},{9,13},{14,2},{2,6},{... | collective-permute-start | bytes 393224 | tf_op jit(solution)/shard_map/ppermute | solution.py:481
  14.3 8.9 %collective-permute-start.4 = (bf16[32,2048]{1,0:T(8,128)(2,1)}, bf16[32,2048]{1,0:T(8,128)(2,1)S(1)}, u32[]{:S(2)}, u32[]{:S(2)}) collective-permute-start(bf16[32,2048]{1,0:T(8,128)(2,1)} %get-tuple-element.22), channel_id=1, source_target_pairs={{8,0},{12,4},{0,8},{4,12},{9,1},{13,5},{1,9},{5,13},{10,2},{14,6},... | collective-permute-start | bytes 393224 | tf_op jit(solution)/shard_map/ppermute | solution.py:481
  15.8 7.4 %collective-permute-start.3 = (bf16[32,2048]{1,0:T(8,128)(2,1)}, bf16[32,2048]{1,0:T(8,128)(2,1)S(1)}, u32[]{:S(2)}, u32[]{:S(2)}) collective-permute-start(bf16[32,2048]{1,0:T(8,128)(2,1)} %get-tuple-element.22), channel_id=1, source_target_pairs={{4,0},{8,4},{12,8},{0,12},{5,1},{9,5},{13,9},{1,13},{6,2},{10,6},{... | collective-permute-start | bytes 393224 | tf_op jit(solution)/shard_map/ppermute | solution.py:481
  21.8 13.2 %collective-permute-start = (bf16[32,2048]{1,0:T(8,128)(2,1)}, bf16[32,2048]{1,0:T(8,128)(2,1)S(1)}, u32[]{:S(2)}, u32[]{:S(2)}) collective-permute-start(bf16[32,2048]{1,0:T(8,128)(2,1)} %get-tuple-element.21), channel_id=1, source_target_pairs={{1,0},{2,1},{3,2},{0,3},{5,4},{6,5},{7,6},{4,7},{9,8},{10,9},{11,1... | collective-permute-start | bytes 393224 | tf_op jit(solution)/shard_map/ppermute | solution.py:477
  24.2 32.7 %collective-permute-start.8 = (bf16[32,2048]{1,0:T(8,128)(2,1)S(1)}, bf16[32,2048]{1,0:T(8,128)(2,1)S(1)}, u32[]{:S(2)}, u32[]{:S(2)}) collective-permute-start(bf16[32,2048]{1,0:T(8,128)(2,1)S(1)} %get-tuple-element.46), channel_id=1, source_target_pairs={{3,0},{0,1},{1,2},{2,3},{7,4},{4,5},{5,6},{6,7},{11,8},{8,9},{9,10... | collective-permute-start | bytes 393224 | tf_op jit(solution)/shard_map/ppermute | solution.py:477
  25.0 32.0 %collective-permute-start.7 = (bf16[32,2048]{1,0:T(8,128)(2,1)S(1)}, bf16[32,2048]{1,0:T(8,128)(2,1)S(1)}, u32[]{:S(2)}, u32[]{:S(2)}) collective-permute-start(bf16[32,2048]{1,0:T(8,128)(2,1)S(1)} %get-tuple-element.47), channel_id=1, source_target_pairs={{2,0},{3,1},{0,2},{1,3},{6,4},{7,5},{4,6},{5,7},{10,8},{11,9},{8,1... | collective-permute-start | bytes 393224 | tf_op jit(solution)/shard_map/ppermute | solution.py:477
  35.1 24.4 %collective-permute-start.6 = (bf16[32,2048]{1,0:T(8,128)(2,1)S(1)}, bf16[32,2048]{1,0:T(8,128)(2,1)S(1)}, u32[]{:S(2)}, u32[]{:S(2)}) collective-permute-start(bf16[32,2048]{1,0:T(8,128)(2,1)S(1)} %get-tuple-element.48), channel_id=1, source_target_pairs={{1,0},{2,1},{3,2},{0,3},{5,4},{6,5},{7,6},{4,7},{9,8},{10,9},{11,1... | collective-permute-start | bytes 393224 | tf_op jit(solution)/shard_map/ppermute | solution.py:477
  37.9 0.8 copy-start
  51.4 41.9 %collective-permute-start.15 = (bf16[32,2048]{1,0:T(8,128)(2,1)S(1)}, bf16[32,2048]{1,0:T(8,128)(2,1)S(1)}, u32[]{:S(2)}, u32[]{:S(2)}) collective-permute-start(bf16[32,2048]{1,0:T(8,128)(2,1)S(1)} %get-tuple-element.38), channel_id=1, source_target_pairs={{0,0},{1,4},{2,8},{3,12},{4,1},{5,5},{6,9},{7,13},{8,2},{9,6},{10,... | collective-permute-start | bytes 393224 | tf_op jit(solution)/shard_map/ppermute | solution.py:510
  52.0 42.9 %collective-permute-start.18 = (bf16[32,2048]{1,0:T(8,128)(2,1)S(1)}, bf16[32,2048]{1,0:T(8,128)(2,1)S(1)}, u32[]{:S(2)}, u32[]{:S(2)}) collective-permute-start(bf16[32,2048]{1,0:T(8,128)(2,1)S(1)} %get-tuple-element.39), channel_id=1, source_target_pairs={{0,3},{1,7},{2,11},{3,15},{4,0},{5,4},{6,8},{7,12},{8,1},{9,5},{10... | collective-permute-start | bytes 393224 | tf_op jit(solution)/shard_map/ppermute | solution.py:510
  57.0 38.0 %collective-permute-start.17 = (bf16[32,2048]{1,0:T(8,128)(2,1)S(1)}, bf16[32,2048]{1,0:T(8,128)(2,1)S(1)}, u32[]{:S(2)}, u32[]{:S(2)}) collective-permute-start(bf16[32,2048]{1,0:T(8,128)(2,1)S(1)} %get-tuple-element.40), channel_id=1, source_target_pairs={{0,2},{1,6},{2,10},{3,14},{4,3},{5,7},{6,11},{7,15},{8,0},{9,4},{1... | collective-permute-start | bytes 393224 | tf_op jit(solution)/shard_map/ppermute | solution.py:510
  57.0 38.6 %collective-permute-start.16 = (bf16[32,2048]{1,0:T(8,128)(2,1)S(1)}, bf16[32,2048]{1,0:T(8,128)(2,1)S(1)}, u32[]{:S(2)}, u32[]{:S(2)}) collective-permute-start(bf16[32,2048]{1,0:T(8,128)(2,1)S(1)} %get-tuple-element.41), channel_id=1, source_target_pairs={{0,1},{1,5},{2,9},{3,13},{4,2},{5,6},{6,10},{7,14},{8,3},{9,7},{10... | collective-permute-start | bytes 393224 | tf_op jit(solution)/shard_map/ppermute | solution.py:510
  81.5 18.1 %collective-permute-start.9 = (bf16[256,128]{1,0:T(8,128)(2,1)S(1)}, bf16[256,128]{1,0:T(8,128)(2,1)S(1)}, u32[]{:S(2)}, u32[]{:S(2)}) collective-permute-start(bf16[256,128]{1,0:T(8,128)(2,1)S(1)} %get-tuple-element.49), channel_id=1, source_target_pairs={{12,0},{0,4},{4,8},{8,12},{13,1},{1,5},{5,9},{9,13},{14,2},{2,6},{... | collective-permute-start | bytes 196616 | tf_op jit(solution)/shard_map/ppermute | solution.py:481
  81.5 22.9 %copy-start.1 = (bf16[1024,128]{1,0:T(8,128)(2,1)S(1)}, bf16[1024,128]{1,0:T(8,128)(2,1)}, u32[]{:S(2)}) copy-start(bf16[1024,128]{1,0:T(8,128)(2,1)} %get-tuple-element.36) | copy-start | bytes 786436
  81.5 22.9 %copy-start.2 = (f32[128]{0:T(128)S(1)}, f32[128]{0:T(128)}, u32[]{:S(2)}) copy-start(f32[128]{0:T(128)} %param.16) | copy-start | bytes 1540
  93.3 6.3 %collective-permute-start.11 = (bf16[256,128]{1,0:T(8,128)(2,1)S(1)}, bf16[256,128]{1,0:T(8,128)(2,1)S(1)}, u32[]{:S(2)}, u32[]{:S(2)}) collective-permute-start(bf16[256,128]{1,0:T(8,128)(2,1)S(1)} %get-tuple-element.50), channel_id=1, source_target_pairs={{4,0},{8,4},{12,8},{0,12},{5,1},{9,5},{13,9},{1,13},{6,2},{10,6},{... | collective-permute-start | bytes 196616 | tf_op jit(solution)/shard_map/ppermute | solution.py:481
  95.0 4.6 %collective-permute-start.10 = (bf16[256,128]{1,0:T(8,128)(2,1)S(1)}, bf16[256,128]{1,0:T(8,128)(2,1)S(1)}, u32[]{:S(2)}, u32[]{:S(2)}) collective-permute-start(bf16[256,128]{1,0:T(8,128)(2,1)S(1)} %get-tuple-element.51), channel_id=1, source_target_pairs={{8,0},{12,4},{0,8},{4,12},{9,1},{13,5},{1,9},{5,13},{10,2},{14,6},... | collective-permute-start | bytes 196616 | tf_op jit(solution)/shard_map/ppermute | solution.py:481
  95.0 20.4 %collective-permute-start.12 = (bf16[32,2048]{1,0:T(8,128)(2,1)S(1)}, bf16[32,2048]{1,0:T(8,128)(2,1)S(1)}, u32[]{:S(2)}, u32[]{:S(2)}) collective-permute-start(bf16[32,2048]{1,0:T(8,128)(2,1)S(1)} %get-tuple-element.42), channel_id=1, source_target_pairs={{3,0},{0,1},{1,2},{2,3},{7,4},{4,5},{5,6},{6,7},{11,8},{8,9},{9,10... | collective-permute-start | bytes 393224 | tf_op jit(solution)/shard_map/ppermute | solution.py:477
  95.6 19.9 %collective-permute-start.14 = (bf16[32,2048]{1,0:T(8,128)(2,1)S(1)}, bf16[32,2048]{1,0:T(8,128)(2,1)S(1)}, u32[]{:S(2)}, u32[]{:S(2)}) collective-permute-start(bf16[32,2048]{1,0:T(8,128)(2,1)S(1)} %get-tuple-element.43), channel_id=1, source_target_pairs={{1,0},{2,1},{3,2},{0,3},{5,4},{6,5},{7,6},{4,7},{9,8},{10,9},{11,1... | collective-permute-start | bytes 393224 | tf_op jit(solution)/shard_map/ppermute | solution.py:477
  100.5 10.6 %collective-permute-start.21 = (bf16[256,128]{1,0:T(8,128)(2,1)S(1)}, bf16[256,128]{1,0:T(8,128)(2,1)S(1)}, u32[]{:S(2)}, u32[]{:S(2)}) collective-permute-start(bf16[256,128]{1,0:T(8,128)(2,1)S(1)} %convert_element_type.127), channel_id=1, source_target_pairs={{3,0},{0,1},{1,2},{2,3},{7,4},{4,5},{5,6},{6,7},{11,8},{8,9},{9,10... | collective-permute-start | bytes 196616 | tf_op jit(solution)/shard_map/ppermute | solution.py:477
  100.6 12.6 %collective-permute-start.20 = (bf16[256,128]{1,0:T(8,128)(2,1)S(1)}, bf16[256,128]{1,0:T(8,128)(2,1)S(1)}, u32[]{:S(2)}, u32[]{:S(2)}) collective-permute-start(bf16[256,128]{1,0:T(8,128)(2,1)S(1)} %convert_element_type.127), channel_id=1, source_target_pairs={{2,0},{3,1},{0,2},{1,3},{6,4},{7,5},{4,6},{5,7},{10,8},{11,9},{8,1... | collective-permute-start | bytes 196616 | tf_op jit(solution)/shard_map/ppermute | solution.py:477
  101.2 12.0 %collective-permute-start.19 = (bf16[256,128]{1,0:T(8,128)(2,1)S(1)}, bf16[256,128]{1,0:T(8,128)(2,1)S(1)}, u32[]{:S(2)}, u32[]{:S(2)}) collective-permute-start(bf16[256,128]{1,0:T(8,128)(2,1)S(1)} %convert_element_type.127), channel_id=1, source_target_pairs={{1,0},{2,1},{3,2},{0,3},{5,4},{6,5},{7,6},{4,7},{9,8},{10,9},{11,1... | collective-permute-start | bytes 196616 | tf_op jit(solution)/shard_map/ppermute | solution.py:477
  111.1 8.1 %collective-permute-start.13 = (bf16[32,2048]{1,0:T(8,128)(2,1)S(1)}, bf16[32,2048]{1,0:T(8,128)(2,1)S(1)}, u32[]{:S(2)}, u32[]{:S(2)}) collective-permute-start(bf16[32,2048]{1,0:T(8,128)(2,1)S(1)} %get-tuple-element.44), channel_id=1, source_target_pairs={{2,0},{3,1},{0,2},{1,3},{6,4},{7,5},{4,6},{5,7},{10,8},{11,9},{8,1... | collective-permute-start | bytes 393224 | tf_op jit(solution)/shard_map/ppermute | solution.py:477
  113.2 7.7 %collective-permute-start.24 = (bf16[256,128]{1,0:T(8,128)(2,1)S(1)}, bf16[256,128]{1,0:T(8,128)(2,1)S(1)}, u32[]{:S(2)}, u32[]{:S(2)}) collective-permute-start(bf16[256,128]{1,0:T(8,128)(2,1)S(1)} %add_convert_fusion.2), channel_id=1, source_target_pairs={{4,0},{8,4},{12,8},{0,12},{5,1},{9,5},{13,9},{1,13},{6,2},{10,6},{... | collective-permute-start | bytes 196616 | tf_op jit(solution)/shard_map/ppermute | solution.py:481
  113.3 7.6 %collective-permute-start.23 = (bf16[256,128]{1,0:T(8,128)(2,1)S(1)}, bf16[256,128]{1,0:T(8,128)(2,1)S(1)}, u32[]{:S(2)}, u32[]{:S(2)}) collective-permute-start(bf16[256,128]{1,0:T(8,128)(2,1)S(1)} %add_convert_fusion.2), channel_id=1, source_target_pairs={{8,0},{12,4},{0,8},{4,12},{9,1},{13,5},{1,9},{5,13},{10,2},{14,6},... | collective-permute-start | bytes 196616 | tf_op jit(solution)/shard_map/ppermute | solution.py:481
  115.3 5.6 %collective-permute-start.22 = (bf16[256,128]{1,0:T(8,128)(2,1)S(1)}, bf16[256,128]{1,0:T(8,128)(2,1)S(1)}, u32[]{:S(2)}, u32[]{:S(2)}) collective-permute-start(bf16[256,128]{1,0:T(8,128)(2,1)S(1)} %add_convert_fusion.2), channel_id=1, source_target_pairs={{12,0},{0,4},{4,8},{8,12},{13,1},{1,5},{5,9},{9,13},{14,2},{2,6},{... | collective-permute-start | bytes 196616 | tf_op jit(solution)/shard_map/ppermute | solution.py:481

commit v5 on v4

--- a/solution.py
+++ b/solution.py
@@ -13,6 +13,8 @@
 WIDE = 256
 F32 = jnp.float32
 BF16 = jnp.bfloat16
+VMEM = pl.BlockSpec(memory_space=pltpu.VMEM)
+KERNEL = pltpu.CompilerParams(dimension_semantics=("arbitrary",), vmem_limit_bytes=24 << 20)
 
 
 def swap_blocks(parts):
@@ -94,6 +96,7 @@
             pltpu.VMEM((here * rows // LANES * PROJ, LANES), F32),
             pltpu.VMEM((here, LANES), F32),
         ],
+        compiler_params=pltpu.CompilerParams(vmem_limit_bytes=24 << 20),
         name="project",
     )(x, gain, shift, w)
 
@@ -142,11 +145,10 @@
 def prep_call(at, labels, counts, w, rows, cols, seqs):
     pairs = CHAINS // 2
     width = w.shape[1]
-    vmem = pl.BlockSpec(memory_space=pltpu.VMEM)
     return pl.pallas_call(
         lambda *refs: prep_body(*refs, rows=rows, cols=cols, seqs=seqs),
-        in_specs=[pl.BlockSpec(memory_space=pltpu.SMEM), vmem, vmem, vmem],
-        out_specs=[vmem] * 6,
+        in_specs=[pl.BlockSpec(memory_space=pltpu.SMEM), VMEM, VMEM, VMEM],
+        out_specs=[VMEM] * 6,
         out_shape=[
             jax.ShapeDtypeStruct((1, rows * PROJ), jnp.int32),
             jax.ShapeDtypeStruct((pairs, 2, 2 * seqs, LANES), BF16),
@@ -156,6 +158,7 @@
             jax.ShapeDtypeStruct((width, PROJ * PROJ), BF16),
         ],
         scratch_shapes=[pltpu.VMEM(w.shape, F32)],
+        compiler_params=pltpu.CompilerParams(vmem_limit_bytes=24 << 20),
         name="prep",
     )(at, labels[None, :], counts, w)
 
@@ -168,6 +171,7 @@
 
 def back_body(grad_ref, wt_ref, out_ref):
     rows, cols, width = grad_ref.shape
+    g = pl.program_id(0)
     block = grad_ref[...].reshape(rows * cols, width)
     for u in range(PROJ * PROJ // WIDE):
         prod = nn_dot(block, wt_ref[:, u * WIDE : (u + 1) * WIDE]).astype(BF16)
@@ -180,7 +184,7 @@
                 ]
                 for q, part in enumerate(swap_blocks(parts)):
                     e = u * (WIDE // PROJ) + t * PER_TILE + q
-                    out_ref[0, e * cols : (e + 1) * cols, half * LANES : (half + 1) * LANES] = part
+                    out_ref[g, e * cols : (e + 1) * cols, half * LANES : (half + 1) * LANES] = part
 
 
 def back_call(grad, wt):
@@ -193,9 +197,9 @@
             pl.BlockSpec((step, cols, width), lambda g: (g, 0, 0)),
             pl.BlockSpec((width, PROJ * PROJ), lambda g: (0, 0)),
         ],
-        out_specs=pl.BlockSpec((1, PROJ * cols, WIDE), lambda g: (g, 0, 0)),
-        out_shape=jax.ShapeDtypeStruct((rows // step, PROJ * cols, WIDE), BF16),
-        compiler_params=pltpu.CompilerParams(dimension_semantics=("arbitrary",)),
+        out_specs=VMEM,
+        out_shape=pltpu.VMEM((rows // step, PROJ * cols, WIDE), BF16),
+        compiler_params=KERNEL,
         cost_estimate=cost(10, PROJ * cols, rows * PROJ, width),
         name="back",
     )(grad, wt)
@@ -241,7 +245,7 @@
 
     def one_pair(pair):
         masked_left(left_ref, lab_ref, lb_ref, pair)
-        q_ref[pair] += nt_dot(back_ref[0], lb_ref[...])
+        q_ref[pair] += nt_dot(back_ref[g], lb_ref[...])
 
     lax.fori_loop(first_pair(at_ref, labels_ref, g), last_pair(at_ref, labels_ref, g) + 1, over_pairs(one_pair), 0)
 
@@ -272,7 +276,7 @@
             num_scalar_prefetch=2,
             grid=(total // WIDE,),
             in_specs=[
-                pl.BlockSpec((1, span, WIDE), lambda g, *_: (g, 0, 0)),
+                VMEM,
                 pl.BlockSpec((seqs, WIDE), lambda g, *_: (0, g)),
                 pl.BlockSpec((1, WIDE), lambda g, *_: (0, g)),
                 whole(wide.shape),
@@ -286,7 +290,7 @@
             ],
         ),
         out_shape=jax.ShapeDtypeStruct((seqs, span), BF16),
-        compiler_params=pltpu.CompilerParams(dimension_semantics=("arbitrary",)),
+        compiler_params=KERNEL,
         cost_estimate=cost(10, span, total, seqs),
         name="right_grad",
     )(at, labels, back, left, lab, wide)
@@ -317,7 +321,7 @@
         lax.fori_loop(first_pair(at_ref, labels_ref, 0), last_pair(at_ref, labels_ref, last) + 1, build, 0)
 
     def one_pair(pair, total):
-        part = nn_dot(rm_ref[pair], back_ref[0])
+        part = nn_dot(rm_ref[pair], back_ref[g])
         keep0 = lab_ref[...] == 2 * pair
         keep1 = lab_ref[...] == 2 * pair + 1
         return total + jnp.where(keep0, part[:seqs], 0.0) + jnp.where(keep1, part[seqs:], 0.0)
@@ -337,7 +341,7 @@
             num_scalar_prefetch=2,
             grid=(total // WIDE,),
             in_specs=[
-                pl.BlockSpec((1, span, WIDE), lambda g, *_: (g, 0, 0)),
+                VMEM,
                 pl.BlockSpec((1, WIDE), lambda g, *_: (0, g)),
                 whole(right.shape),
                 whole(tall.shape),
@@ -349,14 +353,14 @@
             ],
         ),
         out_shape=jax.ShapeDtypeStruct((seqs, total), BF16),
-        compiler_params=pltpu.CompilerParams(dimension_semantics=("arbitrary",)),
+        compiler_params=KERNEL,
         cost_estimate=cost(10, span, total, seqs),
         name="left_grad",
     )(at, labels, back, lab, right, tall)
 
 
 def outer_body(at_ref, labels_ref, left_ref, lab_ref, right_ref, wide_ref, grad_ref,
-               x_ref, weight_out, rm_ref, lb_ref, acc_ref, sum_ref, turn_ref, flip_ref, part_ref):
+               outer_ref, weight_out, rm_ref, lb_ref, acc_ref, sum_ref, turn_ref, flip_ref, part_ref):
     g = pl.program_id(0)
     seqs = left_ref.shape[0]
     span = right_ref.shape[1]
@@ -409,10 +413,10 @@
             turned = swap_blocks(parts)
             for p in range(PER_TILE):
                 i = half * PER_TILE + p
-                x_ref[i * cols : (i + 1) * cols, t * LANES : (t + 1) * LANES] = turned[p]
+                outer_ref[g, i * cols : (i + 1) * cols, t * LANES : (t + 1) * LANES] = turned[p]
 
     flat = grad_ref[...].reshape(rows_here * cols, width)
-    sum_ref[...] += nn_dot(flat.T, x_ref[...])
+    sum_ref[...] += nn_dot(flat.T, outer_ref[g])
 
     @pl.when(g == last)
     def _():
@@ -442,7 +446,7 @@
                 pl.BlockSpec((step, cols, width), lambda g, *_: (g, 0, 0)),
             ],
             out_specs=[
-                pl.BlockSpec((step * cols, PROJ * PROJ), lambda g, *_: (g, 0)),
+                VMEM,
                 whole((PROJ * PROJ, width)),
             ],
             scratch_shapes=[
@@ -456,13 +460,41 @@
             ],
         ),
         out_shape=[
-            jax.ShapeDtypeStruct((rows * cols, PROJ * PROJ), BF16),
+            pltpu.VMEM((rows // step, step * cols, PROJ * PROJ), BF16),
             jax.ShapeDtypeStruct((PROJ * PROJ, width), F32),
         ],
-        compiler_params=pltpu.CompilerParams(dimension_semantics=("arbitrary",)),
+        compiler_params=KERNEL,
         cost_estimate=cost(20, span, total, seqs),
         name="outer",
     )(at, labels, left, lab, right, wide, grad)
+
+
+def pair_body(outer_ref, w_ref, offset_ref, pair_ref):
+    pair = nn_dot(outer_ref[pl.program_id(0)], w_ref[...]) + offset_ref[...]
+    pair_ref[...] = pair.astype(BF16)
+
+
+def pair_call(outer, w, offset):
+    groups, pairs, feats = outer.shape
+    width = w.shape[1]
+    return pl.pallas_call(
+        pair_body,
+        grid=(groups,),
+        in_specs=[
+            VMEM,
+            pl.BlockSpec(w.shape, lambda g: (0, 0)),
+            pl.BlockSpec(offset.shape, lambda g: (0, 0)),
+        ],
+        out_specs=pl.BlockSpec((pairs, width), lambda g: (g, 0)),
+        out_shape=jax.ShapeDtypeStruct((groups * pairs, width), BF16),
+        compiler_params=KERNEL,
+        cost_estimate=pl.CostEstimate(
+            flops=2 * groups * pairs * feats * width,
+            bytes_accessed=2 * groups * pairs * width,
+            transcendentals=0,
+        ),
+        name="pair",
+    )(outer, w, offset)
 
 
 class Ring:
@@ -536,6 +568,10 @@
         return shares.reshape(n * mine.shape[0], mine.shape[1])
 
 
+def in_vmem(value):
+    return pltpu.with_memory_space_constraint(value, pltpu.VMEM)
+
+
 def after(value, *others):
     return lax.optimization_barrier((value,) + others)[0]
 
@@ -558,6 +594,7 @@
     )
     back = back_call(after(grad, *pieces), wt)
     mine = ring.right_along_col(pieces)
+    back = in_vmem(back)
     right_grad = right_grad_call(at, labels, back, left, lab, plain)
 
     right = after(mine, right_grad)
@@ -566,15 +603,15 @@
         at, labels, left, lab, right, wide, grad
     )
     share = ring.weight_over_row(weight)
-    left_grad = left_grad_call(at, labels, after(back, weight), lab, right, tall)
+    left_grad = left_grad_call(at, labels, back, after(lab, weight), right, tall)
     share = after(share, left_grad)
 
     total = left_grad[:here].astype(F32)
     for k in range(1, n_col):
         total += ring.col_shift(left_grad[k * here : (k + 1) * here], n_col - k).astype(F32)
     adjoint_first = total.astype(BF16)
-    pair = jnp.dot(after(outer, left_grad, share), w, preferred_element_type=F32) + final_offset
-    pair_update = pair.astype(BF16).reshape(rows, cols, width)
+    pair_update = pair_call(in_vmem(outer), after(w, left_grad, share), final_offset[None, :])
+    pair_update = pair_update.reshape(rows, cols, width)
     mine = after(ring.weight_over_col(share), pair_update)
     grad_w_out = ring.weight_to_all(mine).astype(F32) / (n_row * rows)
     return pair_update, adjoint_first, grad_right, grad_w_out

time: 123 us -> 99 us (0.80)
  Pallas kernels: 60.3 us -> 46.5 us
  matrix products: 6.7 us -> 0 us
  other arithmetic: 8.85 us -> 3.11 us
  local copies, waits for them, and re-layouts: 5.93 us -> 8.25 us
    dot_general x1 -> x0, matrix products: 6.7 us -> none  [shards(): jnp.dot(after(outer, left_grad, share), w, preferred_element_type=F32)]
    pallas_call x1, Pallas kernels: 10.7 us -> 5.74 us  [left_grad_call(): pl.pallas_call(left_grad_body, grid_spec=pltpu.PrefetchScalarGridSpec(num...]
    pallas_call x1, Pallas kernels: 11.5 us -> 6.58 us  [right_grad_call(): pl.pallas_call(right_grad_body, grid_spec=pltpu.PrefetchScalarGridSpec(nu...]
    pallas_call x0 -> x1, Pallas kernels: none -> 4.82 us  [pair_call(): pl.pallas_call(pair_body, grid=(groups,), in_specs=[VMEM, pl.BlockSpec(w....]
    unnamed x11 -> x25, local copies, waits for them, and re-layouts: 3.41 us -> 7.84 us
    pallas_call x1, Pallas kernels: 9.73 us -> 6.85 us  [back_call(): pl.pallas_call(back_body, grid=(rows // step,), in_specs=[pl.BlockSpec((s...]
    pallas_call x1, Pallas kernels: 20 us -> 17.4 us  [outer_call(): pl.pallas_call(outer_body, grid_spec=pltpu.PrefetchScalarGridSpec(num_sca...]
    pallas_call x1, Pallas kernels: 5.64 us -> 3.73 us  [project_call(): pl.pallas_call(lambda *refs: project_body(*refs, cols=cols), out_shape=[j...]
  transfers between devices with their start and end apart: 25 -> 25, of which waited for: 1 -> 1; matrix products, arithmetic and copies ran while one was open for 14% -> 2% of each run, Pallas kernels for 45% -> 43%
where the time goes in v5:
time: 99 us; the launch traced here: 98.6 us
  Pallas kernels  46.5 us (47%)
  starting transfers between devices  35.9 us (36%)
  local copies, waits for them, and re-layouts  8.25 us (8%)
  waiting for transfers between devices  3.87 us (4%)
  other arithmetic  3.11 us (3%)
    ppermute x12, starting transfers between devices, col_shift(): return lax.ppermute(value, 'col', [((t + k) % n, t) for t in range(n)])  20.8 us
    pallas_call x1, Pallas kernels, outer_call(): pl.pallas_call(outer_body, grid_spec=pltpu.PrefetchScalarGridSpec(num_sca...  17.4 us
    ppermute x4, starting transfers between devices, right_grad_home(): got = lax.ppermute(block, ('row', 'col'), pairs).astype(F32)[None]  8.1 us
    unnamed x25, local copies, waits for them, and re-layouts  7.84 us
    ppermute x9, starting transfers between devices, row_shift(): return lax.ppermute(value, 'row', [((t + k) % n, t) for t in range(n)])  7.02 us
    pallas_call x1, Pallas kernels, back_call(): pl.pallas_call(back_body, grid=(rows // step,), in_specs=[pl.BlockSpec((s...  6.85 us
    pallas_call x1, Pallas kernels, right_grad_call(): pl.pallas_call(right_grad_body, grid_spec=pltpu.PrefetchScalarGridSpec(nu...  6.58 us
    pallas_call x1, Pallas kernels, left_grad_call(): pl.pallas_call(left_grad_body, grid_spec=pltpu.PrefetchScalarGridSpec(num...  5.74 us
  transfers between devices with their start and end apart: 25, of which 1 were waited for; matrix products, arithmetic and copies ran while one was open for 2% of the time, Pallas kernels for 43%

profile of v5, /device:TPU:0, one launch (start us, length us, event | category | flops | bytes accessed | tf_op | source)
XLA Modules:
  0.0 98.6 jit_solution(15127610995413787540)
XLA Ops:
  0.6 0.8 copy.14
  1.5 0.8 copy.15
  2.4 1.2 %copy-done = bf16[32,64,256]{2,1,0:T(8,128)(2,1)S(1)} copy-done((bf16[32,64,256]{2,1,0:T(8,128)(2,1)S(1)}, bf16[32,64,256]{2,1,0:T(8,128)(2,1)}, u32[]{:S(2)}) %copy-start) | copy-done | bytes 1048600
  5.0 3.7 %project.1 = (bf16[32,2048]{1,0:T(8,128)(2,1)S(1)}, bf16[32,2048]{1,0:T(8,128)(2,1)S(1)}) custom-call(bf16[32,64,256]{2,1,0:T(8,128)(2,1)S(1)} %copy-done, f32[1,256]{1,0:T(1,128)S(1)} %bitcast.51, f32[1,256]{1,0:T(1,128)S(1)} %bitcast.52, bf16[256,128]{1,0:T(8,128)(2,1)S(1)} %fusion.6.refs_3_), custom_call_target="tpu_custom_call" | custom-call | tf_op jit(solution)/shard_map/project/pallas_call | solution.py:91
  8.7 3.1 %collective-permute-start.2 = (bf16[32,2048]{1,0:T(8,128)(2,1)S(1)}, bf16[32,2048]{1,0:T(8,128)(2,1)S(1)}, u32[]{:S(2)}, u32[]{:S(2)}) collective-permute-start(bf16[32,2048]{1,0:T(8,128)(2,1)S(1)} %get-tuple-element.21), channel_id=1, source_target_pairs={{3,0},{0,1},{1,2},{2,3},{7,4},{4,5},{5,6},{6,7},{11,8},{8,9},{9,10... | collective-permute-start | bytes 393224 | tf_op jit(solution)/shard_map/ppermute | solution.py:509
  11.8 2.6 %collective-permute-start.1 = (bf16[32,2048]{1,0:T(8,128)(2,1)S(1)}, bf16[32,2048]{1,0:T(8,128)(2,1)S(1)}, u32[]{:S(2)}, u32[]{:S(2)}) collective-permute-start(bf16[32,2048]{1,0:T(8,128)(2,1)S(1)} %get-tuple-element.21), channel_id=1, source_target_pairs={{2,0},{3,1},{0,2},{1,3},{6,4},{7,5},{4,6},{5,7},{10,8},{11,9},{8,1... | collective-permute-start | bytes 393224 | tf_op jit(solution)/shard_map/ppermute | solution.py:509
  14.4 1.5 %collective-permute-start.4 = (bf16[32,2048]{1,0:T(8,128)(2,1)S(1)}, bf16[32,2048]{1,0:T(8,128)(2,1)S(1)}, u32[]{:S(2)}, u32[]{:S(2)}) collective-permute-start(bf16[32,2048]{1,0:T(8,128)(2,1)S(1)} %get-tuple-element.22), channel_id=1, source_target_pairs={{8,0},{12,4},{0,8},{4,12},{9,1},{13,5},{1,9},{5,13},{10,2},{14,6},... | collective-permute-start | bytes 393224 | tf_op jit(solution)/shard_map/ppermute | solution.py:513
  15.9 1.5 %collective-permute-start.3 = (bf16[32,2048]{1,0:T(8,128)(2,1)S(1)}, bf16[32,2048]{1,0:T(8,128)(2,1)S(1)}, u32[]{:S(2)}, u32[]{:S(2)}) collective-permute-start(bf16[32,2048]{1,0:T(8,128)(2,1)S(1)} %get-tuple-element.22), channel_id=1, source_target_pairs={{4,0},{8,4},{12,8},{0,12},{5,1},{9,5},{13,9},{1,13},{6,2},{10,6},{... | collective-permute-start | bytes 393224 | tf_op jit(solution)/shard_map/ppermute | solution.py:513
  17.8 0.9 copy-done.1
  18.7 0.7 copy-done.2
  20.1 1.4 %prep.1 = (s32[1,2048]{1,0:T(1,128)S(1)}, bf16[4,2,256,128]{3,2,1,0:T(8,128)(2,1)S(1)}, bf16[4,2,64,256]{3,2,1,0:T(8,128)(2,1)S(1)}, f32[4,64,256]{2,1,0:T(8,128...) custom-call(s32[3]{0:T(128)S(1)} %add_convert_fusion.3.refs_0_.at_ref, s32[1,256]{1,0:T(1,128)S(1)} %bitcast.50, ...), custom_call_target="tpu_custom_call" | custom-call | tf_op jit(solution)/shard_map/prep/pallas_call | solution.py:148
  21.5 1.4 %collective-permute-start = (bf16[32,2048]{1,0:T(8,128)(2,1)S(1)}, bf16[32,2048]{1,0:T(8,128)(2,1)S(1)}, u32[]{:S(2)}, u32[]{:S(2)}) collective-permute-start(bf16[32,2048]{1,0:T(8,128)(2,1)S(1)} %get-tuple-element.21), channel_id=1, source_target_pairs={{1,0},{2,1},{3,2},{0,3},{5,4},{6,5},{7,6},{4,7},{9,8},{10,9},{11,1... | collective-permute-start | bytes 393224 | tf_op jit(solution)/shard_map/ppermute | solution.py:509
  23.0 0.7 collective-permute-start.8
  24.1 1.2 %copy-done.8 = bf16[64,64,128]{2,1,0:T(8,128)(2,1)S(1)} copy-done((bf16[64,64,128]{2,1,0:T(8,128)(2,1)S(1)}, bf16[64,64,128]{2,1,0:T(8,128)(2,1)}, u32[]{:S(2)}) %copy-start.8) | copy-done | bytes 1048600
  25.3 6.9 %back.1.back_ref = bf16[8,2048,256]{2,1,0:T(8,128)(2,1)S(1)} custom-call(bf16[64,64,128]{2,1,0:T(8,128)(2,1)S(1)} %copy-done.8, bf16[128,1024]{1,0:T(8,128)(2,1)S(1)} %get-tuple-element.26.wt_ref), custom_call_target="tpu_custom_call" | custom-call | flops 21474836480 | bytes 8388608 | tf_op jit(solution)/shard_map/back/pallas_call | solution.py:193
  32.2 2.8 %collective-permute-start.6 = (bf16[32,2048]{1,0:T(8,128)(2,1)S(1)}, bf16[32,2048]{1,0:T(8,128)(2,1)S(1)}, u32[]{:S(2)}, u32[]{:S(2)}) collective-permute-start(bf16[32,2048]{1,0:T(8,128)(2,1)S(1)} %get-tuple-element.48), channel_id=1, source_target_pairs={{1,0},{2,1},{3,2},{0,3},{5,4},{6,5},{7,6},{4,7},{9,8},{10,9},{11,1... | collective-permute-start | bytes 393224 | tf_op jit(solution)/shard_map/ppermute | solution.py:509
  35.1 6.6 %right_grad.1 = bf16[128,2048]{1,0:T(8,128)(2,1)S(1)} custom-call(s32[3]{0:T(128)S(1)} %add_convert_fusion.3.refs_0_.at_ref, s32[256]{0:T(256)S(1)} %copy-done.4, bf16[8,2048,256]{2,1,0:T(8,128)(2,1)S(1)} %back.1.back_ref, bf16[128,2048]{1,0:T(8,128)(2,1)S(1)} %constant_dynamic-update-slice_fusion.left_ref, s32[1,2048]{1,0:T(1,128)S(1)} %get-tuple-element.33.lab_ref, ...), custom_call_target="tpu_custom_call" | custom-call | flops 21474836480 | bytes 8388608 | tf_op jit(solution)/shard_map/right_grad/pallas_call | solution.py:273
  42.5 5.3 %collective-permute-start.18 = (bf16[32,2048]{1,0:T(8,128)(2,1)S(1)}, bf16[32,2048]{1,0:T(8,128)(2,1)S(1)}, u32[]{:S(2)}, u32[]{:S(2)}) collective-permute-start(bf16[32,2048]{1,0:T(8,128)(2,1)S(1)} %get-tuple-element.39), channel_id=1, source_target_pairs={{0,3},{1,7},{2,11},{3,15},{4,0},{5,4},{6,8},{7,12},{8,1},{9,5},{10... | collective-permute-start | bytes 393224 | tf_op jit(solution)/shard_map/ppermute | solution.py:542
  47.8 2.1 %collective-permute-start.16 = (bf16[32,2048]{1,0:T(8,128)(2,1)S(1)}, bf16[32,2048]{1,0:T(8,128)(2,1)S(1)}, u32[]{:S(2)}, u32[]{:S(2)}) collective-permute-start(bf16[32,2048]{1,0:T(8,128)(2,1)S(1)} %get-tuple-element.41), channel_id=1, source_target_pairs={{0,1},{1,5},{2,9},{3,13},{4,2},{5,6},{6,10},{7,14},{8,3},{9,7},{10... | collective-permute-start | bytes 393224 | tf_op jit(solution)/shard_map/ppermute | solution.py:542
  50.0 17.4 %outer.1 = (bf16[8,512,1024]{2,1,0:T(8,128)(2,1)S(1)}, f32[1024,128]{1,0:T(8,128)S(1)}) custom-call(s32[3]{0:T(128)S(1)} %add_convert_fusion.3.refs_0_.at_ref, s32[256]{0:T(256)S(1)} %copy-done.4, bf16[128,2048]{1,0:T(8,128)(2,1)S(1)} %constant_dynamic-update-slice_fusion.left_ref, s32[1,2048]{1,0:T(1,128)S(1)} %get-tuple-element.33.lab_ref, ...), custom_call_target="tpu_custom_call" | custom-call | flops 42949672960 | bytes 8388608 | tf_op jit(solution)/shard_map/outer/pallas_call | solution.py:436
  67.5 5.7 %left_grad.1 = bf16[128,2048]{1,0:T(8,128)(2,1)S(1)} custom-call(s32[3]{0:T(128)S(1)} %add_convert_fusion.3.refs_0_.at_ref, s32[256]{0:T(256)S(1)} %copy-done.4, bf16[8,2048,256]{2,1,0:T(8,128)(2,1)S(1)} %back.1.back_ref, s32[1,2048]{1,0:T(1,128)S(1)} %get-tuple-element.33.lab_ref, bf16[128,2048]{1,0:T(8,128)(2,1)S(1)} %pad_maximum_fusion.1.right_ref, ...), custom_call_target="tpu_custom_call" | custom-call | flops 21474836480 | bytes 8388608 | tf_op jit(solution)/shard_map/left_grad/pallas_call | solution.py:338
  73.3 1.8 %collective-permute-start.11 = (bf16[256,128]{1,0:T(8,128)(2,1)S(1)}, bf16[256,128]{1,0:T(8,128)(2,1)S(1)}, u32[]{:S(2)}, u32[]{:S(2)}) collective-permute-start(bf16[256,128]{1,0:T(8,128)(2,1)S(1)} %get-tuple-element.50), channel_id=1, source_target_pairs={{4,0},{8,4},{12,8},{0,12},{5,1},{9,5},{13,9},{1,13},{6,2},{10,6},{... | collective-permute-start | bytes 196616 | tf_op jit(solution)/shard_map/ppermute | solution.py:513
  75.1 0.7 collective-permute-start.12
  75.8 3.2 %collective-permute-start.14 = (bf16[32,2048]{1,0:T(8,128)(2,1)S(1)}, bf16[32,2048]{1,0:T(8,128)(2,1)S(1)}, u32[]{:S(2)}, u32[]{:S(2)}) collective-permute-start(bf16[32,2048]{1,0:T(8,128)(2,1)S(1)} %get-tuple-element.43), channel_id=1, source_target_pairs={{1,0},{2,1},{3,2},{0,3},{5,4},{6,5},{7,6},{4,7},{9,8},{10,9},{11,1... | collective-permute-start | bytes 393224 | tf_op jit(solution)/shard_map/ppermute | solution.py:509
  79.0 0.7 add_convert_fusion
  80.4 3.3 %collective-permute-start.19 = (bf16[256,128]{1,0:T(8,128)(2,1)S(1)}, bf16[256,128]{1,0:T(8,128)(2,1)S(1)}, u32[]{:S(2)}, u32[]{:S(2)}) collective-permute-start(bf16[256,128]{1,0:T(8,128)(2,1)S(1)} %convert_element_type.123), channel_id=1, source_target_pairs={{1,0},{2,1},{3,2},{0,3},{5,4},{6,5},{7,6},{4,7},{9,8},{10,9},{11,1... | collective-permute-start | bytes 196616 | tf_op jit(solution)/shard_map/ppermute | solution.py:509
  83.6 4.8 %pair.1 = bf16[4096,128]{1,0:T(8,128)(2,1)} custom-call(bf16[8,512,1024]{2,1,0:T(8,128)(2,1)S(1)} %get-tuple-element.30.outer_ref, bf16[1024,128]{1,0:T(8,128)(2,1)S(1)} %get-tuple-element.36.w_ref, f32[1,128]{1,0:T(1,128)S(1)} %bitcast.53), custom_call_target="tpu_custom_call" | custom-call | flops 1073741824 | bytes 1048576 | tf_op jit(solution)/shard_map/pair/pallas_call | solution.py:480
  88.5 2.0 %collective-permute-start.13 = (bf16[32,2048]{1,0:T(8,128)(2,1)S(1)}, bf16[32,2048]{1,0:T(8,128)(2,1)S(1)}, u32[]{:S(2)}, u32[]{:S(2)}) collective-permute-start(bf16[32,2048]{1,0:T(8,128)(2,1)S(1)} %get-tuple-element.44), channel_id=1, source_target_pairs={{2,0},{3,1},{0,2},{1,3},{6,4},{7,5},{4,6},{5,7},{10,8},{11,9},{8,1... | collective-permute-start | bytes 393224 | tf_op jit(solution)/shard_map/ppermute | solution.py:509
  90.6 2.0 %collective-permute-start.23 = (bf16[256,128]{1,0:T(8,128)(2,1)S(1)}, bf16[256,128]{1,0:T(8,128)(2,1)S(1)}, u32[]{:S(2)}, u32[]{:S(2)}) collective-permute-start(bf16[256,128]{1,0:T(8,128)(2,1)S(1)} %add_convert_fusion.2), channel_id=1, source_target_pairs={{8,0},{12,4},{0,8},{4,12},{9,1},{13,5},{1,9},{5,13},{10,2},{14,6},... | collective-permute-start | bytes 196616 | tf_op jit(solution)/shard_map/ppermute | solution.py:513
  92.8 3.8 %collective-permute-done.13 = bf16[32,2048]{1,0:T(8,128)(2,1)S(1)} collective-permute-done((bf16[32,2048]{1,0:T(8,128)(2,1)S(1)}, bf16[32,2048]{1,0:T(8,128)(2,1)S(1)}, u32[]{:S(2)}, u32[]{:S(2)}) %collective-permute-start.13) | collective-permute-done | bytes 131104 | tf_op jit(solution)/shard_map/ppermute | solution.py:509
  96.6 0.7 add_convert_fusion.1
  97.3 1.3 %convert_multiply_fusion = f32[1024,128]{1,0:T(8,128)} fusion(pred[1024]{0:T(1024)(128)(4,1)S(1)} %broadcast_in_dim.105, pred[1024]{0:T(1024)(128)(4,1)S(1)} %broadcast_in_dim.100, pred[1024]{0:T(1024)(128)(4,1)S(1)} %broadcast_in_dim.95, bf16[256,128]{1,0:T(8,128)(2,1)S(1)} %add_convert_fusion.2, bf16[256,128]{1,0:T(8,128)(2,1)S(1)} %collective-permute-done.24, ...), kind=kLoop, calls=%fused_computation.2 | loop fusion | flops 655360 | bytes 789504 | tf_op jit(solution)/shard_map/div | solution.py:616
  (74 shorter events, 4.9 us)
Async XLA Ops:
  2.4 1.2 %copy-start = (bf16[32,64,256]{2,1,0:T(8,128)(2,1)S(1)}, bf16[32,64,256]{2,1,0:T(8,128)(2,1)}, u32[]{:S(2)}) copy-start(bf16[32,64,256]{2,1,0:T(8,128)(2,1)} %refs_0_.1) | copy-start | bytes 3145732
  8.7 26.4 %collective-permute-start.2 = (bf16[32,2048]{1,0:T(8,128)(2,1)S(1)}, bf16[32,2048]{1,0:T(8,128)(2,1)S(1)}, u32[]{:S(2)}, u32[]{:S(2)}) collective-permute-start(bf16[32,2048]{1,0:T(8,128)(2,1)S(1)} %get-tuple-element.21), channel_id=1, source_target_pairs={{3,0},{0,1},{1,2},{2,3},{7,4},{4,5},{5,6},{6,7},{11,8},{8,9},{9,10... | collective-permute-start | bytes 393224 | tf_op jit(solution)/shard_map/ppermute | solution.py:509
  11.8 23.2 %collective-permute-start.1 = (bf16[32,2048]{1,0:T(8,128)(2,1)S(1)}, bf16[32,2048]{1,0:T(8,128)(2,1)S(1)}, u32[]{:S(2)}, u32[]{:S(2)}) collective-permute-start(bf16[32,2048]{1,0:T(8,128)(2,1)S(1)} %get-tuple-element.21), channel_id=1, source_target_pairs={{2,0},{3,1},{0,2},{1,3},{6,4},{7,5},{4,6},{5,7},{10,8},{11,9},{8,1... | collective-permute-start | bytes 393224 | tf_op jit(solution)/shard_map/ppermute | solution.py:509
  14.4 7.1 %collective-permute-start.5 = (bf16[32,2048]{1,0:T(8,128)(2,1)S(1)}, bf16[32,2048]{1,0:T(8,128)(2,1)S(1)}, u32[]{:S(2)}, u32[]{:S(2)}) collective-permute-start(bf16[32,2048]{1,0:T(8,128)(2,1)S(1)} %get-tuple-element.22), channel_id=1, source_target_pairs={{12,0},{0,4},{4,8},{8,12},{13,1},{1,5},{5,9},{9,13},{14,2},{2,6},{... | collective-permute-start | bytes 393224 | tf_op jit(solution)/shard_map/ppermute | solution.py:513
  14.4 8.5 %collective-permute-start.4 = (bf16[32,2048]{1,0:T(8,128)(2,1)S(1)}, bf16[32,2048]{1,0:T(8,128)(2,1)S(1)}, u32[]{:S(2)}, u32[]{:S(2)}) collective-permute-start(bf16[32,2048]{1,0:T(8,128)(2,1)S(1)} %get-tuple-element.22), channel_id=1, source_target_pairs={{8,0},{12,4},{0,8},{4,12},{9,1},{13,5},{1,9},{5,13},{10,2},{14,6},... | collective-permute-start | bytes 393224 | tf_op jit(solution)/shard_map/ppermute | solution.py:513
  15.9 7.0 %collective-permute-start.3 = (bf16[32,2048]{1,0:T(8,128)(2,1)S(1)}, bf16[32,2048]{1,0:T(8,128)(2,1)S(1)}, u32[]{:S(2)}, u32[]{:S(2)}) collective-permute-start(bf16[32,2048]{1,0:T(8,128)(2,1)S(1)} %get-tuple-element.22), channel_id=1, source_target_pairs={{4,0},{8,4},{12,8},{0,12},{5,1},{9,5},{13,9},{1,13},{6,2},{10,6},{... | collective-permute-start | bytes 393224 | tf_op jit(solution)/shard_map/ppermute | solution.py:513
  17.8 1.0 copy-start.1
  18.7 0.7 copy-start.2
  21.5 10.7 %collective-permute-start = (bf16[32,2048]{1,0:T(8,128)(2,1)S(1)}, bf16[32,2048]{1,0:T(8,128)(2,1)S(1)}, u32[]{:S(2)}, u32[]{:S(2)}) collective-permute-start(bf16[32,2048]{1,0:T(8,128)(2,1)S(1)} %get-tuple-element.21), channel_id=1, source_target_pairs={{1,0},{2,1},{3,2},{0,3},{5,4},{6,5},{7,6},{4,7},{9,8},{10,9},{11,1... | collective-permute-start | bytes 393224 | tf_op jit(solution)/shard_map/ppermute | solution.py:509
  23.0 24.8 %collective-permute-start.8 = (bf16[32,2048]{1,0:T(8,128)(2,1)S(1)}, bf16[32,2048]{1,0:T(8,128)(2,1)S(1)}, u32[]{:S(2)}, u32[]{:S(2)}) collective-permute-start(bf16[32,2048]{1,0:T(8,128)(2,1)S(1)} %get-tuple-element.46), channel_id=1, source_target_pairs={{3,0},{0,1},{1,2},{2,3},{7,4},{4,5},{5,6},{6,7},{11,8},{8,9},{9,10... | collective-permute-start | bytes 393224 | tf_op jit(solution)/shard_map/ppermute | solution.py:509
  23.7 24.0 %collective-permute-start.7 = (bf16[32,2048]{1,0:T(8,128)(2,1)S(1)}, bf16[32,2048]{1,0:T(8,128)(2,1)S(1)}, u32[]{:S(2)}, u32[]{:S(2)}) collective-permute-start(bf16[32,2048]{1,0:T(8,128)(2,1)S(1)} %get-tuple-element.47), channel_id=1, source_target_pairs={{2,0},{3,1},{0,2},{1,3},{6,4},{7,5},{4,6},{5,7},{10,8},{11,9},{8,1... | collective-permute-start | bytes 393224 | tf_op jit(solution)/shard_map/ppermute | solution.py:509
  24.1 1.2 %copy-start.8 = (bf16[64,64,128]{2,1,0:T(8,128)(2,1)S(1)}, bf16[64,64,128]{2,1,0:T(8,128)(2,1)}, u32[]{:S(2)}) copy-start(bf16[64,64,128]{2,1,0:T(8,128)(2,1)} %grad_ref.2) | copy-start | bytes 3145732
  25.3 9.8 %copy-start.4 = (s32[256]{0:T(256)S(1)}, s32[256]{0:T(256)}, u32[]{:S(2)}) copy-start(s32[256]{0:T(256)} %labels_ref.5) | copy-start | bytes 3076
  32.2 17.7 %collective-permute-start.6 = (bf16[32,2048]{1,0:T(8,128)(2,1)S(1)}, bf16[32,2048]{1,0:T(8,128)(2,1)S(1)}, u32[]{:S(2)}, u32[]{:S(2)}) collective-permute-start(bf16[32,2048]{1,0:T(8,128)(2,1)S(1)} %get-tuple-element.48), channel_id=1, source_target_pairs={{1,0},{2,1},{3,2},{0,3},{5,4},{6,5},{7,6},{4,7},{9,8},{10,9},{11,1... | collective-permute-start | bytes 393224 | tf_op jit(solution)/shard_map/ppermute | solution.py:509
  35.1 14.8 %copy-start.9 = (bf16[64,64,128]{2,1,0:T(8,128)(2,1)S(1)}, bf16[64,64,128]{2,1,0:T(8,128)(2,1)}, u32[]{:S(2)}) copy-start(bf16[64,64,128]{2,1,0:T(8,128)(2,1)} %grad_ref.2) | copy-start | bytes 3145732
  41.8 31.5 %collective-permute-start.15 = (bf16[32,2048]{1,0:T(8,128)(2,1)S(1)}, bf16[32,2048]{1,0:T(8,128)(2,1)S(1)}, u32[]{:S(2)}, u32[]{:S(2)}) collective-permute-start(bf16[32,2048]{1,0:T(8,128)(2,1)S(1)} %get-tuple-element.38), channel_id=1, source_target_pairs={{0,0},{1,4},{2,8},{3,12},{4,1},{5,5},{6,9},{7,13},{8,2},{9,6},{10,... | collective-permute-start | bytes 393224 | tf_op jit(solution)/shard_map/ppermute | solution.py:542
  42.5 32.6 %collective-permute-start.18 = (bf16[32,2048]{1,0:T(8,128)(2,1)S(1)}, bf16[32,2048]{1,0:T(8,128)(2,1)S(1)}, u32[]{:S(2)}, u32[]{:S(2)}) collective-permute-start(bf16[32,2048]{1,0:T(8,128)(2,1)S(1)} %get-tuple-element.39), channel_id=1, source_target_pairs={{0,3},{1,7},{2,11},{3,15},{4,0},{5,4},{6,8},{7,12},{8,1},{9,5},{10... | collective-permute-start | bytes 393224 | tf_op jit(solution)/shard_map/ppermute | solution.py:542
  47.8 27.3 %collective-permute-start.17 = (bf16[32,2048]{1,0:T(8,128)(2,1)S(1)}, bf16[32,2048]{1,0:T(8,128)(2,1)S(1)}, u32[]{:S(2)}, u32[]{:S(2)}) collective-permute-start(bf16[32,2048]{1,0:T(8,128)(2,1)S(1)} %get-tuple-element.40), channel_id=1, source_target_pairs={{0,2},{1,6},{2,10},{3,14},{4,3},{5,7},{6,11},{7,15},{8,0},{9,4},{1... | collective-permute-start | bytes 393224 | tf_op jit(solution)/shard_map/ppermute | solution.py:542
  47.8 28.0 %collective-permute-start.16 = (bf16[32,2048]{1,0:T(8,128)(2,1)S(1)}, bf16[32,2048]{1,0:T(8,128)(2,1)S(1)}, u32[]{:S(2)}, u32[]{:S(2)}) collective-permute-start(bf16[32,2048]{1,0:T(8,128)(2,1)S(1)} %get-tuple-element.41), channel_id=1, source_target_pairs={{0,1},{1,5},{2,9},{3,13},{4,2},{5,6},{6,10},{7,14},{8,3},{9,7},{10... | collective-permute-start | bytes 393224 | tf_op jit(solution)/shard_map/ppermute | solution.py:542
  67.4 12.2 %collective-permute-start.9 = (bf16[256,128]{1,0:T(8,128)(2,1)S(1)}, bf16[256,128]{1,0:T(8,128)(2,1)S(1)}, u32[]{:S(2)}, u32[]{:S(2)}) collective-permute-start(bf16[256,128]{1,0:T(8,128)(2,1)S(1)} %get-tuple-element.49), channel_id=1, source_target_pairs={{12,0},{0,4},{4,8},{8,12},{13,1},{1,5},{5,9},{9,13},{14,2},{2,6},{... | collective-permute-start | bytes 196616 | tf_op jit(solution)/shard_map/ppermute | solution.py:513
  67.5 16.1 %copy-start.7 = (f32[128]{0:T(128)S(1)}, f32[128]{0:T(128)}, u32[]{:S(2)}) copy-start(f32[128]{0:T(128)} %param.16) | copy-start | bytes 1540
  73.3 6.4 %collective-permute-start.11 = (bf16[256,128]{1,0:T(8,128)(2,1)S(1)}, bf16[256,128]{1,0:T(8,128)(2,1)S(1)}, u32[]{:S(2)}, u32[]{:S(2)}) collective-permute-start(bf16[256,128]{1,0:T(8,128)(2,1)S(1)} %get-tuple-element.50), channel_id=1, source_target_pairs={{4,0},{8,4},{12,8},{0,12},{5,1},{9,5},{13,9},{1,13},{6,2},{10,6},{... | collective-permute-start | bytes 196616 | tf_op jit(solution)/shard_map/ppermute | solution.py:513
  75.1 4.6 %collective-permute-start.10 = (bf16[256,128]{1,0:T(8,128)(2,1)S(1)}, bf16[256,128]{1,0:T(8,128)(2,1)S(1)}, u32[]{:S(2)}, u32[]{:S(2)}) collective-permute-start(bf16[256,128]{1,0:T(8,128)(2,1)S(1)} %get-tuple-element.51), channel_id=1, source_target_pairs={{8,0},{12,4},{0,8},{4,12},{9,1},{13,5},{1,9},{5,13},{10,2},{14,6},... | collective-permute-start | bytes 196616 | tf_op jit(solution)/shard_map/ppermute | solution.py:513
  75.1 17.6 %collective-permute-start.12 = (bf16[32,2048]{1,0:T(8,128)(2,1)S(1)}, bf16[32,2048]{1,0:T(8,128)(2,1)S(1)}, u32[]{:S(2)}, u32[]{:S(2)}) collective-permute-start(bf16[32,2048]{1,0:T(8,128)(2,1)S(1)} %get-tuple-element.42), channel_id=1, source_target_pairs={{3,0},{0,1},{1,2},{2,3},{7,4},{4,5},{5,6},{6,7},{11,8},{8,9},{9,10... | collective-permute-start | bytes 393224 | tf_op jit(solution)/shard_map/ppermute | solution.py:509
  75.8 17.0 %collective-permute-start.14 = (bf16[32,2048]{1,0:T(8,128)(2,1)S(1)}, bf16[32,2048]{1,0:T(8,128)(2,1)S(1)}, u32[]{:S(2)}, u32[]{:S(2)}) collective-permute-start(bf16[32,2048]{1,0:T(8,128)(2,1)S(1)} %get-tuple-element.43), channel_id=1, source_target_pairs={{1,0},{2,1},{3,2},{0,3},{5,4},{6,5},{7,6},{4,7},{9,8},{10,9},{11,1... | collective-permute-start | bytes 393224 | tf_op jit(solution)/shard_map/ppermute | solution.py:509
  79.7 8.7 %collective-permute-start.21 = (bf16[256,128]{1,0:T(8,128)(2,1)S(1)}, bf16[256,128]{1,0:T(8,128)(2,1)S(1)}, u32[]{:S(2)}, u32[]{:S(2)}) collective-permute-start(bf16[256,128]{1,0:T(8,128)(2,1)S(1)} %convert_element_type.123), channel_id=1, source_target_pairs={{3,0},{0,1},{1,2},{2,3},{7,4},{4,5},{5,6},{6,7},{11,8},{8,9},{9,10... | collective-permute-start | bytes 196616 | tf_op jit(solution)/shard_map/ppermute | solution.py:509
  79.8 10.7 %collective-permute-start.20 = (bf16[256,128]{1,0:T(8,128)(2,1)S(1)}, bf16[256,128]{1,0:T(8,128)(2,1)S(1)}, u32[]{:S(2)}, u32[]{:S(2)}) collective-permute-start(bf16[256,128]{1,0:T(8,128)(2,1)S(1)} %convert_element_type.123), channel_id=1, source_target_pairs={{2,0},{3,1},{0,2},{1,3},{6,4},{7,5},{4,6},{5,7},{10,8},{11,9},{8,1... | collective-permute-start | bytes 196616 | tf_op jit(solution)/shard_map/ppermute | solution.py:509
  80.4 10.1 %collective-permute-start.19 = (bf16[256,128]{1,0:T(8,128)(2,1)S(1)}, bf16[256,128]{1,0:T(8,128)(2,1)S(1)}, u32[]{:S(2)}, u32[]{:S(2)}) collective-permute-start(bf16[256,128]{1,0:T(8,128)(2,1)S(1)} %convert_element_type.123), channel_id=1, source_target_pairs={{1,0},{2,1},{3,2},{0,3},{5,4},{6,5},{7,6},{4,7},{9,8},{10,9},{11,1... | collective-permute-start | bytes 196616 | tf_op jit(solution)/shard_map/ppermute | solution.py:509
  88.5 8.1 %collective-permute-start.13 = (bf16[32,2048]{1,0:T(8,128)(2,1)S(1)}, bf16[32,2048]{1,0:T(8,128)(2,1)S(1)}, u32[]{:S(2)}, u32[]{:S(2)}) collective-permute-start(bf16[32,2048]{1,0:T(8,128)(2,1)S(1)} %get-tuple-element.44), channel_id=1, source_target_pairs={{2,0},{3,1},{0,2},{1,3},{6,4},{7,5},{4,6},{5,7},{10,8},{11,9},{8,1... | collective-permute-start | bytes 393224 | tf_op jit(solution)/shard_map/ppermute | solution.py:509
  90.5 6.8 %collective-permute-start.24 = (bf16[256,128]{1,0:T(8,128)(2,1)S(1)}, bf16[256,128]{1,0:T(8,128)(2,1)S(1)}, u32[]{:S(2)}, u32[]{:S(2)}) collective-permute-start(bf16[256,128]{1,0:T(8,128)(2,1)S(1)} %add_convert_fusion.2), channel_id=1, source_target_pairs={{4,0},{8,4},{12,8},{0,12},{5,1},{9,5},{13,9},{1,13},{6,2},{10,6},{... | collective-permute-start | bytes 196616 | tf_op jit(solution)/shard_map/ppermute | solution.py:513
  90.6 6.7 %collective-permute-start.23 = (bf16[256,128]{1,0:T(8,128)(2,1)S(1)}, bf16[256,128]{1,0:T(8,128)(2,1)S(1)}, u32[]{:S(2)}, u32[]{:S(2)}) collective-permute-start(bf16[256,128]{1,0:T(8,128)(2,1)S(1)} %add_convert_fusion.2), channel_id=1, source_target_pairs={{8,0},{12,4},{0,8},{4,12},{9,1},{13,5},{1,9},{5,13},{10,2},{14,6},... | collective-permute-start | bytes 196616 | tf_op jit(solution)/shard_map/ppermute | solution.py:513
  92.6 4.7 %collective-permute-start.22 = (bf16[256,128]{1,0:T(8,128)(2,1)S(1)}, bf16[256,128]{1,0:T(8,128)(2,1)S(1)}, u32[]{:S(2)}, u32[]{:S(2)}) collective-permute-start(bf16[256,128]{1,0:T(8,128)(2,1)S(1)} %add_convert_fusion.2), channel_id=1, source_target_pairs={{12,0},{0,4},{4,8},{8,12},{13,1},{1,5},{5,9},{9,13},{14,2},{2,6},{... | collective-permute-start | bytes 196616 | tf_op jit(solution)/shard_map/ppermute | solution.py:513
  (3 other events, 2.0 us)

commit v6 on v5

--- a/solution.py
+++ b/solution.py
@@ -19,17 +19,22 @@
 
 def swap_blocks(parts):
     lane = lax.broadcasted_iota(jnp.int32, parts[0].shape, 1)
-    for bit in (2, 1):
-        shift = bit * PROJ
-        low = (lane & shift) == 0
-        out = list(parts)
-        for p in range(PER_TILE):
-            if not p & bit:
-                a, b = parts[p], parts[p | bit]
-                out[p] = jnp.where(low, a, pltpu.roll(b, shift, 1))
-                out[p | bit] = jnp.where(low, pltpu.roll(a, LANES - shift, 1), b)
-        parts = out
-    return parts
+    outs = []
+    for q in range(PER_TILE):
+        out = parts[(PER_TILE - 1 - q) % PER_TILE]
+        for block in range(PER_TILE - 2, -1, -1):
+            out = jnp.where(lane < (block + 1) * PROJ, parts[(block - q) % PER_TILE], out)
+        outs.append(pltpu.roll(out, LANES - q * PROJ, 1) if q else out)
+    return outs
+
+
+def rolled(value, p):
+    if not p:
+        return value
+    return jnp.concatenate(
+        [pltpu.roll(value[:, t : t + LANES], p * PROJ, 1) for t in range(0, value.shape[1], LANES)],
+        axis=1,
+    )
 
 
 def nt_dot(a, b):
@@ -40,10 +45,20 @@
     return lax.dot_general(a, b, (((1,), (0,)), ((), ())), preferred_element_type=F32)
 
 
-def project_body(x_ref, gain_ref, shift_ref, w_ref, left_ref, right_ref, proj_ref, turn_ref, out_ref,
+def in_vmem(value):
+    return pltpu.with_memory_space_constraint(value, pltpu.VMEM)
+
+
+def in_hbm(value):
+    return pltpu.with_memory_space_constraint(value, pltpu.HBM)
+
+
+def project_body(x_ref, gain_ref, shift_ref, first_ref, second_ref, left_ref, right_ref, proj_ref, turn_ref, out_ref,
                  *, cols):
     here, rows, feats = x_ref.shape
     chunk = max(1, WIDE // rows)
+    blank = jnp.zeros((LANES - 2 * PROJ, feats), BF16)
+    w = jnp.concatenate([first_ref[...], second_ref[...], blank], axis=0)
 
     def norm(step, carry):
         x = x_ref[pl.ds(step * chunk, chunk)].astype(F32).reshape(chunk * rows, feats)
@@ -51,7 +66,7 @@
         spread = jnp.mean(center * center, axis=-1, keepdims=True)
         normed = center * lax.rsqrt(spread + 1e-05) * gain_ref[...] + shift_ref[...]
         at = pl.multiple_of(step * (chunk * rows), chunk * rows)
-        proj_ref[pl.ds(at, chunk * rows)] = nn_dot(normed.astype(BF16), w_ref[...])
+        proj_ref[pl.ds(at, chunk * rows)] = nt_dot(normed.astype(BF16), w)
         return carry
 
     lax.fori_loop(0, here // chunk, norm, 0)
@@ -86,7 +101,7 @@
             right_ref[:, at : at + LANES] = out_ref[...].astype(BF16)
 
 
-def project_call(x, gain, shift, w, cols):
+def project_call(x, gain, shift, first, second, cols):
     here, rows, _ = x.shape
     return pl.pallas_call(
         lambda *refs: project_body(*refs, cols=cols),
@@ -98,7 +113,7 @@
         ],
         compiler_params=pltpu.CompilerParams(vmem_limit_bytes=24 << 20),
         name="project",
-    )(x, gain, shift, w)
+    )(*map(in_hbm, (x, gain, shift, first, second)))
 
 
 def prep_body(at_ref, labels_ref, counts_ref, w_ref, lab_ref, tall_ref, wide_ref, plain_ref,
@@ -139,7 +154,8 @@
             e = t * PER_TILE + q
             w_out[e * PROJ : (e + 1) * PROJ] = wide_w_ref[pl.ds(e, PROJ, stride=PROJ)].astype(BF16)
         block = w_out[t * LANES : (t + 1) * LANES].astype(F32)
-        wt_out[:, t * LANES : (t + 1) * LANES] = block.T.astype(BF16)
+        for p in range(PER_TILE):
+            wt_out[p, :, t * LANES : (t + 1) * LANES] = rolled(block.T, p).astype(BF16)
 
 
 def prep_call(at, labels, counts, w, rows, cols, seqs):
@@ -155,12 +171,12 @@
             jax.ShapeDtypeStruct((pairs, 2, cols, 2 * seqs), BF16),
             jax.ShapeDtypeStruct((pairs, cols, 2 * seqs), F32),
             jax.ShapeDtypeStruct(w.shape, BF16),
-            jax.ShapeDtypeStruct((width, PROJ * PROJ), BF16),
+            jax.ShapeDtypeStruct((PER_TILE, width, PROJ * PROJ), BF16),
         ],
         scratch_shapes=[pltpu.VMEM(w.shape, F32)],
         compiler_params=pltpu.CompilerParams(vmem_limit_bytes=24 << 20),
         name="prep",
-    )(at, labels[None, :], counts, w)
+    )(at, in_hbm(labels[None, :]), in_hbm(counts), in_hbm(w))
 
 
 def cost(passes, span, total, seqs):
@@ -170,17 +186,23 @@
 
 
 def back_body(grad_ref, wt_ref, out_ref):
-    rows, cols, width = grad_ref.shape
+    rows, cols, _ = grad_ref.shape
     g = pl.program_id(0)
-    block = grad_ref[...].reshape(rows * cols, width)
+    halves = rows // PER_TILE
+    blocks = [
+        jnp.concatenate([grad_ref[half * PER_TILE + p] for half in range(halves)], axis=0)
+        for p in range(PER_TILE)
+    ]
     for u in range(PROJ * PROJ // WIDE):
-        prod = nn_dot(block, wt_ref[:, u * WIDE : (u + 1) * WIDE]).astype(BF16)
-        for half in range(rows // PER_TILE):
+        prods = [
+            nn_dot(block, wt_ref[p, :, u * WIDE : (u + 1) * WIDE]).astype(BF16)
+            for p, block in enumerate(blocks)
+        ]
+        for half in range(halves):
             for t in range(WIDE // LANES):
                 parts = [
-                    prod[(half * PER_TILE + p) * cols : (half * PER_TILE + p + 1) * cols,
-                         t * LANES : (t + 1) * LANES]
-                    for p in range(PER_TILE)
+                    prod[half * cols : (half + 1) * cols, t * LANES : (t + 1) * LANES]
+                    for prod in prods
                 ]
                 for q, part in enumerate(swap_blocks(parts)):
                     e = u * (WIDE // PROJ) + t * PER_TILE + q
@@ -195,14 +217,14 @@
         grid=(rows // step,),
         in_specs=[
             pl.BlockSpec((step, cols, width), lambda g: (g, 0, 0)),
-            pl.BlockSpec((width, PROJ * PROJ), lambda g: (0, 0)),
+            pl.BlockSpec(wt.shape, lambda g: (0, 0, 0)),
         ],
         out_specs=VMEM,
         out_shape=pltpu.VMEM((rows // step, PROJ * cols, WIDE), BF16),
         compiler_params=KERNEL,
         cost_estimate=cost(10, PROJ * cols, rows * PROJ, width),
         name="back",
-    )(grad, wt)
+    )(in_hbm(grad), wt)
 
 
 def first_pair(at_ref, labels_ref, group):
@@ -381,9 +403,11 @@
             plain, third = wide_ref[pair, 0], wide_ref[pair, 1]
             for e in range(PROJ):
                 rows = slice(e * cols, (e + 1) * cols)
+                to = e % PER_TILE * (PROJ // PER_TILE) + e // PER_TILE
+                into = slice(to * cols, (to + 1) * cols)
                 for side in range(2):
                     lanes = slice(side * seqs, (side + 1) * seqs)
-                    rm_ref[pair, rows, lanes] = (
+                    rm_ref[pair, into, lanes] = (
                         flip_ref[rows] * plain[:, lanes] + part_ref[rows] * third[:, lanes]
                     )
             return carry
@@ -391,24 +415,31 @@
         lax.fori_loop(first_pair(at_ref, labels_ref, 0), last_pair(at_ref, labels_ref, last) + 1, build, 0)
         sum_ref[...] = jnp.zeros_like(sum_ref)
 
-    def product(pair):
+    quarter = span // PER_TILE
+
+    def product(pair, add):
         masked_left(left_ref, lab_ref, lb_ref, pair)
-        return nn_dot(rm_ref[pair], lb_ref[...])
-
-    acc_ref[...] = product(first_pair(at_ref, labels_ref, g))
+        for q in range(PER_TILE):
+            rows = slice(q * quarter, (q + 1) * quarter)
+            part = nn_dot(rm_ref[pair, rows], rolled(lb_ref[...], q))
+            acc_ref[rows] = acc_ref[rows] + part if add else part
+
+    product(first_pair(at_ref, labels_ref, g), False)
 
     def more(pair, carry):
-        acc_ref[...] += product(pair)
+        product(pair, True)
         return carry
 
-    lax.fori_loop(first_pair(at_ref, labels_ref, g) + 1, last_pair(at_ref, labels_ref, g) + 1, more, 0)
+    lax.fori_loop(
+        first_pair(at_ref, labels_ref, g) + 1, last_pair(at_ref, labels_ref, g) + 1, more, 0
+    )
 
     for half in range(WIDE // LANES):
         lanes = slice(half * LANES, (half + 1) * LANES)
         for t in range(PROJ // PER_TILE):
             parts = []
             for q in range(PER_TILE):
-                e = t * PER_TILE + q
+                e = q * (PROJ // PER_TILE) + t
                 parts.append(acc_ref[e * cols : (e + 1) * cols, lanes].astype(BF16))
             turned = swap_blocks(parts)
             for p in range(PER_TILE):
@@ -568,10 +599,6 @@
         return shares.reshape(n * mine.shape[0], mine.shape[1])
 
 
-def in_vmem(value):
-    return pltpu.with_memory_space_constraint(value, pltpu.VMEM)
-
-
 def after(value, *others):
     return lax.optimization_barrier((value,) + others)[0]
 
@@ -582,9 +609,9 @@
     here, rows, _ = alignment_tensor.shape
     cols, width = grad.shape[1:]
     seqs = here * n_col
-    both = jnp.concatenate([first_projector, second_projector], axis=1)
-    both = jnp.pad(both, ((0, 0), (0, LANES - 2 * PROJ)))
-    left, right = project_call(alignment_tensor, gain[None, :], shift[None, :], both, cols)
+    left, right = project_call(
+        alignment_tensor, gain[None, :], shift[None, :], first_projector.T, second_projector.T, cols
+    )
     pieces = ring.right_along_row(right)
     left = jnp.concatenate([left] + [ring.col_shift(left, k) for k in range(1, n_col)])
 

time: 99 us -> 87.7 us (0.89)
  local copies, waits for them, and re-layouts: 8.25 us -> 0.46 us
  Pallas kernels: 46.5 us -> 42.5 us
    unnamed x25 -> x9, local copies, waits for them, and re-layouts: 7.84 us -> 0.05 us
    pallas_call x1, Pallas kernels: 17.4 us -> 11.5 us  [outer_call(): pl.pallas_call(outer_body, grid_spec=pltpu.PrefetchScalarGridSpec(num_sca...]
    pallas_call x1, Pallas kernels: 3.73 us -> 5.01 us  [project_call(): pl.pallas_call(lambda *refs: project_body(*refs, cols=cols), out_shape=[j...]
  transfers between devices with their start and end apart: 25 -> 25, of which waited for: 1 -> 2; matrix products, arithmetic and copies ran while one was open for 2% -> 3% of each run, Pallas kernels for 43% -> 43%
where the time goes in v6:
time: 87.7 us; the launch traced here: 87.5 us
  Pallas kernels  42.5 us (48%)
  starting transfers between devices  35.9 us (41%)
  waiting for transfers between devices  4.6 us (5%)
  other arithmetic  3.03 us (3%)
  between operations  0.94 us (1%)
    ppermute x12, starting transfers between devices, col_shift(): return lax.ppermute(value, 'col', [((t + k) % n, t) for t in range(n)])  20.7 us
    pallas_call x1, Pallas kernels, outer_call(): pl.pallas_call(outer_body, grid_spec=pltpu.PrefetchScalarGridSpec(num_sca...  11.5 us
    ppermute x4, starting transfers between devices, right_grad_home(): got = lax.ppermute(block, ('row', 'col'), pairs).astype(F32)[None]  8.08 us
    ppermute x9, starting transfers between devices, row_shift(): return lax.ppermute(value, 'row', [((t + k) % n, t) for t in range(n)])  7.08 us
    pallas_call x1, Pallas kernels, right_grad_call(): pl.pallas_call(right_grad_body, grid_spec=pltpu.PrefetchScalarGridSpec(nu...  6.82 us
    pallas_call x1, Pallas kernels, back_call(): pl.pallas_call(back_body, grid=(rows // step,), in_specs=[pl.BlockSpec((s...  6.42 us
    pallas_call x1, Pallas kernels, left_grad_call(): pl.pallas_call(left_grad_body, grid_spec=pltpu.PrefetchScalarGridSpec(num...  5.88 us
    pallas_call x1, Pallas kernels, project_call(): pl.pallas_call(lambda *refs: project_body(*refs, cols=cols), out_shape=[j...  5.01 us
  transfers between devices with their start and end apart: 25, of which 2 were waited for; matrix products, arithmetic and copies ran while one was open for 3% of the time, Pallas kernels for 43%

profile of v6, /device:TPU:0, one launch (start us, length us, event | category | flops | bytes accessed | tf_op | source)
XLA Modules:
  0.0 87.5 jit_solution(12436524591800926261)
XLA Ops:
  0.6 5.0 %project.1 = (bf16[32,2048]{1,0:T(8,128)(2,1)S(1)}, bf16[32,2048]{1,0:T(8,128)(2,1)S(1)}) custom-call(bf16[32,64,256]{2,1,0:T(8,128)(2,1)} %refs_0_.1, f32[1,256]{1,0:T(1,128)} %bitcast.61, f32[1,256]{1,0:T(1,128)} %bitcast.62, bf16[32,256]{1,0:T(8,128)(2,1)} %bitcast.59, bf16[32,256]{1,0:T(8,128)(2,1)} %bitcast.60), custom_call_target="tpu_custom_call" | custom-call | tf_op jit(solution)/shard_map/project/pallas_call | solution.py:106
  5.6 3.1 %collective-permute-start.2 = (bf16[32,2048]{1,0:T(8,128)(2,1)S(1)}, bf16[32,2048]{1,0:T(8,128)(2,1)S(1)}, u32[]{:S(2)}, u32[]{:S(2)}) collective-permute-start(bf16[32,2048]{1,0:T(8,128)(2,1)S(1)} %get-tuple-element.21), channel_id=1, source_target_pairs={{3,0},{0,1},{1,2},{2,3},{7,4},{4,5},{5,6},{6,7},{11,8},{8,9},{9,10... | collective-permute-start | bytes 393224 | tf_op jit(solution)/shard_map/ppermute | solution.py:540
  8.7 2.6 %collective-permute-start.1 = (bf16[32,2048]{1,0:T(8,128)(2,1)S(1)}, bf16[32,2048]{1,0:T(8,128)(2,1)S(1)}, u32[]{:S(2)}, u32[]{:S(2)}) collective-permute-start(bf16[32,2048]{1,0:T(8,128)(2,1)S(1)} %get-tuple-element.21), channel_id=1, source_target_pairs={{2,0},{3,1},{0,2},{1,3},{6,4},{7,5},{4,6},{5,7},{10,8},{11,9},{8,1... | collective-permute-start | bytes 393224 | tf_op jit(solution)/shard_map/ppermute | solution.py:540
  11.3 1.5 %collective-permute-start.4 = (bf16[32,2048]{1,0:T(8,128)(2,1)S(1)}, bf16[32,2048]{1,0:T(8,128)(2,1)S(1)}, u32[]{:S(2)}, u32[]{:S(2)}) collective-permute-start(bf16[32,2048]{1,0:T(8,128)(2,1)S(1)} %get-tuple-element.22), channel_id=1, source_target_pairs={{8,0},{12,4},{0,8},{4,12},{9,1},{13,5},{1,9},{5,13},{10,2},{14,6},... | collective-permute-start | bytes 393224 | tf_op jit(solution)/shard_map/ppermute | solution.py:544
  12.8 1.5 %collective-permute-start.3 = (bf16[32,2048]{1,0:T(8,128)(2,1)S(1)}, bf16[32,2048]{1,0:T(8,128)(2,1)S(1)}, u32[]{:S(2)}, u32[]{:S(2)}) collective-permute-start(bf16[32,2048]{1,0:T(8,128)(2,1)S(1)} %get-tuple-element.22), channel_id=1, source_target_pairs={{4,0},{8,4},{12,8},{0,12},{5,1},{9,5},{13,9},{1,13},{6,2},{10,6},{... | collective-permute-start | bytes 393224 | tf_op jit(solution)/shard_map/ppermute | solution.py:544
  14.7 2.1 %prep.1 = (s32[1,2048]{1,0:T(1,128)S(1)}, bf16[4,2,256,128]{3,2,1,0:T(8,128)(2,1)S(1)}, bf16[4,2,64,256]{3,2,1,0:T(8,128)(2,1)S(1)}, f32[4,64,256]{2,1,0:T(8,128...) custom-call(s32[3]{0:T(128)S(1)} %add_convert_fusion.3.refs_0_.at_ref, s32[1,256]{1,0:T(1,128)} %bitcast.52, ...), custom_call_target="tpu_custom_call" | custom-call | tf_op jit(solution)/shard_map/prep/pallas_call | solution.py:164
  16.8 1.4 %collective-permute-start = (bf16[32,2048]{1,0:T(8,128)(2,1)S(1)}, bf16[32,2048]{1,0:T(8,128)(2,1)S(1)}, u32[]{:S(2)}, u32[]{:S(2)}) collective-permute-start(bf16[32,2048]{1,0:T(8,128)(2,1)S(1)} %get-tuple-element.21), channel_id=1, source_target_pairs={{1,0},{2,1},{3,2},{0,3},{5,4},{6,5},{7,6},{4,7},{9,8},{10,9},{11,1... | collective-permute-start | bytes 393224 | tf_op jit(solution)/shard_map/ppermute | solution.py:540
  18.2 0.7 collective-permute-done.3
  19.1 0.3 collective-permute-start.8
  19.3 1.7 %collective-permute-start.7 = (bf16[32,2048]{1,0:T(8,128)(2,1)S(1)}, bf16[32,2048]{1,0:T(8,128)(2,1)S(1)}, u32[]{:S(2)}, u32[]{:S(2)}) collective-permute-start(bf16[32,2048]{1,0:T(8,128)(2,1)S(1)} %get-tuple-element.47), channel_id=1, source_target_pairs={{2,0},{3,1},{0,2},{1,3},{6,4},{7,5},{4,6},{5,7},{10,8},{11,9},{8,1... | collective-permute-start | bytes 393224 | tf_op jit(solution)/shard_map/ppermute | solution.py:540
  21.0 6.4 %back.1.back_ref = bf16[8,2048,256]{2,1,0:T(8,128)(2,1)S(1)} custom-call(bf16[64,64,128]{2,1,0:T(8,128)(2,1)} %grad_ref.2, bf16[4,128,1024]{2,1,0:T(8,128)(2,1)S(1)} %get-tuple-element.26.wt_ref), custom_call_target="tpu_custom_call" | custom-call | flops 21474836480 | bytes 8388608 | tf_op jit(solution)/shard_map/back/pallas_call | solution.py:215
  27.5 2.0 %collective-permute-start.6 = (bf16[32,2048]{1,0:T(8,128)(2,1)S(1)}, bf16[32,2048]{1,0:T(8,128)(2,1)S(1)}, u32[]{:S(2)}, u32[]{:S(2)}) collective-permute-start(bf16[32,2048]{1,0:T(8,128)(2,1)S(1)} %get-tuple-element.48), channel_id=1, source_target_pairs={{1,0},{2,1},{3,2},{0,3},{5,4},{6,5},{7,6},{4,7},{9,8},{10,9},{11,1... | collective-permute-start | bytes 393224 | tf_op jit(solution)/shard_map/ppermute | solution.py:540
  29.5 6.8 %right_grad.1 = bf16[128,2048]{1,0:T(8,128)(2,1)S(1)} custom-call(s32[3]{0:T(128)S(1)} %add_convert_fusion.3.refs_0_.at_ref, s32[256]{0:T(256)S(1)} %copy-done, bf16[8,2048,256]{2,1,0:T(8,128)(2,1)S(1)} %back.1.back_ref, bf16[128,2048]{1,0:T(8,128)(2,1)S(1)} %constant_dynamic-update-slice_fusion.left_ref, s32[1,2048]{1,0:T(1,128)S(1)} %get-tuple-element.33.lab_ref, ...), custom_call_target="tpu_custom_call" | custom-call | flops 21474836480 | bytes 8388608 | tf_op jit(solution)/shard_map/right_grad/pallas_call | solution.py:295
  36.4 0.7 collective-permute-start.15
  37.1 6.2 %collective-permute-start.18 = (bf16[32,2048]{1,0:T(8,128)(2,1)S(1)}, bf16[32,2048]{1,0:T(8,128)(2,1)S(1)}, u32[]{:S(2)}, u32[]{:S(2)}) collective-permute-start(bf16[32,2048]{1,0:T(8,128)(2,1)S(1)} %get-tuple-element.39), channel_id=1, source_target_pairs={{0,3},{1,7},{2,11},{3,15},{4,0},{5,4},{6,8},{7,12},{8,1},{9,5},{10... | collective-permute-start | bytes 393224 | tf_op jit(solution)/shard_map/ppermute | solution.py:573
  43.3 1.2 %collective-permute-start.16 = (bf16[32,2048]{1,0:T(8,128)(2,1)S(1)}, bf16[32,2048]{1,0:T(8,128)(2,1)S(1)}, u32[]{:S(2)}, u32[]{:S(2)}) collective-permute-start(bf16[32,2048]{1,0:T(8,128)(2,1)S(1)} %get-tuple-element.41), channel_id=1, source_target_pairs={{0,1},{1,5},{2,9},{3,13},{4,2},{5,6},{6,10},{7,14},{8,3},{9,7},{10... | collective-permute-start | bytes 393224 | tf_op jit(solution)/shard_map/ppermute | solution.py:573
  44.6 11.5 %outer.1 = (bf16[8,512,1024]{2,1,0:T(8,128)(2,1)S(1)}, f32[1024,128]{1,0:T(8,128)S(1)}) custom-call(s32[3]{0:T(128)S(1)} %add_convert_fusion.3.refs_0_.at_ref, s32[256]{0:T(256)S(1)} %copy-done, bf16[128,2048]{1,0:T(8,128)(2,1)S(1)} %constant_dynamic-update-slice_fusion.left_ref, s32[1,2048]{1,0:T(1,128)S(1)} %get-tuple-element.33.lab_ref, ...), custom_call_target="tpu_custom_call" | custom-call | flops 42949672960 | bytes 8388608 | tf_op jit(solution)/shard_map/outer/pallas_call | solution.py:467
  56.2 5.9 %left_grad.1 = bf16[128,2048]{1,0:T(8,128)(2,1)S(1)} custom-call(s32[3]{0:T(128)S(1)} %add_convert_fusion.3.refs_0_.at_ref, s32[256]{0:T(256)S(1)} %copy-done, bf16[8,2048,256]{2,1,0:T(8,128)(2,1)S(1)} %back.1.back_ref, s32[1,2048]{1,0:T(1,128)S(1)} %get-tuple-element.33.lab_ref, bf16[128,2048]{1,0:T(8,128)(2,1)S(1)} %pad_maximum_fusion.1.right_ref, ...), custom_call_target="tpu_custom_call" | custom-call | flops 21474836480 | bytes 8388608 | tf_op jit(solution)/shard_map/left_grad/pallas_call | solution.py:360
  62.2 1.8 %collective-permute-start.11 = (bf16[256,128]{1,0:T(8,128)(2,1)S(1)}, bf16[256,128]{1,0:T(8,128)(2,1)S(1)}, u32[]{:S(2)}, u32[]{:S(2)}) collective-permute-start(bf16[256,128]{1,0:T(8,128)(2,1)S(1)} %get-tuple-element.50), channel_id=1, source_target_pairs={{4,0},{8,4},{12,8},{0,12},{5,1},{9,5},{13,9},{1,13},{6,2},{10,6},{... | collective-permute-start | bytes 196616 | tf_op jit(solution)/shard_map/ppermute | solution.py:544
  63.9 0.1 collective-permute-start.10
  64.0 0.1 collective-permute-start.12
  64.1 3.7 %collective-permute-start.14 = (bf16[32,2048]{1,0:T(8,128)(2,1)S(1)}, bf16[32,2048]{1,0:T(8,128)(2,1)S(1)}, u32[]{:S(2)}, u32[]{:S(2)}) collective-permute-start(bf16[32,2048]{1,0:T(8,128)(2,1)S(1)} %get-tuple-element.43), channel_id=1, source_target_pairs={{1,0},{2,1},{3,2},{0,3},{5,4},{6,5},{7,6},{4,7},{9,8},{10,9},{11,1... | collective-permute-start | bytes 393224 | tf_op jit(solution)/shard_map/ppermute | solution.py:540
  67.9 0.7 add_convert_fusion
  68.7 1.4 %collective-permute-start.20 = (bf16[256,128]{1,0:T(8,128)(2,1)S(1)}, bf16[256,128]{1,0:T(8,128)(2,1)S(1)}, u32[]{:S(2)}, u32[]{:S(2)}) collective-permute-start(bf16[256,128]{1,0:T(8,128)(2,1)S(1)} %convert_element_type.121), channel_id=1, source_target_pairs={{2,0},{3,1},{0,2},{1,3},{6,4},{7,5},{4,6},{5,7},{10,8},{11,9},{8,1... | collective-permute-start | bytes 196616 | tf_op jit(solution)/shard_map/ppermute | solution.py:540
  70.1 2.8 %collective-permute-start.19 = (bf16[256,128]{1,0:T(8,128)(2,1)S(1)}, bf16[256,128]{1,0:T(8,128)(2,1)S(1)}, u32[]{:S(2)}, u32[]{:S(2)}) collective-permute-start(bf16[256,128]{1,0:T(8,128)(2,1)S(1)} %convert_element_type.121), channel_id=1, source_target_pairs={{1,0},{2,1},{3,2},{0,3},{5,4},{6,5},{7,6},{4,7},{9,8},{10,9},{11,1... | collective-permute-start | bytes 196616 | tf_op jit(solution)/shard_map/ppermute | solution.py:540
  73.0 4.8 %pair.1 = bf16[4096,128]{1,0:T(8,128)(2,1)} custom-call(bf16[8,512,1024]{2,1,0:T(8,128)(2,1)S(1)} %get-tuple-element.30.outer_ref, bf16[1024,128]{1,0:T(8,128)(2,1)S(1)} %get-tuple-element.36.w_ref, f32[1,128]{1,0:T(1,128)S(1)} %bitcast.53), custom_call_target="tpu_custom_call" | custom-call | flops 1073741824 | bytes 1048576 | tf_op jit(solution)/shard_map/pair/pallas_call | solution.py:511
  77.8 1.6 %collective-permute-start.13 = (bf16[32,2048]{1,0:T(8,128)(2,1)S(1)}, bf16[32,2048]{1,0:T(8,128)(2,1)S(1)}, u32[]{:S(2)}, u32[]{:S(2)}) collective-permute-start(bf16[32,2048]{1,0:T(8,128)(2,1)S(1)} %get-tuple-element.44), channel_id=1, source_target_pairs={{2,0},{3,1},{0,2},{1,3},{6,4},{7,5},{4,6},{5,7},{10,8},{11,9},{8,1... | collective-permute-start | bytes 393224 | tf_op jit(solution)/shard_map/ppermute | solution.py:540
  79.5 2.0 %collective-permute-start.23 = (bf16[256,128]{1,0:T(8,128)(2,1)S(1)}, bf16[256,128]{1,0:T(8,128)(2,1)S(1)}, u32[]{:S(2)}, u32[]{:S(2)}) collective-permute-start(bf16[256,128]{1,0:T(8,128)(2,1)S(1)} %add_convert_fusion.2), channel_id=1, source_target_pairs={{8,0},{12,4},{0,8},{4,12},{9,1},{13,5},{1,9},{5,13},{10,2},{14,6},... | collective-permute-start | bytes 196616 | tf_op jit(solution)/shard_map/ppermute | solution.py:544
  81.5 0.2 collective-permute-start.22
  81.7 3.8 %collective-permute-done.13 = bf16[32,2048]{1,0:T(8,128)(2,1)S(1)} collective-permute-done((bf16[32,2048]{1,0:T(8,128)(2,1)S(1)}, bf16[32,2048]{1,0:T(8,128)(2,1)S(1)}, u32[]{:S(2)}, u32[]{:S(2)}) %collective-permute-start.13) | collective-permute-done | bytes 131104 | tf_op jit(solution)/shard_map/ppermute | solution.py:540
  85.5 0.7 add_convert_fusion.1
  86.2 1.3 %convert_multiply_fusion = f32[1024,128]{1,0:T(8,128)} fusion(pred[1024]{0:T(1024)(128)(4,1)S(1)} %broadcast_in_dim.105, pred[1024]{0:T(1024)(128)(4,1)S(1)} %broadcast_in_dim.100, pred[1024]{0:T(1024)(128)(4,1)S(1)} %broadcast_in_dim.95, bf16[256,128]{1,0:T(8,128)(2,1)S(1)} %add_convert_fusion.2, bf16[256,128]{1,0:T(8,128)(2,1)S(1)} %collective-permute-done.24, ...), kind=kLoop, calls=%fused_computation.2 | loop fusion | flops 655360 | bytes 789504 | tf_op jit(solution)/shard_map/div | solution.py:643
  (57 shorter events, 1.0 us)
Async XLA Ops:
  5.6 23.9 %collective-permute-start.2 = (bf16[32,2048]{1,0:T(8,128)(2,1)S(1)}, bf16[32,2048]{1,0:T(8,128)(2,1)S(1)}, u32[]{:S(2)}, u32[]{:S(2)}) collective-permute-start(bf16[32,2048]{1,0:T(8,128)(2,1)S(1)} %get-tuple-element.21), channel_id=1, source_target_pairs={{3,0},{0,1},{1,2},{2,3},{7,4},{4,5},{5,6},{6,7},{11,8},{8,9},{9,10... | collective-permute-start | bytes 393224 | tf_op jit(solution)/shard_map/ppermute | solution.py:540
  8.7 20.7 %collective-permute-start.1 = (bf16[32,2048]{1,0:T(8,128)(2,1)S(1)}, bf16[32,2048]{1,0:T(8,128)(2,1)S(1)}, u32[]{:S(2)}, u32[]{:S(2)}) collective-permute-start(bf16[32,2048]{1,0:T(8,128)(2,1)S(1)} %get-tuple-element.21), channel_id=1, source_target_pairs={{2,0},{3,1},{0,2},{1,3},{6,4},{7,5},{4,6},{5,7},{10,8},{11,9},{8,1... | collective-permute-start | bytes 393224 | tf_op jit(solution)/shard_map/ppermute | solution.py:540
  11.3 5.5 %collective-permute-start.5 = (bf16[32,2048]{1,0:T(8,128)(2,1)S(1)}, bf16[32,2048]{1,0:T(8,128)(2,1)S(1)}, u32[]{:S(2)}, u32[]{:S(2)}) collective-permute-start(bf16[32,2048]{1,0:T(8,128)(2,1)S(1)} %get-tuple-element.22), channel_id=1, source_target_pairs={{12,0},{0,4},{4,8},{8,12},{13,1},{1,5},{5,9},{9,13},{14,2},{2,6},{... | collective-permute-start | bytes 393224 | tf_op jit(solution)/shard_map/ppermute | solution.py:544
  11.3 6.9 %collective-permute-start.4 = (bf16[32,2048]{1,0:T(8,128)(2,1)S(1)}, bf16[32,2048]{1,0:T(8,128)(2,1)S(1)}, u32[]{:S(2)}, u32[]{:S(2)}) collective-permute-start(bf16[32,2048]{1,0:T(8,128)(2,1)S(1)} %get-tuple-element.22), channel_id=1, source_target_pairs={{8,0},{12,4},{0,8},{4,12},{9,1},{13,5},{1,9},{5,13},{10,2},{14,6},... | collective-permute-start | bytes 393224 | tf_op jit(solution)/shard_map/ppermute | solution.py:544
  12.8 6.1 %collective-permute-start.3 = (bf16[32,2048]{1,0:T(8,128)(2,1)S(1)}, bf16[32,2048]{1,0:T(8,128)(2,1)S(1)}, u32[]{:S(2)}, u32[]{:S(2)}) collective-permute-start(bf16[32,2048]{1,0:T(8,128)(2,1)S(1)} %get-tuple-element.22), channel_id=1, source_target_pairs={{4,0},{8,4},{12,8},{0,12},{5,1},{9,5},{13,9},{1,13},{6,2},{10,6},{... | collective-permute-start | bytes 393224 | tf_op jit(solution)/shard_map/ppermute | solution.py:544
  16.8 10.7 %collective-permute-start = (bf16[32,2048]{1,0:T(8,128)(2,1)S(1)}, bf16[32,2048]{1,0:T(8,128)(2,1)S(1)}, u32[]{:S(2)}, u32[]{:S(2)}) collective-permute-start(bf16[32,2048]{1,0:T(8,128)(2,1)S(1)} %get-tuple-element.21), channel_id=1, source_target_pairs={{1,0},{2,1},{3,2},{0,3},{5,4},{6,5},{7,6},{4,7},{9,8},{10,9},{11,1... | collective-permute-start | bytes 393224 | tf_op jit(solution)/shard_map/ppermute | solution.py:540
  19.1 24.2 %collective-permute-start.8 = (bf16[32,2048]{1,0:T(8,128)(2,1)S(1)}, bf16[32,2048]{1,0:T(8,128)(2,1)S(1)}, u32[]{:S(2)}, u32[]{:S(2)}) collective-permute-start(bf16[32,2048]{1,0:T(8,128)(2,1)S(1)} %get-tuple-element.46), channel_id=1, source_target_pairs={{3,0},{0,1},{1,2},{2,3},{7,4},{4,5},{5,6},{6,7},{11,8},{8,9},{9,10... | collective-permute-start | bytes 393224 | tf_op jit(solution)/shard_map/ppermute | solution.py:540
  19.3 24.0 %collective-permute-start.7 = (bf16[32,2048]{1,0:T(8,128)(2,1)S(1)}, bf16[32,2048]{1,0:T(8,128)(2,1)S(1)}, u32[]{:S(2)}, u32[]{:S(2)}) collective-permute-start(bf16[32,2048]{1,0:T(8,128)(2,1)S(1)} %get-tuple-element.47), channel_id=1, source_target_pairs={{2,0},{3,1},{0,2},{1,3},{6,4},{7,5},{4,6},{5,7},{10,8},{11,9},{8,1... | collective-permute-start | bytes 393224 | tf_op jit(solution)/shard_map/ppermute | solution.py:540
  21.0 8.5 %copy-start = (s32[256]{0:T(256)S(1)}, s32[256]{0:T(256)}, u32[]{:S(2)}) copy-start(s32[256]{0:T(256)} %labels_ref.5) | copy-start | bytes 3076
  27.5 17.0 %collective-permute-start.6 = (bf16[32,2048]{1,0:T(8,128)(2,1)S(1)}, bf16[32,2048]{1,0:T(8,128)(2,1)S(1)}, u32[]{:S(2)}, u32[]{:S(2)}) collective-permute-start(bf16[32,2048]{1,0:T(8,128)(2,1)S(1)} %get-tuple-element.48), channel_id=1, source_target_pairs={{1,0},{2,1},{3,2},{0,3},{5,4},{6,5},{7,6},{4,7},{9,8},{10,9},{11,1... | collective-permute-start | bytes 393224 | tf_op jit(solution)/shard_map/ppermute | solution.py:540
  29.5 15.0 %copy-start.2 = (bf16[64,64,128]{2,1,0:T(8,128)(2,1)S(1)}, bf16[64,64,128]{2,1,0:T(8,128)(2,1)}, u32[]{:S(2)}) copy-start(bf16[64,64,128]{2,1,0:T(8,128)(2,1)} %grad_ref.2) | copy-start | bytes 3145732
  36.4 25.7 %collective-permute-start.15 = (bf16[32,2048]{1,0:T(8,128)(2,1)S(1)}, bf16[32,2048]{1,0:T(8,128)(2,1)S(1)}, u32[]{:S(2)}, u32[]{:S(2)}) collective-permute-start(bf16[32,2048]{1,0:T(8,128)(2,1)S(1)} %get-tuple-element.38), channel_id=1, source_target_pairs={{0,0},{1,4},{2,8},{3,12},{4,1},{5,5},{6,9},{7,13},{8,2},{9,6},{10,... | collective-permute-start | bytes 393224 | tf_op jit(solution)/shard_map/ppermute | solution.py:573
  37.1 26.8 %collective-permute-start.18 = (bf16[32,2048]{1,0:T(8,128)(2,1)S(1)}, bf16[32,2048]{1,0:T(8,128)(2,1)S(1)}, u32[]{:S(2)}, u32[]{:S(2)}) collective-permute-start(bf16[32,2048]{1,0:T(8,128)(2,1)S(1)} %get-tuple-element.39), channel_id=1, source_target_pairs={{0,3},{1,7},{2,11},{3,15},{4,0},{5,4},{6,8},{7,12},{8,1},{9,5},{10... | collective-permute-start | bytes 393224 | tf_op jit(solution)/shard_map/ppermute | solution.py:573
  43.3 20.7 %collective-permute-start.17 = (bf16[32,2048]{1,0:T(8,128)(2,1)S(1)}, bf16[32,2048]{1,0:T(8,128)(2,1)S(1)}, u32[]{:S(2)}, u32[]{:S(2)}) collective-permute-start(bf16[32,2048]{1,0:T(8,128)(2,1)S(1)} %get-tuple-element.40), channel_id=1, source_target_pairs={{0,2},{1,6},{2,10},{3,14},{4,3},{5,7},{6,11},{7,15},{8,0},{9,4},{1... | collective-permute-start | bytes 393224 | tf_op jit(solution)/shard_map/ppermute | solution.py:573
  43.3 20.8 %collective-permute-start.16 = (bf16[32,2048]{1,0:T(8,128)(2,1)S(1)}, bf16[32,2048]{1,0:T(8,128)(2,1)S(1)}, u32[]{:S(2)}, u32[]{:S(2)}) collective-permute-start(bf16[32,2048]{1,0:T(8,128)(2,1)S(1)} %get-tuple-element.41), channel_id=1, source_target_pairs={{0,1},{1,5},{2,9},{3,13},{4,2},{5,6},{6,10},{7,14},{8,3},{9,7},{10... | collective-permute-start | bytes 393224 | tf_op jit(solution)/shard_map/ppermute | solution.py:573
  56.1 12.4 %collective-permute-start.9 = (bf16[256,128]{1,0:T(8,128)(2,1)S(1)}, bf16[256,128]{1,0:T(8,128)(2,1)S(1)}, u32[]{:S(2)}, u32[]{:S(2)}) collective-permute-start(bf16[256,128]{1,0:T(8,128)(2,1)S(1)} %get-tuple-element.49), channel_id=1, source_target_pairs={{12,0},{0,4},{4,8},{8,12},{13,1},{1,5},{5,9},{9,13},{14,2},{2,6},{... | collective-permute-start | bytes 196616 | tf_op jit(solution)/shard_map/ppermute | solution.py:544
  56.2 16.8 %copy-start.1 = (f32[128]{0:T(128)S(1)}, f32[128]{0:T(128)}, u32[]{:S(2)}) copy-start(f32[128]{0:T(128)} %param.16) | copy-start | bytes 1540
  62.2 6.4 %collective-permute-start.11 = (bf16[256,128]{1,0:T(8,128)(2,1)S(1)}, bf16[256,128]{1,0:T(8,128)(2,1)S(1)}, u32[]{:S(2)}, u32[]{:S(2)}) collective-permute-start(bf16[256,128]{1,0:T(8,128)(2,1)S(1)} %get-tuple-element.50), channel_id=1, source_target_pairs={{4,0},{8,4},{12,8},{0,12},{5,1},{9,5},{13,9},{1,13},{6,2},{10,6},{... | collective-permute-start | bytes 196616 | tf_op jit(solution)/shard_map/ppermute | solution.py:544
  63.9 4.7 %collective-permute-start.10 = (bf16[256,128]{1,0:T(8,128)(2,1)S(1)}, bf16[256,128]{1,0:T(8,128)(2,1)S(1)}, u32[]{:S(2)}, u32[]{:S(2)}) collective-permute-start(bf16[256,128]{1,0:T(8,128)(2,1)S(1)} %get-tuple-element.51), channel_id=1, source_target_pairs={{8,0},{12,4},{0,8},{4,12},{9,1},{13,5},{1,9},{5,13},{10,2},{14,6},... | collective-permute-start | bytes 196616 | tf_op jit(solution)/shard_map/ppermute | solution.py:544
  64.0 17.5 %collective-permute-start.12 = (bf16[32,2048]{1,0:T(8,128)(2,1)S(1)}, bf16[32,2048]{1,0:T(8,128)(2,1)S(1)}, u32[]{:S(2)}, u32[]{:S(2)}) collective-permute-start(bf16[32,2048]{1,0:T(8,128)(2,1)S(1)} %get-tuple-element.42), channel_id=1, source_target_pairs={{3,0},{0,1},{1,2},{2,3},{7,4},{4,5},{5,6},{6,7},{11,8},{8,9},{9,10... | collective-permute-start | bytes 393224 | tf_op jit(solution)/shard_map/ppermute | solution.py:540
  64.1 17.5 %collective-permute-start.14 = (bf16[32,2048]{1,0:T(8,128)(2,1)S(1)}, bf16[32,2048]{1,0:T(8,128)(2,1)S(1)}, u32[]{:S(2)}, u32[]{:S(2)}) collective-permute-start(bf16[32,2048]{1,0:T(8,128)(2,1)S(1)} %get-tuple-element.43), channel_id=1, source_target_pairs={{1,0},{2,1},{3,2},{0,3},{5,4},{6,5},{7,6},{4,7},{9,8},{10,9},{11,1... | collective-permute-start | bytes 393224 | tf_op jit(solution)/shard_map/ppermute | solution.py:540
  68.7 9.1 %collective-permute-start.21 = (bf16[256,128]{1,0:T(8,128)(2,1)S(1)}, bf16[256,128]{1,0:T(8,128)(2,1)S(1)}, u32[]{:S(2)}, u32[]{:S(2)}) collective-permute-start(bf16[256,128]{1,0:T(8,128)(2,1)S(1)} %convert_element_type.121), channel_id=1, source_target_pairs={{3,0},{0,1},{1,2},{2,3},{7,4},{4,5},{5,6},{6,7},{11,8},{8,9},{9,10... | collective-permute-start | bytes 196616 | tf_op jit(solution)/shard_map/ppermute | solution.py:540
  68.7 10.7 %collective-permute-start.20 = (bf16[256,128]{1,0:T(8,128)(2,1)S(1)}, bf16[256,128]{1,0:T(8,128)(2,1)S(1)}, u32[]{:S(2)}, u32[]{:S(2)}) collective-permute-start(bf16[256,128]{1,0:T(8,128)(2,1)S(1)} %convert_element_type.121), channel_id=1, source_target_pairs={{2,0},{3,1},{0,2},{1,3},{6,4},{7,5},{4,6},{5,7},{10,8},{11,9},{8,1... | collective-permute-start | bytes 196616 | tf_op jit(solution)/shard_map/ppermute | solution.py:540
  70.1 9.3 %collective-permute-start.19 = (bf16[256,128]{1,0:T(8,128)(2,1)S(1)}, bf16[256,128]{1,0:T(8,128)(2,1)S(1)}, u32[]{:S(2)}, u32[]{:S(2)}) collective-permute-start(bf16[256,128]{1,0:T(8,128)(2,1)S(1)} %convert_element_type.121), channel_id=1, source_target_pairs={{1,0},{2,1},{3,2},{0,3},{5,4},{6,5},{7,6},{4,7},{9,8},{10,9},{11,1... | collective-permute-start | bytes 196616 | tf_op jit(solution)/shard_map/ppermute | solution.py:540
  77.8 7.7 %collective-permute-start.13 = (bf16[32,2048]{1,0:T(8,128)(2,1)S(1)}, bf16[32,2048]{1,0:T(8,128)(2,1)S(1)}, u32[]{:S(2)}, u32[]{:S(2)}) collective-permute-start(bf16[32,2048]{1,0:T(8,128)(2,1)S(1)} %get-tuple-element.44), channel_id=1, source_target_pairs={{2,0},{3,1},{0,2},{1,3},{6,4},{7,5},{4,6},{5,7},{10,8},{11,9},{8,1... | collective-permute-start | bytes 393224 | tf_op jit(solution)/shard_map/ppermute | solution.py:540
  79.4 6.7 %collective-permute-start.24 = (bf16[256,128]{1,0:T(8,128)(2,1)S(1)}, bf16[256,128]{1,0:T(8,128)(2,1)S(1)}, u32[]{:S(2)}, u32[]{:S(2)}) collective-permute-start(bf16[256,128]{1,0:T(8,128)(2,1)S(1)} %add_convert_fusion.2), channel_id=1, source_target_pairs={{4,0},{8,4},{12,8},{0,12},{5,1},{9,5},{13,9},{1,13},{6,2},{10,6},{... | collective-permute-start | bytes 196616 | tf_op jit(solution)/shard_map/ppermute | solution.py:544
  79.5 6.7 %collective-permute-start.23 = (bf16[256,128]{1,0:T(8,128)(2,1)S(1)}, bf16[256,128]{1,0:T(8,128)(2,1)S(1)}, u32[]{:S(2)}, u32[]{:S(2)}) collective-permute-start(bf16[256,128]{1,0:T(8,128)(2,1)S(1)} %add_convert_fusion.2), channel_id=1, source_target_pairs={{8,0},{12,4},{0,8},{4,12},{9,1},{13,5},{1,9},{5,13},{10,2},{14,6},... | collective-permute-start | bytes 196616 | tf_op jit(solution)/shard_map/ppermute | solution.py:544
  81.5 4.7 %collective-permute-start.22 = (bf16[256,128]{1,0:T(8,128)(2,1)S(1)}, bf16[256,128]{1,0:T(8,128)(2,1)S(1)}, u32[]{:S(2)}, u32[]{:S(2)}) collective-permute-start(bf16[256,128]{1,0:T(8,128)(2,1)S(1)} %add_convert_fusion.2), channel_id=1, source_target_pairs={{12,0},{0,4},{4,8},{8,12},{13,1},{1,5},{5,9},{9,13},{14,2},{2,6},{... | collective-permute-start | bytes 196616 | tf_op jit(solution)/shard_map/ppermute | solution.py:544

commit v7 on v6

--- a/solution.py
+++ b/solution.py
@@ -56,7 +56,7 @@
 def project_body(x_ref, gain_ref, shift_ref, first_ref, second_ref, left_ref, right_ref, proj_ref, turn_ref, out_ref,
                  *, cols):
     here, rows, feats = x_ref.shape
-    chunk = max(1, WIDE // rows)
+    chunk = max(1, 2 * WIDE // rows)
     blank = jnp.zeros((LANES - 2 * PROJ, feats), BF16)
     w = jnp.concatenate([first_ref[...], second_ref[...], blank], axis=0)
 
@@ -544,10 +544,14 @@
         return lax.ppermute(value, "row", [((t + k) % n, t) for t in range(n)])
 
     def right_along_row(self, right):
+        others = [self.row_shift(right, k) for k in range(1, self.n_row)]
+        return [right] + others
+
+    def right_pieces(self, by_row):
         n, m = self.n_row, self.per_row
-        here, lanes = right.shape
+        here, lanes = by_row[0].shape
         lanes //= m
-        by_row = jnp.stack([right] + [self.row_shift(right, k) for k in range(1, n)])
+        by_row = jnp.stack(by_row)
         pieces = []
         for k in range(self.n_col):
             q = (self.col + (self.n_col - k)) % self.n_col
@@ -612,15 +616,15 @@
     left, right = project_call(
         alignment_tensor, gain[None, :], shift[None, :], first_projector.T, second_projector.T, cols
     )
-    pieces = ring.right_along_row(right)
+    by_row = ring.right_along_row(right)
     left = jnp.concatenate([left] + [ring.col_shift(left, k) for k in range(1, n_col)])
 
     at = jnp.stack([ring.row * rows, ring.col * cols, ring.col * here]).astype(jnp.int32)
     lab, tall, wide, plain, w, wt = prep_call(
         at, labels, counts, after(final_projector, right), rows, cols, seqs
     )
-    back = back_call(after(grad, *pieces), wt)
-    mine = ring.right_along_col(pieces)
+    back = back_call(grad, wt)
+    mine = ring.right_along_col(ring.right_pieces(by_row))
     back = in_vmem(back)
     right_grad = right_grad_call(at, labels, back, left, lab, plain)
 

time: 87.7 us -> 89.4 us (1.019)
  waiting for transfers between devices: 4.6 us -> 8.58 us
  starting transfers between devices: 35.9 us -> 34.7 us
  Pallas kernels: 42.5 us -> 41.4 us
    ppermute x12, waiting for transfers between devices: 3.83 us -> 8.55 us  [col_shift(): return lax.ppermute(value, 'col', [((t + k) % n, t) for t in range(n)])]
    pallas_call x1, Pallas kernels: 5.01 us -> 3.92 us  [project_call(): pl.pallas_call(lambda *refs: project_body(*refs, cols=cols), out_shape=[j...]
  transfers between devices with their start and end apart: 25 -> 25, of which waited for: 2 -> 2; matrix products, arithmetic and copies ran while one was open for 3% -> 2% of each run, Pallas kernels for 43% -> 42%
where the time goes in v7:
time: 89.4 us; the launch traced here: 89.1 us
  Pallas kernels  41.4 us (46%)
  starting transfers between devices  34.7 us (39%)
  waiting for transfers between devices  8.58 us (10%)
  other arithmetic  3.03 us (3%)
  between operations  0.95 us (1%)
    ppermute x12, starting transfers between devices, col_shift(): return lax.ppermute(value, 'col', [((t + k) % n, t) for t in range(n)])  20.2 us
    pallas_call x1, Pallas kernels, outer_call(): pl.pallas_call(outer_body, grid_spec=pltpu.PrefetchScalarGridSpec(num_sca...  11.5 us
    ppermute x12, waiting for transfers between devices, col_shift(): return lax.ppermute(value, 'col', [((t + k) % n, t) for t in range(n)])  8.55 us
    ppermute x4, starting transfers between devices, right_grad_home(): got = lax.ppermute(block, ('row', 'col'), pairs).astype(F32)[None]  7.45 us
    ppermute x9, starting transfers between devices, row_shift(): return lax.ppermute(value, 'row', [((t + k) % n, t) for t in range(n)])  7.03 us
    pallas_call x1, Pallas kernels, right_grad_call(): pl.pallas_call(right_grad_body, grid_spec=pltpu.PrefetchScalarGridSpec(nu...  6.81 us
    pallas_call x1, Pallas kernels, back_call(): pl.pallas_call(back_body, grid=(rows // step,), in_specs=[pl.BlockSpec((s...  6.42 us
    pallas_call x1, Pallas kernels, left_grad_call(): pl.pallas_call(left_grad_body, grid_spec=pltpu.PrefetchScalarGridSpec(num...  5.88 us
  transfers between devices with their start and end apart: 25, of which 2 were waited for; matrix products, arithmetic and copies ran while one was open for 2% of the time, Pallas kernels for 42%

profile of v7, /device:TPU:0, one launch (start us, length us, event | category | flops | bytes accessed | tf_op | source)
XLA Modules:
  0.0 89.1 jit_solution(10636622885660963974)
XLA Ops:
  0.6 3.9 %project.1 = (bf16[32,2048]{1,0:T(8,128)(2,1)S(1)}, bf16[32,2048]{1,0:T(8,128)(2,1)S(1)}) custom-call(bf16[32,64,256]{2,1,0:T(8,128)(2,1)} %refs_0_.1, f32[1,256]{1,0:T(1,128)} %bitcast.61, f32[1,256]{1,0:T(1,128)} %bitcast.62, bf16[32,256]{1,0:T(8,128)(2,1)} %bitcast.59, bf16[32,256]{1,0:T(8,128)(2,1)} %bitcast.60), custom_call_target="tpu_custom_call" | custom-call | tf_op jit(solution)/shard_map/project/pallas_call | solution.py:106
  4.6 3.1 %collective-permute-start.2 = (bf16[32,2048]{1,0:T(8,128)(2,1)S(1)}, bf16[32,2048]{1,0:T(8,128)(2,1)S(1)}, u32[]{:S(2)}, u32[]{:S(2)}) collective-permute-start(bf16[32,2048]{1,0:T(8,128)(2,1)S(1)} %get-tuple-element.20), channel_id=1, source_target_pairs={{3,0},{0,1},{1,2},{2,3},{7,4},{4,5},{5,6},{6,7},{11,8},{8,9},{9,10... | collective-permute-start | bytes 393224 | tf_op jit(solution)/shard_map/ppermute | solution.py:540
  7.7 2.6 %collective-permute-start.1 = (bf16[32,2048]{1,0:T(8,128)(2,1)S(1)}, bf16[32,2048]{1,0:T(8,128)(2,1)S(1)}, u32[]{:S(2)}, u32[]{:S(2)}) collective-permute-start(bf16[32,2048]{1,0:T(8,128)(2,1)S(1)} %get-tuple-element.20), channel_id=1, source_target_pairs={{2,0},{3,1},{0,2},{1,3},{6,4},{7,5},{4,6},{5,7},{10,8},{11,9},{8,1... | collective-permute-start | bytes 393224 | tf_op jit(solution)/shard_map/ppermute | solution.py:540
  10.2 1.5 %collective-permute-start.4 = (bf16[32,2048]{1,0:T(8,128)(2,1)S(1)}, bf16[32,2048]{1,0:T(8,128)(2,1)S(1)}, u32[]{:S(2)}, u32[]{:S(2)}) collective-permute-start(bf16[32,2048]{1,0:T(8,128)(2,1)S(1)} %get-tuple-element.21), channel_id=1, source_target_pairs={{8,0},{12,4},{0,8},{4,12},{9,1},{13,5},{1,9},{5,13},{10,2},{14,6},... | collective-permute-start | bytes 393224 | tf_op jit(solution)/shard_map/ppermute | solution.py:544
  11.7 1.5 %collective-permute-start.3 = (bf16[32,2048]{1,0:T(8,128)(2,1)S(1)}, bf16[32,2048]{1,0:T(8,128)(2,1)S(1)}, u32[]{:S(2)}, u32[]{:S(2)}) collective-permute-start(bf16[32,2048]{1,0:T(8,128)(2,1)S(1)} %get-tuple-element.21), channel_id=1, source_target_pairs={{4,0},{8,4},{12,8},{0,12},{5,1},{9,5},{13,9},{1,13},{6,2},{10,6},{... | collective-permute-start | bytes 393224 | tf_op jit(solution)/shard_map/ppermute | solution.py:544
  13.6 2.1 %prep.1 = (s32[1,2048]{1,0:T(1,128)S(1)}, bf16[4,2,256,128]{3,2,1,0:T(8,128)(2,1)S(1)}, bf16[4,2,64,256]{3,2,1,0:T(8,128)(2,1)S(1)}, f32[4,64,256]{2,1,0:T(8,128...) custom-call(s32[3]{0:T(128)S(1)} %add_convert_fusion.3.refs_0_.at_ref, s32[1,256]{1,0:T(1,128)} %bitcast.52, ...), custom_call_target="tpu_custom_call" | custom-call | tf_op jit(solution)/shard_map/prep/pallas_call | solution.py:164
  15.7 6.4 %back.1.back_ref = bf16[8,2048,256]{2,1,0:T(8,128)(2,1)S(1)} custom-call(bf16[64,64,128]{2,1,0:T(8,128)(2,1)} %grad_ref.3, bf16[4,128,1024]{2,1,0:T(8,128)(2,1)S(1)} %get-tuple-element.24.wt_ref), custom_call_target="tpu_custom_call" | custom-call | flops 21474836480 | bytes 8388608 | tf_op jit(solution)/shard_map/back/pallas_call | solution.py:215
  22.2 1.4 %collective-permute-start = (bf16[32,2048]{1,0:T(8,128)(2,1)S(1)}, bf16[32,2048]{1,0:T(8,128)(2,1)S(1)}, u32[]{:S(2)}, u32[]{:S(2)}) collective-permute-start(bf16[32,2048]{1,0:T(8,128)(2,1)S(1)} %get-tuple-element.20), channel_id=1, source_target_pairs={{1,0},{2,1},{3,2},{0,3},{5,4},{6,5},{7,6},{4,7},{9,8},{10,9},{11,1... | collective-permute-start | bytes 393224 | tf_op jit(solution)/shard_map/ppermute | solution.py:540
  23.7 0.7 collective-permute-start.8
  24.4 0.3 collective-permute-start.7
  24.8 4.7 %collective-permute-done = bf16[32,2048]{1,0:T(8,128)(2,1)S(1)} collective-permute-done((bf16[32,2048]{1,0:T(8,128)(2,1)S(1)}, bf16[32,2048]{1,0:T(8,128)(2,1)S(1)}, u32[]{:S(2)}, u32[]{:S(2)}) %collective-permute-start) | collective-permute-done | bytes 131104 | tf_op jit(solution)/shard_map/ppermute | solution.py:540
  29.5 2.3 %collective-permute-start.6 = (bf16[32,2048]{1,0:T(8,128)(2,1)S(1)}, bf16[32,2048]{1,0:T(8,128)(2,1)S(1)}, u32[]{:S(2)}, u32[]{:S(2)}) collective-permute-start(bf16[32,2048]{1,0:T(8,128)(2,1)S(1)} %get-tuple-element.46), channel_id=1, source_target_pairs={{1,0},{2,1},{3,2},{0,3},{5,4},{6,5},{7,6},{4,7},{9,8},{10,9},{11,1... | collective-permute-start | bytes 393224 | tf_op jit(solution)/shard_map/ppermute | solution.py:540
  31.8 6.8 %right_grad.1 = bf16[128,2048]{1,0:T(8,128)(2,1)S(1)} custom-call(s32[3]{0:T(128)S(1)} %add_convert_fusion.3.refs_0_.at_ref, s32[256]{0:T(256)S(1)} %copy-done, bf16[8,2048,256]{2,1,0:T(8,128)(2,1)S(1)} %back.1.back_ref, bf16[128,2048]{1,0:T(8,128)(2,1)S(1)} %constant_dynamic-update-slice_fusion.left_ref, s32[1,2048]{1,0:T(1,128)S(1)} %get-tuple-element.31.lab_ref, ...), custom_call_target="tpu_custom_call" | custom-call | flops 21474836480 | bytes 8388608 | tf_op jit(solution)/shard_map/right_grad/pallas_call | solution.py:295
  38.7 0.7 collective-permute-start.15
  39.4 2.4 %collective-permute-start.18 = (bf16[32,2048]{1,0:T(8,128)(2,1)S(1)}, bf16[32,2048]{1,0:T(8,128)(2,1)S(1)}, u32[]{:S(2)}, u32[]{:S(2)}) collective-permute-start(bf16[32,2048]{1,0:T(8,128)(2,1)S(1)} %get-tuple-element.37), channel_id=1, source_target_pairs={{0,3},{1,7},{2,11},{3,15},{4,0},{5,4},{6,8},{7,12},{8,1},{9,5},{10... | collective-permute-start | bytes 393224 | tf_op jit(solution)/shard_map/ppermute | solution.py:577
  41.8 1.1 %collective-permute-start.17 = (bf16[32,2048]{1,0:T(8,128)(2,1)S(1)}, bf16[32,2048]{1,0:T(8,128)(2,1)S(1)}, u32[]{:S(2)}, u32[]{:S(2)}) collective-permute-start(bf16[32,2048]{1,0:T(8,128)(2,1)S(1)} %get-tuple-element.38), channel_id=1, source_target_pairs={{0,2},{1,6},{2,10},{3,14},{4,3},{5,7},{6,11},{7,15},{8,0},{9,4},{1... | collective-permute-start | bytes 393224 | tf_op jit(solution)/shard_map/ppermute | solution.py:577
  42.9 3.3 %collective-permute-start.16 = (bf16[32,2048]{1,0:T(8,128)(2,1)S(1)}, bf16[32,2048]{1,0:T(8,128)(2,1)S(1)}, u32[]{:S(2)}, u32[]{:S(2)}) collective-permute-start(bf16[32,2048]{1,0:T(8,128)(2,1)S(1)} %get-tuple-element.39), channel_id=1, source_target_pairs={{0,1},{1,5},{2,9},{3,13},{4,2},{5,6},{6,10},{7,14},{8,3},{9,7},{10... | collective-permute-start | bytes 393224 | tf_op jit(solution)/shard_map/ppermute | solution.py:577
  46.2 11.5 %outer.1 = (bf16[8,512,1024]{2,1,0:T(8,128)(2,1)S(1)}, f32[1024,128]{1,0:T(8,128)S(1)}) custom-call(s32[3]{0:T(128)S(1)} %add_convert_fusion.3.refs_0_.at_ref, s32[256]{0:T(256)S(1)} %copy-done, bf16[128,2048]{1,0:T(8,128)(2,1)S(1)} %constant_dynamic-update-slice_fusion.left_ref, s32[1,2048]{1,0:T(1,128)S(1)} %get-tuple-element.31.lab_ref, ...), custom_call_target="tpu_custom_call" | custom-call | flops 42949672960 | bytes 8388608 | tf_op jit(solution)/shard_map/outer/pallas_call | solution.py:467
  57.9 5.9 %left_grad.1 = bf16[128,2048]{1,0:T(8,128)(2,1)S(1)} custom-call(s32[3]{0:T(128)S(1)} %add_convert_fusion.3.refs_0_.at_ref, s32[256]{0:T(256)S(1)} %copy-done, bf16[8,2048,256]{2,1,0:T(8,128)(2,1)S(1)} %back.1.back_ref, s32[1,2048]{1,0:T(1,128)S(1)} %get-tuple-element.31.lab_ref, bf16[128,2048]{1,0:T(8,128)(2,1)S(1)} %pad_maximum_fusion.1.right_ref, ...), custom_call_target="tpu_custom_call" | custom-call | flops 21474836480 | bytes 8388608 | tf_op jit(solution)/shard_map/left_grad/pallas_call | solution.py:360
  63.8 1.8 %collective-permute-start.11 = (bf16[256,128]{1,0:T(8,128)(2,1)S(1)}, bf16[256,128]{1,0:T(8,128)(2,1)S(1)}, u32[]{:S(2)}, u32[]{:S(2)}) collective-permute-start(bf16[256,128]{1,0:T(8,128)(2,1)S(1)} %get-tuple-element.48), channel_id=1, source_target_pairs={{4,0},{8,4},{12,8},{0,12},{5,1},{9,5},{13,9},{1,13},{6,2},{10,6},{... | collective-permute-start | bytes 196616 | tf_op jit(solution)/shard_map/ppermute | solution.py:544
  65.6 0.1 collective-permute-start.12
  65.7 3.8 %collective-permute-start.14 = (bf16[32,2048]{1,0:T(8,128)(2,1)S(1)}, bf16[32,2048]{1,0:T(8,128)(2,1)S(1)}, u32[]{:S(2)}, u32[]{:S(2)}) collective-permute-start(bf16[32,2048]{1,0:T(8,128)(2,1)S(1)} %get-tuple-element.41), channel_id=1, source_target_pairs={{1,0},{2,1},{3,2},{0,3},{5,4},{6,5},{7,6},{4,7},{9,8},{10,9},{11,1... | collective-permute-start | bytes 393224 | tf_op jit(solution)/shard_map/ppermute | solution.py:540
  69.5 0.7 add_convert_fusion
  70.3 0.6 collective-permute-start.20
  70.9 3.3 %collective-permute-start.19 = (bf16[256,128]{1,0:T(8,128)(2,1)S(1)}, bf16[256,128]{1,0:T(8,128)(2,1)S(1)}, u32[]{:S(2)}, u32[]{:S(2)}) collective-permute-start(bf16[256,128]{1,0:T(8,128)(2,1)S(1)} %convert_element_type.121), channel_id=1, source_target_pairs={{1,0},{2,1},{3,2},{0,3},{5,4},{6,5},{7,6},{4,7},{9,8},{10,9},{11,1... | collective-permute-start | bytes 196616 | tf_op jit(solution)/shard_map/ppermute | solution.py:540
  74.2 4.8 %pair.1 = bf16[4096,128]{1,0:T(8,128)(2,1)} custom-call(bf16[8,512,1024]{2,1,0:T(8,128)(2,1)S(1)} %get-tuple-element.28.outer_ref, bf16[1024,128]{1,0:T(8,128)(2,1)S(1)} %get-tuple-element.34.w_ref, f32[1,128]{1,0:T(1,128)S(1)} %bitcast.53), custom_call_target="tpu_custom_call" | custom-call | flops 1073741824 | bytes 1048576 | tf_op jit(solution)/shard_map/pair/pallas_call | solution.py:511
  79.0 2.0 %collective-permute-start.13 = (bf16[32,2048]{1,0:T(8,128)(2,1)S(1)}, bf16[32,2048]{1,0:T(8,128)(2,1)S(1)}, u32[]{:S(2)}, u32[]{:S(2)}) collective-permute-start(bf16[32,2048]{1,0:T(8,128)(2,1)S(1)} %get-tuple-element.42), channel_id=1, source_target_pairs={{2,0},{3,1},{0,2},{1,3},{6,4},{7,5},{4,6},{5,7},{10,8},{11,9},{8,1... | collective-permute-start | bytes 393224 | tf_op jit(solution)/shard_map/ppermute | solution.py:540
  81.1 2.0 %collective-permute-start.23 = (bf16[256,128]{1,0:T(8,128)(2,1)S(1)}, bf16[256,128]{1,0:T(8,128)(2,1)S(1)}, u32[]{:S(2)}, u32[]{:S(2)}) collective-permute-start(bf16[256,128]{1,0:T(8,128)(2,1)S(1)} %add_convert_fusion.2), channel_id=1, source_target_pairs={{8,0},{12,4},{0,8},{4,12},{9,1},{13,5},{1,9},{5,13},{10,2},{14,6},... | collective-permute-start | bytes 196616 | tf_op jit(solution)/shard_map/ppermute | solution.py:544
  83.2 0.2 collective-permute-start.22
  83.3 3.8 %collective-permute-done.13 = bf16[32,2048]{1,0:T(8,128)(2,1)S(1)} collective-permute-done((bf16[32,2048]{1,0:T(8,128)(2,1)S(1)}, bf16[32,2048]{1,0:T(8,128)(2,1)S(1)}, u32[]{:S(2)}, u32[]{:S(2)}) %collective-permute-start.13) | collective-permute-done | bytes 131104 | tf_op jit(solution)/shard_map/ppermute | solution.py:540
  87.1 0.7 add_convert_fusion.1
  87.8 1.3 %convert_multiply_fusion = f32[1024,128]{1,0:T(8,128)} fusion(pred[1024]{0:T(1024)(128)(4,1)S(1)} %broadcast_in_dim.105, pred[1024]{0:T(1024)(128)(4,1)S(1)} %broadcast_in_dim.100, pred[1024]{0:T(1024)(128)(4,1)S(1)} %broadcast_in_dim.95, bf16[256,128]{1,0:T(8,128)(2,1)S(1)} %add_convert_fusion.2, bf16[256,128]{1,0:T(8,128)(2,1)S(1)} %collective-permute-done.24, ...), kind=kLoop, calls=%fused_computation.2 | loop fusion | flops 655360 | bytes 789504 | tf_op jit(solution)/shard_map/div | solution.py:647
  (57 shorter events, 1.0 us)
Async XLA Ops:
  4.6 27.2 %collective-permute-start.2 = (bf16[32,2048]{1,0:T(8,128)(2,1)S(1)}, bf16[32,2048]{1,0:T(8,128)(2,1)S(1)}, u32[]{:S(2)}, u32[]{:S(2)}) collective-permute-start(bf16[32,2048]{1,0:T(8,128)(2,1)S(1)} %get-tuple-element.20), channel_id=1, source_target_pairs={{3,0},{0,1},{1,2},{2,3},{7,4},{4,5},{5,6},{6,7},{11,8},{8,9},{9,10... | collective-permute-start | bytes 393224 | tf_op jit(solution)/shard_map/ppermute | solution.py:540
  7.7 24.1 %collective-permute-start.1 = (bf16[32,2048]{1,0:T(8,128)(2,1)S(1)}, bf16[32,2048]{1,0:T(8,128)(2,1)S(1)}, u32[]{:S(2)}, u32[]{:S(2)}) collective-permute-start(bf16[32,2048]{1,0:T(8,128)(2,1)S(1)} %get-tuple-element.20), channel_id=1, source_target_pairs={{2,0},{3,1},{0,2},{1,3},{6,4},{7,5},{4,6},{5,7},{10,8},{11,9},{8,1... | collective-permute-start | bytes 393224 | tf_op jit(solution)/shard_map/ppermute | solution.py:540
  10.2 11.9 %collective-permute-start.5 = (bf16[32,2048]{1,0:T(8,128)(2,1)S(1)}, bf16[32,2048]{1,0:T(8,128)(2,1)S(1)}, u32[]{:S(2)}, u32[]{:S(2)}) collective-permute-start(bf16[32,2048]{1,0:T(8,128)(2,1)S(1)} %get-tuple-element.21), channel_id=1, source_target_pairs={{12,0},{0,4},{4,8},{8,12},{13,1},{1,5},{5,9},{9,13},{14,2},{2,6},{... | collective-permute-start | bytes 393224 | tf_op jit(solution)/shard_map/ppermute | solution.py:544
  10.2 13.3 %collective-permute-start.4 = (bf16[32,2048]{1,0:T(8,128)(2,1)S(1)}, bf16[32,2048]{1,0:T(8,128)(2,1)S(1)}, u32[]{:S(2)}, u32[]{:S(2)}) collective-permute-start(bf16[32,2048]{1,0:T(8,128)(2,1)S(1)} %get-tuple-element.21), channel_id=1, source_target_pairs={{8,0},{12,4},{0,8},{4,12},{9,1},{13,5},{1,9},{5,13},{10,2},{14,6},... | collective-permute-start | bytes 393224 | tf_op jit(solution)/shard_map/ppermute | solution.py:544
  11.7 11.8 %collective-permute-start.3 = (bf16[32,2048]{1,0:T(8,128)(2,1)S(1)}, bf16[32,2048]{1,0:T(8,128)(2,1)S(1)}, u32[]{:S(2)}, u32[]{:S(2)}) collective-permute-start(bf16[32,2048]{1,0:T(8,128)(2,1)S(1)} %get-tuple-element.21), channel_id=1, source_target_pairs={{4,0},{8,4},{12,8},{0,12},{5,1},{9,5},{13,9},{1,13},{6,2},{10,6},{... | collective-permute-start | bytes 393224 | tf_op jit(solution)/shard_map/ppermute | solution.py:544
  15.7 16.1 %copy-start = (s32[256]{0:T(256)S(1)}, s32[256]{0:T(256)}, u32[]{:S(2)}) copy-start(s32[256]{0:T(256)} %labels_ref.5) | copy-start | bytes 3076
  22.2 7.3 %collective-permute-start = (bf16[32,2048]{1,0:T(8,128)(2,1)S(1)}, bf16[32,2048]{1,0:T(8,128)(2,1)S(1)}, u32[]{:S(2)}, u32[]{:S(2)}) collective-permute-start(bf16[32,2048]{1,0:T(8,128)(2,1)S(1)} %get-tuple-element.20), channel_id=1, source_target_pairs={{1,0},{2,1},{3,2},{0,3},{5,4},{6,5},{7,6},{4,7},{9,8},{10,9},{11,1... | collective-permute-start | bytes 393224 | tf_op jit(solution)/shard_map/ppermute | solution.py:540
  23.7 18.1 %collective-permute-start.8 = (bf16[32,2048]{1,0:T(8,128)(2,1)S(1)}, bf16[32,2048]{1,0:T(8,128)(2,1)S(1)}, u32[]{:S(2)}, u32[]{:S(2)}) collective-permute-start(bf16[32,2048]{1,0:T(8,128)(2,1)S(1)} %get-tuple-element.44), channel_id=1, source_target_pairs={{3,0},{0,1},{1,2},{2,3},{7,4},{4,5},{5,6},{6,7},{11,8},{8,9},{9,10... | collective-permute-start | bytes 393224 | tf_op jit(solution)/shard_map/ppermute | solution.py:540
  24.4 18.4 %collective-permute-start.7 = (bf16[32,2048]{1,0:T(8,128)(2,1)S(1)}, bf16[32,2048]{1,0:T(8,128)(2,1)S(1)}, u32[]{:S(2)}, u32[]{:S(2)}) collective-permute-start(bf16[32,2048]{1,0:T(8,128)(2,1)S(1)} %get-tuple-element.45), channel_id=1, source_target_pairs={{2,0},{3,1},{0,2},{1,3},{6,4},{7,5},{4,6},{5,7},{10,8},{11,9},{8,1... | collective-permute-start | bytes 393224 | tf_op jit(solution)/shard_map/ppermute | solution.py:540
  29.5 16.7 %collective-permute-start.6 = (bf16[32,2048]{1,0:T(8,128)(2,1)S(1)}, bf16[32,2048]{1,0:T(8,128)(2,1)S(1)}, u32[]{:S(2)}, u32[]{:S(2)}) collective-permute-start(bf16[32,2048]{1,0:T(8,128)(2,1)S(1)} %get-tuple-element.46), channel_id=1, source_target_pairs={{1,0},{2,1},{3,2},{0,3},{5,4},{6,5},{7,6},{4,7},{9,8},{10,9},{11,1... | collective-permute-start | bytes 393224 | tf_op jit(solution)/shard_map/ppermute | solution.py:540
  31.8 14.4 %copy-start.2 = (bf16[64,64,128]{2,1,0:T(8,128)(2,1)S(1)}, bf16[64,64,128]{2,1,0:T(8,128)(2,1)}, u32[]{:S(2)}) copy-start(bf16[64,64,128]{2,1,0:T(8,128)(2,1)} %grad_ref.3) | copy-start | bytes 3145732
  38.7 25.1 %collective-permute-start.15 = (bf16[32,2048]{1,0:T(8,128)(2,1)S(1)}, bf16[32,2048]{1,0:T(8,128)(2,1)S(1)}, u32[]{:S(2)}, u32[]{:S(2)}) collective-permute-start(bf16[32,2048]{1,0:T(8,128)(2,1)S(1)} %get-tuple-element.36), channel_id=1, source_target_pairs={{0,0},{1,4},{2,8},{3,12},{4,1},{5,5},{6,9},{7,13},{8,2},{9,6},{10,... | collective-permute-start | bytes 393224 | tf_op jit(solution)/shard_map/ppermute | solution.py:577
  39.4 26.2 %collective-permute-start.18 = (bf16[32,2048]{1,0:T(8,128)(2,1)S(1)}, bf16[32,2048]{1,0:T(8,128)(2,1)S(1)}, u32[]{:S(2)}, u32[]{:S(2)}) collective-permute-start(bf16[32,2048]{1,0:T(8,128)(2,1)S(1)} %get-tuple-element.37), channel_id=1, source_target_pairs={{0,3},{1,7},{2,11},{3,15},{4,0},{5,4},{6,8},{7,12},{8,1},{9,5},{10... | collective-permute-start | bytes 393224 | tf_op jit(solution)/shard_map/ppermute | solution.py:577
  41.8 23.8 %collective-permute-start.17 = (bf16[32,2048]{1,0:T(8,128)(2,1)S(1)}, bf16[32,2048]{1,0:T(8,128)(2,1)S(1)}, u32[]{:S(2)}, u32[]{:S(2)}) collective-permute-start(bf16[32,2048]{1,0:T(8,128)(2,1)S(1)} %get-tuple-element.38), channel_id=1, source_target_pairs={{0,2},{1,6},{2,10},{3,14},{4,3},{5,7},{6,11},{7,15},{8,0},{9,4},{1... | collective-permute-start | bytes 393224 | tf_op jit(solution)/shard_map/ppermute | solution.py:577
  42.9 22.8 %collective-permute-start.16 = (bf16[32,2048]{1,0:T(8,128)(2,1)S(1)}, bf16[32,2048]{1,0:T(8,128)(2,1)S(1)}, u32[]{:S(2)}, u32[]{:S(2)}) collective-permute-start(bf16[32,2048]{1,0:T(8,128)(2,1)S(1)} %get-tuple-element.39), channel_id=1, source_target_pairs={{0,1},{1,5},{2,9},{3,13},{4,2},{5,6},{6,10},{7,14},{8,3},{9,7},{10... | collective-permute-start | bytes 393224 | tf_op jit(solution)/shard_map/ppermute | solution.py:577
  57.8 12.4 %collective-permute-start.9 = (bf16[256,128]{1,0:T(8,128)(2,1)S(1)}, bf16[256,128]{1,0:T(8,128)(2,1)S(1)}, u32[]{:S(2)}, u32[]{:S(2)}) collective-permute-start(bf16[256,128]{1,0:T(8,128)(2,1)S(1)} %get-tuple-element.47), channel_id=1, source_target_pairs={{12,0},{0,4},{4,8},{8,12},{13,1},{1,5},{5,9},{9,13},{14,2},{2,6},{... | collective-permute-start | bytes 196616 | tf_op jit(solution)/shard_map/ppermute | solution.py:544
  57.9 16.3 %copy-start.1 = (f32[128]{0:T(128)S(1)}, f32[128]{0:T(128)}, u32[]{:S(2)}) copy-start(f32[128]{0:T(128)} %param.16) | copy-start | bytes 1540
  63.8 6.4 %collective-permute-start.11 = (bf16[256,128]{1,0:T(8,128)(2,1)S(1)}, bf16[256,128]{1,0:T(8,128)(2,1)S(1)}, u32[]{:S(2)}, u32[]{:S(2)}) collective-permute-start(bf16[256,128]{1,0:T(8,128)(2,1)S(1)} %get-tuple-element.48), channel_id=1, source_target_pairs={{4,0},{8,4},{12,8},{0,12},{5,1},{9,5},{13,9},{1,13},{6,2},{10,6},{... | collective-permute-start | bytes 196616 | tf_op jit(solution)/shard_map/ppermute | solution.py:544
  65.6 4.6 %collective-permute-start.10 = (bf16[256,128]{1,0:T(8,128)(2,1)S(1)}, bf16[256,128]{1,0:T(8,128)(2,1)S(1)}, u32[]{:S(2)}, u32[]{:S(2)}) collective-permute-start(bf16[256,128]{1,0:T(8,128)(2,1)S(1)} %get-tuple-element.49), channel_id=1, source_target_pairs={{8,0},{12,4},{0,8},{4,12},{9,1},{13,5},{1,9},{5,13},{10,2},{14,6},... | collective-permute-start | bytes 196616 | tf_op jit(solution)/shard_map/ppermute | solution.py:544
  65.6 17.6 %collective-permute-start.12 = (bf16[32,2048]{1,0:T(8,128)(2,1)S(1)}, bf16[32,2048]{1,0:T(8,128)(2,1)S(1)}, u32[]{:S(2)}, u32[]{:S(2)}) collective-permute-start(bf16[32,2048]{1,0:T(8,128)(2,1)S(1)} %get-tuple-element.40), channel_id=1, source_target_pairs={{3,0},{0,1},{1,2},{2,3},{7,4},{4,5},{5,6},{6,7},{11,8},{8,9},{9,10... | collective-permute-start | bytes 393224 | tf_op jit(solution)/shard_map/ppermute | solution.py:540
  65.7 17.6 %collective-permute-start.14 = (bf16[32,2048]{1,0:T(8,128)(2,1)S(1)}, bf16[32,2048]{1,0:T(8,128)(2,1)S(1)}, u32[]{:S(2)}, u32[]{:S(2)}) collective-permute-start(bf16[32,2048]{1,0:T(8,128)(2,1)S(1)} %get-tuple-element.41), channel_id=1, source_target_pairs={{1,0},{2,1},{3,2},{0,3},{5,4},{6,5},{7,6},{4,7},{9,8},{10,9},{11,1... | collective-permute-start | bytes 393224 | tf_op jit(solution)/shard_map/ppermute | solution.py:540
  70.3 8.7 %collective-permute-start.21 = (bf16[256,128]{1,0:T(8,128)(2,1)S(1)}, bf16[256,128]{1,0:T(8,128)(2,1)S(1)}, u32[]{:S(2)}, u32[]{:S(2)}) collective-permute-start(bf16[256,128]{1,0:T(8,128)(2,1)S(1)} %convert_element_type.121), channel_id=1, source_target_pairs={{3,0},{0,1},{1,2},{2,3},{7,4},{4,5},{5,6},{6,7},{11,8},{8,9},{9,10... | collective-permute-start | bytes 196616 | tf_op jit(solution)/shard_map/ppermute | solution.py:540
  70.3 10.7 %collective-permute-start.20 = (bf16[256,128]{1,0:T(8,128)(2,1)S(1)}, bf16[256,128]{1,0:T(8,128)(2,1)S(1)}, u32[]{:S(2)}, u32[]{:S(2)}) collective-permute-start(bf16[256,128]{1,0:T(8,128)(2,1)S(1)} %convert_element_type.121), channel_id=1, source_target_pairs={{2,0},{3,1},{0,2},{1,3},{6,4},{7,5},{4,6},{5,7},{10,8},{11,9},{8,1... | collective-permute-start | bytes 196616 | tf_op jit(solution)/shard_map/ppermute | solution.py:540
  70.9 10.1 %collective-permute-start.19 = (bf16[256,128]{1,0:T(8,128)(2,1)S(1)}, bf16[256,128]{1,0:T(8,128)(2,1)S(1)}, u32[]{:S(2)}, u32[]{:S(2)}) collective-permute-start(bf16[256,128]{1,0:T(8,128)(2,1)S(1)} %convert_element_type.121), channel_id=1, source_target_pairs={{1,0},{2,1},{3,2},{0,3},{5,4},{6,5},{7,6},{4,7},{9,8},{10,9},{11,1... | collective-permute-start | bytes 196616 | tf_op jit(solution)/shard_map/ppermute | solution.py:540
  79.0 8.1 %collective-permute-start.13 = (bf16[32,2048]{1,0:T(8,128)(2,1)S(1)}, bf16[32,2048]{1,0:T(8,128)(2,1)S(1)}, u32[]{:S(2)}, u32[]{:S(2)}) collective-permute-start(bf16[32,2048]{1,0:T(8,128)(2,1)S(1)} %get-tuple-element.42), channel_id=1, source_target_pairs={{2,0},{3,1},{0,2},{1,3},{6,4},{7,5},{4,6},{5,7},{10,8},{11,9},{8,1... | collective-permute-start | bytes 393224 | tf_op jit(solution)/shard_map/ppermute | solution.py:540
  81.1 6.8 %collective-permute-start.24 = (bf16[256,128]{1,0:T(8,128)(2,1)S(1)}, bf16[256,128]{1,0:T(8,128)(2,1)S(1)}, u32[]{:S(2)}, u32[]{:S(2)}) collective-permute-start(bf16[256,128]{1,0:T(8,128)(2,1)S(1)} %add_convert_fusion.2), channel_id=1, source_target_pairs={{4,0},{8,4},{12,8},{0,12},{5,1},{9,5},{13,9},{1,13},{6,2},{10,6},{... | collective-permute-start | bytes 196616 | tf_op jit(solution)/shard_map/ppermute | solution.py:544
  81.1 6.7 %collective-permute-start.23 = (bf16[256,128]{1,0:T(8,128)(2,1)S(1)}, bf16[256,128]{1,0:T(8,128)(2,1)S(1)}, u32[]{:S(2)}, u32[]{:S(2)}) collective-permute-start(bf16[256,128]{1,0:T(8,128)(2,1)S(1)} %add_convert_fusion.2), channel_id=1, source_target_pairs={{8,0},{12,4},{0,8},{4,12},{9,1},{13,5},{1,9},{5,13},{10,2},{14,6},... | collective-permute-start | bytes 196616 | tf_op jit(solution)/shard_map/ppermute | solution.py:544
  83.2 4.7 %collective-permute-start.22 = (bf16[256,128]{1,0:T(8,128)(2,1)S(1)}, bf16[256,128]{1,0:T(8,128)(2,1)S(1)}, u32[]{:S(2)}, u32[]{:S(2)}) collective-permute-start(bf16[256,128]{1,0:T(8,128)(2,1)S(1)} %add_convert_fusion.2), channel_id=1, source_target_pairs={{12,0},{0,4},{4,8},{8,12},{13,1},{1,5},{5,9},{9,13},{14,2},{2,6},{... | collective-permute-start | bytes 196616 | tf_op jit(solution)/shard_map/ppermute | solution.py:544

commit v8 on v7

--- a/solution.py
+++ b/solution.py
@@ -55,22 +55,25 @@
 
 def project_body(x_ref, gain_ref, shift_ref, first_ref, second_ref, left_ref, right_ref, proj_ref, turn_ref, out_ref,
                  *, cols):
-    here, rows, feats = x_ref.shape
-    chunk = max(1, 2 * WIDE // rows)
+    chunk, rows, feats = x_ref.shape
+    g = pl.program_id(0)
     blank = jnp.zeros((LANES - 2 * PROJ, feats), BF16)
     w = jnp.concatenate([first_ref[...], second_ref[...], blank], axis=0)
 
-    def norm(step, carry):
-        x = x_ref[pl.ds(step * chunk, chunk)].astype(F32).reshape(chunk * rows, feats)
-        center = x - jnp.mean(x, axis=-1, keepdims=True)
-        spread = jnp.mean(center * center, axis=-1, keepdims=True)
-        normed = center * lax.rsqrt(spread + 1e-05) * gain_ref[...] + shift_ref[...]
-        at = pl.multiple_of(step * (chunk * rows), chunk * rows)
-        proj_ref[pl.ds(at, chunk * rows)] = nt_dot(normed.astype(BF16), w)
-        return carry
-
-    lax.fori_loop(0, here // chunk, norm, 0)
-
+    x = x_ref[...].astype(F32).reshape(chunk * rows, feats)
+    center = x - jnp.mean(x, axis=-1, keepdims=True)
+    spread = jnp.mean(center * center, axis=-1, keepdims=True)
+    normed = center * lax.rsqrt(spread + 1e-05) * gain_ref[...] + shift_ref[...]
+    at = pl.multiple_of(g * (chunk * rows), chunk * rows)
+    proj_ref[pl.ds(at, chunk * rows)] = nt_dot(normed.astype(BF16), w)
+
+    @pl.when(g == pl.num_programs(0) - 1)
+    def _():
+        project_layout(proj_ref, turn_ref, out_ref, left_ref, right_ref, rows, cols)
+
+
+def project_layout(proj_ref, turn_ref, out_ref, left_ref, right_ref, rows, cols):
+    here = left_ref.shape[0]
     lane = lax.broadcasted_iota(jnp.int32, (here, LANES), 1)
     for t in range(rows // PER_TILE):
         tile = proj_ref[pl.ds(t * PER_TILE, here, stride=rows)]
@@ -102,16 +105,22 @@
 
 
 def project_call(x, gain, shift, first, second, cols):
-    here, rows, _ = x.shape
+    here, rows, feats = x.shape
+    chunk = min(here, max(1, 2 * WIDE // rows))
+    whole = lambda a: pl.BlockSpec(a.shape, lambda g: (0,) * a.ndim)
     return pl.pallas_call(
         lambda *refs: project_body(*refs, cols=cols),
+        grid=(here // chunk,),
+        in_specs=[pl.BlockSpec((chunk, rows, feats), lambda g: (g, 0, 0))]
+        + [whole(a) for a in (gain, shift, first, second)],
+        out_specs=[VMEM] * 2,
         out_shape=[jax.ShapeDtypeStruct((here, rows * PROJ), BF16)] * 2,
         scratch_shapes=[
             pltpu.VMEM((here * rows, LANES), F32),
             pltpu.VMEM((here * rows // LANES * PROJ, LANES), F32),
             pltpu.VMEM((here, LANES), F32),
         ],
-        compiler_params=pltpu.CompilerParams(vmem_limit_bytes=24 << 20),
+        compiler_params=KERNEL,
         name="project",
     )(*map(in_hbm, (x, gain, shift, first, second)))
 
@@ -217,7 +226,7 @@
         grid=(rows // step,),
         in_specs=[
             pl.BlockSpec((step, cols, width), lambda g: (g, 0, 0)),
-            pl.BlockSpec(wt.shape, lambda g: (0, 0, 0)),
+            VMEM,
         ],
         out_specs=VMEM,
         out_shape=pltpu.VMEM((rows // step, PROJ * cols, WIDE), BF16),
@@ -235,11 +244,16 @@
     return labels_ref[at_ref[0] + (group + 1) * (WIDE // PROJ) - 1] // 2
 
 
+def lanes_of(group):
+    return pl.ds(pl.multiple_of(group * WIDE, WIDE), WIDE)
+
+
 def masked_left(left_ref, lab_ref, lb_ref, pair):
     seqs = left_ref.shape[0]
+    lanes = lanes_of(pl.program_id(0))
     for side in range(2):
-        keep = (lab_ref[...] == 2 * pair + side).astype(F32).astype(BF16)
-        lb_ref[side * seqs : (side + 1) * seqs] = left_ref[...] * keep
+        keep = (lab_ref[:, lanes] == 2 * pair + side).astype(F32).astype(BF16)
+        lb_ref[side * seqs : (side + 1) * seqs] = left_ref[:, lanes] * keep
 
 
 def right_grad_body(at_ref, labels_ref, back_ref, left_ref, lab_ref, wide_ref,
@@ -291,7 +305,6 @@
     groups, span, _ = back.shape
     total = groups * WIDE
     seqs = left.shape[0]
-    whole = lambda shape: pl.BlockSpec(shape, lambda g, *_: (0,) * len(shape))
     return pl.pallas_call(
         right_grad_body,
         grid_spec=pltpu.PrefetchScalarGridSpec(
@@ -299,11 +312,11 @@
             grid=(total // WIDE,),
             in_specs=[
                 VMEM,
-                pl.BlockSpec((seqs, WIDE), lambda g, *_: (0, g)),
-                pl.BlockSpec((1, WIDE), lambda g, *_: (0, g)),
-                whole(wide.shape),
+                VMEM,
+                VMEM,
+                VMEM,
             ],
-            out_specs=whole((seqs, span)),
+            out_specs=VMEM,
             scratch_shapes=[
                 pltpu.VMEM((CHAINS // 2, span, 2 * seqs), F32),
                 pltpu.VMEM((2 * seqs, WIDE), BF16),
@@ -344,19 +357,18 @@
 
     def one_pair(pair, total):
         part = nn_dot(rm_ref[pair], back_ref[g])
-        keep0 = lab_ref[...] == 2 * pair
-        keep1 = lab_ref[...] == 2 * pair + 1
+        lab = lab_ref[:, lanes_of(g)]
+        keep0, keep1 = lab == 2 * pair, lab == 2 * pair + 1
         return total + jnp.where(keep0, part[:seqs], 0.0) + jnp.where(keep1, part[seqs:], 0.0)
 
-    total = lax.fori_loop(first_pair(at_ref, labels_ref, g), last_pair(at_ref, labels_ref, g) + 1, one_pair, jnp.zeros(left_out.shape, F32))
-    left_out[...] = total.astype(BF16)
+    total = lax.fori_loop(first_pair(at_ref, labels_ref, g), last_pair(at_ref, labels_ref, g) + 1, one_pair, jnp.zeros((seqs, WIDE), F32))
+    left_out[:, lanes_of(g)] = total.astype(BF16)
 
 
 def left_grad_call(at, labels, back, lab, right, tall):
     groups, span, _ = back.shape
     total = groups * WIDE
     seqs = right.shape[0]
-    whole = lambda shape: pl.BlockSpec(shape, lambda g, *_: (0,) * len(shape))
     return pl.pallas_call(
         left_grad_body,
         grid_spec=pltpu.PrefetchScalarGridSpec(
@@ -364,11 +376,11 @@
             grid=(total // WIDE,),
             in_specs=[
                 VMEM,
-                pl.BlockSpec((1, WIDE), lambda g, *_: (0, g)),
-                whole(right.shape),
-                whole(tall.shape),
+                VMEM,
+                VMEM,
+                VMEM,
             ],
-            out_specs=pl.BlockSpec((seqs, WIDE), lambda g, *_: (0, g)),
+            out_specs=VMEM,
             scratch_shapes=[
                 pltpu.VMEM((CHAINS // 2, 2 * seqs, span), BF16),
                 pltpu.VMEM((seqs, span), BF16),
@@ -463,22 +475,21 @@
     seqs, total = left.shape
     span = right.shape[1]
     step = WIDE // PROJ
-    whole = lambda shape: pl.BlockSpec(shape, lambda g, *_: (0,) * len(shape))
     return pl.pallas_call(
         outer_body,
         grid_spec=pltpu.PrefetchScalarGridSpec(
             num_scalar_prefetch=2,
             grid=(total // WIDE,),
             in_specs=[
-                pl.BlockSpec((seqs, WIDE), lambda g, *_: (0, g)),
-                pl.BlockSpec((1, WIDE), lambda g, *_: (0, g)),
-                whole(right.shape),
-                whole(wide.shape),
+                VMEM,
+                VMEM,
+                VMEM,
+                VMEM,
                 pl.BlockSpec((step, cols, width), lambda g, *_: (g, 0, 0)),
             ],
             out_specs=[
                 VMEM,
-                whole((PROJ * PROJ, width)),
+                VMEM,
             ],
             scratch_shapes=[
                 pltpu.VMEM((CHAINS // 2, span, 2 * seqs), BF16),
@@ -513,8 +524,8 @@
         grid=(groups,),
         in_specs=[
             VMEM,
-            pl.BlockSpec(w.shape, lambda g: (0, 0)),
-            pl.BlockSpec(offset.shape, lambda g: (0, 0)),
+            VMEM,
+            VMEM,
         ],
         out_specs=pl.BlockSpec((pairs, width), lambda g: (g, 0)),
         out_shape=jax.ShapeDtypeStruct((groups * pairs, width), BF16),

time: 89.4 us -> 89.4 us (level)
  no operation moved by 1% of the time
where the time goes in v8:
time: 89.4 us; the launch traced here: 89.1 us
  Pallas kernels  41.4 us (46%)
  starting transfers between devices  34.6 us (39%)
  waiting for transfers between devices  8.62 us (10%)
  other arithmetic  3.03 us (3%)
  between operations  0.96 us (1%)
    ppermute x12, starting transfers between devices, col_shift(): return lax.ppermute(value, 'col', [((t + k) % n, t) for t in range(n)])  20.1 us
    pallas_call x1, Pallas kernels, outer_call(): pl.pallas_call(outer_body, grid_spec=pltpu.PrefetchScalarGridSpec(num_sca...  11.4 us
    ppermute x12, waiting for transfers between devices, col_shift(): return lax.ppermute(value, 'col', [((t + k) % n, t) for t in range(n)])  8.59 us
    ppermute x4, starting transfers between devices, right_grad_home(): got = lax.ppermute(block, ('row', 'col'), pairs).astype(F32)[None]  7.44 us
    ppermute x9, starting transfers between devices, row_shift(): return lax.ppermute(value, 'row', [((t + k) % n, t) for t in range(n)])  7.04 us
    pallas_call x1, Pallas kernels, right_grad_call(): pl.pallas_call(right_grad_body, grid_spec=pltpu.PrefetchScalarGridSpec(nu...  6.73 us
    pallas_call x1, Pallas kernels, back_call(): pl.pallas_call(back_body, grid=(rows // step,), in_specs=[pl.BlockSpec((s...  6.42 us
    pallas_call x1, Pallas kernels, left_grad_call(): pl.pallas_call(left_grad_body, grid_spec=pltpu.PrefetchScalarGridSpec(num...  5.81 us
  transfers between devices with their start and end apart: 25, of which 2 were waited for; matrix products, arithmetic and copies ran while one was open for 2% of the time, Pallas kernels for 42%

profile of v8, /device:TPU:0, one launch (start us, length us, event | category | flops | bytes accessed | tf_op | source)
XLA Modules:
  0.0 89.1 jit_solution(8145618166230081666)
XLA Ops:
  0.6 4.2 %project.1 = (bf16[32,2048]{1,0:T(8,128)(2,1)S(1)}, bf16[32,2048]{1,0:T(8,128)(2,1)S(1)}) custom-call(bf16[32,64,256]{2,1,0:T(8,128)(2,1)} %refs_0_.1, f32[1,256]{1,0:T(1,128)} %bitcast.61, f32[1,256]{1,0:T(1,128)} %bitcast.62, bf16[32,256]{1,0:T(8,128)(2,1)} %bitcast.59, bf16[32,256]{1,0:T(8,128)(2,1)} %bitcast.60), custom_call_target="tpu_custom_call" | custom-call | tf_op jit(solution)/shard_map/project/pallas_call | solution.py:111
  4.8 3.1 %collective-permute-start.2 = (bf16[32,2048]{1,0:T(8,128)(2,1)S(1)}, bf16[32,2048]{1,0:T(8,128)(2,1)S(1)}, u32[]{:S(2)}, u32[]{:S(2)}) collective-permute-start(bf16[32,2048]{1,0:T(8,128)(2,1)S(1)} %get-tuple-element.20), channel_id=1, source_target_pairs={{3,0},{0,1},{1,2},{2,3},{7,4},{4,5},{5,6},{6,7},{11,8},{8,9},{9,10... | collective-permute-start | bytes 393224 | tf_op jit(solution)/shard_map/ppermute | solution.py:551
  7.9 2.6 %collective-permute-start.1 = (bf16[32,2048]{1,0:T(8,128)(2,1)S(1)}, bf16[32,2048]{1,0:T(8,128)(2,1)S(1)}, u32[]{:S(2)}, u32[]{:S(2)}) collective-permute-start(bf16[32,2048]{1,0:T(8,128)(2,1)S(1)} %get-tuple-element.20), channel_id=1, source_target_pairs={{2,0},{3,1},{0,2},{1,3},{6,4},{7,5},{4,6},{5,7},{10,8},{11,9},{8,1... | collective-permute-start | bytes 393224 | tf_op jit(solution)/shard_map/ppermute | solution.py:551
  10.5 1.5 %collective-permute-start.4 = (bf16[32,2048]{1,0:T(8,128)(2,1)S(1)}, bf16[32,2048]{1,0:T(8,128)(2,1)S(1)}, u32[]{:S(2)}, u32[]{:S(2)}) collective-permute-start(bf16[32,2048]{1,0:T(8,128)(2,1)S(1)} %get-tuple-element.21), channel_id=1, source_target_pairs={{8,0},{12,4},{0,8},{4,12},{9,1},{13,5},{1,9},{5,13},{10,2},{14,6},... | collective-permute-start | bytes 393224 | tf_op jit(solution)/shard_map/ppermute | solution.py:555
  12.0 1.5 %collective-permute-start.3 = (bf16[32,2048]{1,0:T(8,128)(2,1)S(1)}, bf16[32,2048]{1,0:T(8,128)(2,1)S(1)}, u32[]{:S(2)}, u32[]{:S(2)}) collective-permute-start(bf16[32,2048]{1,0:T(8,128)(2,1)S(1)} %get-tuple-element.21), channel_id=1, source_target_pairs={{4,0},{8,4},{12,8},{0,12},{5,1},{9,5},{13,9},{1,13},{6,2},{10,6},{... | collective-permute-start | bytes 393224 | tf_op jit(solution)/shard_map/ppermute | solution.py:555
  13.9 2.1 %prep.1 = (s32[1,2048]{1,0:T(1,128)S(1)}, bf16[4,2,256,128]{3,2,1,0:T(8,128)(2,1)S(1)}, bf16[4,2,64,256]{3,2,1,0:T(8,128)(2,1)S(1)}, f32[4,64,256]{2,1,0:T(8,128...) custom-call(s32[3]{0:T(128)S(1)} %add_convert_fusion.3.refs_0_.at_ref, s32[1,256]{1,0:T(1,128)} %bitcast.52, ...), custom_call_target="tpu_custom_call" | custom-call | tf_op jit(solution)/shard_map/prep/pallas_call | solution.py:173
  16.0 6.4 %back.1.back_ref = bf16[8,2048,256]{2,1,0:T(8,128)(2,1)S(1)} custom-call(bf16[64,64,128]{2,1,0:T(8,128)(2,1)} %grad_ref.3, bf16[4,128,1024]{2,1,0:T(8,128)(2,1)S(1)} %get-tuple-element.24.wt_ref), custom_call_target="tpu_custom_call" | custom-call | flops 21474836480 | bytes 8388608 | tf_op jit(solution)/shard_map/back/pallas_call | solution.py:224
  22.4 1.4 %collective-permute-start = (bf16[32,2048]{1,0:T(8,128)(2,1)S(1)}, bf16[32,2048]{1,0:T(8,128)(2,1)S(1)}, u32[]{:S(2)}, u32[]{:S(2)}) collective-permute-start(bf16[32,2048]{1,0:T(8,128)(2,1)S(1)} %get-tuple-element.20), channel_id=1, source_target_pairs={{1,0},{2,1},{3,2},{0,3},{5,4},{6,5},{7,6},{4,7},{9,8},{10,9},{11,1... | collective-permute-start | bytes 393224 | tf_op jit(solution)/shard_map/ppermute | solution.py:551
  24.0 0.7 collective-permute-start.8
  24.7 0.3 collective-permute-start.7
  25.0 4.8 %collective-permute-done = bf16[32,2048]{1,0:T(8,128)(2,1)S(1)} collective-permute-done((bf16[32,2048]{1,0:T(8,128)(2,1)S(1)}, bf16[32,2048]{1,0:T(8,128)(2,1)S(1)}, u32[]{:S(2)}, u32[]{:S(2)}) %collective-permute-start) | collective-permute-done | bytes 131104 | tf_op jit(solution)/shard_map/ppermute | solution.py:551
  29.8 2.2 %collective-permute-start.6 = (bf16[32,2048]{1,0:T(8,128)(2,1)S(1)}, bf16[32,2048]{1,0:T(8,128)(2,1)S(1)}, u32[]{:S(2)}, u32[]{:S(2)}) collective-permute-start(bf16[32,2048]{1,0:T(8,128)(2,1)S(1)} %get-tuple-element.46), channel_id=1, source_target_pairs={{1,0},{2,1},{3,2},{0,3},{5,4},{6,5},{7,6},{4,7},{9,8},{10,9},{11,1... | collective-permute-start | bytes 393224 | tf_op jit(solution)/shard_map/ppermute | solution.py:551
  32.1 6.7 %right_grad.1 = bf16[128,2048]{1,0:T(8,128)(2,1)S(1)} custom-call(s32[3]{0:T(128)S(1)} %add_convert_fusion.3.refs_0_.at_ref, s32[256]{0:T(256)S(1)} %copy-done, bf16[8,2048,256]{2,1,0:T(8,128)(2,1)S(1)} %back.1.back_ref, bf16[128,2048]{1,0:T(8,128)(2,1)S(1)} %constant_dynamic-update-slice_fusion.left_ref, s32[1,2048]{1,0:T(1,128)S(1)} %get-tuple-element.31.lab_ref, ...), custom_call_target="tpu_custom_call" | custom-call | flops 21474836480 | bytes 8388608 | tf_op jit(solution)/shard_map/right_grad/pallas_call | solution.py:308
  38.9 0.7 collective-permute-start.15
  39.6 2.4 %collective-permute-start.18 = (bf16[32,2048]{1,0:T(8,128)(2,1)S(1)}, bf16[32,2048]{1,0:T(8,128)(2,1)S(1)}, u32[]{:S(2)}, u32[]{:S(2)}) collective-permute-start(bf16[32,2048]{1,0:T(8,128)(2,1)S(1)} %get-tuple-element.37), channel_id=1, source_target_pairs={{0,3},{1,7},{2,11},{3,15},{4,0},{5,4},{6,8},{7,12},{8,1},{9,5},{10... | collective-permute-start | bytes 393224 | tf_op jit(solution)/shard_map/ppermute | solution.py:588
  42.0 1.0 %collective-permute-start.17 = (bf16[32,2048]{1,0:T(8,128)(2,1)S(1)}, bf16[32,2048]{1,0:T(8,128)(2,1)S(1)}, u32[]{:S(2)}, u32[]{:S(2)}) collective-permute-start(bf16[32,2048]{1,0:T(8,128)(2,1)S(1)} %get-tuple-element.38), channel_id=1, source_target_pairs={{0,2},{1,6},{2,10},{3,14},{4,3},{5,7},{6,11},{7,15},{8,0},{9,4},{1... | collective-permute-start | bytes 393224 | tf_op jit(solution)/shard_map/ppermute | solution.py:588
  43.0 3.3 %collective-permute-start.16 = (bf16[32,2048]{1,0:T(8,128)(2,1)S(1)}, bf16[32,2048]{1,0:T(8,128)(2,1)S(1)}, u32[]{:S(2)}, u32[]{:S(2)}) collective-permute-start(bf16[32,2048]{1,0:T(8,128)(2,1)S(1)} %get-tuple-element.39), channel_id=1, source_target_pairs={{0,1},{1,5},{2,9},{3,13},{4,2},{5,6},{6,10},{7,14},{8,3},{9,7},{10... | collective-permute-start | bytes 393224 | tf_op jit(solution)/shard_map/ppermute | solution.py:588
  46.4 11.4 %outer.1 = (bf16[8,512,1024]{2,1,0:T(8,128)(2,1)S(1)}, f32[1024,128]{1,0:T(8,128)S(1)}) custom-call(s32[3]{0:T(128)S(1)} %add_convert_fusion.3.refs_0_.at_ref, s32[256]{0:T(256)S(1)} %copy-done, bf16[128,2048]{1,0:T(8,128)(2,1)S(1)} %constant_dynamic-update-slice_fusion.left_ref, s32[1,2048]{1,0:T(1,128)S(1)} %get-tuple-element.31.lab_ref, ...), custom_call_target="tpu_custom_call" | custom-call | flops 42949672960 | bytes 8388608 | tf_op jit(solution)/shard_map/outer/pallas_call | solution.py:478
  57.9 5.8 %left_grad.1 = bf16[128,2048]{1,0:T(8,128)(2,1)S(1)} custom-call(s32[3]{0:T(128)S(1)} %add_convert_fusion.3.refs_0_.at_ref, s32[256]{0:T(256)S(1)} %copy-done, bf16[8,2048,256]{2,1,0:T(8,128)(2,1)S(1)} %back.1.back_ref, s32[1,2048]{1,0:T(1,128)S(1)} %get-tuple-element.31.lab_ref, bf16[128,2048]{1,0:T(8,128)(2,1)S(1)} %pad_maximum_fusion.1.right_ref, ...), custom_call_target="tpu_custom_call" | custom-call | flops 21474836480 | bytes 8388608 | tf_op jit(solution)/shard_map/left_grad/pallas_call | solution.py:372
  63.8 1.8 %collective-permute-start.11 = (bf16[256,128]{1,0:T(8,128)(2,1)S(1)}, bf16[256,128]{1,0:T(8,128)(2,1)S(1)}, u32[]{:S(2)}, u32[]{:S(2)}) collective-permute-start(bf16[256,128]{1,0:T(8,128)(2,1)S(1)} %get-tuple-element.48), channel_id=1, source_target_pairs={{4,0},{8,4},{12,8},{0,12},{5,1},{9,5},{13,9},{1,13},{6,2},{10,6},{... | collective-permute-start | bytes 196616 | tf_op jit(solution)/shard_map/ppermute | solution.py:555
  65.6 0.1 collective-permute-start.12
  65.7 3.8 %collective-permute-start.14 = (bf16[32,2048]{1,0:T(8,128)(2,1)S(1)}, bf16[32,2048]{1,0:T(8,128)(2,1)S(1)}, u32[]{:S(2)}, u32[]{:S(2)}) collective-permute-start(bf16[32,2048]{1,0:T(8,128)(2,1)S(1)} %get-tuple-element.41), channel_id=1, source_target_pairs={{1,0},{2,1},{3,2},{0,3},{5,4},{6,5},{7,6},{4,7},{9,8},{10,9},{11,1... | collective-permute-start | bytes 393224 | tf_op jit(solution)/shard_map/ppermute | solution.py:551
  69.5 0.7 add_convert_fusion
  70.3 0.6 collective-permute-start.20
  70.9 3.3 %collective-permute-start.19 = (bf16[256,128]{1,0:T(8,128)(2,1)S(1)}, bf16[256,128]{1,0:T(8,128)(2,1)S(1)}, u32[]{:S(2)}, u32[]{:S(2)}) collective-permute-start(bf16[256,128]{1,0:T(8,128)(2,1)S(1)} %convert_element_type.121), channel_id=1, source_target_pairs={{1,0},{2,1},{3,2},{0,3},{5,4},{6,5},{7,6},{4,7},{9,8},{10,9},{11,1... | collective-permute-start | bytes 196616 | tf_op jit(solution)/shard_map/ppermute | solution.py:551
  74.2 4.8 %pair.1 = bf16[4096,128]{1,0:T(8,128)(2,1)} custom-call(bf16[8,512,1024]{2,1,0:T(8,128)(2,1)S(1)} %get-tuple-element.28.outer_ref, bf16[1024,128]{1,0:T(8,128)(2,1)S(1)} %get-tuple-element.34.w_ref, f32[1,128]{1,0:T(1,128)S(1)} %bitcast.53), custom_call_target="tpu_custom_call" | custom-call | flops 1073741824 | bytes 1048576 | tf_op jit(solution)/shard_map/pair/pallas_call | solution.py:522
  79.0 2.0 %collective-permute-start.13 = (bf16[32,2048]{1,0:T(8,128)(2,1)S(1)}, bf16[32,2048]{1,0:T(8,128)(2,1)S(1)}, u32[]{:S(2)}, u32[]{:S(2)}) collective-permute-start(bf16[32,2048]{1,0:T(8,128)(2,1)S(1)} %get-tuple-element.42), channel_id=1, source_target_pairs={{2,0},{3,1},{0,2},{1,3},{6,4},{7,5},{4,6},{5,7},{10,8},{11,9},{8,1... | collective-permute-start | bytes 393224 | tf_op jit(solution)/shard_map/ppermute | solution.py:551
  81.1 2.0 %collective-permute-start.23 = (bf16[256,128]{1,0:T(8,128)(2,1)S(1)}, bf16[256,128]{1,0:T(8,128)(2,1)S(1)}, u32[]{:S(2)}, u32[]{:S(2)}) collective-permute-start(bf16[256,128]{1,0:T(8,128)(2,1)S(1)} %add_convert_fusion.2), channel_id=1, source_target_pairs={{8,0},{12,4},{0,8},{4,12},{9,1},{13,5},{1,9},{5,13},{10,2},{14,6},... | collective-permute-start | bytes 196616 | tf_op jit(solution)/shard_map/ppermute | solution.py:555
  83.2 0.2 collective-permute-start.22
  83.3 3.8 %collective-permute-done.13 = bf16[32,2048]{1,0:T(8,128)(2,1)S(1)} collective-permute-done((bf16[32,2048]{1,0:T(8,128)(2,1)S(1)}, bf16[32,2048]{1,0:T(8,128)(2,1)S(1)}, u32[]{:S(2)}, u32[]{:S(2)}) %collective-permute-start.13) | collective-permute-done | bytes 131104 | tf_op jit(solution)/shard_map/ppermute | solution.py:551
  87.1 0.7 add_convert_fusion.1
  87.8 1.3 %convert_multiply_fusion = f32[1024,128]{1,0:T(8,128)} fusion(pred[1024]{0:T(1024)(128)(4,1)S(1)} %broadcast_in_dim.105, pred[1024]{0:T(1024)(128)(4,1)S(1)} %broadcast_in_dim.100, pred[1024]{0:T(1024)(128)(4,1)S(1)} %broadcast_in_dim.95, bf16[256,128]{1,0:T(8,128)(2,1)S(1)} %add_convert_fusion.2, bf16[256,128]{1,0:T(8,128)(2,1)S(1)} %collective-permute-done.24, ...), kind=kLoop, calls=%fused_computation.2 | loop fusion | flops 655360 | bytes 789504 | tf_op jit(solution)/shard_map/div | solution.py:658
  (57 shorter events, 1.0 us)
Async XLA Ops:
  4.8 27.2 %collective-permute-start.2 = (bf16[32,2048]{1,0:T(8,128)(2,1)S(1)}, bf16[32,2048]{1,0:T(8,128)(2,1)S(1)}, u32[]{:S(2)}, u32[]{:S(2)}) collective-permute-start(bf16[32,2048]{1,0:T(8,128)(2,1)S(1)} %get-tuple-element.20), channel_id=1, source_target_pairs={{3,0},{0,1},{1,2},{2,3},{7,4},{4,5},{5,6},{6,7},{11,8},{8,9},{9,10... | collective-permute-start | bytes 393224 | tf_op jit(solution)/shard_map/ppermute | solution.py:551
  7.9 24.1 %collective-permute-start.1 = (bf16[32,2048]{1,0:T(8,128)(2,1)S(1)}, bf16[32,2048]{1,0:T(8,128)(2,1)S(1)}, u32[]{:S(2)}, u32[]{:S(2)}) collective-permute-start(bf16[32,2048]{1,0:T(8,128)(2,1)S(1)} %get-tuple-element.20), channel_id=1, source_target_pairs={{2,0},{3,1},{0,2},{1,3},{6,4},{7,5},{4,6},{5,7},{10,8},{11,9},{8,1... | collective-permute-start | bytes 393224 | tf_op jit(solution)/shard_map/ppermute | solution.py:551
  10.5 11.9 %collective-permute-start.5 = (bf16[32,2048]{1,0:T(8,128)(2,1)S(1)}, bf16[32,2048]{1,0:T(8,128)(2,1)S(1)}, u32[]{:S(2)}, u32[]{:S(2)}) collective-permute-start(bf16[32,2048]{1,0:T(8,128)(2,1)S(1)} %get-tuple-element.21), channel_id=1, source_target_pairs={{12,0},{0,4},{4,8},{8,12},{13,1},{1,5},{5,9},{9,13},{14,2},{2,6},{... | collective-permute-start | bytes 393224 | tf_op jit(solution)/shard_map/ppermute | solution.py:555
  10.5 13.3 %collective-permute-start.4 = (bf16[32,2048]{1,0:T(8,128)(2,1)S(1)}, bf16[32,2048]{1,0:T(8,128)(2,1)S(1)}, u32[]{:S(2)}, u32[]{:S(2)}) collective-permute-start(bf16[32,2048]{1,0:T(8,128)(2,1)S(1)} %get-tuple-element.21), channel_id=1, source_target_pairs={{8,0},{12,4},{0,8},{4,12},{9,1},{13,5},{1,9},{5,13},{10,2},{14,6},... | collective-permute-start | bytes 393224 | tf_op jit(solution)/shard_map/ppermute | solution.py:555
  12.0 11.8 %collective-permute-start.3 = (bf16[32,2048]{1,0:T(8,128)(2,1)S(1)}, bf16[32,2048]{1,0:T(8,128)(2,1)S(1)}, u32[]{:S(2)}, u32[]{:S(2)}) collective-permute-start(bf16[32,2048]{1,0:T(8,128)(2,1)S(1)} %get-tuple-element.21), channel_id=1, source_target_pairs={{4,0},{8,4},{12,8},{0,12},{5,1},{9,5},{13,9},{1,13},{6,2},{10,6},{... | collective-permute-start | bytes 393224 | tf_op jit(solution)/shard_map/ppermute | solution.py:555
  16.0 16.1 %copy-start = (s32[256]{0:T(256)S(1)}, s32[256]{0:T(256)}, u32[]{:S(2)}) copy-start(s32[256]{0:T(256)} %labels_ref.5) | copy-start | bytes 3076
  22.4 7.4 %collective-permute-start = (bf16[32,2048]{1,0:T(8,128)(2,1)S(1)}, bf16[32,2048]{1,0:T(8,128)(2,1)S(1)}, u32[]{:S(2)}, u32[]{:S(2)}) collective-permute-start(bf16[32,2048]{1,0:T(8,128)(2,1)S(1)} %get-tuple-element.20), channel_id=1, source_target_pairs={{1,0},{2,1},{3,2},{0,3},{5,4},{6,5},{7,6},{4,7},{9,8},{10,9},{11,1... | collective-permute-start | bytes 393224 | tf_op jit(solution)/shard_map/ppermute | solution.py:551
  24.0 18.0 %collective-permute-start.8 = (bf16[32,2048]{1,0:T(8,128)(2,1)S(1)}, bf16[32,2048]{1,0:T(8,128)(2,1)S(1)}, u32[]{:S(2)}, u32[]{:S(2)}) collective-permute-start(bf16[32,2048]{1,0:T(8,128)(2,1)S(1)} %get-tuple-element.44), channel_id=1, source_target_pairs={{3,0},{0,1},{1,2},{2,3},{7,4},{4,5},{5,6},{6,7},{11,8},{8,9},{9,10... | collective-permute-start | bytes 393224 | tf_op jit(solution)/shard_map/ppermute | solution.py:551
  24.7 18.3 %collective-permute-start.7 = (bf16[32,2048]{1,0:T(8,128)(2,1)S(1)}, bf16[32,2048]{1,0:T(8,128)(2,1)S(1)}, u32[]{:S(2)}, u32[]{:S(2)}) collective-permute-start(bf16[32,2048]{1,0:T(8,128)(2,1)S(1)} %get-tuple-element.45), channel_id=1, source_target_pairs={{2,0},{3,1},{0,2},{1,3},{6,4},{7,5},{4,6},{5,7},{10,8},{11,9},{8,1... | collective-permute-start | bytes 393224 | tf_op jit(solution)/shard_map/ppermute | solution.py:551
  29.8 16.6 %collective-permute-start.6 = (bf16[32,2048]{1,0:T(8,128)(2,1)S(1)}, bf16[32,2048]{1,0:T(8,128)(2,1)S(1)}, u32[]{:S(2)}, u32[]{:S(2)}) collective-permute-start(bf16[32,2048]{1,0:T(8,128)(2,1)S(1)} %get-tuple-element.46), channel_id=1, source_target_pairs={{1,0},{2,1},{3,2},{0,3},{5,4},{6,5},{7,6},{4,7},{9,8},{10,9},{11,1... | collective-permute-start | bytes 393224 | tf_op jit(solution)/shard_map/ppermute | solution.py:551
  32.1 14.3 %copy-start.2 = (bf16[64,64,128]{2,1,0:T(8,128)(2,1)S(1)}, bf16[64,64,128]{2,1,0:T(8,128)(2,1)}, u32[]{:S(2)}) copy-start(bf16[64,64,128]{2,1,0:T(8,128)(2,1)} %grad_ref.3) | copy-start | bytes 3145732
  38.9 24.9 %collective-permute-start.15 = (bf16[32,2048]{1,0:T(8,128)(2,1)S(1)}, bf16[32,2048]{1,0:T(8,128)(2,1)S(1)}, u32[]{:S(2)}, u32[]{:S(2)}) collective-permute-start(bf16[32,2048]{1,0:T(8,128)(2,1)S(1)} %get-tuple-element.36), channel_id=1, source_target_pairs={{0,0},{1,4},{2,8},{3,12},{4,1},{5,5},{6,9},{7,13},{8,2},{9,6},{10,... | collective-permute-start | bytes 393224 | tf_op jit(solution)/shard_map/ppermute | solution.py:588
  39.6 26.0 %collective-permute-start.18 = (bf16[32,2048]{1,0:T(8,128)(2,1)S(1)}, bf16[32,2048]{1,0:T(8,128)(2,1)S(1)}, u32[]{:S(2)}, u32[]{:S(2)}) collective-permute-start(bf16[32,2048]{1,0:T(8,128)(2,1)S(1)} %get-tuple-element.37), channel_id=1, source_target_pairs={{0,3},{1,7},{2,11},{3,15},{4,0},{5,4},{6,8},{7,12},{8,1},{9,5},{10... | collective-permute-start | bytes 393224 | tf_op jit(solution)/shard_map/ppermute | solution.py:588
  42.0 23.6 %collective-permute-start.17 = (bf16[32,2048]{1,0:T(8,128)(2,1)S(1)}, bf16[32,2048]{1,0:T(8,128)(2,1)S(1)}, u32[]{:S(2)}, u32[]{:S(2)}) collective-permute-start(bf16[32,2048]{1,0:T(8,128)(2,1)S(1)} %get-tuple-element.38), channel_id=1, source_target_pairs={{0,2},{1,6},{2,10},{3,14},{4,3},{5,7},{6,11},{7,15},{8,0},{9,4},{1... | collective-permute-start | bytes 393224 | tf_op jit(solution)/shard_map/ppermute | solution.py:588
  43.0 22.7 %collective-permute-start.16 = (bf16[32,2048]{1,0:T(8,128)(2,1)S(1)}, bf16[32,2048]{1,0:T(8,128)(2,1)S(1)}, u32[]{:S(2)}, u32[]{:S(2)}) collective-permute-start(bf16[32,2048]{1,0:T(8,128)(2,1)S(1)} %get-tuple-element.39), channel_id=1, source_target_pairs={{0,1},{1,5},{2,9},{3,13},{4,2},{5,6},{6,10},{7,14},{8,3},{9,7},{10... | collective-permute-start | bytes 393224 | tf_op jit(solution)/shard_map/ppermute | solution.py:588
  57.9 12.3 %collective-permute-start.9 = (bf16[256,128]{1,0:T(8,128)(2,1)S(1)}, bf16[256,128]{1,0:T(8,128)(2,1)S(1)}, u32[]{:S(2)}, u32[]{:S(2)}) collective-permute-start(bf16[256,128]{1,0:T(8,128)(2,1)S(1)} %get-tuple-element.47), channel_id=1, source_target_pairs={{12,0},{0,4},{4,8},{8,12},{13,1},{1,5},{5,9},{9,13},{14,2},{2,6},{... | collective-permute-start | bytes 196616 | tf_op jit(solution)/shard_map/ppermute | solution.py:555
  57.9 16.2 %copy-start.1 = (f32[128]{0:T(128)S(1)}, f32[128]{0:T(128)}, u32[]{:S(2)}) copy-start(f32[128]{0:T(128)} %param.16) | copy-start | bytes 1540
  63.8 6.4 %collective-permute-start.11 = (bf16[256,128]{1,0:T(8,128)(2,1)S(1)}, bf16[256,128]{1,0:T(8,128)(2,1)S(1)}, u32[]{:S(2)}, u32[]{:S(2)}) collective-permute-start(bf16[256,128]{1,0:T(8,128)(2,1)S(1)} %get-tuple-element.48), channel_id=1, source_target_pairs={{4,0},{8,4},{12,8},{0,12},{5,1},{9,5},{13,9},{1,13},{6,2},{10,6},{... | collective-permute-start | bytes 196616 | tf_op jit(solution)/shard_map/ppermute | solution.py:555
  65.6 4.6 %collective-permute-start.10 = (bf16[256,128]{1,0:T(8,128)(2,1)S(1)}, bf16[256,128]{1,0:T(8,128)(2,1)S(1)}, u32[]{:S(2)}, u32[]{:S(2)}) collective-permute-start(bf16[256,128]{1,0:T(8,128)(2,1)S(1)} %get-tuple-element.49), channel_id=1, source_target_pairs={{8,0},{12,4},{0,8},{4,12},{9,1},{13,5},{1,9},{5,13},{10,2},{14,6},... | collective-permute-start | bytes 196616 | tf_op jit(solution)/shard_map/ppermute | solution.py:555
  65.6 17.6 %collective-permute-start.12 = (bf16[32,2048]{1,0:T(8,128)(2,1)S(1)}, bf16[32,2048]{1,0:T(8,128)(2,1)S(1)}, u32[]{:S(2)}, u32[]{:S(2)}) collective-permute-start(bf16[32,2048]{1,0:T(8,128)(2,1)S(1)} %get-tuple-element.40), channel_id=1, source_target_pairs={{3,0},{0,1},{1,2},{2,3},{7,4},{4,5},{5,6},{6,7},{11,8},{8,9},{9,10... | collective-permute-start | bytes 393224 | tf_op jit(solution)/shard_map/ppermute | solution.py:551
  65.7 17.6 %collective-permute-start.14 = (bf16[32,2048]{1,0:T(8,128)(2,1)S(1)}, bf16[32,2048]{1,0:T(8,128)(2,1)S(1)}, u32[]{:S(2)}, u32[]{:S(2)}) collective-permute-start(bf16[32,2048]{1,0:T(8,128)(2,1)S(1)} %get-tuple-element.41), channel_id=1, source_target_pairs={{1,0},{2,1},{3,2},{0,3},{5,4},{6,5},{7,6},{4,7},{9,8},{10,9},{11,1... | collective-permute-start | bytes 393224 | tf_op jit(solution)/shard_map/ppermute | solution.py:551
  70.3 8.7 %collective-permute-start.21 = (bf16[256,128]{1,0:T(8,128)(2,1)S(1)}, bf16[256,128]{1,0:T(8,128)(2,1)S(1)}, u32[]{:S(2)}, u32[]{:S(2)}) collective-permute-start(bf16[256,128]{1,0:T(8,128)(2,1)S(1)} %convert_element_type.121), channel_id=1, source_target_pairs={{3,0},{0,1},{1,2},{2,3},{7,4},{4,5},{5,6},{6,7},{11,8},{8,9},{9,10... | collective-permute-start | bytes 196616 | tf_op jit(solution)/shard_map/ppermute | solution.py:551
  70.3 10.7 %collective-permute-start.20 = (bf16[256,128]{1,0:T(8,128)(2,1)S(1)}, bf16[256,128]{1,0:T(8,128)(2,1)S(1)}, u32[]{:S(2)}, u32[]{:S(2)}) collective-permute-start(bf16[256,128]{1,0:T(8,128)(2,1)S(1)} %convert_element_type.121), channel_id=1, source_target_pairs={{2,0},{3,1},{0,2},{1,3},{6,4},{7,5},{4,6},{5,7},{10,8},{11,9},{8,1... | collective-permute-start | bytes 196616 | tf_op jit(solution)/shard_map/ppermute | solution.py:551
  70.9 10.1 %collective-permute-start.19 = (bf16[256,128]{1,0:T(8,128)(2,1)S(1)}, bf16[256,128]{1,0:T(8,128)(2,1)S(1)}, u32[]{:S(2)}, u32[]{:S(2)}) collective-permute-start(bf16[256,128]{1,0:T(8,128)(2,1)S(1)} %convert_element_type.121), channel_id=1, source_target_pairs={{1,0},{2,1},{3,2},{0,3},{5,4},{6,5},{7,6},{4,7},{9,8},{10,9},{11,1... | collective-permute-start | bytes 196616 | tf_op jit(solution)/shard_map/ppermute | solution.py:551
  79.0 8.1 %collective-permute-start.13 = (bf16[32,2048]{1,0:T(8,128)(2,1)S(1)}, bf16[32,2048]{1,0:T(8,128)(2,1)S(1)}, u32[]{:S(2)}, u32[]{:S(2)}) collective-permute-start(bf16[32,2048]{1,0:T(8,128)(2,1)S(1)} %get-tuple-element.42), channel_id=1, source_target_pairs={{2,0},{3,1},{0,2},{1,3},{6,4},{7,5},{4,6},{5,7},{10,8},{11,9},{8,1... | collective-permute-start | bytes 393224 | tf_op jit(solution)/shard_map/ppermute | solution.py:551
  81.1 6.8 %collective-permute-start.24 = (bf16[256,128]{1,0:T(8,128)(2,1)S(1)}, bf16[256,128]{1,0:T(8,128)(2,1)S(1)}, u32[]{:S(2)}, u32[]{:S(2)}) collective-permute-start(bf16[256,128]{1,0:T(8,128)(2,1)S(1)} %add_convert_fusion.2), channel_id=1, source_target_pairs={{4,0},{8,4},{12,8},{0,12},{5,1},{9,5},{13,9},{1,13},{6,2},{10,6},{... | collective-permute-start | bytes 196616 | tf_op jit(solution)/shard_map/ppermute | solution.py:555
  81.1 6.7 %collective-permute-start.23 = (bf16[256,128]{1,0:T(8,128)(2,1)S(1)}, bf16[256,128]{1,0:T(8,128)(2,1)S(1)}, u32[]{:S(2)}, u32[]{:S(2)}) collective-permute-start(bf16[256,128]{1,0:T(8,128)(2,1)S(1)} %add_convert_fusion.2), channel_id=1, source_target_pairs={{8,0},{12,4},{0,8},{4,12},{9,1},{13,5},{1,9},{5,13},{10,2},{14,6},... | collective-permute-start | bytes 196616 | tf_op jit(solution)/shard_map/ppermute | solution.py:555
  83.2 4.7 %collective-permute-start.22 = (bf16[256,128]{1,0:T(8,128)(2,1)S(1)}, bf16[256,128]{1,0:T(8,128)(2,1)S(1)}, u32[]{:S(2)}, u32[]{:S(2)}) collective-permute-start(bf16[256,128]{1,0:T(8,128)(2,1)S(1)} %add_convert_fusion.2), channel_id=1, source_target_pairs={{12,0},{0,4},{4,8},{8,12},{13,1},{1,5},{5,9},{9,13},{14,2},{2,6},{... | collective-permute-start | bytes 196616 | tf_op jit(solution)/shard_map/ppermute | solution.py:555

commit v9 on v8

v9 whole, which is shorter than its diff:
```python
import jax
import jax.numpy as jnp
from jax import lax
from jax.experimental import pallas as pl
from jax.experimental.pallas import tpu as pltpu
from jax.sharding import PartitionSpec as P


PROJ = 32
CHAINS = 8
LANES = 128
PER_TILE = LANES // PROJ
WIDE = 256
F32 = jnp.float32
BF16 = jnp.bfloat16
VMEM = pl.BlockSpec(memory_space=pltpu.VMEM)
KERNEL = pltpu.CompilerParams(vmem_limit_bytes=24 << 20)
HBM = pl.BlockSpec(memory_space=pltpu.HBM)
SMEM = pl.BlockSpec(memory_space=pltpu.SMEM)


def swap_blocks(parts):
    lane = lax.broadcasted_iota(jnp.int32, parts[0].shape, 1)
    outs = []
    for q in range(PER_TILE):
        out = parts[(PER_TILE - 1 - q) % PER_TILE]
        for block in range(PER_TILE - 2, -1, -1):
            out = jnp.where(lane < (block + 1) * PROJ, parts[(block - q) % PER_TILE], out)
        outs.append(pltpu.roll(out, LANES - q * PROJ, 1) if q else out)
    return outs


def rolled(value, p):
    if not p:
        return value
    return jnp.concatenate(
        [pltpu.roll(value[:, t : t + LANES], p * PROJ, 1) for t in range(0, value.shape[1], LANES)],
        axis=1,
    )


def nt_dot(a, b):
    return lax.dot_general(a, b, (((1,), (1,)), ((), ())), preferred_element_type=F32)


def nn_dot(a, b):
    return lax.dot_general(a, b, (((1,), (0,)), ((), ())), preferred_element_type=F32)


def in_vmem(value):
    return pltpu.with_memory_space_constraint(value, pltpu.VMEM)


def in_hbm(value):
    return pltpu.with_memory_space_constraint(value, pltpu.HBM)


def project_body(x_hbm, gain_hbm, shift_hbm, first_hbm, second_hbm, left_ref, right_ref,
                 x_ref, gain_ref, shift_ref, w_ref, proj_ref, turn_ref, out_ref, sems, *, cols):
    chunks, chunk, rows, feats = x_ref.shape
    small = [
        pltpu.make_async_copy(gain_hbm, gain_ref, sems.at[chunks]),
        pltpu.make_async_copy(shift_hbm, shift_ref, sems.at[chunks + 1]),
        pltpu.make_async_copy(first_hbm, w_ref.at[pl.ds(0, PROJ)], sems.at[chunks + 2]),
        pltpu.make_async_copy(second_hbm, w_ref.at[pl.ds(PROJ, PROJ)], sems.at[chunks + 3]),
    ]
    big = [
        pltpu.make_async_copy(x_hbm.at[pl.ds(g * chunk, chunk)], x_ref.at[g], sems.at[g])
        for g in range(chunks)
    ]
    for copy in big[:1] + small + big[1:]:
        copy.start()
    w_ref[2 * PROJ :] = jnp.zeros((LANES - 2 * PROJ, feats), BF16)
    for copy in small:
        copy.wait()
    for g in range(chunks):
        big[g].wait()
        x = x_ref[g].astype(F32).reshape(chunk * rows, feats)
        center = x - jnp.mean(x, axis=-1, keepdims=True)
        spread = jnp.mean(center * center, axis=-1, keepdims=True)
        normed = center * lax.rsqrt(spread + 1e-05) * gain_ref[...] + shift_ref[...]
        at = slice(g * chunk * rows, (g + 1) * chunk * rows)
        proj_ref[at] = nt_dot(normed.astype(BF16), w_ref[...])
    project_layout(proj_ref, turn_ref, out_ref, left_ref, right_ref, rows, cols)


def project_layout(proj_ref, turn_ref, out_ref, left_ref, right_ref, rows, cols):
    here = left_ref.shape[0]
    lane = lax.broadcasted_iota(jnp.int32, (here, LANES), 1)
    for t in range(rows // PER_TILE):
        tile = proj_ref[pl.ds(t * PER_TILE, here, stride=rows)]
        for p in range(1, PER_TILE):
            part = proj_ref[pl.ds(t * PER_TILE + p, here, stride=rows)]
            tile = jnp.where(lane < p * PROJ, tile, pltpu.roll(part, p * PROJ, 1))
        left_ref[:, t * LANES : (t + 1) * LANES] = tile.astype(BF16)

    tiles = here * rows // LANES
    for t in range(tiles):
        flipped = proj_ref[t * LANES : (t + 1) * LANES].T
        turn_ref[t * PROJ : (t + 1) * PROJ] = flipped[PROJ : 2 * PROJ]
    seqs = LANES // rows
    per = LANES // cols
    lane = lax.broadcasted_iota(jnp.int32, (tiles, LANES), 1)
    for block in range(rows // cols):
        for t in range(PROJ // per):
            at = (block * (PROJ // per) + t) * LANES
            parts = [turn_ref[pl.ds(t * per + p, tiles, stride=PROJ)] for p in range(per)]
            for u in range(seqs):
                start = u * rows + block * cols
                tile = None
                for p, part in enumerate(parts):
                    amount = (p * cols - start) % LANES
                    part = pltpu.roll(part, amount, 1) if amount else part
                    tile = part if tile is None else jnp.where(lane < p * cols, tile, part)
                out_ref[pl.ds(u, tiles, stride=seqs), :] = tile
            right_ref[:, at : at + LANES] = out_ref[...].astype(BF16)


def project_call(x, gain, shift, first, second, cols):
    here, rows, feats = x.shape
    chunk = min(here, max(1, 2 * WIDE // rows))
    return pl.pallas_call(
        lambda *refs: project_body(*refs, cols=cols),
        in_specs=[HBM] * 5,
        out_specs=[VMEM] * 2,
        out_shape=[jax.ShapeDtypeStruct((here, rows * PROJ), BF16)] * 2,
        scratch_shapes=[
            pltpu.VMEM((here // chunk, chunk, rows, feats), BF16),
            pltpu.VMEM(gain.shape, F32),
            pltpu.VMEM(shift.shape, F32),
            pltpu.VMEM((LANES, feats), BF16),
            pltpu.VMEM((here * rows, LANES), F32),
            pltpu.VMEM((here * rows // LANES * PROJ, LANES), F32),
            pltpu.VMEM((here, LANES), F32),
            pltpu.SemaphoreType.DMA((here // chunk + 4,)),
        ],
        compiler_params=KERNEL,
        name="project",
    )(*map(in_hbm, (x, gain, shift, first, second)))


def masks(at_ref, labels_ref, counts_ref, lab_ref, tall_ref, wide_ref, plain_ref, rows, cols, seqs):
    res = labels_ref.shape[1]
    labels = jnp.broadcast_to(labels_ref[...], (8, res))
    own = pltpu.roll(labels, (res - at_ref[0]) % res, 1)[:, :rows]
    spread = (
        lax.broadcasted_iota(jnp.int32, (rows, rows * PROJ), 1) // PROJ
        == lax.broadcasted_iota(jnp.int32, (rows, rows * PROJ), 0)
    )
    lab = nn_dot(own.astype(F32).astype(BF16), spread.astype(F32).astype(BF16))
    lab_ref[...] = lab[:1].astype(jnp.int32)

    there = pltpu.roll(labels, (res - at_ref[1]) % res, 1)[:, :LANES]
    there = jnp.where(lax.broadcasted_iota(jnp.int32, (8, LANES), 1) < cols, there, 0)
    reach = cols
    while reach < LANES:
        there = there + pltpu.roll(there, reach, 1)
        reach *= 2
    depth = jnp.zeros((CHAINS, LANES), jnp.int32)
    for b in range(CHAINS):
        depth += jnp.where(there == b, counts_ref[:, b : b + 1], 0)
    seq = (lax.broadcasted_iota(jnp.int32, (seqs, LANES), 0) + at_ref[2]) % seqs
    for a in range(CHAINS):
        deep = jnp.broadcast_to(depth[a : a + 1], (seqs, LANES))
        weight = jnp.where(seq < deep, 1.0 / deep.astype(F32), 0.0)
        three = deep % 3 == 0
        side = slice((a % 2) * seqs, (a % 2 + 1) * seqs)
        for x, part in enumerate((jnp.where(three, 0.0, weight), jnp.where(three, 3.0 * weight, 0.0))):
            tall_ref[a // 2, x, side] = part.astype(BF16)
            wide_ref[a // 2, x, :, side] = part.T[:cols].astype(BF16)
        plain_ref[a // 2, :, side] = weight.T[:cols]


def projector(w_ref, wide_w_ref, w_out, wt_ref):
    wide_w_ref[...] = w_ref[...].astype(F32)
    for t in range(PROJ // PER_TILE):
        for q in range(PER_TILE):
            e = t * PER_TILE + q
            w_out[e * PROJ : (e + 1) * PROJ] = wide_w_ref[pl.ds(e, PROJ, stride=PROJ)].astype(BF16)
        block = w_out[t * LANES : (t + 1) * LANES].astype(F32)
        for p in range(PER_TILE):
            wt_ref[p, :, t * LANES : (t + 1) * LANES] = rolled(block.T, p).astype(BF16)


def cost(passes, span, total, seqs):
    return pl.CostEstimate(
        flops=4 * passes * span * total * seqs, bytes_accessed=2 * span * total, transcendentals=0
    )


def back_body(at_ref, labels_hbm, counts_hbm, w_hbm, grad_hbm,
              lab_ref, tall_ref, wide_ref, plain_ref, w_out, back_ref, grad_ref,
              labels_ref, counts_ref, w_ref, wide_w_ref, wt_ref, sems, *, seqs):
    groups, step, cols, _ = grad_ref.shape
    copies = [
        pltpu.make_async_copy(w_hbm, w_ref, sems.at[groups]),
        pltpu.make_async_copy(labels_hbm, labels_ref, sems.at[groups + 1]),
        pltpu.make_async_copy(counts_hbm, counts_ref, sems.at[groups + 2]),
    ]
    for copy in copies:
        copy.start()

    def grad_of(g):
        return pltpu.make_async_copy(grad_hbm.at[pl.ds(g * step, step)], grad_ref.at[g], sems.at[g])

    for g in range(groups):
        grad_of(g).start()
    for copy in copies:
        copy.wait()
    projector(w_ref, wide_w_ref, w_out, wt_ref)
    masks(at_ref, labels_ref, counts_ref, lab_ref, tall_ref, wide_ref, plain_ref,
          groups * step, cols, seqs)
    halves = step // PER_TILE

    def group(g, carry):
        grad_of(g).wait()
        blocks = [
            jnp.concatenate([grad_ref[g, half * PER_TILE + p] for half in range(halves)], axis=0)
            for p in range(PER_TILE)
        ]
        for u in range(PROJ * PROJ // WIDE):
            prods = [
                nn_dot(block, wt_ref[p, :, u * WIDE : (u + 1) * WIDE]).astype(BF16)
                for p, block in enumerate(blocks)
            ]
            for half in range(halves):
                for t in range(WIDE // LANES):
                    parts = [
                        prod[half * cols : (half + 1) * cols, t * LANES : (t + 1) * LANES]
                        for prod in prods
                    ]
                    for q, part in enumerate(swap_blocks(parts)):
                        e = u * (WIDE // PROJ) + t * PER_TILE + q
                        at = (g, slice(e * cols, (e + 1) * cols))
                        back_ref[at + (slice(half * LANES, (half + 1) * LANES),)] = part
        return carry

    lax.fori_loop(0, groups, group, 0)


def back_call(at, labels, counts, w, grad, seqs):
    rows, cols, width = grad.shape
    step = WIDE // PROJ
    groups = rows // step
    pairs = CHAINS // 2
    labels = labels[None, :]
    return pl.pallas_call(
        lambda *refs: back_body(*refs, seqs=seqs),
        in_specs=[SMEM] + [HBM] * 4,
        out_specs=[VMEM] * 7,
        out_shape=[
            jax.ShapeDtypeStruct((1, rows * PROJ), jnp.int32),
            jax.ShapeDtypeStruct((pairs, 2, 2 * seqs, LANES), BF16),
            jax.ShapeDtypeStruct((pairs, 2, cols, 2 * seqs), BF16),
            jax.ShapeDtypeStruct((pairs, cols, 2 * seqs), F32),
            jax.ShapeDtypeStruct(w.shape, BF16),
            pltpu.VMEM((groups, PROJ * cols, WIDE), BF16),
            pltpu.VMEM((groups, step, cols, width), BF16),
        ],
        scratch_shapes=[
            pltpu.VMEM(labels.shape, jnp.int32),
            pltpu.VMEM(counts.shape, jnp.int32),
            pltpu.VMEM(w.shape, BF16),
            pltpu.VMEM(w.shape, F32),
            pltpu.VMEM((PER_TILE, width, PROJ * PROJ), BF16),
            pltpu.SemaphoreType.DMA((groups + 3,)),
        ],
        compiler_params=KERNEL,
        cost_estimate=cost(10, PROJ * cols, rows * PROJ, width),
        name="back",
    )(at, *map(in_hbm, (labels, counts, w, grad)))


def first_pair(at_ref, labels_ref, group):
    return labels_ref[at_ref[0] + group * (WIDE // PROJ)] // 2


def last_pair(at_ref, labels_ref, group):
    return labels_ref[at_ref[0] + (group + 1) * (WIDE // PROJ) - 1] // 2


def each(first, last, fn):
    def step(k, carry):
        fn(k)
        return carry

    lax.fori_loop(first, last + 1, step, 0)


def lanes_of(group):
    return pl.ds(pl.multiple_of(group * WIDE, WIDE), WIDE)


def masked_left(left_ref, lab_ref, lb_ref, pair, group):
    seqs = left_ref.shape[0]
    lanes = lanes_of(group)
    for side in range(2):
        keep = (lab_ref[:, lanes] == 2 * pair + side).astype(F32).astype(BF16)
        lb_ref[side * seqs : (side + 1) * seqs] = left_ref[:, lanes] * keep


def right_grad_body(at_ref, labels_ref, back_ref, left_ref, lab_ref, wide_ref,
                    right_out, q_ref, lb_ref, flip_ref, turn_ref):
    seqs = left_ref.shape[0]
    groups, span, _ = back_ref.shape
    cols = span // PROJ
    first = lambda g: first_pair(at_ref, labels_ref, g)
    last = lambda g: last_pair(at_ref, labels_ref, g)

    def clear(pair):
        q_ref[pair] = jnp.zeros(q_ref.shape[1:], F32)

    each(first(0), last(groups - 1), clear)

    def group(g):
        def one_pair(pair):
            masked_left(left_ref, lab_ref, lb_ref, pair, g)
            q_ref[pair] += nt_dot(back_ref[g], lb_ref[...])

        each(first(g), last(g), one_pair)

    each(0, groups - 1, group)

    def combine(pair, start):
        for e in range(PROJ):
            rows = slice(e * cols, (e + 1) * cols)
            both = q_ref[pair, rows] * wide_ref[pair]
            total = both[:, :seqs] + both[:, seqs:]
            flip_ref[rows] = total if start else flip_ref[rows] + total

    combine(first(0), True)
    each(first(0) + 1, last(groups - 1), lambda pair: combine(pair, False))
    for j in range(cols):
        turn_ref[j * PROJ : (j + 1) * PROJ] = flip_ref[pl.ds(j, PROJ, stride=cols)]
    for t in range(span // LANES):
        rows = slice(t * LANES, (t + 1) * LANES)
        right_out[:, rows] = turn_ref[rows].T.astype(BF16)


def right_grad_call(at, labels, back, left, lab, wide):
    groups, span, _ = back.shape
    total = groups * WIDE
    seqs = left.shape[0]
    return pl.pallas_call(
        right_grad_body,
        in_specs=[SMEM] * 2 + [VMEM] * 4,
        out_specs=VMEM,
        out_shape=jax.ShapeDtypeStruct((seqs, span), BF16),
        scratch_shapes=[
            pltpu.VMEM((CHAINS // 2, span, 2 * seqs), F32),
            pltpu.VMEM((2 * seqs, WIDE), BF16),
            pltpu.VMEM((span, seqs), F32),
            pltpu.VMEM((span, seqs), F32),
        ],
        compiler_params=KERNEL,
        cost_estimate=cost(10, span, total, seqs),
        name="right_grad",
    )(at, labels, back, left, lab, wide)


def left_grad_body(at_ref, labels_ref, back_ref, lab_ref, right_ref, tall_ref,
                   left_out, rm_ref, part_ref):
    seqs = right_ref.shape[0]
    groups, span, _ = back_ref.shape
    first = lambda g: first_pair(at_ref, labels_ref, g)
    last = lambda g: last_pair(at_ref, labels_ref, g)
    part_ref[...] = (right_ref[...].astype(F32) / 3).astype(BF16)

    def build(pair):
        for side in range(2):
            rows = slice(side * seqs, (side + 1) * seqs)
            plain, third = tall_ref[pair, 0, rows], tall_ref[pair, 1, rows]
            for t in range(span // LANES):
                lanes = slice(t * LANES, (t + 1) * LANES)
                rm_ref[pair, rows, lanes] = (
                    right_ref[:, lanes] * plain + part_ref[:, lanes] * third
                )

    each(first(0), last(groups - 1), build)

    def group(g):
        lab = lab_ref[:, lanes_of(g)]

        def one_pair(pair, total):
            part = nn_dot(rm_ref[pair], back_ref[g])
            keep0, keep1 = lab == 2 * pair, lab == 2 * pair + 1
            return total + jnp.where(keep0, part[:seqs], 0.0) + jnp.where(keep1, part[seqs:], 0.0)

        total = lax.fori_loop(first(g), last(g) + 1, one_pair, jnp.zeros((seqs, WIDE), F32))
        left_out[:, lanes_of(g)] = total.astype(BF16)

    each(0, groups - 1, group)


def left_grad_call(at, labels, back, lab, right, tall):
    groups, span, _ = back.shape
    total = groups * WIDE
    seqs = right.shape[0]
    return pl.pallas_call(
        left_grad_body,
        in_specs=[SMEM] * 2 + [VMEM] * 4,
        out_specs=VMEM,
        out_shape=jax.ShapeDtypeStruct((seqs, total), BF16),
        scratch_shapes=[
            pltpu.VMEM((CHAINS // 2, 2 * seqs, span), BF16),
            pltpu.VMEM((seqs, span), BF16),
        ],
        compiler_params=KERNEL,
        cost_estimate=cost(10, span, total, seqs),
        name="left_grad",
    )(at, labels, back, lab, right, tall)


def outer_body(at_ref, labels_ref, left_ref, lab_ref, right_ref, wide_ref, grad_ref,
               outer_ref, weight_out, rm_ref, lb_ref, acc_ref, sum_ref, turn_ref, flip_ref, part_ref):
    seqs = left_ref.shape[0]
    span = right_ref.shape[1]
    cols = span // PROJ
    groups, step, _, width = grad_ref.shape
    first = lambda g: first_pair(at_ref, labels_ref, g)
    last = lambda g: last_pair(at_ref, labels_ref, g)
    for t in range(span // LANES):
        lanes = slice(t * LANES, (t + 1) * LANES)
        flipped = right_ref[:, lanes].astype(F32).T
        flip_ref[lanes] = flipped.astype(BF16)
        part_ref[lanes] = (flipped / 3).astype(BF16)

    def build(pair):
        plain, third = wide_ref[pair, 0], wide_ref[pair, 1]
        for e in range(PROJ):
            rows = slice(e * cols, (e + 1) * cols)
            to = e % PER_TILE * (PROJ // PER_TILE) + e // PER_TILE
            into = slice(to * cols, (to + 1) * cols)
            for side in range(2):
                lanes = slice(side * seqs, (side + 1) * seqs)
                rm_ref[pair, into, lanes] = (
                    flip_ref[rows] * plain[:, lanes] + part_ref[rows] * third[:, lanes]
                )

    each(first(0), last(groups - 1), build)
    sum_ref[...] = jnp.zeros_like(sum_ref)
    quarter = span // PER_TILE

    def product(pair, g, add):
        masked_left(left_ref, lab_ref, lb_ref, pair, g)
        for q in range(PER_TILE):
            rows = slice(q * quarter, (q + 1) * quarter)
            part = nn_dot(rm_ref[pair, rows], rolled(lb_ref[...], q))
            acc_ref[rows] = acc_ref[rows] + part if add else part

    def group(g):
        product(first(g), g, False)
        each(first(g) + 1, last(g), lambda pair: product(pair, g, True))
        for half in range(WIDE // LANES):
            lanes = slice(half * LANES, (half + 1) * LANES)
            for t in range(PROJ // PER_TILE):
                parts = []
                for q in range(PER_TILE):
                    e = q * (PROJ // PER_TILE) + t
                    parts.append(acc_ref[e * cols : (e + 1) * cols, lanes].astype(BF16))
                turned = swap_blocks(parts)
                for p in range(PER_TILE):
                    i = half * PER_TILE + p
                    at = (g, slice(i * cols, (i + 1) * cols), slice(t * LANES, (t + 1) * LANES))
                    outer_ref[at] = turned[p]
        flat = grad_ref[g].reshape(step * cols, width)
        sum_ref[...] += nn_dot(flat.T, outer_ref[g])

    each(0, groups - 1, group)
    for t in range(PROJ * PROJ // LANES):
        part = slice(t * LANES, (t + 1) * LANES)
        turn_ref[part] = sum_ref[:, part].T
    for c in range(PROJ):
        weight_out[c * PROJ : (c + 1) * PROJ] = turn_ref[pl.ds(c, PROJ, stride=PROJ)]


def outer_call(at, labels, left, lab, right, wide, grad):
    groups, step, cols, width = grad.shape
    seqs, total = left.shape
    span = right.shape[1]
    return pl.pallas_call(
        outer_body,
        in_specs=[SMEM] * 2 + [VMEM] * 5,
        out_specs=[VMEM] * 2,
        out_shape=[
            pltpu.VMEM((groups, step * cols, PROJ * PROJ), BF16),
            jax.ShapeDtypeStruct((PROJ * PROJ, width), F32),
        ],
        scratch_shapes=[
            pltpu.VMEM((CHAINS // 2, span, 2 * seqs), BF16),
            pltpu.VMEM((2 * seqs, WIDE), BF16),
            pltpu.VMEM((span, WIDE), F32),
            pltpu.VMEM((width, PROJ * PROJ), F32),
            pltpu.VMEM((PROJ * PROJ, width), F32),
            pltpu.VMEM((span, seqs), BF16),
            pltpu.VMEM((span, seqs), BF16),
        ],
        compiler_params=KERNEL,
        cost_estimate=cost(20, span, total, seqs),
        name="outer",
    )(at, labels, left, lab, right, wide, grad)


def pair_body(outer_ref, w_ref, offset_ref, pair_ref):
    _, pairs, _ = outer_ref.shape
    here = pair_ref.shape[0] // pairs
    for g in range(here):
        pair = nn_dot(outer_ref[pl.program_id(0) * here + g], w_ref[...]) + offset_ref[...]
        pair_ref[g * pairs : (g + 1) * pairs] = pair.astype(BF16)


def pair_call(outer, w, offset):
    groups, pairs, feats = outer.shape
    width = w.shape[1]
    steps = 2
    return pl.pallas_call(
        pair_body,
        grid=(steps,),
        in_specs=[VMEM] * 3,
        out_specs=pl.BlockSpec((groups * pairs // steps, width), lambda g: (g, 0)),
        out_shape=jax.ShapeDtypeStruct((groups * pairs, width), BF16),
        compiler_params=KERNEL,
        cost_estimate=pl.CostEstimate(
            flops=2 * groups * pairs * feats * width,
            bytes_accessed=2 * groups * pairs * width,
            transcendentals=0,
        ),
        name="pair",
    )(outer, w, offset)


class Ring:
    def __init__(self, n_row, n_col):
        self.n_row, self.n_col = n_row, n_col
        self.per_row = n_col // n_row
        self.row = lax.axis_index("row").astype(jnp.uint32)
        self.col = lax.axis_index("col").astype(jnp.uint32)

    def col_shift(self, value, k):
        n = self.n_col
        return lax.ppermute(value, "col", [((t + k) % n, t) for t in range(n)])

    def row_shift(self, value, k):
        n = self.n_row
        return lax.ppermute(value, "row", [((t + k) % n, t) for t in range(n)])

    def right_along_row(self, right):
        others = [self.row_shift(right, k) for k in range(1, self.n_row)]
        return [right] + others

    def right_pieces(self, by_row):
        n, m = self.n_row, self.per_row
        here, lanes = by_row[0].shape
        lanes //= m
        by_row = jnp.stack(by_row)
        pieces = []
        for k in range(self.n_col):
            q = (self.col + (self.n_col - k)) % self.n_col
            at = ((q // m + (n - self.row)) % n, jnp.uint32(0), (q % m) * lanes)
            pieces.append(lax.dynamic_slice(by_row, at, (1, here, lanes))[0])
        return pieces

    def right_along_col(self, pieces):
        return jnp.concatenate([self.col_shift(p, k) if k else p for k, p in enumerate(pieces)])

    def right_grad_home(self, grad):
        n, m = self.n_col, self.per_row
        here, lanes = grad.shape[0] // n, grad.shape[1]
        total = jnp.zeros((m, here, lanes), F32)
        slot = lax.broadcasted_iota(jnp.uint32, (m, 1, 1), 0)
        for k in range(n):
            t = (self.row * m + self.col % m + k) % n
            block = lax.dynamic_slice_in_dim(grad, ((t + n - self.col) % n) * here, here, 0)
            pairs = []
            for r in range(self.n_row):
                for q in range(n):
                    pairs.append((r * n + q, (q // m) * n + (r * m + q % m + k) % n))
            got = lax.ppermute(block, ("row", "col"), pairs).astype(F32)[None]
            total += got if m == 1 else jnp.where(slot == (self.col + (n - k)) % n % m, got, 0)
        return total.swapaxes(0, 1).reshape(here, m * lanes).astype(BF16)

    def weight_over_row(self, weight):
        n = self.n_row
        size = weight.shape[0] // n
        sent = weight.astype(BF16).reshape(n, size, -1)
        total = lax.dynamic_index_in_dim(weight.reshape(n, size, -1), self.row, 0, keepdims=False)
        for k in range(1, n):
            piece = lax.dynamic_index_in_dim(sent, (self.row + k) % n, 0, keepdims=False)
            total += self.row_shift(piece, n - k).astype(F32)
        return total

    def weight_over_col(self, total):
        mine = total.astype(BF16)
        for k in range(1, self.n_col):
            total += self.col_shift(mine, k).astype(F32)
        return total.astype(BF16)

    def weight_to_all(self, mine):
        n = self.n_row
        which = (lax.broadcasted_iota(jnp.uint32, (n, 1, 1), 0) + (n - self.row)) % n
        shares = mine[None]
        for k in range(1, n):
            shares = jnp.where(which == k, self.row_shift(mine, k)[None], shares)
        return shares.reshape(n * mine.shape[0], mine.shape[1])


def after(value, *others):
    return lax.optimization_barrier((value,) + others)[0]


def shards(n_row, n_col, alignment_tensor, gain, shift, first_projector, second_projector,
           final_projector, final_offset, labels, counts, grad):
    ring = Ring(n_row, n_col)
    here, rows, _ = alignment_tensor.shape
    cols, width = grad.shape[1:]
    seqs = here * n_col
    left, right = project_call(
        alignment_tensor, gain[None, :], shift[None, :], first_projector.T, second_projector.T, cols
    )
    by_row = ring.right_along_row(right)
    left = jnp.concatenate([left] + [ring.col_shift(left, k) for k in range(1, n_col)])

    at = jnp.stack([ring.row * rows, ring.col * cols, ring.col * here]).astype(jnp.int32)
    lab, tall, wide, plain, w, back, grad = back_call(
        at, labels, counts, after(final_projector, right), grad, seqs
    )
    mine = ring.right_along_col(ring.right_pieces(by_row))
    back, grad = in_vmem(back), in_vmem(grad)
    right_grad = right_grad_call(at, labels, back, left, lab, plain)

    right = after(mine, right_grad)
    grad_right = ring.right_grad_home(right_grad)
    outer, weight = outer_call(
        at, labels, left, lab, right, wide, grad
    )
    share = ring.weight_over_row(weight)
    left_grad = left_grad_call(at, labels, back, after(lab, weight), right, tall)
    share = after(share, left_grad)

    total = left_grad[:here].astype(F32)
    for k in range(1, n_col):
        total += ring.col_shift(left_grad[k * here : (k + 1) * here], n_col - k).astype(F32)
    adjoint_first = total.astype(BF16)
    pair_update = pair_call(in_vmem(outer), after(w, left_grad, share), final_offset[None, :])
    pair_update = pair_update.reshape(rows, cols, width)
    mine = after(ring.weight_over_col(share), pair_update)
    grad_w_out = ring.weight_to_all(mine).astype(F32) / (n_row * rows)
    return pair_update, adjoint_first, grad_right, grad_w_out


def solution(mesh):
    in_specs = (
        P(("parts", "col"), "row", None),
        P(),
        P(),
        P(),
        P(),
        P(),
        P(),
        P("parts"),
        P("parts", None),
        P(("parts", "row"), "col", None),
    )
    out_specs = (
        P(("parts", "row"), "col", None),
        P(("parts", "col"), "row"),
        P(("parts", "col"), "row"),
        P("parts", None),
    )

    def body(*args):
        return shards(mesh.shape["row"], mesh.shape["col"], *args)

    return jax.shard_map(body, mesh=mesh, in_specs=in_specs, out_specs=out_specs, check_vma=False)
```

time: 89.4 us -> 86 us (0.962)
  Pallas kernels: 41.4 us -> 37.2 us
    pallas_call x7 -> x6, Pallas kernels: 41.4 us -> 37.2 us  [the longest x1 11.2 us: outer_call(): pl.pallas_call(outer_body, in_specs=[SMEM] * 2 + [VMEM] * 5, out_specs=[V...]
  transfers between devices with their start and end apart: 25 -> 25, of which waited for: 2 -> 3; matrix products, arithmetic and copies ran while one was open for 2% -> 3% of each run, Pallas kernels for 42% -> 39%
where the time goes in v9:
time: 86 us; the launch traced here: 84.9 us
  Pallas kernels  37.2 us (43%)
  starting transfers between devices  34 us (40%)
  waiting for transfers between devices  9.23 us (11%)
  other arithmetic  3.03 us (4%)
  between operations  0.93 us (1%)
    ppermute x12, starting transfers between devices, col_shift(): return lax.ppermute(value, 'col', [((t + k) % n, t) for t in range(n)])  19.6 us
    pallas_call x1, Pallas kernels, outer_call(): pl.pallas_call(outer_body, in_specs=[SMEM] * 2 + [VMEM] * 5, out_specs=[V...  11.2 us
    ppermute x12, waiting for transfers between devices, col_shift(): return lax.ppermute(value, 'col', [((t + k) % n, t) for t in range(n)])  9.2 us
    ppermute x4, starting transfers between devices, right_grad_home(): got = lax.ppermute(block, ('row', 'col'), pairs).astype(F32)[None]  7.42 us
    ppermute x9, starting transfers between devices, row_shift(): return lax.ppermute(value, 'row', [((t + k) % n, t) for t in range(n)])  7.03 us
    pallas_call x1, Pallas kernels, back_call(): pl.pallas_call(lambda *refs: back_body(*refs, seqs=seqs), in_specs=[SMEM]...  6.93 us
    pallas_call x1, Pallas kernels, right_grad_call(): pl.pallas_call(right_grad_body, in_specs=[SMEM] * 2 + [VMEM] * 4, out_spe...  6.32 us
    pallas_call x1, Pallas kernels, left_grad_call(): pl.pallas_call(left_grad_body, in_specs=[SMEM] * 2 + [VMEM] * 4, out_spec...  5.67 us
  transfers between devices with their start and end apart: 25, of which 3 were waited for; matrix products, arithmetic and copies ran while one was open for 3% of the time, Pallas kernels for 39%

profile of v9, /device:TPU:0, one launch (start us, length us, event | category | flops | bytes accessed | tf_op | source)
XLA Modules:
  0.0 84.9 jit_solution(8248188997417908122)
XLA Ops:
  0.6 3.7 %project.1 = (bf16[32,2048]{1,0:T(8,128)(2,1)S(1)}, bf16[32,2048]{1,0:T(8,128)(2,1)S(1)}) custom-call(bf16[32,64,256]{2,1,0:T(8,128)(2,1)} %refs_0_.1, f32[1,256]{1,0:T(1,128)} %bitcast.61, f32[1,256]{1,0:T(1,128)} %bitcast.62, bf16[32,256]{1,0:T(8,128)(2,1)} %bitcast.59, bf16[32,256]{1,0:T(8,128)(2,1)} %bitcast.60), custom_call_target="tpu_custom_call" | custom-call | tf_op jit(solution)/shard_map/project/pallas_call | solution.py:122
  4.4 3.1 %collective-permute-start.2 = (bf16[32,2048]{1,0:T(8,128)(2,1)S(1)}, bf16[32,2048]{1,0:T(8,128)(2,1)S(1)}, u32[]{:S(2)}, u32[]{:S(2)}) collective-permute-start(bf16[32,2048]{1,0:T(8,128)(2,1)S(1)} %get-tuple-element.21), channel_id=1, source_target_pairs={{3,0},{0,1},{1,2},{2,3},{7,4},{4,5},{5,6},{6,7},{11,8},{8,9},{9,10... | collective-permute-start | bytes 393224 | tf_op jit(solution)/shard_map/ppermute | solution.py:541
  7.5 2.6 %collective-permute-start.1 = (bf16[32,2048]{1,0:T(8,128)(2,1)S(1)}, bf16[32,2048]{1,0:T(8,128)(2,1)S(1)}, u32[]{:S(2)}, u32[]{:S(2)}) collective-permute-start(bf16[32,2048]{1,0:T(8,128)(2,1)S(1)} %get-tuple-element.21), channel_id=1, source_target_pairs={{2,0},{3,1},{0,2},{1,3},{6,4},{7,5},{4,6},{5,7},{10,8},{11,9},{8,1... | collective-permute-start | bytes 393224 | tf_op jit(solution)/shard_map/ppermute | solution.py:541
  10.1 1.5 %collective-permute-start.4 = (bf16[32,2048]{1,0:T(8,128)(2,1)S(1)}, bf16[32,2048]{1,0:T(8,128)(2,1)S(1)}, u32[]{:S(2)}, u32[]{:S(2)}) collective-permute-start(bf16[32,2048]{1,0:T(8,128)(2,1)S(1)} %get-tuple-element.22), channel_id=1, source_target_pairs={{8,0},{12,4},{0,8},{4,12},{9,1},{13,5},{1,9},{5,13},{10,2},{14,6},... | collective-permute-start | bytes 393224 | tf_op jit(solution)/shard_map/ppermute | solution.py:545
  11.6 1.5 %collective-permute-start.3 = (bf16[32,2048]{1,0:T(8,128)(2,1)S(1)}, bf16[32,2048]{1,0:T(8,128)(2,1)S(1)}, u32[]{:S(2)}, u32[]{:S(2)}) collective-permute-start(bf16[32,2048]{1,0:T(8,128)(2,1)S(1)} %get-tuple-element.22), channel_id=1, source_target_pairs={{4,0},{8,4},{12,8},{0,12},{5,1},{9,5},{13,9},{1,13},{6,2},{10,6},{... | collective-permute-start | bytes 393224 | tf_op jit(solution)/shard_map/ppermute | solution.py:545
  13.4 6.9 %back.1 = (s32[1,2048]{1,0:T(1,128)S(1)}, bf16[4,2,256,128]{3,2,1,0:T(8,128)(2,1)S(1)}, bf16[4,2,64,256]{3,2,1,0:T(8,128)(2,1)S(1)}, f32[4,64,256]{2,1,0:T(8,128...) custom-call(s32[3]{0:T(128)S(1)} %add_convert_fusion.3.refs_0_.at_ref, ...), custom_call_target="tpu_custom_call" | custom-call | flops 21474836480 | bytes 8388608 | tf_op jit(solution)/shard_map/back/pallas_call | solution.py:247
  20.4 1.4 %collective-permute-start = (bf16[32,2048]{1,0:T(8,128)(2,1)S(1)}, bf16[32,2048]{1,0:T(8,128)(2,1)S(1)}, u32[]{:S(2)}, u32[]{:S(2)}) collective-permute-start(bf16[32,2048]{1,0:T(8,128)(2,1)S(1)} %get-tuple-element.21), channel_id=1, source_target_pairs={{1,0},{2,1},{3,2},{0,3},{5,4},{6,5},{7,6},{4,7},{9,8},{10,9},{11,1... | collective-permute-start | bytes 393224 | tf_op jit(solution)/shard_map/ppermute | solution.py:541
  21.9 0.7 collective-permute-start.8
  22.7 0.3 collective-permute-start.7
  23.0 4.7 %collective-permute-done = bf16[32,2048]{1,0:T(8,128)(2,1)S(1)} collective-permute-done((bf16[32,2048]{1,0:T(8,128)(2,1)S(1)}, bf16[32,2048]{1,0:T(8,128)(2,1)S(1)}, u32[]{:S(2)}, u32[]{:S(2)}) %collective-permute-start) | collective-permute-done | bytes 131104 | tf_op jit(solution)/shard_map/ppermute | solution.py:541
  27.7 2.3 %collective-permute-start.6 = (bf16[32,2048]{1,0:T(8,128)(2,1)S(1)}, bf16[32,2048]{1,0:T(8,128)(2,1)S(1)}, u32[]{:S(2)}, u32[]{:S(2)}) collective-permute-start(bf16[32,2048]{1,0:T(8,128)(2,1)S(1)} %get-tuple-element.48), channel_id=1, source_target_pairs={{1,0},{2,1},{3,2},{0,3},{5,4},{6,5},{7,6},{4,7},{9,8},{10,9},{11,1... | collective-permute-start | bytes 393224 | tf_op jit(solution)/shard_map/ppermute | solution.py:541
  30.1 6.3 %right_grad.1 = bf16[128,2048]{1,0:T(8,128)(2,1)S(1)} custom-call(s32[3]{0:T(128)S(1)} %add_convert_fusion.3.refs_0_.at_ref, s32[256]{0:T(256)S(1)} %copy-done.1, bf16[8,2048,256]{2,1,0:T(8,128)(2,1)S(1)} %get-tuple-element.25.back_ref, bf16[128,2048]{1,0:T(8,128)(2,1)S(1)} %constant_dynamic-update-slice_fusion.left_ref, ...), custom_call_target="tpu_custom_call" | custom-call | flops 21474836480 | bytes 8388608 | tf_op jit(solution)/shard_map/right_grad/pallas_call | solution.py:344
  36.4 0.7 collective-permute-start.15
  37.1 2.4 %collective-permute-start.18 = (bf16[32,2048]{1,0:T(8,128)(2,1)S(1)}, bf16[32,2048]{1,0:T(8,128)(2,1)S(1)}, u32[]{:S(2)}, u32[]{:S(2)}) collective-permute-start(bf16[32,2048]{1,0:T(8,128)(2,1)S(1)} %get-tuple-element.39), channel_id=1, source_target_pairs={{0,3},{1,7},{2,11},{3,15},{4,0},{5,4},{6,8},{7,12},{8,1},{9,5},{10... | collective-permute-start | bytes 393224 | tf_op jit(solution)/shard_map/ppermute | solution.py:578
  39.5 1.1 %collective-permute-start.17 = (bf16[32,2048]{1,0:T(8,128)(2,1)S(1)}, bf16[32,2048]{1,0:T(8,128)(2,1)S(1)}, u32[]{:S(2)}, u32[]{:S(2)}) collective-permute-start(bf16[32,2048]{1,0:T(8,128)(2,1)S(1)} %get-tuple-element.40), channel_id=1, source_target_pairs={{0,2},{1,6},{2,10},{3,14},{4,3},{5,7},{6,11},{7,15},{8,0},{9,4},{1... | collective-permute-start | bytes 393224 | tf_op jit(solution)/shard_map/ppermute | solution.py:578
  40.6 3.3 %collective-permute-start.16 = (bf16[32,2048]{1,0:T(8,128)(2,1)S(1)}, bf16[32,2048]{1,0:T(8,128)(2,1)S(1)}, u32[]{:S(2)}, u32[]{:S(2)}) collective-permute-start(bf16[32,2048]{1,0:T(8,128)(2,1)S(1)} %get-tuple-element.41), channel_id=1, source_target_pairs={{0,1},{1,5},{2,9},{3,13},{4,2},{5,6},{6,10},{7,14},{8,3},{9,7},{10... | collective-permute-start | bytes 393224 | tf_op jit(solution)/shard_map/ppermute | solution.py:578
  43.9 11.2 %outer.1 = (bf16[8,512,1024]{2,1,0:T(8,128)(2,1)S(1)}, f32[1024,128]{1,0:T(8,128)S(1)}) custom-call(s32[3]{0:T(128)S(1)} %add_convert_fusion.3.refs_0_.at_ref, s32[256]{0:T(256)S(1)} %copy-done.1, bf16[128,2048]{1,0:T(8,128)(2,1)S(1)} %constant_dynamic-update-slice_fusion.left_ref, s32[1,2048]{1,0:T(1,128)S(1)} %get-tuple-element.33.lab_ref, ...), custom_call_target="tpu_custom_call" | custom-call | flops 42949672960 | bytes 8388608 | tf_op jit(solution)/shard_map/outer/pallas_call | solution.py:481
  55.3 5.7 %left_grad.1 = bf16[128,2048]{1,0:T(8,128)(2,1)S(1)} custom-call(s32[3]{0:T(128)S(1)} %add_convert_fusion.3.refs_0_.at_ref, s32[256]{0:T(256)S(1)} %copy-done.1, bf16[8,2048,256]{2,1,0:T(8,128)(2,1)S(1)} %get-tuple-element.25.back_ref, s32[1,2048]{1,0:T(1,128)S(1)} %get-tuple-element.33.lab_ref, bf16[128,2048]{1,0:T(8,128)(2,1)S(1)} %pad_maximum_fusion.1.right_ref, ...), custom_call_target="tpu_custom_call" | custom-call | flops 21474836480 | bytes 8388608 | tf_op jit(solution)/shard_map/left_grad/pallas_call | solution.py:399
  61.0 1.8 %collective-permute-start.11 = (bf16[256,128]{1,0:T(8,128)(2,1)S(1)}, bf16[256,128]{1,0:T(8,128)(2,1)S(1)}, u32[]{:S(2)}, u32[]{:S(2)}) collective-permute-start(bf16[256,128]{1,0:T(8,128)(2,1)S(1)} %get-tuple-element.50), channel_id=1, source_target_pairs={{4,0},{8,4},{12,8},{0,12},{5,1},{9,5},{13,9},{1,13},{6,2},{10,6},{... | collective-permute-start | bytes 196616 | tf_op jit(solution)/shard_map/ppermute | solution.py:545
  62.8 0.1 collective-permute-start.12
  62.9 3.8 %collective-permute-start.14 = (bf16[32,2048]{1,0:T(8,128)(2,1)S(1)}, bf16[32,2048]{1,0:T(8,128)(2,1)S(1)}, u32[]{:S(2)}, u32[]{:S(2)}) collective-permute-start(bf16[32,2048]{1,0:T(8,128)(2,1)S(1)} %get-tuple-element.43), channel_id=1, source_target_pairs={{1,0},{2,1},{3,2},{0,3},{5,4},{6,5},{7,6},{4,7},{9,8},{10,9},{11,1... | collective-permute-start | bytes 393224 | tf_op jit(solution)/shard_map/ppermute | solution.py:541
  66.7 0.7 add_convert_fusion
  67.6 0.6 collective-permute-start.20
  68.1 3.3 %collective-permute-start.19 = (bf16[256,128]{1,0:T(8,128)(2,1)S(1)}, bf16[256,128]{1,0:T(8,128)(2,1)S(1)}, u32[]{:S(2)}, u32[]{:S(2)}) collective-permute-start(bf16[256,128]{1,0:T(8,128)(2,1)S(1)} %convert_element_type.121), channel_id=1, source_target_pairs={{1,0},{2,1},{3,2},{0,3},{5,4},{6,5},{7,6},{4,7},{9,8},{10,9},{11,1... | collective-permute-start | bytes 196616 | tf_op jit(solution)/shard_map/ppermute | solution.py:541
  71.4 3.3 %pair.1 = bf16[4096,128]{1,0:T(8,128)(2,1)} custom-call(bf16[8,512,1024]{2,1,0:T(8,128)(2,1)S(1)} %get-tuple-element.30.outer_ref, bf16[1024,128]{1,0:T(8,128)(2,1)S(1)} %get-tuple-element.36.w_ref, f32[1,128]{1,0:T(1,128)S(1)} %bitcast.52), custom_call_target="tpu_custom_call" | custom-call | flops 1073741824 | bytes 1048576 | tf_op jit(solution)/shard_map/pair/pallas_call | solution.py:516
  74.7 0.6 collective-permute-done.21
  75.3 1.4 %collective-permute-start.13 = (bf16[32,2048]{1,0:T(8,128)(2,1)S(1)}, bf16[32,2048]{1,0:T(8,128)(2,1)S(1)}, u32[]{:S(2)}, u32[]{:S(2)}) collective-permute-start(bf16[32,2048]{1,0:T(8,128)(2,1)S(1)} %get-tuple-element.44), channel_id=1, source_target_pairs={{2,0},{3,1},{0,2},{1,3},{6,4},{7,5},{4,6},{5,7},{10,8},{11,9},{8,1... | collective-permute-start | bytes 393224 | tf_op jit(solution)/shard_map/ppermute | solution.py:541
  76.8 2.0 %collective-permute-start.23 = (bf16[256,128]{1,0:T(8,128)(2,1)S(1)}, bf16[256,128]{1,0:T(8,128)(2,1)S(1)}, u32[]{:S(2)}, u32[]{:S(2)}) collective-permute-start(bf16[256,128]{1,0:T(8,128)(2,1)S(1)} %add_convert_fusion.2), channel_id=1, source_target_pairs={{8,0},{12,4},{0,8},{4,12},{9,1},{13,5},{1,9},{5,13},{10,2},{14,6},... | collective-permute-start | bytes 196616 | tf_op jit(solution)/shard_map/ppermute | solution.py:545
  78.9 0.2 collective-permute-start.22
  79.0 3.8 %collective-permute-done.13 = bf16[32,2048]{1,0:T(8,128)(2,1)S(1)} collective-permute-done((bf16[32,2048]{1,0:T(8,128)(2,1)S(1)}, bf16[32,2048]{1,0:T(8,128)(2,1)S(1)}, u32[]{:S(2)}, u32[]{:S(2)}) %collective-permute-start.13) | collective-permute-done | bytes 131104 | tf_op jit(solution)/shard_map/ppermute | solution.py:541
  82.9 0.7 add_convert_fusion.1
  83.6 1.3 %convert_multiply_fusion = f32[1024,128]{1,0:T(8,128)} fusion(pred[1024]{0:T(1024)(128)(4,1)S(1)} %broadcast_in_dim.105, pred[1024]{0:T(1024)(128)(4,1)S(1)} %broadcast_in_dim.100, pred[1024]{0:T(1024)(128)(4,1)S(1)} %broadcast_in_dim.95, bf16[256,128]{1,0:T(8,128)(2,1)S(1)} %add_convert_fusion.2, bf16[256,128]{1,0:T(8,128)(2,1)S(1)} %collective-permute-done.24, ...), kind=kLoop, calls=%fused_computation.2 | loop fusion | flops 655360 | bytes 789504 | tf_op jit(solution)/shard_map/div | solution.py:647
  (54 shorter events, 1.0 us)
Async XLA Ops:
  4.4 25.6 %collective-permute-start.2 = (bf16[32,2048]{1,0:T(8,128)(2,1)S(1)}, bf16[32,2048]{1,0:T(8,128)(2,1)S(1)}, u32[]{:S(2)}, u32[]{:S(2)}) collective-permute-start(bf16[32,2048]{1,0:T(8,128)(2,1)S(1)} %get-tuple-element.21), channel_id=1, source_target_pairs={{3,0},{0,1},{1,2},{2,3},{7,4},{4,5},{5,6},{6,7},{11,8},{8,9},{9,10... | collective-permute-start | bytes 393224 | tf_op jit(solution)/shard_map/ppermute | solution.py:541
  7.5 22.5 %collective-permute-start.1 = (bf16[32,2048]{1,0:T(8,128)(2,1)S(1)}, bf16[32,2048]{1,0:T(8,128)(2,1)S(1)}, u32[]{:S(2)}, u32[]{:S(2)}) collective-permute-start(bf16[32,2048]{1,0:T(8,128)(2,1)S(1)} %get-tuple-element.21), channel_id=1, source_target_pairs={{2,0},{3,1},{0,2},{1,3},{6,4},{7,5},{4,6},{5,7},{10,8},{11,9},{8,1... | collective-permute-start | bytes 393224 | tf_op jit(solution)/shard_map/ppermute | solution.py:541
  10.1 10.3 %collective-permute-start.5 = (bf16[32,2048]{1,0:T(8,128)(2,1)S(1)}, bf16[32,2048]{1,0:T(8,128)(2,1)S(1)}, u32[]{:S(2)}, u32[]{:S(2)}) collective-permute-start(bf16[32,2048]{1,0:T(8,128)(2,1)S(1)} %get-tuple-element.22), channel_id=1, source_target_pairs={{12,0},{0,4},{4,8},{8,12},{13,1},{1,5},{5,9},{9,13},{14,2},{2,6},{... | collective-permute-start | bytes 393224 | tf_op jit(solution)/shard_map/ppermute | solution.py:545
  10.1 11.7 %collective-permute-start.4 = (bf16[32,2048]{1,0:T(8,128)(2,1)S(1)}, bf16[32,2048]{1,0:T(8,128)(2,1)S(1)}, u32[]{:S(2)}, u32[]{:S(2)}) collective-permute-start(bf16[32,2048]{1,0:T(8,128)(2,1)S(1)} %get-tuple-element.22), channel_id=1, source_target_pairs={{8,0},{12,4},{0,8},{4,12},{9,1},{13,5},{1,9},{5,13},{10,2},{14,6},... | collective-permute-start | bytes 393224 | tf_op jit(solution)/shard_map/ppermute | solution.py:545
  11.6 10.2 %collective-permute-start.3 = (bf16[32,2048]{1,0:T(8,128)(2,1)S(1)}, bf16[32,2048]{1,0:T(8,128)(2,1)S(1)}, u32[]{:S(2)}, u32[]{:S(2)}) collective-permute-start(bf16[32,2048]{1,0:T(8,128)(2,1)S(1)} %get-tuple-element.22), channel_id=1, source_target_pairs={{4,0},{8,4},{12,8},{0,12},{5,1},{9,5},{13,9},{1,13},{6,2},{10,6},{... | collective-permute-start | bytes 393224 | tf_op jit(solution)/shard_map/ppermute | solution.py:545
  13.4 16.6 %copy-start.1 = (s32[256]{0:T(256)S(1)}, s32[256]{0:T(256)}, u32[]{:S(2)}) copy-start(s32[256]{0:T(256)} %labels_ref.5) | copy-start | bytes 3076
  20.4 7.3 %collective-permute-start = (bf16[32,2048]{1,0:T(8,128)(2,1)S(1)}, bf16[32,2048]{1,0:T(8,128)(2,1)S(1)}, u32[]{:S(2)}, u32[]{:S(2)}) collective-permute-start(bf16[32,2048]{1,0:T(8,128)(2,1)S(1)} %get-tuple-element.21), channel_id=1, source_target_pairs={{1,0},{2,1},{3,2},{0,3},{5,4},{6,5},{7,6},{4,7},{9,8},{10,9},{11,1... | collective-permute-start | bytes 393224 | tf_op jit(solution)/shard_map/ppermute | solution.py:541
  21.9 17.6 %collective-permute-start.8 = (bf16[32,2048]{1,0:T(8,128)(2,1)S(1)}, bf16[32,2048]{1,0:T(8,128)(2,1)S(1)}, u32[]{:S(2)}, u32[]{:S(2)}) collective-permute-start(bf16[32,2048]{1,0:T(8,128)(2,1)S(1)} %get-tuple-element.46), channel_id=1, source_target_pairs={{3,0},{0,1},{1,2},{2,3},{7,4},{4,5},{5,6},{6,7},{11,8},{8,9},{9,10... | collective-permute-start | bytes 393224 | tf_op jit(solution)/shard_map/ppermute | solution.py:541
  22.7 17.9 %collective-permute-start.7 = (bf16[32,2048]{1,0:T(8,128)(2,1)S(1)}, bf16[32,2048]{1,0:T(8,128)(2,1)S(1)}, u32[]{:S(2)}, u32[]{:S(2)}) collective-permute-start(bf16[32,2048]{1,0:T(8,128)(2,1)S(1)} %get-tuple-element.47), channel_id=1, source_target_pairs={{2,0},{3,1},{0,2},{1,3},{6,4},{7,5},{4,6},{5,7},{10,8},{11,9},{8,1... | collective-permute-start | bytes 393224 | tf_op jit(solution)/shard_map/ppermute | solution.py:541
  27.7 16.2 %collective-permute-start.6 = (bf16[32,2048]{1,0:T(8,128)(2,1)S(1)}, bf16[32,2048]{1,0:T(8,128)(2,1)S(1)}, u32[]{:S(2)}, u32[]{:S(2)}) collective-permute-start(bf16[32,2048]{1,0:T(8,128)(2,1)S(1)} %get-tuple-element.48), channel_id=1, source_target_pairs={{1,0},{2,1},{3,2},{0,3},{5,4},{6,5},{7,6},{4,7},{9,8},{10,9},{11,1... | collective-permute-start | bytes 393224 | tf_op jit(solution)/shard_map/ppermute | solution.py:541
  36.4 24.6 %collective-permute-start.15 = (bf16[32,2048]{1,0:T(8,128)(2,1)S(1)}, bf16[32,2048]{1,0:T(8,128)(2,1)S(1)}, u32[]{:S(2)}, u32[]{:S(2)}) collective-permute-start(bf16[32,2048]{1,0:T(8,128)(2,1)S(1)} %get-tuple-element.38), channel_id=1, source_target_pairs={{0,0},{1,4},{2,8},{3,12},{4,1},{5,5},{6,9},{7,13},{8,2},{9,6},{10,... | collective-permute-start | bytes 393224 | tf_op jit(solution)/shard_map/ppermute | solution.py:578
  37.1 25.7 %collective-permute-start.18 = (bf16[32,2048]{1,0:T(8,128)(2,1)S(1)}, bf16[32,2048]{1,0:T(8,128)(2,1)S(1)}, u32[]{:S(2)}, u32[]{:S(2)}) collective-permute-start(bf16[32,2048]{1,0:T(8,128)(2,1)S(1)} %get-tuple-element.39), channel_id=1, source_target_pairs={{0,3},{1,7},{2,11},{3,15},{4,0},{5,4},{6,8},{7,12},{8,1},{9,5},{10... | collective-permute-start | bytes 393224 | tf_op jit(solution)/shard_map/ppermute | solution.py:578
  39.5 23.3 %collective-permute-start.17 = (bf16[32,2048]{1,0:T(8,128)(2,1)S(1)}, bf16[32,2048]{1,0:T(8,128)(2,1)S(1)}, u32[]{:S(2)}, u32[]{:S(2)}) collective-permute-start(bf16[32,2048]{1,0:T(8,128)(2,1)S(1)} %get-tuple-element.40), channel_id=1, source_target_pairs={{0,2},{1,6},{2,10},{3,14},{4,3},{5,7},{6,11},{7,15},{8,0},{9,4},{1... | collective-permute-start | bytes 393224 | tf_op jit(solution)/shard_map/ppermute | solution.py:578
  40.6 22.3 %collective-permute-start.16 = (bf16[32,2048]{1,0:T(8,128)(2,1)S(1)}, bf16[32,2048]{1,0:T(8,128)(2,1)S(1)}, u32[]{:S(2)}, u32[]{:S(2)}) collective-permute-start(bf16[32,2048]{1,0:T(8,128)(2,1)S(1)} %get-tuple-element.41), channel_id=1, source_target_pairs={{0,1},{1,5},{2,9},{3,13},{4,2},{5,6},{6,10},{7,14},{8,3},{9,7},{10... | collective-permute-start | bytes 393224 | tf_op jit(solution)/shard_map/ppermute | solution.py:578
  55.2 12.2 %collective-permute-start.9 = (bf16[256,128]{1,0:T(8,128)(2,1)S(1)}, bf16[256,128]{1,0:T(8,128)(2,1)S(1)}, u32[]{:S(2)}, u32[]{:S(2)}) collective-permute-start(bf16[256,128]{1,0:T(8,128)(2,1)S(1)} %get-tuple-element.49), channel_id=1, source_target_pairs={{12,0},{0,4},{4,8},{8,12},{13,1},{1,5},{5,9},{9,13},{14,2},{2,6},{... | collective-permute-start | bytes 196616 | tf_op jit(solution)/shard_map/ppermute | solution.py:545
  55.3 16.1 %copy-start = (f32[128]{0:T(128)S(1)}, f32[128]{0:T(128)}, u32[]{:S(2)}) copy-start(f32[128]{0:T(128)} %param.16) | copy-start | bytes 1540
  61.0 6.4 %collective-permute-start.11 = (bf16[256,128]{1,0:T(8,128)(2,1)S(1)}, bf16[256,128]{1,0:T(8,128)(2,1)S(1)}, u32[]{:S(2)}, u32[]{:S(2)}) collective-permute-start(bf16[256,128]{1,0:T(8,128)(2,1)S(1)} %get-tuple-element.50), channel_id=1, source_target_pairs={{4,0},{8,4},{12,8},{0,12},{5,1},{9,5},{13,9},{1,13},{6,2},{10,6},{... | collective-permute-start | bytes 196616 | tf_op jit(solution)/shard_map/ppermute | solution.py:545
  62.8 4.6 %collective-permute-start.10 = (bf16[256,128]{1,0:T(8,128)(2,1)S(1)}, bf16[256,128]{1,0:T(8,128)(2,1)S(1)}, u32[]{:S(2)}, u32[]{:S(2)}) collective-permute-start(bf16[256,128]{1,0:T(8,128)(2,1)S(1)} %get-tuple-element.51), channel_id=1, source_target_pairs={{8,0},{12,4},{0,8},{4,12},{9,1},{13,5},{1,9},{5,13},{10,2},{14,6},... | collective-permute-start | bytes 196616 | tf_op jit(solution)/shard_map/ppermute | solution.py:545
  62.8 16.0 %collective-permute-start.12 = (bf16[32,2048]{1,0:T(8,128)(2,1)S(1)}, bf16[32,2048]{1,0:T(8,128)(2,1)S(1)}, u32[]{:S(2)}, u32[]{:S(2)}) collective-permute-start(bf16[32,2048]{1,0:T(8,128)(2,1)S(1)} %get-tuple-element.42), channel_id=1, source_target_pairs={{3,0},{0,1},{1,2},{2,3},{7,4},{4,5},{5,6},{6,7},{11,8},{8,9},{9,10... | collective-permute-start | bytes 393224 | tf_op jit(solution)/shard_map/ppermute | solution.py:541
  62.9 16.1 %collective-permute-start.14 = (bf16[32,2048]{1,0:T(8,128)(2,1)S(1)}, bf16[32,2048]{1,0:T(8,128)(2,1)S(1)}, u32[]{:S(2)}, u32[]{:S(2)}) collective-permute-start(bf16[32,2048]{1,0:T(8,128)(2,1)S(1)} %get-tuple-element.43), channel_id=1, source_target_pairs={{1,0},{2,1},{3,2},{0,3},{5,4},{6,5},{7,6},{4,7},{9,8},{10,9},{11,1... | collective-permute-start | bytes 393224 | tf_op jit(solution)/shard_map/ppermute | solution.py:541
  67.5 7.8 %collective-permute-start.21 = (bf16[256,128]{1,0:T(8,128)(2,1)S(1)}, bf16[256,128]{1,0:T(8,128)(2,1)S(1)}, u32[]{:S(2)}, u32[]{:S(2)}) collective-permute-start(bf16[256,128]{1,0:T(8,128)(2,1)S(1)} %convert_element_type.121), channel_id=1, source_target_pairs={{3,0},{0,1},{1,2},{2,3},{7,4},{4,5},{5,6},{6,7},{11,8},{8,9},{9,10... | collective-permute-start | bytes 196616 | tf_op jit(solution)/shard_map/ppermute | solution.py:541
  67.6 9.2 %collective-permute-start.20 = (bf16[256,128]{1,0:T(8,128)(2,1)S(1)}, bf16[256,128]{1,0:T(8,128)(2,1)S(1)}, u32[]{:S(2)}, u32[]{:S(2)}) collective-permute-start(bf16[256,128]{1,0:T(8,128)(2,1)S(1)} %convert_element_type.121), channel_id=1, source_target_pairs={{2,0},{3,1},{0,2},{1,3},{6,4},{7,5},{4,6},{5,7},{10,8},{11,9},{8,1... | collective-permute-start | bytes 196616 | tf_op jit(solution)/shard_map/ppermute | solution.py:541
  68.1 8.6 %collective-permute-start.19 = (bf16[256,128]{1,0:T(8,128)(2,1)S(1)}, bf16[256,128]{1,0:T(8,128)(2,1)S(1)}, u32[]{:S(2)}, u32[]{:S(2)}) collective-permute-start(bf16[256,128]{1,0:T(8,128)(2,1)S(1)} %convert_element_type.121), channel_id=1, source_target_pairs={{1,0},{2,1},{3,2},{0,3},{5,4},{6,5},{7,6},{4,7},{9,8},{10,9},{11,1... | collective-permute-start | bytes 196616 | tf_op jit(solution)/shard_map/ppermute | solution.py:541
  75.3 7.6 %collective-permute-start.13 = (bf16[32,2048]{1,0:T(8,128)(2,1)S(1)}, bf16[32,2048]{1,0:T(8,128)(2,1)S(1)}, u32[]{:S(2)}, u32[]{:S(2)}) collective-permute-start(bf16[32,2048]{1,0:T(8,128)(2,1)S(1)} %get-tuple-element.44), channel_id=1, source_target_pairs={{2,0},{3,1},{0,2},{1,3},{6,4},{7,5},{4,6},{5,7},{10,8},{11,9},{8,1... | collective-permute-start | bytes 393224 | tf_op jit(solution)/shard_map/ppermute | solution.py:541
  76.8 6.8 %collective-permute-start.24 = (bf16[256,128]{1,0:T(8,128)(2,1)S(1)}, bf16[256,128]{1,0:T(8,128)(2,1)S(1)}, u32[]{:S(2)}, u32[]{:S(2)}) collective-permute-start(bf16[256,128]{1,0:T(8,128)(2,1)S(1)} %add_convert_fusion.2), channel_id=1, source_target_pairs={{4,0},{8,4},{12,8},{0,12},{5,1},{9,5},{13,9},{1,13},{6,2},{10,6},{... | collective-permute-start | bytes 196616 | tf_op jit(solution)/shard_map/ppermute | solution.py:545
  76.8 6.8 %collective-permute-start.23 = (bf16[256,128]{1,0:T(8,128)(2,1)S(1)}, bf16[256,128]{1,0:T(8,128)(2,1)S(1)}, u32[]{:S(2)}, u32[]{:S(2)}) collective-permute-start(bf16[256,128]{1,0:T(8,128)(2,1)S(1)} %add_convert_fusion.2), channel_id=1, source_target_pairs={{8,0},{12,4},{0,8},{4,12},{9,1},{13,5},{1,9},{5,13},{10,2},{14,6},... | collective-permute-start | bytes 196616 | tf_op jit(solution)/shard_map/ppermute | solution.py:545
  78.9 4.7 %collective-permute-start.22 = (bf16[256,128]{1,0:T(8,128)(2,1)S(1)}, bf16[256,128]{1,0:T(8,128)(2,1)S(1)}, u32[]{:S(2)}, u32[]{:S(2)}) collective-permute-start(bf16[256,128]{1,0:T(8,128)(2,1)S(1)} %add_convert_fusion.2), channel_id=1, source_target_pairs={{12,0},{0,4},{4,8},{8,12},{13,1},{1,5},{5,9},{9,13},{14,2},{2,6},{... | collective-permute-start | bytes 196616 | tf_op jit(solution)/shard_map/ppermute | solution.py:545

commit v10 on v9

--- a/solution.py
+++ b/solution.py
@@ -164,11 +164,10 @@
         deep = jnp.broadcast_to(depth[a : a + 1], (seqs, LANES))
         weight = jnp.where(seq < deep, 1.0 / deep.astype(F32), 0.0)
         three = deep % 3 == 0
-        side = slice((a % 2) * seqs, (a % 2 + 1) * seqs)
         for x, part in enumerate((jnp.where(three, 0.0, weight), jnp.where(three, 3.0 * weight, 0.0))):
-            tall_ref[a // 2, x, side] = part.astype(BF16)
-            wide_ref[a // 2, x, :, side] = part.T[:cols].astype(BF16)
-        plain_ref[a // 2, :, side] = weight.T[:cols]
+            tall_ref[a, x] = part.astype(BF16)
+            wide_ref[a, x] = part.T[:cols].astype(BF16)
+        plain_ref[a] = weight.T[:cols]
 
 
 def projector(w_ref, wide_w_ref, w_out, wt_ref):
@@ -242,7 +241,6 @@
     rows, cols, width = grad.shape
     step = WIDE // PROJ
     groups = rows // step
-    pairs = CHAINS // 2
     labels = labels[None, :]
     return pl.pallas_call(
         lambda *refs: back_body(*refs, seqs=seqs),
@@ -250,9 +248,9 @@
         out_specs=[VMEM] * 7,
         out_shape=[
             jax.ShapeDtypeStruct((1, rows * PROJ), jnp.int32),
-            jax.ShapeDtypeStruct((pairs, 2, 2 * seqs, LANES), BF16),
-            jax.ShapeDtypeStruct((pairs, 2, cols, 2 * seqs), BF16),
-            jax.ShapeDtypeStruct((pairs, cols, 2 * seqs), F32),
+            jax.ShapeDtypeStruct((CHAINS, 2, seqs, LANES), BF16),
+            jax.ShapeDtypeStruct((CHAINS, 2, cols, seqs), BF16),
+            jax.ShapeDtypeStruct((CHAINS, cols, seqs), F32),
             jax.ShapeDtypeStruct(w.shape, BF16),
             pltpu.VMEM((groups, PROJ * cols, WIDE), BF16),
             pltpu.VMEM((groups, step, cols, width), BF16),
@@ -271,12 +269,16 @@
     )(at, *map(in_hbm, (labels, counts, w, grad)))
 
 
-def first_pair(at_ref, labels_ref, group):
-    return labels_ref[at_ref[0] + group * (WIDE // PROJ)] // 2
-
-
-def last_pair(at_ref, labels_ref, group):
-    return labels_ref[at_ref[0] + (group + 1) * (WIDE // PROJ) - 1] // 2
+def first_chain(at_ref, labels_ref, group):
+    return labels_ref[at_ref[0] + group * (WIDE // PROJ)]
+
+
+def last_chain(at_ref, labels_ref, group):
+    return labels_ref[at_ref[0] + (group + 1) * (WIDE // PROJ) - 1]
+
+
+def slots(chain, count, seqs):
+    return pl.ds(pl.multiple_of(chain * seqs, seqs), count * seqs)
 
 
 def each(first, last, fn):
@@ -291,11 +293,11 @@
     return pl.ds(pl.multiple_of(group * WIDE, WIDE), WIDE)
 
 
-def masked_left(left_ref, lab_ref, lb_ref, pair, group):
+def masked_left(left_ref, lab_ref, lb_ref, chain, group):
     seqs = left_ref.shape[0]
     lanes = lanes_of(group)
     for side in range(2):
-        keep = (lab_ref[:, lanes] == 2 * pair + side).astype(F32).astype(BF16)
+        keep = (lab_ref[:, lanes] == chain + side).astype(F32).astype(BF16)
         lb_ref[side * seqs : (side + 1) * seqs] = left_ref[:, lanes] * keep
 
 
@@ -304,32 +306,32 @@
     seqs = left_ref.shape[0]
     groups, span, _ = back_ref.shape
     cols = span // PROJ
-    first = lambda g: first_pair(at_ref, labels_ref, g)
-    last = lambda g: last_pair(at_ref, labels_ref, g)
-
-    def clear(pair):
-        q_ref[pair] = jnp.zeros(q_ref.shape[1:], F32)
-
-    each(first(0), last(groups - 1), clear)
+    first = lambda g: first_chain(at_ref, labels_ref, g)
+    last = lambda g: last_chain(at_ref, labels_ref, g)
+
+    def clear(chain):
+        q_ref[:, slots(chain, 1, seqs)] = jnp.zeros((span, seqs), F32)
+
+    each(first(0), last(groups - 1) + 1, clear)
 
     def group(g):
-        def one_pair(pair):
-            masked_left(left_ref, lab_ref, lb_ref, pair, g)
-            q_ref[pair] += nt_dot(back_ref[g], lb_ref[...])
-
-        each(first(g), last(g), one_pair)
+        def two_chains(k):
+            chain = first(g) + 2 * k
+            masked_left(left_ref, lab_ref, lb_ref, chain, g)
+            q_ref[:, slots(chain, 2, seqs)] += nt_dot(back_ref[g], lb_ref[...])
+
+        each(0, (last(g) - first(g)) // 2, two_chains)
 
     each(0, groups - 1, group)
 
-    def combine(pair, start):
+    def combine(chain, start):
         for e in range(PROJ):
             rows = slice(e * cols, (e + 1) * cols)
-            both = q_ref[pair, rows] * wide_ref[pair]
-            total = both[:, :seqs] + both[:, seqs:]
-            flip_ref[rows] = total if start else flip_ref[rows] + total
+            part = q_ref[rows, slots(chain, 1, seqs)] * wide_ref[chain]
+            flip_ref[rows] = part if start else flip_ref[rows] + part
 
     combine(first(0), True)
-    each(first(0) + 1, last(groups - 1), lambda pair: combine(pair, False))
+    each(first(0) + 1, last(groups - 1), lambda chain: combine(chain, False))
     for j in range(cols):
         turn_ref[j * PROJ : (j + 1) * PROJ] = flip_ref[pl.ds(j, PROJ, stride=cols)]
     for t in range(span // LANES):
@@ -347,7 +349,7 @@
         out_specs=VMEM,
         out_shape=jax.ShapeDtypeStruct((seqs, span), BF16),
         scratch_shapes=[
-            pltpu.VMEM((CHAINS // 2, span, 2 * seqs), F32),
+            pltpu.VMEM((span, (CHAINS + 1) * seqs), F32),
             pltpu.VMEM((2 * seqs, WIDE), BF16),
             pltpu.VMEM((span, seqs), F32),
             pltpu.VMEM((span, seqs), F32),
@@ -362,31 +364,32 @@
                    left_out, rm_ref, part_ref):
     seqs = right_ref.shape[0]
     groups, span, _ = back_ref.shape
-    first = lambda g: first_pair(at_ref, labels_ref, g)
-    last = lambda g: last_pair(at_ref, labels_ref, g)
+    first = lambda g: first_chain(at_ref, labels_ref, g)
+    last = lambda g: last_chain(at_ref, labels_ref, g)
     part_ref[...] = (right_ref[...].astype(F32) / 3).astype(BF16)
 
-    def build(pair):
-        for side in range(2):
-            rows = slice(side * seqs, (side + 1) * seqs)
-            plain, third = tall_ref[pair, 0, rows], tall_ref[pair, 1, rows]
-            for t in range(span // LANES):
-                lanes = slice(t * LANES, (t + 1) * LANES)
-                rm_ref[pair, rows, lanes] = (
-                    right_ref[:, lanes] * plain + part_ref[:, lanes] * third
-                )
+    def build(chain):
+        plain, third = tall_ref[chain, 0], tall_ref[chain, 1]
+        for t in range(span // LANES):
+            lanes = slice(t * LANES, (t + 1) * LANES)
+            rm_ref[slots(chain, 1, seqs), lanes] = (
+                right_ref[:, lanes] * plain + part_ref[:, lanes] * third
+            )
 
     each(first(0), last(groups - 1), build)
+    rm_ref[slots(last(groups - 1) + 1, 1, seqs)] = jnp.zeros((seqs, span), BF16)
 
     def group(g):
         lab = lab_ref[:, lanes_of(g)]
 
-        def one_pair(pair, total):
-            part = nn_dot(rm_ref[pair], back_ref[g])
-            keep0, keep1 = lab == 2 * pair, lab == 2 * pair + 1
+        def two_chains(k, total):
+            chain = first(g) + 2 * k
+            part = nn_dot(rm_ref[slots(chain, 2, seqs)], back_ref[g])
+            keep0, keep1 = lab == chain, lab == chain + 1
             return total + jnp.where(keep0, part[:seqs], 0.0) + jnp.where(keep1, part[seqs:], 0.0)
 
-        total = lax.fori_loop(first(g), last(g) + 1, one_pair, jnp.zeros((seqs, WIDE), F32))
+        passes = (last(g) - first(g)) // 2 + 1
+        total = lax.fori_loop(0, passes, two_chains, jnp.zeros((seqs, WIDE), F32))
         left_out[:, lanes_of(g)] = total.astype(BF16)
 
     each(0, groups - 1, group)
@@ -402,7 +405,7 @@
         out_specs=VMEM,
         out_shape=jax.ShapeDtypeStruct((seqs, total), BF16),
         scratch_shapes=[
-            pltpu.VMEM((CHAINS // 2, 2 * seqs, span), BF16),
+            pltpu.VMEM(((CHAINS + 1) * seqs, span), BF16),
             pltpu.VMEM((seqs, span), BF16),
         ],
         compiler_params=KERNEL,
@@ -417,40 +420,38 @@
     span = right_ref.shape[1]
     cols = span // PROJ
     groups, step, _, width = grad_ref.shape
-    first = lambda g: first_pair(at_ref, labels_ref, g)
-    last = lambda g: last_pair(at_ref, labels_ref, g)
+    first = lambda g: first_chain(at_ref, labels_ref, g)
+    last = lambda g: last_chain(at_ref, labels_ref, g)
     for t in range(span // LANES):
         lanes = slice(t * LANES, (t + 1) * LANES)
         flipped = right_ref[:, lanes].astype(F32).T
         flip_ref[lanes] = flipped.astype(BF16)
         part_ref[lanes] = (flipped / 3).astype(BF16)
 
-    def build(pair):
-        plain, third = wide_ref[pair, 0], wide_ref[pair, 1]
+    def build(chain):
+        plain, third = wide_ref[chain, 0], wide_ref[chain, 1]
         for e in range(PROJ):
             rows = slice(e * cols, (e + 1) * cols)
             to = e % PER_TILE * (PROJ // PER_TILE) + e // PER_TILE
-            into = slice(to * cols, (to + 1) * cols)
-            for side in range(2):
-                lanes = slice(side * seqs, (side + 1) * seqs)
-                rm_ref[pair, into, lanes] = (
-                    flip_ref[rows] * plain[:, lanes] + part_ref[rows] * third[:, lanes]
-                )
+            rm_ref[to * cols : (to + 1) * cols, slots(chain, 1, seqs)] = (
+                flip_ref[rows] * plain + part_ref[rows] * third
+            )
 
     each(first(0), last(groups - 1), build)
+    rm_ref[:, slots(last(groups - 1) + 1, 1, seqs)] = jnp.zeros((span, seqs), BF16)
     sum_ref[...] = jnp.zeros_like(sum_ref)
     quarter = span // PER_TILE
 
-    def product(pair, g, add):
-        masked_left(left_ref, lab_ref, lb_ref, pair, g)
+    def product(chain, g, add):
+        masked_left(left_ref, lab_ref, lb_ref, chain, g)
         for q in range(PER_TILE):
             rows = slice(q * quarter, (q + 1) * quarter)
-            part = nn_dot(rm_ref[pair, rows], rolled(lb_ref[...], q))
+            part = nn_dot(rm_ref[rows, slots(chain, 2, seqs)], rolled(lb_ref[...], q))
             acc_ref[rows] = acc_ref[rows] + part if add else part
 
     def group(g):
         product(first(g), g, False)
-        each(first(g) + 1, last(g), lambda pair: product(pair, g, True))
+        each(1, (last(g) - first(g)) // 2, lambda k: product(first(g) + 2 * k, g, True))
         for half in range(WIDE // LANES):
             lanes = slice(half * LANES, (half + 1) * LANES)
             for t in range(PROJ // PER_TILE):
@@ -487,7 +488,7 @@
             jax.ShapeDtypeStruct((PROJ * PROJ, width), F32),
         ],
         scratch_shapes=[
-            pltpu.VMEM((CHAINS // 2, span, 2 * seqs), BF16),
+            pltpu.VMEM((span, (CHAINS + 1) * seqs), BF16),
             pltpu.VMEM((2 * seqs, WIDE), BF16),
             pltpu.VMEM((span, WIDE), F32),
             pltpu.VMEM((width, PROJ * PROJ), F32),

time: 86 us -> 84.1 us (0.978); the launches traced: 84.9 us -> 84 us
  Pallas kernels: 37.2 us -> 35.7 us
  starting transfers between devices: 34 us -> 35.2 us
    ppermute x12, starting transfers between devices: 19.6 us -> 21.9 us  [col_shift(): return lax.ppermute(value, 'col', [((t + k) % n, t) for t in range(n)])]
    ppermute x9, starting transfers between devices: 7.03 us -> 5.9 us  [row_shift(): return lax.ppermute(value, 'row', [((t + k) % n, t) for t in range(n)])]
  transfers between devices with their start and end apart: 25 -> 25, of which waited for: 3 -> 2; matrix products, arithmetic and copies ran while one was open for 3% -> 3% of each run, Pallas kernels for 39% -> 38%
where the time goes in v10:
time: 84.1 us; the launch traced here: 84 us
  Pallas kernels  35.7 us (42%)
  starting transfers between devices  35.2 us (42%)
  waiting for transfers between devices  8.69 us (10%)
  other arithmetic  3.03 us (4%)
  between operations  0.93 us (1%)
    ppermute x12, starting transfers between devices, col_shift(): return lax.ppermute(value, 'col', [((t + k) % n, t) for t in range(n)])  21.9 us
    pallas_call x1, Pallas kernels, outer_call(): pl.pallas_call(outer_body, in_specs=[SMEM] * 2 + [VMEM] * 5, out_specs=[V...  10.7 us
    ppermute x12, waiting for transfers between devices, col_shift(): return lax.ppermute(value, 'col', [((t + k) % n, t) for t in range(n)])  8.66 us
    ppermute x4, starting transfers between devices, right_grad_home(): got = lax.ppermute(block, ('row', 'col'), pairs).astype(F32)[None]  7.38 us
    pallas_call x1, Pallas kernels, back_call(): pl.pallas_call(lambda *refs: back_body(*refs, seqs=seqs), in_specs=[SMEM]...  6.94 us
    ppermute x9, starting transfers between devices, row_shift(): return lax.ppermute(value, 'row', [((t + k) % n, t) for t in range(n)])  5.9 us
    pallas_call x1, Pallas kernels, right_grad_call(): pl.pallas_call(right_grad_body, in_specs=[SMEM] * 2 + [VMEM] * 4, out_spe...  5.9 us
    pallas_call x1, Pallas kernels, left_grad_call(): pl.pallas_call(left_grad_body, in_specs=[SMEM] * 2 + [VMEM] * 4, out_spec...  5.05 us
  transfers between devices with their start and end apart: 25, of which 2 were waited for; matrix products, arithmetic and copies ran while one was open for 3% of the time, Pallas kernels for 38%

profile of v10, /device:TPU:0, one launch (start us, length us, event | category | flops | bytes accessed | tf_op | source)
XLA Modules:
  0.0 84.0 jit_solution(17860307648267001012)
XLA Ops:
  0.6 3.7 %project.1 = (bf16[32,2048]{1,0:T(8,128)(2,1)S(1)}, bf16[32,2048]{1,0:T(8,128)(2,1)S(1)}) custom-call(bf16[32,64,256]{2,1,0:T(8,128)(2,1)} %refs_0_.1, f32[1,256]{1,0:T(1,128)} %bitcast.61, f32[1,256]{1,0:T(1,128)} %bitcast.62, bf16[32,256]{1,0:T(8,128)(2,1)} %bitcast.59, bf16[32,256]{1,0:T(8,128)(2,1)} %bitcast.60), custom_call_target="tpu_custom_call" | custom-call | tf_op jit(solution)/shard_map/project/pallas_call | solution.py:122
  4.4 3.1 %collective-permute-start.2 = (bf16[32,2048]{1,0:T(8,128)(2,1)S(1)}, bf16[32,2048]{1,0:T(8,128)(2,1)S(1)}, u32[]{:S(2)}, u32[]{:S(2)}) collective-permute-start(bf16[32,2048]{1,0:T(8,128)(2,1)S(1)} %get-tuple-element.21), channel_id=1, source_target_pairs={{3,0},{0,1},{1,2},{2,3},{7,4},{4,5},{5,6},{6,7},{11,8},{8,9},{9,10... | collective-permute-start | bytes 393224 | tf_op jit(solution)/shard_map/ppermute | solution.py:542
  7.5 2.6 %collective-permute-start.1 = (bf16[32,2048]{1,0:T(8,128)(2,1)S(1)}, bf16[32,2048]{1,0:T(8,128)(2,1)S(1)}, u32[]{:S(2)}, u32[]{:S(2)}) collective-permute-start(bf16[32,2048]{1,0:T(8,128)(2,1)S(1)} %get-tuple-element.21), channel_id=1, source_target_pairs={{2,0},{3,1},{0,2},{1,3},{6,4},{7,5},{4,6},{5,7},{10,8},{11,9},{8,1... | collective-permute-start | bytes 393224 | tf_op jit(solution)/shard_map/ppermute | solution.py:542
  10.1 1.5 %collective-permute-start.4 = (bf16[32,2048]{1,0:T(8,128)(2,1)S(1)}, bf16[32,2048]{1,0:T(8,128)(2,1)S(1)}, u32[]{:S(2)}, u32[]{:S(2)}) collective-permute-start(bf16[32,2048]{1,0:T(8,128)(2,1)S(1)} %get-tuple-element.22), channel_id=1, source_target_pairs={{8,0},{12,4},{0,8},{4,12},{9,1},{13,5},{1,9},{5,13},{10,2},{14,6},... | collective-permute-start | bytes 393224 | tf_op jit(solution)/shard_map/ppermute | solution.py:546
  11.6 1.5 %collective-permute-start.3 = (bf16[32,2048]{1,0:T(8,128)(2,1)S(1)}, bf16[32,2048]{1,0:T(8,128)(2,1)S(1)}, u32[]{:S(2)}, u32[]{:S(2)}) collective-permute-start(bf16[32,2048]{1,0:T(8,128)(2,1)S(1)} %get-tuple-element.22), channel_id=1, source_target_pairs={{4,0},{8,4},{12,8},{0,12},{5,1},{9,5},{13,9},{1,13},{6,2},{10,6},{... | collective-permute-start | bytes 393224 | tf_op jit(solution)/shard_map/ppermute | solution.py:546
  13.4 0.1 add_convert_fusion.3.refs_0_.at_ref
  13.4 6.9 %back.1 = (s32[1,2048]{1,0:T(1,128)S(1)}, bf16[8,2,128,128]{3,2,1,0:T(8,128)(2,1)S(1)}, bf16[8,2,64,128]{3,2,1,0:T(8,128)(2,1)S(1)}, f32[8,64,128]{2,1,0:T(8,128...) custom-call(s32[3]{0:T(128)S(1)} %add_convert_fusion.3.refs_0_.at_ref, ...), custom_call_target="tpu_custom_call" | custom-call | flops 21474836480 | bytes 8388608 | tf_op jit(solution)/shard_map/back/pallas_call | solution.py:245
  20.4 1.4 %collective-permute-start = (bf16[32,2048]{1,0:T(8,128)(2,1)S(1)}, bf16[32,2048]{1,0:T(8,128)(2,1)S(1)}, u32[]{:S(2)}, u32[]{:S(2)}) collective-permute-start(bf16[32,2048]{1,0:T(8,128)(2,1)S(1)} %get-tuple-element.21), channel_id=1, source_target_pairs={{1,0},{2,1},{3,2},{0,3},{5,4},{6,5},{7,6},{4,7},{9,8},{10,9},{11,1... | collective-permute-start | bytes 393224 | tf_op jit(solution)/shard_map/ppermute | solution.py:542
  21.9 0.7 collective-permute-start.8
  22.7 0.3 collective-permute-start.7
  23.0 4.7 %collective-permute-done = bf16[32,2048]{1,0:T(8,128)(2,1)S(1)} collective-permute-done((bf16[32,2048]{1,0:T(8,128)(2,1)S(1)}, bf16[32,2048]{1,0:T(8,128)(2,1)S(1)}, u32[]{:S(2)}, u32[]{:S(2)}) %collective-permute-start) | collective-permute-done | bytes 131104 | tf_op jit(solution)/shard_map/ppermute | solution.py:542
  27.7 2.2 %collective-permute-start.6 = (bf16[32,2048]{1,0:T(8,128)(2,1)S(1)}, bf16[32,2048]{1,0:T(8,128)(2,1)S(1)}, u32[]{:S(2)}, u32[]{:S(2)}) collective-permute-start(bf16[32,2048]{1,0:T(8,128)(2,1)S(1)} %get-tuple-element.48), channel_id=1, source_target_pairs={{1,0},{2,1},{3,2},{0,3},{5,4},{6,5},{7,6},{4,7},{9,8},{10,9},{11,1... | collective-permute-start | bytes 393224 | tf_op jit(solution)/shard_map/ppermute | solution.py:542
  30.0 5.9 %right_grad.1 = bf16[128,2048]{1,0:T(8,128)(2,1)S(1)} custom-call(s32[3]{0:T(128)S(1)} %add_convert_fusion.3.refs_0_.at_ref, s32[256]{0:T(256)S(1)} %copy-done.1, bf16[8,2048,256]{2,1,0:T(8,128)(2,1)S(1)} %get-tuple-element.25.back_ref, bf16[128,2048]{1,0:T(8,128)(2,1)S(1)} %constant_dynamic-update-slice_fusion.left_ref, ...), custom_call_target="tpu_custom_call" | custom-call | flops 21474836480 | bytes 8388608 | tf_op jit(solution)/shard_map/right_grad/pallas_call | solution.py:346
  36.0 0.7 collective-permute-start.15
  36.7 2.5 %collective-permute-start.18 = (bf16[32,2048]{1,0:T(8,128)(2,1)S(1)}, bf16[32,2048]{1,0:T(8,128)(2,1)S(1)}, u32[]{:S(2)}, u32[]{:S(2)}) collective-permute-start(bf16[32,2048]{1,0:T(8,128)(2,1)S(1)} %get-tuple-element.39), channel_id=1, source_target_pairs={{0,3},{1,7},{2,11},{3,15},{4,0},{5,4},{6,8},{7,12},{8,1},{9,5},{10... | collective-permute-start | bytes 393224 | tf_op jit(solution)/shard_map/ppermute | solution.py:579
  39.2 1.4 %collective-permute-start.17 = (bf16[32,2048]{1,0:T(8,128)(2,1)S(1)}, bf16[32,2048]{1,0:T(8,128)(2,1)S(1)}, u32[]{:S(2)}, u32[]{:S(2)}) collective-permute-start(bf16[32,2048]{1,0:T(8,128)(2,1)S(1)} %get-tuple-element.40), channel_id=1, source_target_pairs={{0,2},{1,6},{2,10},{3,14},{4,3},{5,7},{6,11},{7,15},{8,0},{9,4},{1... | collective-permute-start | bytes 393224 | tf_op jit(solution)/shard_map/ppermute | solution.py:579
  40.6 2.8 %collective-permute-start.16 = (bf16[32,2048]{1,0:T(8,128)(2,1)S(1)}, bf16[32,2048]{1,0:T(8,128)(2,1)S(1)}, u32[]{:S(2)}, u32[]{:S(2)}) collective-permute-start(bf16[32,2048]{1,0:T(8,128)(2,1)S(1)} %get-tuple-element.41), channel_id=1, source_target_pairs={{0,1},{1,5},{2,9},{3,13},{4,2},{5,6},{6,10},{7,14},{8,3},{9,7},{10... | collective-permute-start | bytes 393224 | tf_op jit(solution)/shard_map/ppermute | solution.py:579
  43.4 10.7 %outer.1 = (bf16[8,512,1024]{2,1,0:T(8,128)(2,1)S(1)}, f32[1024,128]{1,0:T(8,128)S(1)}) custom-call(s32[3]{0:T(128)S(1)} %add_convert_fusion.3.refs_0_.at_ref, s32[256]{0:T(256)S(1)} %copy-done.1, bf16[128,2048]{1,0:T(8,128)(2,1)S(1)} %constant_dynamic-update-slice_fusion.left_ref, s32[1,2048]{1,0:T(1,128)S(1)} %get-tuple-element.33.lab_ref, ...), custom_call_target="tpu_custom_call" | custom-call | flops 42949672960 | bytes 8388608 | tf_op jit(solution)/shard_map/outer/pallas_call | solution.py:482
  54.3 5.1 %left_grad.1 = bf16[128,2048]{1,0:T(8,128)(2,1)S(1)} custom-call(s32[3]{0:T(128)S(1)} %add_convert_fusion.3.refs_0_.at_ref, s32[256]{0:T(256)S(1)} %copy-done.1, bf16[8,2048,256]{2,1,0:T(8,128)(2,1)S(1)} %get-tuple-element.25.back_ref, s32[1,2048]{1,0:T(1,128)S(1)} %get-tuple-element.33.lab_ref, bf16[128,2048]{1,0:T(8,128)(2,1)S(1)} %pad_maximum_fusion.1.right_ref, ...), custom_call_target="tpu_custom_call" | custom-call | flops 21474836480 | bytes 8388608 | tf_op jit(solution)/shard_map/left_grad/pallas_call | solution.py:402
  59.4 1.8 %collective-permute-start.11 = (bf16[256,128]{1,0:T(8,128)(2,1)S(1)}, bf16[256,128]{1,0:T(8,128)(2,1)S(1)}, u32[]{:S(2)}, u32[]{:S(2)}) collective-permute-start(bf16[256,128]{1,0:T(8,128)(2,1)S(1)} %get-tuple-element.50), channel_id=1, source_target_pairs={{4,0},{8,4},{12,8},{0,12},{5,1},{9,5},{13,9},{1,13},{6,2},{10,6},{... | collective-permute-start | bytes 196616 | tf_op jit(solution)/shard_map/ppermute | solution.py:546
  61.2 1.4 %collective-permute-start.12 = (bf16[32,2048]{1,0:T(8,128)(2,1)S(1)}, bf16[32,2048]{1,0:T(8,128)(2,1)S(1)}, u32[]{:S(2)}, u32[]{:S(2)}) collective-permute-start(bf16[32,2048]{1,0:T(8,128)(2,1)S(1)} %get-tuple-element.42), channel_id=1, source_target_pairs={{3,0},{0,1},{1,2},{2,3},{7,4},{4,5},{5,6},{6,7},{11,8},{8,9},{9,10... | collective-permute-start | bytes 393224 | tf_op jit(solution)/shard_map/ppermute | solution.py:542
  62.6 2.5 %collective-permute-start.14 = (bf16[32,2048]{1,0:T(8,128)(2,1)S(1)}, bf16[32,2048]{1,0:T(8,128)(2,1)S(1)}, u32[]{:S(2)}, u32[]{:S(2)}) collective-permute-start(bf16[32,2048]{1,0:T(8,128)(2,1)S(1)} %get-tuple-element.43), channel_id=1, source_target_pairs={{1,0},{2,1},{3,2},{0,3},{5,4},{6,5},{7,6},{4,7},{9,8},{10,9},{11,1... | collective-permute-start | bytes 393224 | tf_op jit(solution)/shard_map/ppermute | solution.py:542
  65.1 0.7 add_convert_fusion
  66.0 1.6 %collective-permute-start.20 = (bf16[256,128]{1,0:T(8,128)(2,1)S(1)}, bf16[256,128]{1,0:T(8,128)(2,1)S(1)}, u32[]{:S(2)}, u32[]{:S(2)}) collective-permute-start(bf16[256,128]{1,0:T(8,128)(2,1)S(1)} %convert_element_type.121), channel_id=1, source_target_pairs={{2,0},{3,1},{0,2},{1,3},{6,4},{7,5},{4,6},{5,7},{10,8},{11,9},{8,1... | collective-permute-start | bytes 196616 | tf_op jit(solution)/shard_map/ppermute | solution.py:542
  67.6 2.8 %collective-permute-start.19 = (bf16[256,128]{1,0:T(8,128)(2,1)S(1)}, bf16[256,128]{1,0:T(8,128)(2,1)S(1)}, u32[]{:S(2)}, u32[]{:S(2)}) collective-permute-start(bf16[256,128]{1,0:T(8,128)(2,1)S(1)} %convert_element_type.121), channel_id=1, source_target_pairs={{1,0},{2,1},{3,2},{0,3},{5,4},{6,5},{7,6},{4,7},{9,8},{10,9},{11,1... | collective-permute-start | bytes 196616 | tf_op jit(solution)/shard_map/ppermute | solution.py:542
  70.4 3.3 %pair.1 = bf16[4096,128]{1,0:T(8,128)(2,1)} custom-call(bf16[8,512,1024]{2,1,0:T(8,128)(2,1)S(1)} %get-tuple-element.30.outer_ref, bf16[1024,128]{1,0:T(8,128)(2,1)S(1)} %get-tuple-element.36.w_ref, f32[1,128]{1,0:T(1,128)S(1)} %bitcast.52), custom_call_target="tpu_custom_call" | custom-call | flops 1073741824 | bytes 1048576 | tf_op jit(solution)/shard_map/pair/pallas_call | solution.py:517
  73.7 3.1 %collective-permute-start.13 = (bf16[32,2048]{1,0:T(8,128)(2,1)S(1)}, bf16[32,2048]{1,0:T(8,128)(2,1)S(1)}, u32[]{:S(2)}, u32[]{:S(2)}) collective-permute-start(bf16[32,2048]{1,0:T(8,128)(2,1)S(1)} %get-tuple-element.44), channel_id=1, source_target_pairs={{2,0},{3,1},{0,2},{1,3},{6,4},{7,5},{4,6},{5,7},{10,8},{11,9},{8,1... | collective-permute-start | bytes 393224 | tf_op jit(solution)/shard_map/ppermute | solution.py:542
  77.0 0.9 %collective-permute-start.23 = (bf16[256,128]{1,0:T(8,128)(2,1)S(1)}, bf16[256,128]{1,0:T(8,128)(2,1)S(1)}, u32[]{:S(2)}, u32[]{:S(2)}) collective-permute-start(bf16[256,128]{1,0:T(8,128)(2,1)S(1)} %add_convert_fusion.2), channel_id=1, source_target_pairs={{8,0},{12,4},{0,8},{4,12},{9,1},{13,5},{1,9},{5,13},{10,2},{14,6},... | collective-permute-start | bytes 196616 | tf_op jit(solution)/shard_map/ppermute | solution.py:546
  77.9 0.2 collective-permute-start.22
  78.0 3.9 %collective-permute-done.13 = bf16[32,2048]{1,0:T(8,128)(2,1)S(1)} collective-permute-done((bf16[32,2048]{1,0:T(8,128)(2,1)S(1)}, bf16[32,2048]{1,0:T(8,128)(2,1)S(1)}, u32[]{:S(2)}, u32[]{:S(2)}) %collective-permute-start.13) | collective-permute-done | bytes 131104 | tf_op jit(solution)/shard_map/ppermute | solution.py:542
  82.0 0.7 add_convert_fusion.1
  82.7 1.3 %convert_multiply_fusion = f32[1024,128]{1,0:T(8,128)} fusion(pred[1024]{0:T(1024)(128)(4,1)S(1)} %broadcast_in_dim.105, pred[1024]{0:T(1024)(128)(4,1)S(1)} %broadcast_in_dim.100, pred[1024]{0:T(1024)(128)(4,1)S(1)} %broadcast_in_dim.95, bf16[256,128]{1,0:T(8,128)(2,1)S(1)} %add_convert_fusion.2, bf16[256,128]{1,0:T(8,128)(2,1)S(1)} %collective-permute-done.24, ...), kind=kLoop, calls=%fused_computation.2 | loop fusion | flops 655360 | bytes 789504 | tf_op jit(solution)/shard_map/div | solution.py:648
  (54 shorter events, 0.9 us)
Async XLA Ops:
  4.4 25.6 %collective-permute-start.2 = (bf16[32,2048]{1,0:T(8,128)(2,1)S(1)}, bf16[32,2048]{1,0:T(8,128)(2,1)S(1)}, u32[]{:S(2)}, u32[]{:S(2)}) collective-permute-start(bf16[32,2048]{1,0:T(8,128)(2,1)S(1)} %get-tuple-element.21), channel_id=1, source_target_pairs={{3,0},{0,1},{1,2},{2,3},{7,4},{4,5},{5,6},{6,7},{11,8},{8,9},{9,10... | collective-permute-start | bytes 393224 | tf_op jit(solution)/shard_map/ppermute | solution.py:542
  7.5 22.5 %collective-permute-start.1 = (bf16[32,2048]{1,0:T(8,128)(2,1)S(1)}, bf16[32,2048]{1,0:T(8,128)(2,1)S(1)}, u32[]{:S(2)}, u32[]{:S(2)}) collective-permute-start(bf16[32,2048]{1,0:T(8,128)(2,1)S(1)} %get-tuple-element.21), channel_id=1, source_target_pairs={{2,0},{3,1},{0,2},{1,3},{6,4},{7,5},{4,6},{5,7},{10,8},{11,9},{8,1... | collective-permute-start | bytes 393224 | tf_op jit(solution)/shard_map/ppermute | solution.py:542
  10.1 10.3 %collective-permute-start.5 = (bf16[32,2048]{1,0:T(8,128)(2,1)S(1)}, bf16[32,2048]{1,0:T(8,128)(2,1)S(1)}, u32[]{:S(2)}, u32[]{:S(2)}) collective-permute-start(bf16[32,2048]{1,0:T(8,128)(2,1)S(1)} %get-tuple-element.22), channel_id=1, source_target_pairs={{12,0},{0,4},{4,8},{8,12},{13,1},{1,5},{5,9},{9,13},{14,2},{2,6},{... | collective-permute-start | bytes 393224 | tf_op jit(solution)/shard_map/ppermute | solution.py:546
  10.1 11.7 %collective-permute-start.4 = (bf16[32,2048]{1,0:T(8,128)(2,1)S(1)}, bf16[32,2048]{1,0:T(8,128)(2,1)S(1)}, u32[]{:S(2)}, u32[]{:S(2)}) collective-permute-start(bf16[32,2048]{1,0:T(8,128)(2,1)S(1)} %get-tuple-element.22), channel_id=1, source_target_pairs={{8,0},{12,4},{0,8},{4,12},{9,1},{13,5},{1,9},{5,13},{10,2},{14,6},... | collective-permute-start | bytes 393224 | tf_op jit(solution)/shard_map/ppermute | solution.py:546
  11.6 10.2 %collective-permute-start.3 = (bf16[32,2048]{1,0:T(8,128)(2,1)S(1)}, bf16[32,2048]{1,0:T(8,128)(2,1)S(1)}, u32[]{:S(2)}, u32[]{:S(2)}) collective-permute-start(bf16[32,2048]{1,0:T(8,128)(2,1)S(1)} %get-tuple-element.22), channel_id=1, source_target_pairs={{4,0},{8,4},{12,8},{0,12},{5,1},{9,5},{13,9},{1,13},{6,2},{10,6},{... | collective-permute-start | bytes 393224 | tf_op jit(solution)/shard_map/ppermute | solution.py:546
  13.4 16.6 %copy-start.1 = (s32[256]{0:T(256)S(1)}, s32[256]{0:T(256)}, u32[]{:S(2)}) copy-start(s32[256]{0:T(256)} %labels_ref.5) | copy-start | bytes 3076
  20.4 7.3 %collective-permute-start = (bf16[32,2048]{1,0:T(8,128)(2,1)S(1)}, bf16[32,2048]{1,0:T(8,128)(2,1)S(1)}, u32[]{:S(2)}, u32[]{:S(2)}) collective-permute-start(bf16[32,2048]{1,0:T(8,128)(2,1)S(1)} %get-tuple-element.21), channel_id=1, source_target_pairs={{1,0},{2,1},{3,2},{0,3},{5,4},{6,5},{7,6},{4,7},{9,8},{10,9},{11,1... | collective-permute-start | bytes 393224 | tf_op jit(solution)/shard_map/ppermute | solution.py:542
  21.9 17.3 %collective-permute-start.8 = (bf16[32,2048]{1,0:T(8,128)(2,1)S(1)}, bf16[32,2048]{1,0:T(8,128)(2,1)S(1)}, u32[]{:S(2)}, u32[]{:S(2)}) collective-permute-start(bf16[32,2048]{1,0:T(8,128)(2,1)S(1)} %get-tuple-element.46), channel_id=1, source_target_pairs={{3,0},{0,1},{1,2},{2,3},{7,4},{4,5},{5,6},{6,7},{11,8},{8,9},{9,10... | collective-permute-start | bytes 393224 | tf_op jit(solution)/shard_map/ppermute | solution.py:542
  22.7 17.9 %collective-permute-start.7 = (bf16[32,2048]{1,0:T(8,128)(2,1)S(1)}, bf16[32,2048]{1,0:T(8,128)(2,1)S(1)}, u32[]{:S(2)}, u32[]{:S(2)}) collective-permute-start(bf16[32,2048]{1,0:T(8,128)(2,1)S(1)} %get-tuple-element.47), channel_id=1, source_target_pairs={{2,0},{3,1},{0,2},{1,3},{6,4},{7,5},{4,6},{5,7},{10,8},{11,9},{8,1... | collective-permute-start | bytes 393224 | tf_op jit(solution)/shard_map/ppermute | solution.py:542
  27.7 15.7 %collective-permute-start.6 = (bf16[32,2048]{1,0:T(8,128)(2,1)S(1)}, bf16[32,2048]{1,0:T(8,128)(2,1)S(1)}, u32[]{:S(2)}, u32[]{:S(2)}) collective-permute-start(bf16[32,2048]{1,0:T(8,128)(2,1)S(1)} %get-tuple-element.48), channel_id=1, source_target_pairs={{1,0},{2,1},{3,2},{0,3},{5,4},{6,5},{7,6},{4,7},{9,8},{10,9},{11,1... | collective-permute-start | bytes 393224 | tf_op jit(solution)/shard_map/ppermute | solution.py:542
  36.0 23.4 %collective-permute-start.15 = (bf16[32,2048]{1,0:T(8,128)(2,1)S(1)}, bf16[32,2048]{1,0:T(8,128)(2,1)S(1)}, u32[]{:S(2)}, u32[]{:S(2)}) collective-permute-start(bf16[32,2048]{1,0:T(8,128)(2,1)S(1)} %get-tuple-element.38), channel_id=1, source_target_pairs={{0,0},{1,4},{2,8},{3,12},{4,1},{5,5},{6,9},{7,13},{8,2},{9,6},{10,... | collective-permute-start | bytes 393224 | tf_op jit(solution)/shard_map/ppermute | solution.py:579
  36.7 24.5 %collective-permute-start.18 = (bf16[32,2048]{1,0:T(8,128)(2,1)S(1)}, bf16[32,2048]{1,0:T(8,128)(2,1)S(1)}, u32[]{:S(2)}, u32[]{:S(2)}) collective-permute-start(bf16[32,2048]{1,0:T(8,128)(2,1)S(1)} %get-tuple-element.39), channel_id=1, source_target_pairs={{0,3},{1,7},{2,11},{3,15},{4,0},{5,4},{6,8},{7,12},{8,1},{9,5},{10... | collective-permute-start | bytes 393224 | tf_op jit(solution)/shard_map/ppermute | solution.py:579
  39.2 22.0 %collective-permute-start.17 = (bf16[32,2048]{1,0:T(8,128)(2,1)S(1)}, bf16[32,2048]{1,0:T(8,128)(2,1)S(1)}, u32[]{:S(2)}, u32[]{:S(2)}) collective-permute-start(bf16[32,2048]{1,0:T(8,128)(2,1)S(1)} %get-tuple-element.40), channel_id=1, source_target_pairs={{0,2},{1,6},{2,10},{3,14},{4,3},{5,7},{6,11},{7,15},{8,0},{9,4},{1... | collective-permute-start | bytes 393224 | tf_op jit(solution)/shard_map/ppermute | solution.py:579
  40.6 22.1 %collective-permute-start.16 = (bf16[32,2048]{1,0:T(8,128)(2,1)S(1)}, bf16[32,2048]{1,0:T(8,128)(2,1)S(1)}, u32[]{:S(2)}, u32[]{:S(2)}) collective-permute-start(bf16[32,2048]{1,0:T(8,128)(2,1)S(1)} %get-tuple-element.41), channel_id=1, source_target_pairs={{0,1},{1,5},{2,9},{3,13},{4,2},{5,6},{6,10},{7,14},{8,3},{9,7},{10... | collective-permute-start | bytes 393224 | tf_op jit(solution)/shard_map/ppermute | solution.py:579
  54.3 11.6 %collective-permute-start.9 = (bf16[256,128]{1,0:T(8,128)(2,1)S(1)}, bf16[256,128]{1,0:T(8,128)(2,1)S(1)}, u32[]{:S(2)}, u32[]{:S(2)}) collective-permute-start(bf16[256,128]{1,0:T(8,128)(2,1)S(1)} %get-tuple-element.49), channel_id=1, source_target_pairs={{12,0},{0,4},{4,8},{8,12},{13,1},{1,5},{5,9},{9,13},{14,2},{2,6},{... | collective-permute-start | bytes 196616 | tf_op jit(solution)/shard_map/ppermute | solution.py:546
  54.3 16.1 %copy-start = (f32[128]{0:T(128)S(1)}, f32[128]{0:T(128)}, u32[]{:S(2)}) copy-start(f32[128]{0:T(128)} %param.16) | copy-start | bytes 1540
  59.4 6.4 %collective-permute-start.11 = (bf16[256,128]{1,0:T(8,128)(2,1)S(1)}, bf16[256,128]{1,0:T(8,128)(2,1)S(1)}, u32[]{:S(2)}, u32[]{:S(2)}) collective-permute-start(bf16[256,128]{1,0:T(8,128)(2,1)S(1)} %get-tuple-element.50), channel_id=1, source_target_pairs={{4,0},{8,4},{12,8},{0,12},{5,1},{9,5},{13,9},{1,13},{6,2},{10,6},{... | collective-permute-start | bytes 196616 | tf_op jit(solution)/shard_map/ppermute | solution.py:546
  61.2 4.6 %collective-permute-start.10 = (bf16[256,128]{1,0:T(8,128)(2,1)S(1)}, bf16[256,128]{1,0:T(8,128)(2,1)S(1)}, u32[]{:S(2)}, u32[]{:S(2)}) collective-permute-start(bf16[256,128]{1,0:T(8,128)(2,1)S(1)} %get-tuple-element.51), channel_id=1, source_target_pairs={{8,0},{12,4},{0,8},{4,12},{9,1},{13,5},{1,9},{5,13},{10,2},{14,6},... | collective-permute-start | bytes 196616 | tf_op jit(solution)/shard_map/ppermute | solution.py:546
  61.2 16.7 %collective-permute-start.12 = (bf16[32,2048]{1,0:T(8,128)(2,1)S(1)}, bf16[32,2048]{1,0:T(8,128)(2,1)S(1)}, u32[]{:S(2)}, u32[]{:S(2)}) collective-permute-start(bf16[32,2048]{1,0:T(8,128)(2,1)S(1)} %get-tuple-element.42), channel_id=1, source_target_pairs={{3,0},{0,1},{1,2},{2,3},{7,4},{4,5},{5,6},{6,7},{11,8},{8,9},{9,10... | collective-permute-start | bytes 393224 | tf_op jit(solution)/shard_map/ppermute | solution.py:542
  62.6 15.4 %collective-permute-start.14 = (bf16[32,2048]{1,0:T(8,128)(2,1)S(1)}, bf16[32,2048]{1,0:T(8,128)(2,1)S(1)}, u32[]{:S(2)}, u32[]{:S(2)}) collective-permute-start(bf16[32,2048]{1,0:T(8,128)(2,1)S(1)} %get-tuple-element.43), channel_id=1, source_target_pairs={{1,0},{2,1},{3,2},{0,3},{5,4},{6,5},{7,6},{4,7},{9,8},{10,9},{11,1... | collective-permute-start | bytes 393224 | tf_op jit(solution)/shard_map/ppermute | solution.py:542
  65.9 7.8 %collective-permute-start.21 = (bf16[256,128]{1,0:T(8,128)(2,1)S(1)}, bf16[256,128]{1,0:T(8,128)(2,1)S(1)}, u32[]{:S(2)}, u32[]{:S(2)}) collective-permute-start(bf16[256,128]{1,0:T(8,128)(2,1)S(1)} %convert_element_type.121), channel_id=1, source_target_pairs={{3,0},{0,1},{1,2},{2,3},{7,4},{4,5},{5,6},{6,7},{11,8},{8,9},{9,10... | collective-permute-start | bytes 196616 | tf_op jit(solution)/shard_map/ppermute | solution.py:542
  66.0 10.9 %collective-permute-start.20 = (bf16[256,128]{1,0:T(8,128)(2,1)S(1)}, bf16[256,128]{1,0:T(8,128)(2,1)S(1)}, u32[]{:S(2)}, u32[]{:S(2)}) collective-permute-start(bf16[256,128]{1,0:T(8,128)(2,1)S(1)} %convert_element_type.121), channel_id=1, source_target_pairs={{2,0},{3,1},{0,2},{1,3},{6,4},{7,5},{4,6},{5,7},{10,8},{11,9},{8,1... | collective-permute-start | bytes 196616 | tf_op jit(solution)/shard_map/ppermute | solution.py:542
  67.6 9.3 %collective-permute-start.19 = (bf16[256,128]{1,0:T(8,128)(2,1)S(1)}, bf16[256,128]{1,0:T(8,128)(2,1)S(1)}, u32[]{:S(2)}, u32[]{:S(2)}) collective-permute-start(bf16[256,128]{1,0:T(8,128)(2,1)S(1)} %convert_element_type.121), channel_id=1, source_target_pairs={{1,0},{2,1},{3,2},{0,3},{5,4},{6,5},{7,6},{4,7},{9,8},{10,9},{11,1... | collective-permute-start | bytes 196616 | tf_op jit(solution)/shard_map/ppermute | solution.py:542
  73.7 8.2 %collective-permute-start.13 = (bf16[32,2048]{1,0:T(8,128)(2,1)S(1)}, bf16[32,2048]{1,0:T(8,128)(2,1)S(1)}, u32[]{:S(2)}, u32[]{:S(2)}) collective-permute-start(bf16[32,2048]{1,0:T(8,128)(2,1)S(1)} %get-tuple-element.44), channel_id=1, source_target_pairs={{2,0},{3,1},{0,2},{1,3},{6,4},{7,5},{4,6},{5,7},{10,8},{11,9},{8,1... | collective-permute-start | bytes 393224 | tf_op jit(solution)/shard_map/ppermute | solution.py:542
  76.9 5.8 %collective-permute-start.24 = (bf16[256,128]{1,0:T(8,128)(2,1)S(1)}, bf16[256,128]{1,0:T(8,128)(2,1)S(1)}, u32[]{:S(2)}, u32[]{:S(2)}) collective-permute-start(bf16[256,128]{1,0:T(8,128)(2,1)S(1)} %add_convert_fusion.2), channel_id=1, source_target_pairs={{4,0},{8,4},{12,8},{0,12},{5,1},{9,5},{13,9},{1,13},{6,2},{10,6},{... | collective-permute-start | bytes 196616 | tf_op jit(solution)/shard_map/ppermute | solution.py:546
  77.0 5.7 %collective-permute-start.23 = (bf16[256,128]{1,0:T(8,128)(2,1)S(1)}, bf16[256,128]{1,0:T(8,128)(2,1)S(1)}, u32[]{:S(2)}, u32[]{:S(2)}) collective-permute-start(bf16[256,128]{1,0:T(8,128)(2,1)S(1)} %add_convert_fusion.2), channel_id=1, source_target_pairs={{8,0},{12,4},{0,8},{4,12},{9,1},{13,5},{1,9},{5,13},{10,2},{14,6},... | collective-permute-start | bytes 196616 | tf_op jit(solution)/shard_map/ppermute | solution.py:546
  77.9 4.8 %collective-permute-start.22 = (bf16[256,128]{1,0:T(8,128)(2,1)S(1)}, bf16[256,128]{1,0:T(8,128)(2,1)S(1)}, u32[]{:S(2)}, u32[]{:S(2)}) collective-permute-start(bf16[256,128]{1,0:T(8,128)(2,1)S(1)} %add_convert_fusion.2), channel_id=1, source_target_pairs={{12,0},{0,4},{4,8},{8,12},{13,1},{1,5},{5,9},{9,13},{14,2},{2,6},{... | collective-permute-start | bytes 196616 | tf_op jit(solution)/shard_map/ppermute | solution.py:546

commit v11 on v10

--- a/solution.py
+++ b/solution.py
@@ -139,7 +139,8 @@
     )(*map(in_hbm, (x, gain, shift, first, second)))
 
 
-def masks(at_ref, labels_ref, counts_ref, lab_ref, tall_ref, wide_ref, plain_ref, rows, cols, seqs):
+def masks(at_ref, labels_ref, counts_ref, lab_ref, tall_ref, wide_ref, plain_ref, rows, cols, seqs,
+          n_row, n_col):
     res = labels_ref.shape[1]
     labels = jnp.broadcast_to(labels_ref[...], (8, res))
     own = pltpu.roll(labels, (res - at_ref[0]) % res, 1)[:, :rows]
@@ -159,7 +160,14 @@
     depth = jnp.zeros((CHAINS, LANES), jnp.int32)
     for b in range(CHAINS):
         depth += jnp.where(there == b, counts_ref[:, b : b + 1], 0)
-    seq = (lax.broadcasted_iota(jnp.int32, (seqs, LANES), 0) + at_ref[2]) % seqs
+    here, m = seqs // n_col, n_col // n_row
+    within = lax.broadcasted_iota(jnp.int32, (here, LANES), 0)
+    blocks = []
+    for k in range(n_row):
+        for u in range(m):
+            t = (at_ref[2] ^ k) * m + (lax.rem(at_ref[3] + (m - u), m) if m > 1 else 0)
+            blocks.append(within + t * here)
+    seq = jnp.concatenate(blocks, axis=0)
     for a in range(CHAINS):
         deep = jnp.broadcast_to(depth[a : a + 1], (seqs, LANES))
         weight = jnp.where(seq < deep, 1.0 / deep.astype(F32), 0.0)
@@ -189,7 +197,7 @@
 
 def back_body(at_ref, labels_hbm, counts_hbm, w_hbm, grad_hbm,
               lab_ref, tall_ref, wide_ref, plain_ref, w_out, back_ref, grad_ref,
-              labels_ref, counts_ref, w_ref, wide_w_ref, wt_ref, sems, *, seqs):
+              labels_ref, counts_ref, w_ref, wide_w_ref, wt_ref, sems, *, seqs, n_row, n_col):
     groups, step, cols, _ = grad_ref.shape
     copies = [
         pltpu.make_async_copy(w_hbm, w_ref, sems.at[groups]),
@@ -208,7 +216,7 @@
         copy.wait()
     projector(w_ref, wide_w_ref, w_out, wt_ref)
     masks(at_ref, labels_ref, counts_ref, lab_ref, tall_ref, wide_ref, plain_ref,
-          groups * step, cols, seqs)
+          groups * step, cols, seqs, n_row, n_col)
     halves = step // PER_TILE
 
     def group(g, carry):
@@ -237,13 +245,13 @@
     lax.fori_loop(0, groups, group, 0)
 
 
-def back_call(at, labels, counts, w, grad, seqs):
+def back_call(at, labels, counts, w, grad, seqs, n_row, n_col):
     rows, cols, width = grad.shape
     step = WIDE // PROJ
     groups = rows // step
     labels = labels[None, :]
     return pl.pallas_call(
-        lambda *refs: back_body(*refs, seqs=seqs),
+        lambda *refs: back_body(*refs, seqs=seqs, n_row=n_row, n_col=n_col),
         in_specs=[SMEM] + [HBM] * 4,
         out_specs=[VMEM] * 7,
         out_shape=[
@@ -530,55 +538,79 @@
     )(outer, w, offset)
 
 
-class Ring:
+class Pairs:
     def __init__(self, n_row, n_col):
         self.n_row, self.n_col = n_row, n_col
         self.per_row = n_col // n_row
         self.row = lax.axis_index("row").astype(jnp.uint32)
         self.col = lax.axis_index("col").astype(jnp.uint32)
 
-    def col_shift(self, value, k):
-        n = self.n_col
-        return lax.ppermute(value, "col", [((t + k) % n, t) for t in range(n)])
-
-    def row_shift(self, value, k):
-        n = self.n_row
-        return lax.ppermute(value, "row", [((t + k) % n, t) for t in range(n)])
-
-    def right_along_row(self, right):
-        others = [self.row_shift(right, k) for k in range(1, self.n_row)]
-        return [right] + others
-
-    def right_pieces(self, by_row):
-        n, m = self.n_row, self.per_row
-        here, lanes = by_row[0].shape
-        lanes //= m
-        by_row = jnp.stack(by_row)
+    def col_swap(self, value, k):
+        return lax.ppermute(value, "col", [(t ^ k, t) for t in range(self.n_col)])
+
+    def row_swap(self, value, k):
+        return lax.ppermute(value, "row", [(t ^ k, t) for t in range(self.n_row)])
+
+    def place_of(self, t):
+        m = self.per_row
+        return ((t // m) ^ self.row) * m + (self.col + (m - t % m)) % m
+
+    def home_pairs(self, u):
+        n, m = self.n_col, self.per_row
+        return [
+            (a * n + t, (t // m) * n + a * m + (t + u) % m) for a in range(self.n_row) for t in range(n)
+        ]
+
+    def right_to_col(self, right):
+        m = self.per_row
+        lanes = right.shape[1] // m
         pieces = []
+        for u in range(m):
+            at = (self.col + u) % m * lanes
+            block = lax.dynamic_slice_in_dim(right, at, lanes, 1) if m > 1 else right
+            pieces.append(lax.ppermute(block, ("row", "col"), self.home_pairs(u)))
+        return jnp.concatenate(pieces)
+
+    def right_along_row(self, mine):
+        swaps = [self.row_swap(mine, k) for k in range(1, self.n_row)]
+        return jnp.concatenate([mine] + swaps)
+
+    def right_grad_along_row(self, grad):
+        size = grad.shape[0] // self.n_row
+        total = grad[:size].astype(F32)
+        for k in range(1, self.n_row):
+            total += self.row_swap(grad[k * size : (k + 1) * size], k).astype(F32)
+        return total.astype(BF16)
+
+    def right_grad_home(self, mine):
+        m = self.per_row
+        here, lanes = mine.shape[0] // m, mine.shape[1]
+        slot = lax.broadcasted_iota(jnp.uint32, (m, 1, 1), 0)
+        home = jnp.zeros((m, here, lanes), BF16)
+        for u in range(m):
+            pairs = [(there, origin) for origin, there in self.home_pairs(u)]
+            got = lax.ppermute(mine[u * here : (u + 1) * here], ("row", "col"), pairs)[None]
+            home = got if m == 1 else jnp.where(slot == (self.col + u) % m, got, home)
+        return home.swapaxes(0, 1).reshape(here, m * lanes)
+
+    def left_along_col(self, left):
+        here = left.shape[0]
+        out = jnp.zeros((self.n_col * here, left.shape[1]), left.dtype)
         for k in range(self.n_col):
-            q = (self.col + (self.n_col - k)) % self.n_col
-            at = ((q // m + (n - self.row)) % n, jnp.uint32(0), (q % m) * lanes)
-            pieces.append(lax.dynamic_slice(by_row, at, (1, here, lanes))[0])
-        return pieces
-
-    def right_along_col(self, pieces):
-        return jnp.concatenate([self.col_shift(p, k) if k else p for k, p in enumerate(pieces)])
-
-    def right_grad_home(self, grad):
-        n, m = self.n_col, self.per_row
-        here, lanes = grad.shape[0] // n, grad.shape[1]
-        total = jnp.zeros((m, here, lanes), F32)
-        slot = lax.broadcasted_iota(jnp.uint32, (m, 1, 1), 0)
-        for k in range(n):
-            t = (self.row * m + self.col % m + k) % n
-            block = lax.dynamic_slice_in_dim(grad, ((t + n - self.col) % n) * here, here, 0)
-            pairs = []
-            for r in range(self.n_row):
-                for q in range(n):
-                    pairs.append((r * n + q, (q // m) * n + (r * m + q % m + k) % n))
-            got = lax.ppermute(block, ("row", "col"), pairs).astype(F32)[None]
-            total += got if m == 1 else jnp.where(slot == (self.col + (n - k)) % n % m, got, 0)
-        return total.swapaxes(0, 1).reshape(here, m * lanes).astype(BF16)
+            block = self.col_swap(left, k) if k else left
+            out = lax.dynamic_update_slice_in_dim(out, block, self.place_of(self.col ^ k) * here, 0)
+        return out
+
+    def left_grad_along_col(self, grad):
+        here = grad.shape[0] // self.n_col
+        blocks = [
+            lax.dynamic_slice_in_dim(grad, self.place_of(self.col ^ k) * here, here, 0)
+            for k in range(self.n_col)
+        ]
+        total = blocks[0].astype(F32)
+        for k in range(1, self.n_col):
+            total += self.col_swap(blocks[k], k).astype(F32)
+        return total.astype(BF16)
 
     def weight_over_row(self, weight):
         n = self.n_row
@@ -586,22 +618,22 @@
         sent = weight.astype(BF16).reshape(n, size, -1)
         total = lax.dynamic_index_in_dim(weight.reshape(n, size, -1), self.row, 0, keepdims=False)
         for k in range(1, n):
-            piece = lax.dynamic_index_in_dim(sent, (self.row + k) % n, 0, keepdims=False)
-            total += self.row_shift(piece, n - k).astype(F32)
+            piece = lax.dynamic_index_in_dim(sent, self.row ^ k, 0, keepdims=False)
+            total += self.row_swap(piece, k).astype(F32)
         return total
 
     def weight_over_col(self, total):
         mine = total.astype(BF16)
         for k in range(1, self.n_col):
-            total += self.col_shift(mine, k).astype(F32)
+            total += self.col_swap(mine, k).astype(F32)
         return total.astype(BF16)
 
     def weight_to_all(self, mine):
         n = self.n_row
-        which = (lax.broadcasted_iota(jnp.uint32, (n, 1, 1), 0) + (n - self.row)) % n
+        which = lax.broadcasted_iota(jnp.uint32, (n, 1, 1), 0) ^ self.row
         shares = mine[None]
         for k in range(1, n):
-            shares = jnp.where(which == k, self.row_shift(mine, k)[None], shares)
+            shares = jnp.where(which == k, self.row_swap(mine, k)[None], shares)
         return shares.reshape(n * mine.shape[0], mine.shape[1])
 
 
@@ -611,26 +643,26 @@
 
 def shards(n_row, n_col, alignment_tensor, gain, shift, first_projector, second_projector,
            final_projector, final_offset, labels, counts, grad):
-    ring = Ring(n_row, n_col)
+    ring = Pairs(n_row, n_col)
     here, rows, _ = alignment_tensor.shape
     cols, width = grad.shape[1:]
     seqs = here * n_col
     left, right = project_call(
         alignment_tensor, gain[None, :], shift[None, :], first_projector.T, second_projector.T, cols
     )
-    by_row = ring.right_along_row(right)
-    left = jnp.concatenate([left] + [ring.col_shift(left, k) for k in range(1, n_col)])
-
-    at = jnp.stack([ring.row * rows, ring.col * cols, ring.col * here]).astype(jnp.int32)
+    mine = ring.right_to_col(right)
+    left = ring.left_along_col(left)
+
+    at = jnp.stack([ring.row * rows, ring.col * cols, ring.row, ring.col]).astype(jnp.int32)
     lab, tall, wide, plain, w, back, grad = back_call(
-        at, labels, counts, after(final_projector, right), grad, seqs
+        at, labels, counts, after(final_projector, right), grad, seqs, n_row, n_col
     )
-    mine = ring.right_along_col(ring.right_pieces(by_row))
+    right = ring.right_along_row(mine)
     back, grad = in_vmem(back), in_vmem(grad)
     right_grad = right_grad_call(at, labels, back, left, lab, plain)
 
-    right = after(mine, right_grad)
-    grad_right = ring.right_grad_home(right_grad)
+    right = after(right, right_grad)
+    mine = ring.right_grad_along_row(right_grad)
     outer, weight = outer_call(
         at, labels, left, lab, right, wide, grad
     )
@@ -638,10 +670,8 @@
     left_grad = left_grad_call(at, labels, back, after(lab, weight), right, tall)
     share = after(share, left_grad)
 
-    total = left_grad[:here].astype(F32)
-    for k in range(1, n_col):
-        total += ring.col_shift(left_grad[k * here : (k + 1) * here], n_col - k).astype(F32)
-    adjoint_first = total.astype(BF16)
+    grad_right = ring.right_grad_home(after(mine, weight))
+    adjoint_first = ring.left_grad_along_col(left_grad)
     pair_update = pair_call(in_vmem(outer), after(w, left_grad, share), final_offset[None, :])
     pair_update = pair_update.reshape(rows, cols, width)
     mine = after(ring.weight_over_col(share), pair_update)

time: 84.1 us -> 85 us (1.011)
  waiting for transfers between devices: 8.69 us -> 20 us
  starting transfers between devices: 35.2 us -> 24.8 us
    ppermute x25 -> x23, waiting for transfers between devices: 8.69 us -> 20 us  [the longest x9 15.7 us: col_swap(): return lax.ppermute(value, 'col', [(t ^ k, t) for t in range(self.n_col)])]
    ppermute x25 -> x23, starting transfers between devices: 35.2 us -> 24.8 us  [the longest x9 14.2 us: col_swap(): return lax.ppermute(value, 'col', [(t ^ k, t) for t in range(self.n_col)])]
  transfers between devices with their start and end apart: 25 -> 23, of which waited for: 2 -> 6; matrix products, arithmetic and copies ran while one was open for 3% -> 2% of each run, Pallas kernels for 38% -> 38%
where the time goes in v11:
time: 85 us; the launch traced here: 84.8 us
  Pallas kernels  35.7 us (42%)
  starting transfers between devices  24.8 us (29%)
  waiting for transfers between devices  20 us (24%)
  other arithmetic  2.31 us (3%)
  local copies, waits for them, and re-layouts  1.11 us (1%)
  between operations  0.91 us (1%)
    ppermute x9, waiting for transfers between devices, col_swap(): return lax.ppermute(value, 'col', [(t ^ k, t) for t in range(self.n_col)])  15.7 us
    ppermute x9, starting transfers between devices, col_swap(): return lax.ppermute(value, 'col', [(t ^ k, t) for t in range(self.n_col)])  14.2 us
    pallas_call x1, Pallas kernels, outer_call(): pl.pallas_call(outer_body, in_specs=[SMEM] * 2 + [VMEM] * 5, out_specs=[V...  10.7 us
    ppermute x12, starting transfers between devices, row_swap(): return lax.ppermute(value, 'row', [(t ^ k, t) for t in range(self.n_row)])  9.29 us
    pallas_call x1, Pallas kernels, back_call(): pl.pallas_call(lambda *refs: back_body(*refs, seqs=seqs, n_row=n_row, n_c...  6.92 us
    pallas_call x1, Pallas kernels, right_grad_call(): pl.pallas_call(right_grad_body, in_specs=[SMEM] * 2 + [VMEM] * 4, out_spe...  5.92 us
    pallas_call x1, Pallas kernels, left_grad_call(): pl.pallas_call(left_grad_body, in_specs=[SMEM] * 2 + [VMEM] * 4, out_spec...  5.05 us
    ppermute x12, waiting for transfers between devices, row_swap(): return lax.ppermute(value, 'row', [(t ^ k, t) for t in range(self.n_row)])  4.35 us
  transfers between devices with their start and end apart: 23, of which 6 were waited for; matrix products, arithmetic and copies ran while one was open for 2% of the time, Pallas kernels for 38%

profile of v11, /device:TPU:0, one launch (start us, length us, event | category | flops | bytes accessed | tf_op | source)
XLA Modules:
  0.0 84.8 jit_solution(4026063604889490540)
XLA Ops:
  0.6 3.7 %project.1 = (bf16[32,2048]{1,0:T(8,128)(2,1)S(1)}, bf16[32,2048]{1,0:T(8,128)(2,1)S(1)}) custom-call(bf16[32,64,256]{2,1,0:T(8,128)(2,1)} %refs_0_.1, f32[1,256]{1,0:T(1,128)} %bitcast.46, f32[1,256]{1,0:T(1,128)} %bitcast.47, bf16[32,256]{1,0:T(8,128)(2,1)} %bitcast.44, bf16[32,256]{1,0:T(8,128)(2,1)} %bitcast.45), custom_call_target="tpu_custom_call" | custom-call | tf_op jit(solution)/shard_map/project/pallas_call | solution.py:122
  4.4 5.1 %collective-permute-start.2 = (bf16[32,2048]{1,0:T(8,128)(2,1)S(1)}, bf16[32,2048]{1,0:T(8,128)(2,1)S(1)}, u32[]{:S(2)}, u32[]{:S(2)}) collective-permute-start(bf16[32,2048]{1,0:T(8,128)(2,1)S(1)} %get-tuple-element.22), channel_id=1, source_target_pairs={{3,0},{2,1},{1,2},{0,3},{7,4},{6,5},{5,6},{4,7},{11,8},{10,9},{9,1... | collective-permute-start | bytes 393224 | tf_op jit(solution)/shard_map/ppermute | solution.py:549
  9.5 0.6 collective-permute-start
  10.2 0.7 collective-permute-start.3
  11.2 6.9 %back.1 = (s32[1,2048]{1,0:T(1,128)S(1)}, bf16[8,2,128,128]{3,2,1,0:T(8,128)(2,1)S(1)}, bf16[8,2,64,128]{3,2,1,0:T(8,128)(2,1)S(1)}, f32[8,64,128]{2,1,0:T(8,128...) custom-call(s32[4]{0:T(128)S(1)} %add_convert_fusion.3.refs_0_.at_ref, ...), custom_call_target="tpu_custom_call" | custom-call | flops 21474836480 | bytes 8388608 | tf_op jit(solution)/shard_map/back/pallas_call | solution.py:253
  18.2 0.8 collective-permute-done
  19.0 5.3 %collective-permute-done.1 = bf16[32,2048]{1,0:T(8,128)(2,1)S(1)} collective-permute-done((bf16[32,2048]{1,0:T(8,128)(2,1)S(1)}, bf16[32,2048]{1,0:T(8,128)(2,1)S(1)}, u32[]{:S(2)}, u32[]{:S(2)}) %collective-permute-start.1) | collective-permute-done | bytes 131104 | tf_op jit(solution)/shard_map/ppermute | solution.py:549
  24.4 5.9 %right_grad.1 = bf16[128,2048]{1,0:T(8,128)(2,1)S(1)} custom-call(s32[4]{0:T(128)S(1)} %add_convert_fusion.3.refs_0_.at_ref, s32[256]{0:T(256)S(1)} %copy-done.1, bf16[8,2048,256]{2,1,0:T(8,128)(2,1)S(1)} %get-tuple-element.26.back_ref, bf16[128,2048]{1,0:T(8,128)(2,1)S(1)} %constant_dynamic-update-slice_fusion.left_ref, ...), custom_call_target="tpu_custom_call" | custom-call | flops 21474836480 | bytes 8388608 | tf_op jit(solution)/shard_map/right_grad/pallas_call | solution.py:354
  30.3 0.2 collective-permute-start.6
  30.6 0.4 collective-permute-start.5
  31.0 1.3 %collective-permute-start.4 = (bf16[32,2048]{1,0:T(8,128)(2,1)S(1)}, bf16[32,2048]{1,0:T(8,128)(2,1)S(1)}, u32[]{:S(2)}, u32[]{:S(2)}) collective-permute-start(bf16[32,2048]{1,0:T(8,128)(2,1)S(1)} %collective-permute-done.3), channel_id=1, source_target_pairs={{4,0},{0,4},{12,8},{8,12},{5,1},{1,5},{13,9},{9,13},{6,2},{2,6},{1... | collective-permute-start | bytes 393224 | tf_op jit(solution)/shard_map/ppermute | solution.py:552
  32.4 0.5 collective-permute-start.15
  32.9 3.3 %collective-permute-done.6 = bf16[32,2048]{1,0:T(8,128)(2,1)S(1)} collective-permute-done((bf16[32,2048]{1,0:T(8,128)(2,1)S(1)}, bf16[32,2048]{1,0:T(8,128)(2,1)S(1)}, u32[]{:S(2)}, u32[]{:S(2)}) %collective-permute-start.6) | collective-permute-done | bytes 131104 | tf_op jit(solution)/shard_map/ppermute | solution.py:552
  36.2 1.0 %collective-permute-done.5 = bf16[32,2048]{1,0:T(8,128)(2,1)S(1)} collective-permute-done((bf16[32,2048]{1,0:T(8,128)(2,1)S(1)}, bf16[32,2048]{1,0:T(8,128)(2,1)S(1)}, u32[]{:S(2)}, u32[]{:S(2)}) %collective-permute-start.5) | collective-permute-done | bytes 131104 | tf_op jit(solution)/shard_map/ppermute | solution.py:552
  37.3 10.7 %outer.1 = (bf16[8,512,1024]{2,1,0:T(8,128)(2,1)S(1)}, f32[1024,128]{1,0:T(8,128)S(1)}) custom-call(s32[4]{0:T(128)S(1)} %add_convert_fusion.3.refs_0_.at_ref, s32[256]{0:T(256)S(1)} %copy-done.1, bf16[128,2048]{1,0:T(8,128)(2,1)S(1)} %constant_dynamic-update-slice_fusion.left_ref, s32[1,2048]{1,0:T(1,128)S(1)} %get-tuple-element.34.lab_ref, ...), custom_call_target="tpu_custom_call" | custom-call | flops 42949672960 | bytes 8388608 | tf_op jit(solution)/shard_map/outer/pallas_call | solution.py:490
  48.2 0.7 collective-permute-start.16
  48.9 3.6 %collective-permute-start.7 = (bf16[256,128]{1,0:T(8,128)(2,1)S(1)}, bf16[256,128]{1,0:T(8,128)(2,1)S(1)}, u32[]{:S(2)}, u32[]{:S(2)}) collective-permute-start(bf16[256,128]{1,0:T(8,128)(2,1)S(1)} %get-tuple-element.46), channel_id=1, source_target_pairs={{4,0},{0,4},{12,8},{8,12},{5,1},{1,5},{13,9},{9,13},{6,2},{2,6},{1... | collective-permute-start | bytes 196616 | tf_op jit(solution)/shard_map/ppermute | solution.py:552
  52.5 1.9 %collective-permute-start.9 = (bf16[256,128]{1,0:T(8,128)(2,1)S(1)}, bf16[256,128]{1,0:T(8,128)(2,1)S(1)}, u32[]{:S(2)}, u32[]{:S(2)}) collective-permute-start(bf16[256,128]{1,0:T(8,128)(2,1)S(1)} %get-tuple-element.47), channel_id=1, source_target_pairs={{12,0},{8,4},{4,8},{0,12},{13,1},{9,5},{5,9},{1,13},{14,2},{10,6},... | collective-permute-start | bytes 196616 | tf_op jit(solution)/shard_map/ppermute | solution.py:552
  54.3 0.3 collective-permute-start.8
  54.7 5.1 %left_grad.1 = bf16[128,2048]{1,0:T(8,128)(2,1)S(1)} custom-call(s32[4]{0:T(128)S(1)} %add_convert_fusion.3.refs_0_.at_ref, s32[256]{0:T(256)S(1)} %copy-done.1, bf16[8,2048,256]{2,1,0:T(8,128)(2,1)S(1)} %get-tuple-element.26.back_ref, s32[1,2048]{1,0:T(1,128)S(1)} %get-tuple-element.34.lab_ref, bf16[128,2048]{1,0:T(8,128)(2,1)S(1)} %pad_maximum_fusion.right_ref, ...), custom_call_target="tpu_custom_call" | custom-call | flops 21474836480 | bytes 8388608 | tf_op jit(solution)/shard_map/left_grad/pallas_call | solution.py:410
  59.8 1.6 %collective-permute-start.10 = (bf16[32,2048]{1,0:T(8,128)(2,1)S(1)}, bf16[32,2048]{1,0:T(8,128)(2,1)S(1)}, u32[]{:S(2)}, u32[]{:S(2)}) collective-permute-start(bf16[32,2048]{1,0:T(8,128)(2,1)S(1)} %get-tuple-element.43), channel_id=1, source_target_pairs={{1,0},{0,1},{3,2},{2,3},{5,4},{4,5},{7,6},{6,7},{9,8},{8,9},{11,10... | collective-permute-start | bytes 393224 | tf_op jit(solution)/shard_map/ppermute | solution.py:549
  61.5 1.8 %collective-permute-start.19 = (bf16[256,128]{1,0:T(8,128)(2,1)S(1)}, bf16[256,128]{1,0:T(8,128)(2,1)S(1)}, u32[]{:S(2)}, u32[]{:S(2)}) collective-permute-start(bf16[256,128]{1,0:T(8,128)(2,1)S(1)} %convert_element_type.112), channel_id=1, source_target_pairs={{3,0},{2,1},{1,2},{0,3},{7,4},{6,5},{5,6},{4,7},{11,8},{10,9},{9,1... | collective-permute-start | bytes 196616 | tf_op jit(solution)/shard_map/ppermute | solution.py:549
  63.5 2.5 %collective-permute-start.17 = (bf16[256,128]{1,0:T(8,128)(2,1)S(1)}, bf16[256,128]{1,0:T(8,128)(2,1)S(1)}, u32[]{:S(2)}, u32[]{:S(2)}) collective-permute-start(bf16[256,128]{1,0:T(8,128)(2,1)S(1)} %convert_element_type.112), channel_id=1, source_target_pairs={{1,0},{0,1},{3,2},{2,3},{5,4},{4,5},{7,6},{6,7},{9,8},{8,9},{11,10... | collective-permute-start | bytes 196616 | tf_op jit(solution)/shard_map/ppermute | solution.py:549
  65.9 3.3 %pair.1 = bf16[4096,128]{1,0:T(8,128)(2,1)} custom-call(bf16[8,512,1024]{2,1,0:T(8,128)(2,1)S(1)} %get-tuple-element.31.outer_ref, bf16[1024,128]{1,0:T(8,128)(2,1)S(1)} %get-tuple-element.37.w_ref, f32[1,128]{1,0:T(1,128)S(1)} %bitcast.40), custom_call_target="tpu_custom_call" | custom-call | flops 1073741824 | bytes 1048576 | tf_op jit(solution)/shard_map/pair/pallas_call | solution.py:525
  69.2 1.8 %collective-permute-start.12 = (bf16[32,2048]{1,0:T(8,128)(2,1)S(1)}, bf16[32,2048]{1,0:T(8,128)(2,1)S(1)}, u32[]{:S(2)}, u32[]{:S(2)}) collective-permute-start(bf16[32,2048]{1,0:T(8,128)(2,1)S(1)} %get-tuple-element.44), channel_id=1, source_target_pairs={{3,0},{2,1},{1,2},{0,3},{7,4},{6,5},{5,6},{4,7},{11,8},{10,9},{9,1... | collective-permute-start | bytes 393224 | tf_op jit(solution)/shard_map/ppermute | solution.py:549
  71.1 0.4 collective-permute-start.11
  71.7 0.9 %collective-permute-start.21 = (bf16[256,128]{1,0:T(8,128)(2,1)S(1)}, bf16[256,128]{1,0:T(8,128)(2,1)S(1)}, u32[]{:S(2)}, u32[]{:S(2)}) collective-permute-start(bf16[256,128]{1,0:T(8,128)(2,1)S(1)} %add_convert_fusion.2), channel_id=1, source_target_pairs={{8,0},{12,4},{0,8},{4,12},{9,1},{13,5},{1,9},{5,13},{10,2},{14,6},... | collective-permute-start | bytes 196616 | tf_op jit(solution)/shard_map/ppermute | solution.py:552
  72.6 4.7 %collective-permute-done.12 = bf16[32,2048]{1,0:T(8,128)(2,1)S(1)} collective-permute-done((bf16[32,2048]{1,0:T(8,128)(2,1)S(1)}, bf16[32,2048]{1,0:T(8,128)(2,1)S(1)}, u32[]{:S(2)}, u32[]{:S(2)}) %collective-permute-start.12) | collective-permute-done | bytes 131104 | tf_op jit(solution)/shard_map/ppermute | solution.py:549
  77.3 4.8 %collective-permute-done.11 = bf16[32,2048]{1,0:T(8,128)(2,1)S(1)} collective-permute-done((bf16[32,2048]{1,0:T(8,128)(2,1)S(1)}, bf16[32,2048]{1,0:T(8,128)(2,1)S(1)}, u32[]{:S(2)}, u32[]{:S(2)}) %collective-permute-start.11) | collective-permute-done | bytes 131104 | tf_op jit(solution)/shard_map/ppermute | solution.py:549
  82.1 0.7 add_convert_fusion.1
  82.9 1.3 %convert_multiply_fusion = f32[1024,128]{1,0:T(8,128)} fusion(pred[1024]{0:T(1024)(128)(4,1)S(1)} %broadcast_in_dim.105, pred[1024]{0:T(1024)(128)(4,1)S(1)} %broadcast_in_dim.100, pred[1024]{0:T(1024)(128)(4,1)S(1)} %broadcast_in_dim.95, bf16[256,128]{1,0:T(8,128)(2,1)S(1)} %add_convert_fusion.2, bf16[256,128]{1,0:T(8,128)(2,1)S(1)} %collective-permute-done.22, ...), kind=kLoop, calls=%fused_computation.1 | loop fusion | flops 655360 | bytes 789504 | tf_op jit(solution)/shard_map/div | solution.py:678
  84.1 0.7 copy.19
  (50 shorter events, 1.1 us)
Async XLA Ops:
  4.4 20.0 %collective-permute-start.2 = (bf16[32,2048]{1,0:T(8,128)(2,1)S(1)}, bf16[32,2048]{1,0:T(8,128)(2,1)S(1)}, u32[]{:S(2)}, u32[]{:S(2)}) collective-permute-start(bf16[32,2048]{1,0:T(8,128)(2,1)S(1)} %get-tuple-element.22), channel_id=1, source_target_pairs={{3,0},{2,1},{1,2},{0,3},{7,4},{6,5},{5,6},{4,7},{11,8},{10,9},{9,1... | collective-permute-start | bytes 393224 | tf_op jit(solution)/shard_map/ppermute | solution.py:549
  9.5 14.8 %collective-permute-start.1 = (bf16[32,2048]{1,0:T(8,128)(2,1)S(1)}, bf16[32,2048]{1,0:T(8,128)(2,1)S(1)}, u32[]{:S(2)}, u32[]{:S(2)}) collective-permute-start(bf16[32,2048]{1,0:T(8,128)(2,1)S(1)} %get-tuple-element.22), channel_id=1, source_target_pairs={{2,0},{3,1},{0,2},{1,3},{6,4},{7,5},{4,6},{5,7},{10,8},{11,9},{8,1... | collective-permute-start | bytes 393224 | tf_op jit(solution)/shard_map/ppermute | solution.py:549
  9.5 9.5 %collective-permute-start = (bf16[32,2048]{1,0:T(8,128)(2,1)S(1)}, bf16[32,2048]{1,0:T(8,128)(2,1)S(1)}, u32[]{:S(2)}, u32[]{:S(2)}) collective-permute-start(bf16[32,2048]{1,0:T(8,128)(2,1)S(1)} %get-tuple-element.22), channel_id=1, source_target_pairs={{1,0},{0,1},{3,2},{2,3},{5,4},{4,5},{7,6},{6,7},{9,8},{8,9},{11,10... | collective-permute-start | bytes 393224 | tf_op jit(solution)/shard_map/ppermute | solution.py:549
  10.2 20.2 %collective-permute-start.3 = (bf16[32,2048]{1,0:T(8,128)(2,1)S(1)}, bf16[32,2048]{1,0:T(8,128)(2,1)S(1)}, u32[]{:S(2)}, u32[]{:S(2)}) collective-permute-start(bf16[32,2048]{1,0:T(8,128)(2,1)S(1)} %get-tuple-element.23), channel_id=1, source_target_pairs={{0,0},{1,4},{2,8},{3,12},{4,1},{5,5},{6,9},{7,13},{8,2},{9,6},{10,... | collective-permute-start | bytes 393224 | tf_op jit(solution)/shard_map/ppermute | solution.py:571
  11.2 13.2 %copy-start.1 = (s32[256]{0:T(256)S(1)}, s32[256]{0:T(256)}, u32[]{:S(2)}) copy-start(s32[256]{0:T(256)} %labels_ref.5) | copy-start | bytes 3076
  30.3 5.9 %collective-permute-start.6 = (bf16[32,2048]{1,0:T(8,128)(2,1)S(1)}, bf16[32,2048]{1,0:T(8,128)(2,1)S(1)}, u32[]{:S(2)}, u32[]{:S(2)}) collective-permute-start(bf16[32,2048]{1,0:T(8,128)(2,1)S(1)} %collective-permute-done.3), channel_id=1, source_target_pairs={{12,0},{8,4},{4,8},{0,12},{13,1},{9,5},{5,9},{1,13},{14,2},{10,6},... | collective-permute-start | bytes 393224 | tf_op jit(solution)/shard_map/ppermute | solution.py:552
  30.6 6.6 %collective-permute-start.5 = (bf16[32,2048]{1,0:T(8,128)(2,1)S(1)}, bf16[32,2048]{1,0:T(8,128)(2,1)S(1)}, u32[]{:S(2)}, u32[]{:S(2)}) collective-permute-start(bf16[32,2048]{1,0:T(8,128)(2,1)S(1)} %collective-permute-done.3), channel_id=1, source_target_pairs={{8,0},{12,4},{0,8},{4,12},{9,1},{13,5},{1,9},{5,13},{10,2},{14,6},... | collective-permute-start | bytes 393224 | tf_op jit(solution)/shard_map/ppermute | solution.py:552
  31.0 6.3 %collective-permute-start.4 = (bf16[32,2048]{1,0:T(8,128)(2,1)S(1)}, bf16[32,2048]{1,0:T(8,128)(2,1)S(1)}, u32[]{:S(2)}, u32[]{:S(2)}) collective-permute-start(bf16[32,2048]{1,0:T(8,128)(2,1)S(1)} %collective-permute-done.3), channel_id=1, source_target_pairs={{4,0},{0,4},{12,8},{8,12},{5,1},{1,5},{13,9},{9,13},{6,2},{2,6},{1... | collective-permute-start | bytes 393224 | tf_op jit(solution)/shard_map/ppermute | solution.py:552
  32.3 15.8 %collective-permute-start.13 = (bf16[32,2048]{1,0:T(8,128)(2,1)S(1)}, bf16[32,2048]{1,0:T(8,128)(2,1)S(1)}, u32[]{:S(2)}, u32[]{:S(2)}) collective-permute-start(bf16[32,2048]{1,0:T(8,128)(2,1)S(1)} %get-tuple-element.40), channel_id=1, source_target_pairs={{4,0},{0,4},{12,8},{8,12},{5,1},{1,5},{13,9},{9,13},{6,2},{2,6},{1... | collective-permute-start | bytes 393224 | tf_op jit(solution)/shard_map/ppermute | solution.py:552
  32.4 15.7 %collective-permute-start.15 = (bf16[32,2048]{1,0:T(8,128)(2,1)S(1)}, bf16[32,2048]{1,0:T(8,128)(2,1)S(1)}, u32[]{:S(2)}, u32[]{:S(2)}) collective-permute-start(bf16[32,2048]{1,0:T(8,128)(2,1)S(1)} %get-tuple-element.41), channel_id=1, source_target_pairs={{12,0},{8,4},{4,8},{0,12},{13,1},{9,5},{5,9},{1,13},{14,2},{10,6},... | collective-permute-start | bytes 393224 | tf_op jit(solution)/shard_map/ppermute | solution.py:552
  36.2 11.9 %collective-permute-start.14 = (bf16[32,2048]{1,0:T(8,128)(2,1)S(1)}, bf16[32,2048]{1,0:T(8,128)(2,1)S(1)}, u32[]{:S(2)}, u32[]{:S(2)}) collective-permute-start(bf16[32,2048]{1,0:T(8,128)(2,1)S(1)} %get-tuple-element.42), channel_id=1, source_target_pairs={{8,0},{12,4},{0,8},{4,12},{9,1},{13,5},{1,9},{5,13},{10,2},{14,6},... | collective-permute-start | bytes 393224 | tf_op jit(solution)/shard_map/ppermute | solution.py:552
  48.2 34.7 %collective-permute-start.16 = (bf16[32,2048]{1,0:T(8,128)(2,1)S(1)}, bf16[32,2048]{1,0:T(8,128)(2,1)S(1)}, u32[]{:S(2)}, u32[]{:S(2)}) collective-permute-start(bf16[32,2048]{1,0:T(8,128)(2,1)S(1)} %add_convert_fusion), channel_id=1, source_target_pairs={{0,0},{4,1},{8,2},{12,3},{1,4},{5,5},{9,6},{13,7},{2,8},{6,9},{10,... | collective-permute-start | bytes 393224 | tf_op jit(solution)/shard_map/ppermute | solution.py:592
  48.9 12.5 %collective-permute-start.7 = (bf16[256,128]{1,0:T(8,128)(2,1)S(1)}, bf16[256,128]{1,0:T(8,128)(2,1)S(1)}, u32[]{:S(2)}, u32[]{:S(2)}) collective-permute-start(bf16[256,128]{1,0:T(8,128)(2,1)S(1)} %get-tuple-element.46), channel_id=1, source_target_pairs={{4,0},{0,4},{12,8},{8,12},{5,1},{1,5},{13,9},{9,13},{6,2},{2,6},{1... | collective-permute-start | bytes 196616 | tf_op jit(solution)/shard_map/ppermute | solution.py:552
  52.5 8.9 %collective-permute-start.9 = (bf16[256,128]{1,0:T(8,128)(2,1)S(1)}, bf16[256,128]{1,0:T(8,128)(2,1)S(1)}, u32[]{:S(2)}, u32[]{:S(2)}) collective-permute-start(bf16[256,128]{1,0:T(8,128)(2,1)S(1)} %get-tuple-element.47), channel_id=1, source_target_pairs={{12,0},{8,4},{4,8},{0,12},{13,1},{9,5},{5,9},{1,13},{14,2},{10,6},... | collective-permute-start | bytes 196616 | tf_op jit(solution)/shard_map/ppermute | solution.py:552
  54.3 7.1 %collective-permute-start.8 = (bf16[256,128]{1,0:T(8,128)(2,1)S(1)}, bf16[256,128]{1,0:T(8,128)(2,1)S(1)}, u32[]{:S(2)}, u32[]{:S(2)}) collective-permute-start(bf16[256,128]{1,0:T(8,128)(2,1)S(1)} %get-tuple-element.48), channel_id=1, source_target_pairs={{8,0},{12,4},{0,8},{4,12},{9,1},{13,5},{1,9},{5,13},{10,2},{14,6},... | collective-permute-start | bytes 196616 | tf_op jit(solution)/shard_map/ppermute | solution.py:552
  54.7 11.3 %copy-start = (f32[128]{0:T(128)S(1)}, f32[128]{0:T(128)}, u32[]{:S(2)}) copy-start(f32[128]{0:T(128)} %param.16) | copy-start | bytes 1540
  59.8 11.9 %collective-permute-start.10 = (bf16[32,2048]{1,0:T(8,128)(2,1)S(1)}, bf16[32,2048]{1,0:T(8,128)(2,1)S(1)}, u32[]{:S(2)}, u32[]{:S(2)}) collective-permute-start(bf16[32,2048]{1,0:T(8,128)(2,1)S(1)} %get-tuple-element.43), channel_id=1, source_target_pairs={{1,0},{0,1},{3,2},{2,3},{5,4},{4,5},{7,6},{6,7},{9,8},{8,9},{11,10... | collective-permute-start | bytes 393224 | tf_op jit(solution)/shard_map/ppermute | solution.py:549
  61.5 7.8 %collective-permute-start.19 = (bf16[256,128]{1,0:T(8,128)(2,1)S(1)}, bf16[256,128]{1,0:T(8,128)(2,1)S(1)}, u32[]{:S(2)}, u32[]{:S(2)}) collective-permute-start(bf16[256,128]{1,0:T(8,128)(2,1)S(1)} %convert_element_type.112), channel_id=1, source_target_pairs={{3,0},{2,1},{1,2},{0,3},{7,4},{6,5},{5,6},{4,7},{11,8},{10,9},{9,1... | collective-permute-start | bytes 196616 | tf_op jit(solution)/shard_map/ppermute | solution.py:549
  63.3 7.8 %collective-permute-start.18 = (bf16[256,128]{1,0:T(8,128)(2,1)S(1)}, bf16[256,128]{1,0:T(8,128)(2,1)S(1)}, u32[]{:S(2)}, u32[]{:S(2)}) collective-permute-start(bf16[256,128]{1,0:T(8,128)(2,1)S(1)} %convert_element_type.112), channel_id=1, source_target_pairs={{2,0},{3,1},{0,2},{1,3},{6,4},{7,5},{4,6},{5,7},{10,8},{11,9},{8,1... | collective-permute-start | bytes 196616 | tf_op jit(solution)/shard_map/ppermute | solution.py:549
  63.5 8.1 %collective-permute-start.17 = (bf16[256,128]{1,0:T(8,128)(2,1)S(1)}, bf16[256,128]{1,0:T(8,128)(2,1)S(1)}, u32[]{:S(2)}, u32[]{:S(2)}) collective-permute-start(bf16[256,128]{1,0:T(8,128)(2,1)S(1)} %convert_element_type.112), channel_id=1, source_target_pairs={{1,0},{0,1},{3,2},{2,3},{5,4},{4,5},{7,6},{6,7},{9,8},{8,9},{11,10... | collective-permute-start | bytes 196616 | tf_op jit(solution)/shard_map/ppermute | solution.py:549
  69.2 8.0 %collective-permute-start.12 = (bf16[32,2048]{1,0:T(8,128)(2,1)S(1)}, bf16[32,2048]{1,0:T(8,128)(2,1)S(1)}, u32[]{:S(2)}, u32[]{:S(2)}) collective-permute-start(bf16[32,2048]{1,0:T(8,128)(2,1)S(1)} %get-tuple-element.44), channel_id=1, source_target_pairs={{3,0},{2,1},{1,2},{0,3},{7,4},{6,5},{5,6},{4,7},{11,8},{10,9},{9,1... | collective-permute-start | bytes 393224 | tf_op jit(solution)/shard_map/ppermute | solution.py:549
  71.1 11.0 %collective-permute-start.11 = (bf16[32,2048]{1,0:T(8,128)(2,1)S(1)}, bf16[32,2048]{1,0:T(8,128)(2,1)S(1)}, u32[]{:S(2)}, u32[]{:S(2)}) collective-permute-start(bf16[32,2048]{1,0:T(8,128)(2,1)S(1)} %get-tuple-element.45), channel_id=1, source_target_pairs={{2,0},{3,1},{0,2},{1,3},{6,4},{7,5},{4,6},{5,7},{10,8},{11,9},{8,1... | collective-permute-start | bytes 393224 | tf_op jit(solution)/shard_map/ppermute | solution.py:549
  71.6 11.3 %collective-permute-start.22 = (bf16[256,128]{1,0:T(8,128)(2,1)S(1)}, bf16[256,128]{1,0:T(8,128)(2,1)S(1)}, u32[]{:S(2)}, u32[]{:S(2)}) collective-permute-start(bf16[256,128]{1,0:T(8,128)(2,1)S(1)} %add_convert_fusion.2), channel_id=1, source_target_pairs={{4,0},{0,4},{12,8},{8,12},{5,1},{1,5},{13,9},{9,13},{6,2},{2,6},{1... | collective-permute-start | bytes 196616 | tf_op jit(solution)/shard_map/ppermute | solution.py:552
  71.7 11.2 %collective-permute-start.21 = (bf16[256,128]{1,0:T(8,128)(2,1)S(1)}, bf16[256,128]{1,0:T(8,128)(2,1)S(1)}, u32[]{:S(2)}, u32[]{:S(2)}) collective-permute-start(bf16[256,128]{1,0:T(8,128)(2,1)S(1)} %add_convert_fusion.2), channel_id=1, source_target_pairs={{8,0},{12,4},{0,8},{4,12},{9,1},{13,5},{1,9},{5,13},{10,2},{14,6},... | collective-permute-start | bytes 196616 | tf_op jit(solution)/shard_map/ppermute | solution.py:552
  77.3 5.6 %collective-permute-start.20 = (bf16[256,128]{1,0:T(8,128)(2,1)S(1)}, bf16[256,128]{1,0:T(8,128)(2,1)S(1)}, u32[]{:S(2)}, u32[]{:S(2)}) collective-permute-start(bf16[256,128]{1,0:T(8,128)(2,1)S(1)} %add_convert_fusion.2), channel_id=1, source_target_pairs={{12,0},{8,4},{4,8},{0,12},{13,1},{9,5},{5,9},{1,13},{14,2},{10,6},... | collective-permute-start | bytes 196616 | tf_op jit(solution)/shard_map/ppermute | solution.py:552

commit v12 on v11

--- a/solution.py
+++ b/solution.py
@@ -577,10 +577,8 @@
 
     def right_grad_along_row(self, grad):
         size = grad.shape[0] // self.n_row
-        total = grad[:size].astype(F32)
-        for k in range(1, self.n_row):
-            total += self.row_swap(grad[k * size : (k + 1) * size], k).astype(F32)
-        return total.astype(BF16)
+        swaps = [self.row_swap(grad[k * size : (k + 1) * size], k) for k in range(1, self.n_row)]
+        return [grad[:size]] + swaps
 
     def right_grad_home(self, mine):
         m = self.per_row
@@ -662,7 +660,7 @@
     right_grad = right_grad_call(at, labels, back, left, lab, plain)
 
     right = after(right, right_grad)
-    mine = ring.right_grad_along_row(right_grad)
+    parts = ring.right_grad_along_row(right_grad)
     outer, weight = outer_call(
         at, labels, left, lab, right, wide, grad
     )
@@ -670,7 +668,9 @@
     left_grad = left_grad_call(at, labels, back, after(lab, weight), right, tall)
     share = after(share, left_grad)
 
-    grad_right = ring.right_grad_home(after(mine, weight))
+    parts = lax.optimization_barrier((*parts, share))[:-1]
+    mine = sum(part.astype(F32) for part in parts).astype(BF16)
+    grad_right = ring.right_grad_home(mine)
     adjoint_first = ring.left_grad_along_col(left_grad)
     pair_update = pair_call(in_vmem(outer), after(w, left_grad, share), final_offset[None, :])
     pair_update = pair_update.reshape(rows, cols, width)

time: 85 us -> 89.1 us (1.048)
  starting transfers between devices: 24.8 us -> 27.7 us
  waiting for transfers between devices: 20 us -> 21.2 us
    ppermute x12, waiting for transfers between devices: 4.35 us -> 8.44 us  [row_swap(): return lax.ppermute(value, 'row', [(t ^ k, t) for t in range(self.n_row)])]
    ppermute x9, waiting for transfers between devices: 15.7 us -> 12.8 us  [col_swap(): return lax.ppermute(value, 'col', [(t ^ k, t) for t in range(self.n_col)])]
    ppermute x12, starting transfers between devices: 9.29 us -> 11.1 us  [row_swap(): return lax.ppermute(value, 'row', [(t ^ k, t) for t in range(self.n_row)])]
    ppermute x9, starting transfers between devices: 14.2 us -> 15.3 us  [col_swap(): return lax.ppermute(value, 'col', [(t ^ k, t) for t in range(self.n_col)])]
  transfers between devices with their start and end apart: 23 -> 23, of which waited for: 6 -> 6; matrix products, arithmetic and copies ran while one was open for 2% -> 2% of each run, Pallas kernels for 38% -> 36%
where the time goes in v12:
time: 89.1 us; the launch traced here: 89 us
  Pallas kernels  35.7 us (40%)
  starting transfers between devices  27.7 us (31%)
  waiting for transfers between devices  21.2 us (24%)
  other arithmetic  2.31 us (3%)
  local copies, waits for them, and re-layouts  1.12 us (1%)
  between operations  0.91 us (1%)
    ppermute x9, starting transfers between devices, col_swap(): return lax.ppermute(value, 'col', [(t ^ k, t) for t in range(self.n_col)])  15.3 us
    ppermute x9, waiting for transfers between devices, col_swap(): return lax.ppermute(value, 'col', [(t ^ k, t) for t in range(self.n_col)])  12.8 us
    ppermute x12, starting transfers between devices, row_swap(): return lax.ppermute(value, 'row', [(t ^ k, t) for t in range(self.n_row)])  11.1 us
    pallas_call x1, Pallas kernels, outer_call(): pl.pallas_call(outer_body, in_specs=[SMEM] * 2 + [VMEM] * 5, out_specs=[V...  10.7 us
    ppermute x12, waiting for transfers between devices, row_swap(): return lax.ppermute(value, 'row', [(t ^ k, t) for t in range(self.n_row)])  8.44 us
    pallas_call x1, Pallas kernels, back_call(): pl.pallas_call(lambda *refs: back_body(*refs, seqs=seqs, n_row=n_row, n_c...  6.92 us
    pallas_call x1, Pallas kernels, right_grad_call(): pl.pallas_call(right_grad_body, in_specs=[SMEM] * 2 + [VMEM] * 4, out_spe...  5.91 us
    pallas_call x1, Pallas kernels, left_grad_call(): pl.pallas_call(left_grad_body, in_specs=[SMEM] * 2 + [VMEM] * 4, out_spec...  5.03 us
  transfers between devices with their start and end apart: 23, of which 6 were waited for; matrix products, arithmetic and copies ran while one was open for 2% of the time, Pallas kernels for 36%

profile of v12, /device:TPU:0, one launch (start us, length us, event | category | flops | bytes accessed | tf_op | source)
XLA Modules:
  0.0 89.0 jit_solution(7414742524353315540)
XLA Ops:
  0.6 3.7 %project.1 = (bf16[32,2048]{1,0:T(8,128)(2,1)S(1)}, bf16[32,2048]{1,0:T(8,128)(2,1)S(1)}) custom-call(bf16[32,64,256]{2,1,0:T(8,128)(2,1)} %refs_0_.1, f32[1,256]{1,0:T(1,128)} %bitcast.46, f32[1,256]{1,0:T(1,128)} %bitcast.47, bf16[32,256]{1,0:T(8,128)(2,1)} %bitcast.44, bf16[32,256]{1,0:T(8,128)(2,1)} %bitcast.45), custom_call_target="tpu_custom_call" | custom-call | tf_op jit(solution)/shard_map/project/pallas_call | solution.py:122
  4.4 3.1 %collective-permute-start = (bf16[32,2048]{1,0:T(8,128)(2,1)S(1)}, bf16[32,2048]{1,0:T(8,128)(2,1)S(1)}, u32[]{:S(2)}, u32[]{:S(2)}) collective-permute-start(bf16[32,2048]{1,0:T(8,128)(2,1)S(1)} %get-tuple-element.25), channel_id=1, source_target_pairs={{1,0},{0,1},{3,2},{2,3},{5,4},{4,5},{7,6},{6,7},{9,8},{8,9},{11,10... | collective-permute-start | bytes 393224 | tf_op jit(solution)/shard_map/ppermute | solution.py:549
  7.5 2.6 %collective-permute-start.1 = (bf16[32,2048]{1,0:T(8,128)(2,1)S(1)}, bf16[32,2048]{1,0:T(8,128)(2,1)S(1)}, u32[]{:S(2)}, u32[]{:S(2)}) collective-permute-start(bf16[32,2048]{1,0:T(8,128)(2,1)S(1)} %get-tuple-element.25), channel_id=1, source_target_pairs={{2,0},{3,1},{0,2},{1,3},{6,4},{7,5},{4,6},{5,7},{10,8},{11,9},{8,1... | collective-permute-start | bytes 393224 | tf_op jit(solution)/shard_map/ppermute | solution.py:549
  10.1 0.7 collective-permute-start.3
  11.2 6.9 %back.1 = (s32[1,2048]{1,0:T(1,128)S(1)}, bf16[8,2,128,128]{3,2,1,0:T(8,128)(2,1)S(1)}, bf16[8,2,64,128]{3,2,1,0:T(8,128)(2,1)S(1)}, f32[8,64,128]{2,1,0:T(8,128...) custom-call(s32[4]{0:T(128)S(1)} %add_convert_fusion.3.refs_0_.at_ref, ...), custom_call_target="tpu_custom_call" | custom-call | flops 21474836480 | bytes 8388608 | tf_op jit(solution)/shard_map/back/pallas_call | solution.py:253
  18.2 5.0 %collective-permute-done.1 = bf16[32,2048]{1,0:T(8,128)(2,1)S(1)} collective-permute-done((bf16[32,2048]{1,0:T(8,128)(2,1)S(1)}, bf16[32,2048]{1,0:T(8,128)(2,1)S(1)}, u32[]{:S(2)}, u32[]{:S(2)}) %collective-permute-start.1) | collective-permute-done | bytes 131104 | tf_op jit(solution)/shard_map/ppermute | solution.py:549
  23.3 5.9 %right_grad.1 = bf16[128,2048]{1,0:T(8,128)(2,1)S(1)} custom-call(s32[4]{0:T(128)S(1)} %add_convert_fusion.3.refs_0_.at_ref, s32[256]{0:T(256)S(1)} %copy-done.1, bf16[8,2048,256]{2,1,0:T(8,128)(2,1)S(1)} %get-tuple-element.29.back_ref, bf16[128,2048]{1,0:T(8,128)(2,1)S(1)} %constant_dynamic-update-slice_fusion.left_ref, ...), custom_call_target="tpu_custom_call" | custom-call | flops 21474836480 | bytes 8388608 | tf_op jit(solution)/shard_map/right_grad/pallas_call | solution.py:354
  29.3 1.7 %collective-permute-start.5 = (bf16[32,2048]{1,0:T(8,128)(2,1)S(1)}, bf16[32,2048]{1,0:T(8,128)(2,1)S(1)}, u32[]{:S(2)}, u32[]{:S(2)}) collective-permute-start(bf16[32,2048]{1,0:T(8,128)(2,1)S(1)} %collective-permute-done.3), channel_id=1, source_target_pairs={{8,0},{12,4},{0,8},{4,12},{9,1},{13,5},{1,9},{5,13},{10,2},{14,6},... | collective-permute-start | bytes 393224 | tf_op jit(solution)/shard_map/ppermute | solution.py:552
  31.1 0.4 collective-permute-start.13
  31.6 1.7 %collective-permute-start.14 = (bf16[32,2048]{1,0:T(8,128)(2,1)S(1)}, bf16[32,2048]{1,0:T(8,128)(2,1)S(1)}, u32[]{:S(2)}, u32[]{:S(2)}) collective-permute-start(bf16[32,2048]{1,0:T(8,128)(2,1)S(1)} %get-tuple-element.47), channel_id=1, source_target_pairs={{8,0},{12,4},{0,8},{4,12},{9,1},{13,5},{1,9},{5,13},{10,2},{14,6},... | collective-permute-start | bytes 393224 | tf_op jit(solution)/shard_map/ppermute | solution.py:552
  33.2 2.5 %collective-permute-done.5 = bf16[32,2048]{1,0:T(8,128)(2,1)S(1)} collective-permute-done((bf16[32,2048]{1,0:T(8,128)(2,1)S(1)}, bf16[32,2048]{1,0:T(8,128)(2,1)S(1)}, u32[]{:S(2)}, u32[]{:S(2)}) %collective-permute-start.5) | collective-permute-done | bytes 131104 | tf_op jit(solution)/shard_map/ppermute | solution.py:552
  35.7 2.0 %collective-permute-done.6 = bf16[32,2048]{1,0:T(8,128)(2,1)S(1)} collective-permute-done((bf16[32,2048]{1,0:T(8,128)(2,1)S(1)}, bf16[32,2048]{1,0:T(8,128)(2,1)S(1)}, u32[]{:S(2)}, u32[]{:S(2)}) %collective-permute-start.6) | collective-permute-done | bytes 131104 | tf_op jit(solution)/shard_map/ppermute | solution.py:552
  37.7 10.7 %outer.1 = (bf16[8,512,1024]{2,1,0:T(8,128)(2,1)S(1)}, f32[1024,128]{1,0:T(8,128)S(1)}) custom-call(s32[4]{0:T(128)S(1)} %add_convert_fusion.3.refs_0_.at_ref, s32[256]{0:T(256)S(1)} %copy-done.1, bf16[128,2048]{1,0:T(8,128)(2,1)S(1)} %constant_dynamic-update-slice_fusion.left_ref, s32[1,2048]{1,0:T(1,128)S(1)} %get-tuple-element.37.lab_ref, ...), custom_call_target="tpu_custom_call" | custom-call | flops 42949672960 | bytes 8388608 | tf_op jit(solution)/shard_map/outer/pallas_call | solution.py:490
  48.5 1.4 %collective-permute-start.7 = (bf16[256,128]{1,0:T(8,128)(2,1)S(1)}, bf16[256,128]{1,0:T(8,128)(2,1)S(1)}, u32[]{:S(2)}, u32[]{:S(2)}) collective-permute-start(bf16[256,128]{1,0:T(8,128)(2,1)S(1)} %get-tuple-element.53), channel_id=1, source_target_pairs={{4,0},{0,4},{12,8},{8,12},{5,1},{1,5},{13,9},{9,13},{6,2},{2,6},{1... | collective-permute-start | bytes 196616 | tf_op jit(solution)/shard_map/ppermute | solution.py:552
  49.9 1.0 %collective-permute-start.8 = (bf16[256,128]{1,0:T(8,128)(2,1)S(1)}, bf16[256,128]{1,0:T(8,128)(2,1)S(1)}, u32[]{:S(2)}, u32[]{:S(2)}) collective-permute-start(bf16[256,128]{1,0:T(8,128)(2,1)S(1)} %get-tuple-element.55), channel_id=1, source_target_pairs={{8,0},{12,4},{0,8},{4,12},{9,1},{13,5},{1,9},{5,13},{10,2},{14,6},... | collective-permute-start | bytes 196616 | tf_op jit(solution)/shard_map/ppermute | solution.py:552
  50.9 0.4 collective-permute-start.9
  51.4 5.0 %left_grad.1 = bf16[128,2048]{1,0:T(8,128)(2,1)S(1)} custom-call(s32[4]{0:T(128)S(1)} %add_convert_fusion.3.refs_0_.at_ref, s32[256]{0:T(256)S(1)} %copy-done.1, bf16[8,2048,256]{2,1,0:T(8,128)(2,1)S(1)} %get-tuple-element.29.back_ref, s32[1,2048]{1,0:T(1,128)S(1)} %get-tuple-element.37.lab_ref, bf16[128,2048]{1,0:T(8,128)(2,1)S(1)} %pad_maximum_fusion.right_ref, ...), custom_call_target="tpu_custom_call" | custom-call | flops 21474836480 | bytes 8388608 | tf_op jit(solution)/shard_map/left_grad/pallas_call | solution.py:410
  56.5 1.4 %collective-permute-start.15 = (bf16[32,2048]{1,0:T(8,128)(2,1)S(1)}, bf16[32,2048]{1,0:T(8,128)(2,1)S(1)}, u32[]{:S(2)}, u32[]{:S(2)}) collective-permute-start(bf16[32,2048]{1,0:T(8,128)(2,1)S(1)} %get-tuple-element.46), channel_id=1, source_target_pairs={{12,0},{8,4},{4,8},{0,12},{13,1},{9,5},{5,9},{1,13},{14,2},{10,6},... | collective-permute-start | bytes 393224 | tf_op jit(solution)/shard_map/ppermute | solution.py:552
  57.8 2.4 %collective-permute-start.10 = (bf16[32,2048]{1,0:T(8,128)(2,1)S(1)}, bf16[32,2048]{1,0:T(8,128)(2,1)S(1)}, u32[]{:S(2)}, u32[]{:S(2)}) collective-permute-start(bf16[32,2048]{1,0:T(8,128)(2,1)S(1)} %get-tuple-element.50), channel_id=1, source_target_pairs={{1,0},{0,1},{3,2},{2,3},{5,4},{4,5},{7,6},{6,7},{9,8},{8,9},{11,10... | collective-permute-start | bytes 393224 | tf_op jit(solution)/shard_map/ppermute | solution.py:549
  60.2 1.3 %collective-permute-start.11 = (bf16[32,2048]{1,0:T(8,128)(2,1)S(1)}, bf16[32,2048]{1,0:T(8,128)(2,1)S(1)}, u32[]{:S(2)}, u32[]{:S(2)}) collective-permute-start(bf16[32,2048]{1,0:T(8,128)(2,1)S(1)} %get-tuple-element.52), channel_id=1, source_target_pairs={{2,0},{3,1},{0,2},{1,3},{6,4},{7,5},{4,6},{5,7},{10,8},{11,9},{8,1... | collective-permute-start | bytes 393224 | tf_op jit(solution)/shard_map/ppermute | solution.py:549
  61.5 2.0 %collective-permute-start.17 = (bf16[256,128]{1,0:T(8,128)(2,1)S(1)}, bf16[256,128]{1,0:T(8,128)(2,1)S(1)}, u32[]{:S(2)}, u32[]{:S(2)}) collective-permute-start(bf16[256,128]{1,0:T(8,128)(2,1)S(1)} %convert_element_type.112), channel_id=1, source_target_pairs={{1,0},{0,1},{3,2},{2,3},{5,4},{4,5},{7,6},{6,7},{9,8},{8,9},{11,10... | collective-permute-start | bytes 196616 | tf_op jit(solution)/shard_map/ppermute | solution.py:549
  63.5 2.4 %collective-permute-start.19 = (bf16[256,128]{1,0:T(8,128)(2,1)S(1)}, bf16[256,128]{1,0:T(8,128)(2,1)S(1)}, u32[]{:S(2)}, u32[]{:S(2)}) collective-permute-start(bf16[256,128]{1,0:T(8,128)(2,1)S(1)} %convert_element_type.112), channel_id=1, source_target_pairs={{3,0},{2,1},{1,2},{0,3},{7,4},{6,5},{5,6},{4,7},{11,8},{10,9},{9,1... | collective-permute-start | bytes 196616 | tf_op jit(solution)/shard_map/ppermute | solution.py:549
  66.1 3.3 %pair.1 = bf16[4096,128]{1,0:T(8,128)(2,1)} custom-call(bf16[8,512,1024]{2,1,0:T(8,128)(2,1)S(1)} %get-tuple-element.34.outer_ref, bf16[1024,128]{1,0:T(8,128)(2,1)S(1)} %get-tuple-element.40.w_ref, f32[1,128]{1,0:T(1,128)S(1)} %bitcast.40), custom_call_target="tpu_custom_call" | custom-call | flops 1073741824 | bytes 1048576 | tf_op jit(solution)/shard_map/pair/pallas_call | solution.py:525
  69.4 1.5 %collective-permute-start.12 = (bf16[32,2048]{1,0:T(8,128)(2,1)S(1)}, bf16[32,2048]{1,0:T(8,128)(2,1)S(1)}, u32[]{:S(2)}, u32[]{:S(2)}) collective-permute-start(bf16[32,2048]{1,0:T(8,128)(2,1)S(1)} %get-tuple-element.51), channel_id=1, source_target_pairs={{3,0},{2,1},{1,2},{0,3},{7,4},{6,5},{5,6},{4,7},{11,8},{10,9},{9,1... | collective-permute-start | bytes 393224 | tf_op jit(solution)/shard_map/ppermute | solution.py:549
  70.9 7.8 %collective-permute-done.18 = bf16[256,128]{1,0:T(8,128)(2,1)S(1)} collective-permute-done((bf16[256,128]{1,0:T(8,128)(2,1)S(1)}, bf16[256,128]{1,0:T(8,128)(2,1)S(1)}, u32[]{:S(2)}, u32[]{:S(2)}) %collective-permute-start.18) | collective-permute-done | bytes 65568 | tf_op jit(solution)/shard_map/ppermute | solution.py:549
  78.7 0.7 collective-permute-start.16
  79.4 2.7 %collective-permute-start.20 = (bf16[256,128]{1,0:T(8,128)(2,1)S(1)}, bf16[256,128]{1,0:T(8,128)(2,1)S(1)}, u32[]{:S(2)}, u32[]{:S(2)}) collective-permute-start(bf16[256,128]{1,0:T(8,128)(2,1)S(1)} %add_convert_fusion.2), channel_id=1, source_target_pairs={{12,0},{8,4},{4,8},{0,12},{13,1},{9,5},{5,9},{1,13},{14,2},{10,6},... | collective-permute-start | bytes 196616 | tf_op jit(solution)/shard_map/ppermute | solution.py:552
  82.3 0.7 add_convert_fusion.1
  83.1 2.1 %collective-permute-done.20 = bf16[256,128]{1,0:T(8,128)(2,1)S(1)} collective-permute-done((bf16[256,128]{1,0:T(8,128)(2,1)S(1)}, bf16[256,128]{1,0:T(8,128)(2,1)S(1)}, u32[]{:S(2)}, u32[]{:S(2)}) %collective-permute-start.20) | collective-permute-done | bytes 65568 | tf_op jit(solution)/shard_map/ppermute | solution.py:552
  85.2 1.8 %collective-permute-done.21 = bf16[256,128]{1,0:T(8,128)(2,1)S(1)} collective-permute-done((bf16[256,128]{1,0:T(8,128)(2,1)S(1)}, bf16[256,128]{1,0:T(8,128)(2,1)S(1)}, u32[]{:S(2)}, u32[]{:S(2)}) %collective-permute-start.21) | collective-permute-done | bytes 65568 | tf_op jit(solution)/shard_map/ppermute | solution.py:552
  87.0 1.3 %convert_multiply_fusion = f32[1024,128]{1,0:T(8,128)} fusion(pred[1024]{0:T(1024)(128)(4,1)S(1)} %broadcast_in_dim.105, pred[1024]{0:T(1024)(128)(4,1)S(1)} %broadcast_in_dim.100, pred[1024]{0:T(1024)(128)(4,1)S(1)} %broadcast_in_dim.95, bf16[256,128]{1,0:T(8,128)(2,1)S(1)} %add_convert_fusion.2, bf16[256,128]{1,0:T(8,128)(2,1)S(1)} %collective-permute-done.22, ...), kind=kLoop, calls=%fused_computation.1 | loop fusion | flops 655360 | bytes 789504 | tf_op jit(solution)/shard_map/div | solution.py:678
  88.3 0.7 copy.19
  (50 shorter events, 1.2 us)
Async XLA Ops:
  4.4 13.8 %collective-permute-start = (bf16[32,2048]{1,0:T(8,128)(2,1)S(1)}, bf16[32,2048]{1,0:T(8,128)(2,1)S(1)}, u32[]{:S(2)}, u32[]{:S(2)}) collective-permute-start(bf16[32,2048]{1,0:T(8,128)(2,1)S(1)} %get-tuple-element.25), channel_id=1, source_target_pairs={{1,0},{0,1},{3,2},{2,3},{5,4},{4,5},{7,6},{6,7},{9,8},{8,9},{11,10... | collective-permute-start | bytes 393224 | tf_op jit(solution)/shard_map/ppermute | solution.py:549
  7.5 15.7 %collective-permute-start.1 = (bf16[32,2048]{1,0:T(8,128)(2,1)S(1)}, bf16[32,2048]{1,0:T(8,128)(2,1)S(1)}, u32[]{:S(2)}, u32[]{:S(2)}) collective-permute-start(bf16[32,2048]{1,0:T(8,128)(2,1)S(1)} %get-tuple-element.25), channel_id=1, source_target_pairs={{2,0},{3,1},{0,2},{1,3},{6,4},{7,5},{4,6},{5,7},{10,8},{11,9},{8,1... | collective-permute-start | bytes 393224 | tf_op jit(solution)/shard_map/ppermute | solution.py:549
  10.1 13.1 %collective-permute-start.2 = (bf16[32,2048]{1,0:T(8,128)(2,1)S(1)}, bf16[32,2048]{1,0:T(8,128)(2,1)S(1)}, u32[]{:S(2)}, u32[]{:S(2)}) collective-permute-start(bf16[32,2048]{1,0:T(8,128)(2,1)S(1)} %get-tuple-element.25), channel_id=1, source_target_pairs={{3,0},{2,1},{1,2},{0,3},{7,4},{6,5},{5,6},{4,7},{11,8},{10,9},{9,1... | collective-permute-start | bytes 393224 | tf_op jit(solution)/shard_map/ppermute | solution.py:549
  10.1 19.1 %collective-permute-start.3 = (bf16[32,2048]{1,0:T(8,128)(2,1)S(1)}, bf16[32,2048]{1,0:T(8,128)(2,1)S(1)}, u32[]{:S(2)}, u32[]{:S(2)}) collective-permute-start(bf16[32,2048]{1,0:T(8,128)(2,1)S(1)} %get-tuple-element.26), channel_id=1, source_target_pairs={{0,0},{1,4},{2,8},{3,12},{4,1},{5,5},{6,9},{7,13},{8,2},{9,6},{10,... | collective-permute-start | bytes 393224 | tf_op jit(solution)/shard_map/ppermute | solution.py:571
  11.1 12.1 %copy-start.1 = (s32[256]{0:T(256)S(1)}, s32[256]{0:T(256)}, u32[]{:S(2)}) copy-start(s32[256]{0:T(256)} %labels_ref.5) | copy-start | bytes 3076
  29.2 4.1 %collective-permute-start.4 = (bf16[32,2048]{1,0:T(8,128)(2,1)S(1)}, bf16[32,2048]{1,0:T(8,128)(2,1)S(1)}, u32[]{:S(2)}, u32[]{:S(2)}) collective-permute-start(bf16[32,2048]{1,0:T(8,128)(2,1)S(1)} %collective-permute-done.3), channel_id=1, source_target_pairs={{4,0},{0,4},{12,8},{8,12},{5,1},{1,5},{13,9},{9,13},{6,2},{2,6},{1... | collective-permute-start | bytes 393224 | tf_op jit(solution)/shard_map/ppermute | solution.py:552
  29.3 6.4 %collective-permute-start.5 = (bf16[32,2048]{1,0:T(8,128)(2,1)S(1)}, bf16[32,2048]{1,0:T(8,128)(2,1)S(1)}, u32[]{:S(2)}, u32[]{:S(2)}) collective-permute-start(bf16[32,2048]{1,0:T(8,128)(2,1)S(1)} %collective-permute-done.3), channel_id=1, source_target_pairs={{8,0},{12,4},{0,8},{4,12},{9,1},{13,5},{1,9},{5,13},{10,2},{14,6},... | collective-permute-start | bytes 393224 | tf_op jit(solution)/shard_map/ppermute | solution.py:552
  31.0 6.7 %collective-permute-start.6 = (bf16[32,2048]{1,0:T(8,128)(2,1)S(1)}, bf16[32,2048]{1,0:T(8,128)(2,1)S(1)}, u32[]{:S(2)}, u32[]{:S(2)}) collective-permute-start(bf16[32,2048]{1,0:T(8,128)(2,1)S(1)} %collective-permute-done.3), channel_id=1, source_target_pairs={{12,0},{8,4},{4,8},{0,12},{13,1},{9,5},{5,9},{1,13},{14,2},{10,6},... | collective-permute-start | bytes 393224 | tf_op jit(solution)/shard_map/ppermute | solution.py:552
  31.1 30.4 %collective-permute-start.13 = (bf16[32,2048]{1,0:T(8,128)(2,1)S(1)}, bf16[32,2048]{1,0:T(8,128)(2,1)S(1)}, u32[]{:S(2)}, u32[]{:S(2)}) collective-permute-start(bf16[32,2048]{1,0:T(8,128)(2,1)S(1)} %get-tuple-element.48), channel_id=1, source_target_pairs={{4,0},{0,4},{12,8},{8,12},{5,1},{1,5},{13,9},{9,13},{6,2},{2,6},{1... | collective-permute-start | bytes 393224 | tf_op jit(solution)/shard_map/ppermute | solution.py:552
  31.6 32.0 %collective-permute-start.14 = (bf16[32,2048]{1,0:T(8,128)(2,1)S(1)}, bf16[32,2048]{1,0:T(8,128)(2,1)S(1)}, u32[]{:S(2)}, u32[]{:S(2)}) collective-permute-start(bf16[32,2048]{1,0:T(8,128)(2,1)S(1)} %get-tuple-element.47), channel_id=1, source_target_pairs={{8,0},{12,4},{0,8},{4,12},{9,1},{13,5},{1,9},{5,13},{10,2},{14,6},... | collective-permute-start | bytes 393224 | tf_op jit(solution)/shard_map/ppermute | solution.py:552
  48.5 7.9 %collective-permute-start.7 = (bf16[256,128]{1,0:T(8,128)(2,1)S(1)}, bf16[256,128]{1,0:T(8,128)(2,1)S(1)}, u32[]{:S(2)}, u32[]{:S(2)}) collective-permute-start(bf16[256,128]{1,0:T(8,128)(2,1)S(1)} %get-tuple-element.53), channel_id=1, source_target_pairs={{4,0},{0,4},{12,8},{8,12},{5,1},{1,5},{13,9},{9,13},{6,2},{2,6},{1... | collective-permute-start | bytes 196616 | tf_op jit(solution)/shard_map/ppermute | solution.py:552
  49.9 7.9 %collective-permute-start.8 = (bf16[256,128]{1,0:T(8,128)(2,1)S(1)}, bf16[256,128]{1,0:T(8,128)(2,1)S(1)}, u32[]{:S(2)}, u32[]{:S(2)}) collective-permute-start(bf16[256,128]{1,0:T(8,128)(2,1)S(1)} %get-tuple-element.55), channel_id=1, source_target_pairs={{8,0},{12,4},{0,8},{4,12},{9,1},{13,5},{1,9},{5,13},{10,2},{14,6},... | collective-permute-start | bytes 196616 | tf_op jit(solution)/shard_map/ppermute | solution.py:552
  50.9 9.3 %collective-permute-start.9 = (bf16[256,128]{1,0:T(8,128)(2,1)S(1)}, bf16[256,128]{1,0:T(8,128)(2,1)S(1)}, u32[]{:S(2)}, u32[]{:S(2)}) collective-permute-start(bf16[256,128]{1,0:T(8,128)(2,1)S(1)} %get-tuple-element.54), channel_id=1, source_target_pairs={{12,0},{8,4},{4,8},{0,12},{13,1},{9,5},{5,9},{1,13},{14,2},{10,6},... | collective-permute-start | bytes 196616 | tf_op jit(solution)/shard_map/ppermute | solution.py:552
  51.4 14.7 %copy-start = (f32[128]{0:T(128)S(1)}, f32[128]{0:T(128)}, u32[]{:S(2)}) copy-start(f32[128]{0:T(128)} %param.16) | copy-start | bytes 1540
  56.5 7.1 %collective-permute-start.15 = (bf16[32,2048]{1,0:T(8,128)(2,1)S(1)}, bf16[32,2048]{1,0:T(8,128)(2,1)S(1)}, u32[]{:S(2)}, u32[]{:S(2)}) collective-permute-start(bf16[32,2048]{1,0:T(8,128)(2,1)S(1)} %get-tuple-element.46), channel_id=1, source_target_pairs={{12,0},{8,4},{4,8},{0,12},{13,1},{9,5},{5,9},{1,13},{14,2},{10,6},... | collective-permute-start | bytes 393224 | tf_op jit(solution)/shard_map/ppermute | solution.py:552
  57.8 24.3 %collective-permute-start.10 = (bf16[32,2048]{1,0:T(8,128)(2,1)S(1)}, bf16[32,2048]{1,0:T(8,128)(2,1)S(1)}, u32[]{:S(2)}, u32[]{:S(2)}) collective-permute-start(bf16[32,2048]{1,0:T(8,128)(2,1)S(1)} %get-tuple-element.50), channel_id=1, source_target_pairs={{1,0},{0,1},{3,2},{2,3},{5,4},{4,5},{7,6},{6,7},{9,8},{8,9},{11,10... | collective-permute-start | bytes 393224 | tf_op jit(solution)/shard_map/ppermute | solution.py:549
  60.2 22.0 %collective-permute-start.11 = (bf16[32,2048]{1,0:T(8,128)(2,1)S(1)}, bf16[32,2048]{1,0:T(8,128)(2,1)S(1)}, u32[]{:S(2)}, u32[]{:S(2)}) collective-permute-start(bf16[32,2048]{1,0:T(8,128)(2,1)S(1)} %get-tuple-element.52), channel_id=1, source_target_pairs={{2,0},{3,1},{0,2},{1,3},{6,4},{7,5},{4,6},{5,7},{10,8},{11,9},{8,1... | collective-permute-start | bytes 393224 | tf_op jit(solution)/shard_map/ppermute | solution.py:549
  61.5 7.9 %collective-permute-start.17 = (bf16[256,128]{1,0:T(8,128)(2,1)S(1)}, bf16[256,128]{1,0:T(8,128)(2,1)S(1)}, u32[]{:S(2)}, u32[]{:S(2)}) collective-permute-start(bf16[256,128]{1,0:T(8,128)(2,1)S(1)} %convert_element_type.112), channel_id=1, source_target_pairs={{1,0},{0,1},{3,2},{2,3},{5,4},{4,5},{7,6},{6,7},{9,8},{8,9},{11,10... | collective-permute-start | bytes 196616 | tf_op jit(solution)/shard_map/ppermute | solution.py:549
  63.5 15.2 %collective-permute-start.18 = (bf16[256,128]{1,0:T(8,128)(2,1)S(1)}, bf16[256,128]{1,0:T(8,128)(2,1)S(1)}, u32[]{:S(2)}, u32[]{:S(2)}) collective-permute-start(bf16[256,128]{1,0:T(8,128)(2,1)S(1)} %convert_element_type.112), channel_id=1, source_target_pairs={{2,0},{3,1},{0,2},{1,3},{6,4},{7,5},{4,6},{5,7},{10,8},{11,9},{8,1... | collective-permute-start | bytes 196616 | tf_op jit(solution)/shard_map/ppermute | solution.py:549
  63.5 15.8 %collective-permute-start.19 = (bf16[256,128]{1,0:T(8,128)(2,1)S(1)}, bf16[256,128]{1,0:T(8,128)(2,1)S(1)}, u32[]{:S(2)}, u32[]{:S(2)}) collective-permute-start(bf16[256,128]{1,0:T(8,128)(2,1)S(1)} %convert_element_type.112), channel_id=1, source_target_pairs={{3,0},{2,1},{1,2},{0,3},{7,4},{6,5},{5,6},{4,7},{11,8},{10,9},{9,1... | collective-permute-start | bytes 196616 | tf_op jit(solution)/shard_map/ppermute | solution.py:549
  69.4 12.9 %collective-permute-start.12 = (bf16[32,2048]{1,0:T(8,128)(2,1)S(1)}, bf16[32,2048]{1,0:T(8,128)(2,1)S(1)}, u32[]{:S(2)}, u32[]{:S(2)}) collective-permute-start(bf16[32,2048]{1,0:T(8,128)(2,1)S(1)} %get-tuple-element.51), channel_id=1, source_target_pairs={{3,0},{2,1},{1,2},{0,3},{7,4},{6,5},{5,6},{4,7},{11,8},{10,9},{9,1... | collective-permute-start | bytes 393224 | tf_op jit(solution)/shard_map/ppermute | solution.py:549
  78.7 4.4 %collective-permute-start.16 = (bf16[32,2048]{1,0:T(8,128)(2,1)S(1)}, bf16[32,2048]{1,0:T(8,128)(2,1)S(1)}, u32[]{:S(2)}, u32[]{:S(2)}) collective-permute-start(bf16[32,2048]{1,0:T(8,128)(2,1)S(1)} %add_convert_fusion), channel_id=1, source_target_pairs={{0,0},{4,1},{8,2},{12,3},{1,4},{5,5},{9,6},{13,7},{2,8},{6,9},{10,... | collective-permute-start | bytes 393224 | tf_op jit(solution)/shard_map/ppermute | solution.py:590
  79.4 5.8 %collective-permute-start.20 = (bf16[256,128]{1,0:T(8,128)(2,1)S(1)}, bf16[256,128]{1,0:T(8,128)(2,1)S(1)}, u32[]{:S(2)}, u32[]{:S(2)}) collective-permute-start(bf16[256,128]{1,0:T(8,128)(2,1)S(1)} %add_convert_fusion.2), channel_id=1, source_target_pairs={{12,0},{8,4},{4,8},{0,12},{13,1},{9,5},{5,9},{1,13},{14,2},{10,6},... | collective-permute-start | bytes 196616 | tf_op jit(solution)/shard_map/ppermute | solution.py:552
  82.1 4.9 %collective-permute-start.21 = (bf16[256,128]{1,0:T(8,128)(2,1)S(1)}, bf16[256,128]{1,0:T(8,128)(2,1)S(1)}, u32[]{:S(2)}, u32[]{:S(2)}) collective-permute-start(bf16[256,128]{1,0:T(8,128)(2,1)S(1)} %add_convert_fusion.2), channel_id=1, source_target_pairs={{8,0},{12,4},{0,8},{4,12},{9,1},{13,5},{1,9},{5,13},{10,2},{14,6},... | collective-permute-start | bytes 196616 | tf_op jit(solution)/shard_map/ppermute | solution.py:552
  82.2 4.8 %collective-permute-start.22 = (bf16[256,128]{1,0:T(8,128)(2,1)S(1)}, bf16[256,128]{1,0:T(8,128)(2,1)S(1)}, u32[]{:S(2)}, u32[]{:S(2)}) collective-permute-start(bf16[256,128]{1,0:T(8,128)(2,1)S(1)} %add_convert_fusion.2), channel_id=1, source_target_pairs={{4,0},{0,4},{12,8},{8,12},{5,1},{1,5},{13,9},{9,13},{6,2},{2,6},{1... | collective-permute-start | bytes 196616 | tf_op jit(solution)/shard_map/ppermute | solution.py:552

commit v13 on v10

--- a/solution.py
+++ b/solution.py
@@ -139,7 +139,7 @@
     )(*map(in_hbm, (x, gain, shift, first, second)))
 
 
-def masks(at_ref, labels_ref, counts_ref, lab_ref, tall_ref, wide_ref, plain_ref, rows, cols, seqs):
+def masks(at_ref, labels_ref, counts_ref, lab_ref, tall_ref, wide_ref, plain_ref, rows, cols, seqs, n_col):
     res = labels_ref.shape[1]
     labels = jnp.broadcast_to(labels_ref[...], (8, res))
     own = pltpu.roll(labels, (res - at_ref[0]) % res, 1)[:, :rows]
@@ -159,7 +159,8 @@
     depth = jnp.zeros((CHAINS, LANES), jnp.int32)
     for b in range(CHAINS):
         depth += jnp.where(there == b, counts_ref[:, b : b + 1], 0)
-    seq = (lax.broadcasted_iota(jnp.int32, (seqs, LANES), 0) + at_ref[2]) % seqs
+    here = lax.broadcasted_iota(jnp.int32, (seqs // n_col, LANES), 0)
+    seq = jnp.concatenate([here + (at_ref[2] ^ k) * (seqs // n_col) for k in range(n_col)], axis=0)
     for a in range(CHAINS):
         deep = jnp.broadcast_to(depth[a : a + 1], (seqs, LANES))
         weight = jnp.where(seq < deep, 1.0 / deep.astype(F32), 0.0)
@@ -189,7 +190,7 @@
 
 def back_body(at_ref, labels_hbm, counts_hbm, w_hbm, grad_hbm,
               lab_ref, tall_ref, wide_ref, plain_ref, w_out, back_ref, grad_ref,
-              labels_ref, counts_ref, w_ref, wide_w_ref, wt_ref, sems, *, seqs):
+              labels_ref, counts_ref, w_ref, wide_w_ref, wt_ref, sems, *, seqs, n_col):
     groups, step, cols, _ = grad_ref.shape
     copies = [
         pltpu.make_async_copy(w_hbm, w_ref, sems.at[groups]),
@@ -208,7 +209,7 @@
         copy.wait()
     projector(w_ref, wide_w_ref, w_out, wt_ref)
     masks(at_ref, labels_ref, counts_ref, lab_ref, tall_ref, wide_ref, plain_ref,
-          groups * step, cols, seqs)
+          groups * step, cols, seqs, n_col)
     halves = step // PER_TILE
 
     def group(g, carry):
@@ -237,13 +238,13 @@
     lax.fori_loop(0, groups, group, 0)
 
 
-def back_call(at, labels, counts, w, grad, seqs):
+def back_call(at, labels, counts, w, grad, seqs, n_col):
     rows, cols, width = grad.shape
     step = WIDE // PROJ
     groups = rows // step
     labels = labels[None, :]
     return pl.pallas_call(
-        lambda *refs: back_body(*refs, seqs=seqs),
+        lambda *refs: back_body(*refs, seqs=seqs, n_col=n_col),
         in_specs=[SMEM] + [HBM] * 4,
         out_specs=[VMEM] * 7,
         out_shape=[
@@ -530,39 +531,37 @@
     )(outer, w, offset)
 
 
-class Ring:
+class Pairs:
     def __init__(self, n_row, n_col):
         self.n_row, self.n_col = n_row, n_col
         self.per_row = n_col // n_row
         self.row = lax.axis_index("row").astype(jnp.uint32)
         self.col = lax.axis_index("col").astype(jnp.uint32)
 
-    def col_shift(self, value, k):
-        n = self.n_col
-        return lax.ppermute(value, "col", [((t + k) % n, t) for t in range(n)])
-
-    def row_shift(self, value, k):
-        n = self.n_row
-        return lax.ppermute(value, "row", [((t + k) % n, t) for t in range(n)])
+    def col_swap(self, value, k):
+        return lax.ppermute(value, "col", [(t ^ k, t) for t in range(self.n_col)])
+
+    def row_swap(self, value, k):
+        return lax.ppermute(value, "row", [(t ^ k, t) for t in range(self.n_row)])
 
     def right_along_row(self, right):
-        others = [self.row_shift(right, k) for k in range(1, self.n_row)]
+        others = [self.row_swap(right, k) for k in range(1, self.n_row)]
         return [right] + others
 
     def right_pieces(self, by_row):
-        n, m = self.n_row, self.per_row
+        m = self.per_row
         here, lanes = by_row[0].shape
         lanes //= m
         by_row = jnp.stack(by_row)
         pieces = []
         for k in range(self.n_col):
-            q = (self.col + (self.n_col - k)) % self.n_col
-            at = ((q // m + (n - self.row)) % n, jnp.uint32(0), (q % m) * lanes)
+            q = self.col ^ k
+            at = ((q // m) ^ self.row, jnp.uint32(0), (q % m) * lanes)
             pieces.append(lax.dynamic_slice(by_row, at, (1, here, lanes))[0])
         return pieces
 
     def right_along_col(self, pieces):
-        return jnp.concatenate([self.col_shift(p, k) if k else p for k, p in enumerate(pieces)])
+        return jnp.concatenate([self.col_swap(p, k) if k else p for k, p in enumerate(pieces)])
 
     def right_grad_home(self, grad):
         n, m = self.n_col, self.per_row
@@ -570,14 +569,14 @@
         total = jnp.zeros((m, here, lanes), F32)
         slot = lax.broadcasted_iota(jnp.uint32, (m, 1, 1), 0)
         for k in range(n):
-            t = (self.row * m + self.col % m + k) % n
-            block = lax.dynamic_slice_in_dim(grad, ((t + n - self.col) % n) * here, here, 0)
+            t = (self.row * m + self.col % m) ^ k
+            block = lax.dynamic_slice_in_dim(grad, (t ^ self.col) * here, here, 0)
             pairs = []
             for r in range(self.n_row):
                 for q in range(n):
-                    pairs.append((r * n + q, (q // m) * n + (r * m + q % m + k) % n))
+                    pairs.append((r * n + q, (q // m) * n + ((r * m + q % m) ^ k)))
             got = lax.ppermute(block, ("row", "col"), pairs).astype(F32)[None]
-            total += got if m == 1 else jnp.where(slot == (self.col + (n - k)) % n % m, got, 0)
+            total += got if m == 1 else jnp.where(slot == (self.col ^ k) % m, got, 0)
         return total.swapaxes(0, 1).reshape(here, m * lanes).astype(BF16)
 
     def weight_over_row(self, weight):
@@ -586,22 +585,22 @@
         sent = weight.astype(BF16).reshape(n, size, -1)
         total = lax.dynamic_index_in_dim(weight.reshape(n, size, -1), self.row, 0, keepdims=False)
         for k in range(1, n):
-            piece = lax.dynamic_index_in_dim(sent, (self.row + k) % n, 0, keepdims=False)
-            total += self.row_shift(piece, n - k).astype(F32)
+            piece = lax.dynamic_index_in_dim(sent, self.row ^ k, 0, keepdims=False)
+            total += self.row_swap(piece, k).astype(F32)
         return total
 
     def weight_over_col(self, total):
         mine = total.astype(BF16)
         for k in range(1, self.n_col):
-            total += self.col_shift(mine, k).astype(F32)
+            total += self.col_swap(mine, k).astype(F32)
         return total.astype(BF16)
 
     def weight_to_all(self, mine):
         n = self.n_row
-        which = (lax.broadcasted_iota(jnp.uint32, (n, 1, 1), 0) + (n - self.row)) % n
+        which = lax.broadcasted_iota(jnp.uint32, (n, 1, 1), 0) ^ self.row
         shares = mine[None]
         for k in range(1, n):
-            shares = jnp.where(which == k, self.row_shift(mine, k)[None], shares)
+            shares = jnp.where(which == k, self.row_swap(mine, k)[None], shares)
         return shares.reshape(n * mine.shape[0], mine.shape[1])
 
 
@@ -611,7 +610,7 @@
 
 def shards(n_row, n_col, alignment_tensor, gain, shift, first_projector, second_projector,
            final_projector, final_offset, labels, counts, grad):
-    ring = Ring(n_row, n_col)
+    ring = Pairs(n_row, n_col)
     here, rows, _ = alignment_tensor.shape
     cols, width = grad.shape[1:]
     seqs = here * n_col
@@ -619,11 +618,11 @@
         alignment_tensor, gain[None, :], shift[None, :], first_projector.T, second_projector.T, cols
     )
     by_row = ring.right_along_row(right)
-    left = jnp.concatenate([left] + [ring.col_shift(left, k) for k in range(1, n_col)])
-
-    at = jnp.stack([ring.row * rows, ring.col * cols, ring.col * here]).astype(jnp.int32)
+    left = jnp.concatenate([left] + [ring.col_swap(left, k) for k in range(1, n_col)])
+
+    at = jnp.stack([ring.row * rows, ring.col * cols, ring.col]).astype(jnp.int32)
     lab, tall, wide, plain, w, back, grad = back_call(
-        at, labels, counts, after(final_projector, right), grad, seqs
+        at, labels, counts, after(final_projector, right), grad, seqs, n_col
     )
     mine = ring.right_along_col(ring.right_pieces(by_row))
     back, grad = in_vmem(back), in_vmem(grad)
@@ -640,7 +639,7 @@
 
     total = left_grad[:here].astype(F32)
     for k in range(1, n_col):
-        total += ring.col_shift(left_grad[k * here : (k + 1) * here], n_col - k).astype(F32)
+        total += ring.col_swap(left_grad[k * here : (k + 1) * here], k).astype(F32)
     adjoint_first = total.astype(BF16)
     pair_update = pair_call(in_vmem(outer), after(w, left_grad, share), final_offset[None, :])
     pair_update = pair_update.reshape(rows, cols, width)

time: 84.1 us -> 82.5 us (0.981)
  waiting for transfers between devices: 8.69 us -> 4.13 us
  starting transfers between devices: 35.2 us -> 38 us
    ppermute x21, waiting for transfers between devices: 8.68 us -> 4.12 us  [the longest x12 3.64 us: col_swap(): return lax.ppermute(value, 'col', [(t ^ k, t) for t in range(self.n_col)])]
    ppermute x21, starting transfers between devices: 27.8 us -> 30.5 us  [the longest x12 22.8 us: col_swap(): return lax.ppermute(value, 'col', [(t ^ k, t) for t in range(self.n_col)])]
  transfers between devices with their start and end apart: 25 -> 25, of which waited for: 2 -> 3; matrix products, arithmetic and copies ran while one was open for 3% -> 3% of each run, Pallas kernels for 38% -> 39%
where the time goes in v13:
time: 82.5 us; the launch traced here: 82.3 us
  starting transfers between devices  38 us (46%)
  Pallas kernels  35.9 us (44%)
  waiting for transfers between devices  4.13 us (5%)
  other arithmetic  3.03 us (4%)
  between operations  0.88 us (1%)
    ppermute x12, starting transfers between devices, col_swap(): return lax.ppermute(value, 'col', [(t ^ k, t) for t in range(self.n_col)])  22.8 us
    pallas_call x1, Pallas kernels, outer_call(): pl.pallas_call(outer_body, in_specs=[SMEM] * 2 + [VMEM] * 5, out_specs=[V...  10.7 us
    ppermute x9, starting transfers between devices, row_swap(): return lax.ppermute(value, 'row', [(t ^ k, t) for t in range(self.n_row)])  7.68 us
    ppermute x4, starting transfers between devices, right_grad_home(): got = lax.ppermute(block, ('row', 'col'), pairs).astype(F32)[None]  7.48 us
    pallas_call x1, Pallas kernels, back_call(): pl.pallas_call(lambda *refs: back_body(*refs, seqs=seqs, n_col=n_col), in...  6.94 us
    pallas_call x1, Pallas kernels, right_grad_call(): pl.pallas_call(right_grad_body, in_specs=[SMEM] * 2 + [VMEM] * 4, out_spe...  5.91 us
    pallas_call x1, Pallas kernels, left_grad_call(): pl.pallas_call(left_grad_body, in_specs=[SMEM] * 2 + [VMEM] * 4, out_spec...  5.23 us
    pallas_call x1, Pallas kernels, project_call(): pl.pallas_call(lambda *refs: project_body(*refs, cols=cols), in_specs=[HB...  3.74 us
  transfers between devices with their start and end apart: 25, of which 3 were waited for; matrix products, arithmetic and copies ran while one was open for 3% of the time, Pallas kernels for 39%

profile of v13, /device:TPU:0, one launch (start us, length us, event | category | flops | bytes accessed | tf_op | source)
XLA Modules:
  0.0 82.3 jit_solution(9403757764662497547)
XLA Ops:
  0.6 3.7 %project.1 = (bf16[32,2048]{1,0:T(8,128)(2,1)S(1)}, bf16[32,2048]{1,0:T(8,128)(2,1)S(1)}) custom-call(bf16[32,64,256]{2,1,0:T(8,128)(2,1)} %refs_0_.1, f32[1,256]{1,0:T(1,128)} %bitcast.61, f32[1,256]{1,0:T(1,128)} %bitcast.62, bf16[32,256]{1,0:T(8,128)(2,1)} %bitcast.59, bf16[32,256]{1,0:T(8,128)(2,1)} %bitcast.60), custom_call_target="tpu_custom_call" | custom-call | tf_op jit(solution)/shard_map/project/pallas_call | solution.py:122
  4.4 5.1 %collective-permute-start.2 = (bf16[32,2048]{1,0:T(8,128)(2,1)S(1)}, bf16[32,2048]{1,0:T(8,128)(2,1)S(1)}, u32[]{:S(2)}, u32[]{:S(2)}) collective-permute-start(bf16[32,2048]{1,0:T(8,128)(2,1)S(1)} %get-tuple-element.21), channel_id=1, source_target_pairs={{3,0},{2,1},{1,2},{0,3},{7,4},{6,5},{5,6},{4,7},{11,8},{10,9},{9,1... | collective-permute-start | bytes 393224 | tf_op jit(solution)/shard_map/ppermute | solution.py:542
  9.5 0.7 collective-permute-start.5
  10.2 0.8 %collective-permute-start.4 = (bf16[32,2048]{1,0:T(8,128)(2,1)S(1)}, bf16[32,2048]{1,0:T(8,128)(2,1)S(1)}, u32[]{:S(2)}, u32[]{:S(2)}) collective-permute-start(bf16[32,2048]{1,0:T(8,128)(2,1)S(1)} %get-tuple-element.22), channel_id=1, source_target_pairs={{8,0},{12,4},{0,8},{4,12},{9,1},{13,5},{1,9},{5,13},{10,2},{14,6},... | collective-permute-start | bytes 393224 | tf_op jit(solution)/shard_map/ppermute | solution.py:545
  11.0 0.4 collective-permute-start.3
  11.8 6.9 %back.1 = (s32[1,2048]{1,0:T(1,128)S(1)}, bf16[8,2,128,128]{3,2,1,0:T(8,128)(2,1)S(1)}, bf16[8,2,64,128]{3,2,1,0:T(8,128)(2,1)S(1)}, f32[8,64,128]{2,1,0:T(8,128...) custom-call(s32[3]{0:T(128)S(1)} %add_convert_fusion.3.refs_0_.at_ref, ...), custom_call_target="tpu_custom_call" | custom-call | flops 21474836480 | bytes 8388608 | tf_op jit(solution)/shard_map/back/pallas_call | solution.py:246
  18.7 0.7 collective-permute-start
  19.6 3.8 %collective-permute-start.8 = (bf16[32,2048]{1,0:T(8,128)(2,1)S(1)}, bf16[32,2048]{1,0:T(8,128)(2,1)S(1)}, u32[]{:S(2)}, u32[]{:S(2)}) collective-permute-start(bf16[32,2048]{1,0:T(8,128)(2,1)S(1)} %get-tuple-element.46), channel_id=1, source_target_pairs={{3,0},{2,1},{1,2},{0,3},{7,4},{6,5},{5,6},{4,7},{11,8},{10,9},{9,1... | collective-permute-start | bytes 393224 | tf_op jit(solution)/shard_map/ppermute | solution.py:542
  23.4 1.0 %collective-permute-done = bf16[32,2048]{1,0:T(8,128)(2,1)S(1)} collective-permute-done((bf16[32,2048]{1,0:T(8,128)(2,1)S(1)}, bf16[32,2048]{1,0:T(8,128)(2,1)S(1)}, u32[]{:S(2)}, u32[]{:S(2)}) %collective-permute-start) | collective-permute-done | bytes 131104 | tf_op jit(solution)/shard_map/ppermute | solution.py:542
  24.4 0.8 collective-permute-start.6
  25.2 5.9 %right_grad.1 = bf16[128,2048]{1,0:T(8,128)(2,1)S(1)} custom-call(s32[3]{0:T(128)S(1)} %add_convert_fusion.3.refs_0_.at_ref, s32[256]{0:T(256)S(1)} %copy-done.1, bf16[8,2048,256]{2,1,0:T(8,128)(2,1)S(1)} %get-tuple-element.25.back_ref, bf16[128,2048]{1,0:T(8,128)(2,1)S(1)} %constant_dynamic-update-slice_fusion.left_ref, ...), custom_call_target="tpu_custom_call" | custom-call | flops 21474836480 | bytes 8388608 | tf_op jit(solution)/shard_map/right_grad/pallas_call | solution.py:347
  31.2 0.7 collective-permute-start.15
  31.8 5.7 %collective-permute-start.18 = (bf16[32,2048]{1,0:T(8,128)(2,1)S(1)}, bf16[32,2048]{1,0:T(8,128)(2,1)S(1)}, u32[]{:S(2)}, u32[]{:S(2)}) collective-permute-start(bf16[32,2048]{1,0:T(8,128)(2,1)S(1)} %get-tuple-element.39), channel_id=1, source_target_pairs={{0,3},{1,7},{2,11},{3,15},{4,2},{5,6},{6,10},{7,14},{8,1},{9,5},{1... | collective-permute-start | bytes 393224 | tf_op jit(solution)/shard_map/ppermute | solution.py:578
  37.6 1.1 %collective-permute-start.17 = (bf16[32,2048]{1,0:T(8,128)(2,1)S(1)}, bf16[32,2048]{1,0:T(8,128)(2,1)S(1)}, u32[]{:S(2)}, u32[]{:S(2)}) collective-permute-start(bf16[32,2048]{1,0:T(8,128)(2,1)S(1)} %get-tuple-element.40), channel_id=1, source_target_pairs={{0,2},{1,6},{2,10},{3,14},{4,3},{5,7},{6,11},{7,15},{8,0},{9,4},{1... | collective-permute-start | bytes 393224 | tf_op jit(solution)/shard_map/ppermute | solution.py:578
  38.7 10.7 %outer.1 = (bf16[8,512,1024]{2,1,0:T(8,128)(2,1)S(1)}, f32[1024,128]{1,0:T(8,128)S(1)}) custom-call(s32[3]{0:T(128)S(1)} %add_convert_fusion.3.refs_0_.at_ref, s32[256]{0:T(256)S(1)} %copy-done.1, bf16[128,2048]{1,0:T(8,128)(2,1)S(1)} %constant_dynamic-update-slice_fusion.left_ref, s32[1,2048]{1,0:T(1,128)S(1)} %get-tuple-element.33.lab_ref, ...), custom_call_target="tpu_custom_call" | custom-call | flops 42949672960 | bytes 8388608 | tf_op jit(solution)/shard_map/outer/pallas_call | solution.py:483
  49.5 1.2 %collective-permute-start.9 = (bf16[256,128]{1,0:T(8,128)(2,1)S(1)}, bf16[256,128]{1,0:T(8,128)(2,1)S(1)}, u32[]{:S(2)}, u32[]{:S(2)}) collective-permute-start(bf16[256,128]{1,0:T(8,128)(2,1)S(1)} %get-tuple-element.49), channel_id=1, source_target_pairs={{4,0},{0,4},{12,8},{8,12},{5,1},{1,5},{13,9},{9,13},{6,2},{2,6},{1... | collective-permute-start | bytes 196616 | tf_op jit(solution)/shard_map/ppermute | solution.py:545
  50.8 5.2 %left_grad.1 = bf16[128,2048]{1,0:T(8,128)(2,1)S(1)} custom-call(s32[3]{0:T(128)S(1)} %add_convert_fusion.3.refs_0_.at_ref, s32[256]{0:T(256)S(1)} %copy-done.1, bf16[8,2048,256]{2,1,0:T(8,128)(2,1)S(1)} %get-tuple-element.25.back_ref, s32[1,2048]{1,0:T(1,128)S(1)} %get-tuple-element.33.lab_ref, bf16[128,2048]{1,0:T(8,128)(2,1)S(1)} %pad_maximum_fusion.1.right_ref, ...), custom_call_target="tpu_custom_call" | custom-call | flops 21474836480 | bytes 8388608 | tf_op jit(solution)/shard_map/left_grad/pallas_call | solution.py:403
  56.1 2.7 %collective-permute-start.11 = (bf16[256,128]{1,0:T(8,128)(2,1)S(1)}, bf16[256,128]{1,0:T(8,128)(2,1)S(1)}, u32[]{:S(2)}, u32[]{:S(2)}) collective-permute-start(bf16[256,128]{1,0:T(8,128)(2,1)S(1)} %get-tuple-element.50), channel_id=1, source_target_pairs={{12,0},{8,4},{4,8},{0,12},{13,1},{9,5},{5,9},{1,13},{14,2},{10,6},... | collective-permute-start | bytes 196616 | tf_op jit(solution)/shard_map/ppermute | solution.py:545
  58.7 1.5 %collective-permute-start.12 = (bf16[32,2048]{1,0:T(8,128)(2,1)S(1)}, bf16[32,2048]{1,0:T(8,128)(2,1)S(1)}, u32[]{:S(2)}, u32[]{:S(2)}) collective-permute-start(bf16[32,2048]{1,0:T(8,128)(2,1)S(1)} %get-tuple-element.42), channel_id=1, source_target_pairs={{1,0},{0,1},{3,2},{2,3},{5,4},{4,5},{7,6},{6,7},{9,8},{8,9},{11,10... | collective-permute-start | bytes 393224 | tf_op jit(solution)/shard_map/ppermute | solution.py:542
  60.2 2.6 %collective-permute-start.14 = (bf16[32,2048]{1,0:T(8,128)(2,1)S(1)}, bf16[32,2048]{1,0:T(8,128)(2,1)S(1)}, u32[]{:S(2)}, u32[]{:S(2)}) collective-permute-start(bf16[32,2048]{1,0:T(8,128)(2,1)S(1)} %get-tuple-element.43), channel_id=1, source_target_pairs={{3,0},{2,1},{1,2},{0,3},{7,4},{6,5},{5,6},{4,7},{11,8},{10,9},{9,1... | collective-permute-start | bytes 393224 | tf_op jit(solution)/shard_map/ppermute | solution.py:542
  62.8 0.7 add_convert_fusion
  63.6 1.7 %collective-permute-start.21 = (bf16[256,128]{1,0:T(8,128)(2,1)S(1)}, bf16[256,128]{1,0:T(8,128)(2,1)S(1)}, u32[]{:S(2)}, u32[]{:S(2)}) collective-permute-start(bf16[256,128]{1,0:T(8,128)(2,1)S(1)} %convert_element_type.100), channel_id=1, source_target_pairs={{3,0},{2,1},{1,2},{0,3},{7,4},{6,5},{5,6},{4,7},{11,8},{10,9},{9,1... | collective-permute-start | bytes 196616 | tf_op jit(solution)/shard_map/ppermute | solution.py:542
  65.3 0.7 collective-permute-start.20
  66.0 2.1 %collective-permute-start.19 = (bf16[256,128]{1,0:T(8,128)(2,1)S(1)}, bf16[256,128]{1,0:T(8,128)(2,1)S(1)}, u32[]{:S(2)}, u32[]{:S(2)}) collective-permute-start(bf16[256,128]{1,0:T(8,128)(2,1)S(1)} %convert_element_type.100), channel_id=1, source_target_pairs={{1,0},{0,1},{3,2},{2,3},{5,4},{4,5},{7,6},{6,7},{9,8},{8,9},{11,10... | collective-permute-start | bytes 196616 | tf_op jit(solution)/shard_map/ppermute | solution.py:542
  68.1 3.3 %pair.1 = bf16[4096,128]{1,0:T(8,128)(2,1)} custom-call(bf16[8,512,1024]{2,1,0:T(8,128)(2,1)S(1)} %get-tuple-element.30.outer_ref, bf16[1024,128]{1,0:T(8,128)(2,1)S(1)} %get-tuple-element.36.w_ref, f32[1,128]{1,0:T(1,128)S(1)} %bitcast.52), custom_call_target="tpu_custom_call" | custom-call | flops 1073741824 | bytes 1048576 | tf_op jit(solution)/shard_map/pair/pallas_call | solution.py:518
  71.4 3.8 %collective-permute-start.13 = (bf16[32,2048]{1,0:T(8,128)(2,1)S(1)}, bf16[32,2048]{1,0:T(8,128)(2,1)S(1)}, u32[]{:S(2)}, u32[]{:S(2)}) collective-permute-start(bf16[32,2048]{1,0:T(8,128)(2,1)S(1)} %get-tuple-element.44), channel_id=1, source_target_pairs={{2,0},{3,1},{0,2},{1,3},{6,4},{7,5},{4,6},{5,7},{10,8},{11,9},{8,1... | collective-permute-start | bytes 393224 | tf_op jit(solution)/shard_map/ppermute | solution.py:542
  75.4 1.3 %collective-permute-start.23 = (bf16[256,128]{1,0:T(8,128)(2,1)S(1)}, bf16[256,128]{1,0:T(8,128)(2,1)S(1)}, u32[]{:S(2)}, u32[]{:S(2)}) collective-permute-start(bf16[256,128]{1,0:T(8,128)(2,1)S(1)} %add_convert_fusion.2), channel_id=1, source_target_pairs={{8,0},{12,4},{0,8},{4,12},{9,1},{13,5},{1,9},{5,13},{10,2},{14,6},... | collective-permute-start | bytes 196616 | tf_op jit(solution)/shard_map/ppermute | solution.py:545
  76.7 0.5 collective-permute-start.22
  77.2 2.7 %collective-permute-done.13 = bf16[32,2048]{1,0:T(8,128)(2,1)S(1)} collective-permute-done((bf16[32,2048]{1,0:T(8,128)(2,1)S(1)}, bf16[32,2048]{1,0:T(8,128)(2,1)S(1)}, u32[]{:S(2)}, u32[]{:S(2)}) %collective-permute-start.13) | collective-permute-done | bytes 131104 | tf_op jit(solution)/shard_map/ppermute | solution.py:542
  79.9 0.7 add_convert_fusion.1
  80.6 0.5 collective-permute-done.22
  81.1 1.3 %convert_multiply_fusion = f32[1024,128]{1,0:T(8,128)} fusion(pred[1024]{0:T(1024)(128)(4,1)S(1)} %broadcast_in_dim.105, pred[1024]{0:T(1024)(128)(4,1)S(1)} %broadcast_in_dim.100, pred[1024]{0:T(1024)(128)(4,1)S(1)} %broadcast_in_dim.95, bf16[256,128]{1,0:T(8,128)(2,1)S(1)} %add_convert_fusion.2, bf16[256,128]{1,0:T(8,128)(2,1)S(1)} %collective-permute-done.24, ...), kind=kLoop, calls=%fused_computation.2 | loop fusion | flops 655360 | bytes 789504 | tf_op jit(solution)/shard_map/div | solution.py:647
  (54 shorter events, 0.9 us)
Async XLA Ops:
  4.4 20.8 %collective-permute-start.2 = (bf16[32,2048]{1,0:T(8,128)(2,1)S(1)}, bf16[32,2048]{1,0:T(8,128)(2,1)S(1)}, u32[]{:S(2)}, u32[]{:S(2)}) collective-permute-start(bf16[32,2048]{1,0:T(8,128)(2,1)S(1)} %get-tuple-element.21), channel_id=1, source_target_pairs={{3,0},{2,1},{1,2},{0,3},{7,4},{6,5},{5,6},{4,7},{11,8},{10,9},{9,1... | collective-permute-start | bytes 393224 | tf_op jit(solution)/shard_map/ppermute | solution.py:542
  9.5 15.6 %collective-permute-start.1 = (bf16[32,2048]{1,0:T(8,128)(2,1)S(1)}, bf16[32,2048]{1,0:T(8,128)(2,1)S(1)}, u32[]{:S(2)}, u32[]{:S(2)}) collective-permute-start(bf16[32,2048]{1,0:T(8,128)(2,1)S(1)} %get-tuple-element.21), channel_id=1, source_target_pairs={{2,0},{3,1},{0,2},{1,3},{6,4},{7,5},{4,6},{5,7},{10,8},{11,9},{8,1... | collective-permute-start | bytes 393224 | tf_op jit(solution)/shard_map/ppermute | solution.py:542
  9.5 9.2 %collective-permute-start.5 = (bf16[32,2048]{1,0:T(8,128)(2,1)S(1)}, bf16[32,2048]{1,0:T(8,128)(2,1)S(1)}, u32[]{:S(2)}, u32[]{:S(2)}) collective-permute-start(bf16[32,2048]{1,0:T(8,128)(2,1)S(1)} %get-tuple-element.22), channel_id=1, source_target_pairs={{12,0},{8,4},{4,8},{0,12},{13,1},{9,5},{5,9},{1,13},{14,2},{10,6},... | collective-permute-start | bytes 393224 | tf_op jit(solution)/shard_map/ppermute | solution.py:545
  10.2 9.3 %collective-permute-start.4 = (bf16[32,2048]{1,0:T(8,128)(2,1)S(1)}, bf16[32,2048]{1,0:T(8,128)(2,1)S(1)}, u32[]{:S(2)}, u32[]{:S(2)}) collective-permute-start(bf16[32,2048]{1,0:T(8,128)(2,1)S(1)} %get-tuple-element.22), channel_id=1, source_target_pairs={{8,0},{12,4},{0,8},{4,12},{9,1},{13,5},{1,9},{5,13},{10,2},{14,6},... | collective-permute-start | bytes 393224 | tf_op jit(solution)/shard_map/ppermute | solution.py:545
  11.0 8.4 %collective-permute-start.3 = (bf16[32,2048]{1,0:T(8,128)(2,1)S(1)}, bf16[32,2048]{1,0:T(8,128)(2,1)S(1)}, u32[]{:S(2)}, u32[]{:S(2)}) collective-permute-start(bf16[32,2048]{1,0:T(8,128)(2,1)S(1)} %get-tuple-element.22), channel_id=1, source_target_pairs={{4,0},{0,4},{12,8},{8,12},{5,1},{1,5},{13,9},{9,13},{6,2},{2,6},{1... | collective-permute-start | bytes 393224 | tf_op jit(solution)/shard_map/ppermute | solution.py:545
  11.8 13.4 %copy-start.1 = (s32[256]{0:T(256)S(1)}, s32[256]{0:T(256)}, u32[]{:S(2)}) copy-start(s32[256]{0:T(256)} %labels_ref.5) | copy-start | bytes 3076
  18.7 5.6 %collective-permute-start = (bf16[32,2048]{1,0:T(8,128)(2,1)S(1)}, bf16[32,2048]{1,0:T(8,128)(2,1)S(1)}, u32[]{:S(2)}, u32[]{:S(2)}) collective-permute-start(bf16[32,2048]{1,0:T(8,128)(2,1)S(1)} %get-tuple-element.21), channel_id=1, source_target_pairs={{1,0},{0,1},{3,2},{2,3},{5,4},{4,5},{7,6},{6,7},{9,8},{8,9},{11,10... | collective-permute-start | bytes 393224 | tf_op jit(solution)/shard_map/ppermute | solution.py:542
  19.6 18.0 %collective-permute-start.8 = (bf16[32,2048]{1,0:T(8,128)(2,1)S(1)}, bf16[32,2048]{1,0:T(8,128)(2,1)S(1)}, u32[]{:S(2)}, u32[]{:S(2)}) collective-permute-start(bf16[32,2048]{1,0:T(8,128)(2,1)S(1)} %get-tuple-element.46), channel_id=1, source_target_pairs={{3,0},{2,1},{1,2},{0,3},{7,4},{6,5},{5,6},{4,7},{11,8},{10,9},{9,1... | collective-permute-start | bytes 393224 | tf_op jit(solution)/shard_map/ppermute | solution.py:542
  23.4 15.3 %collective-permute-start.7 = (bf16[32,2048]{1,0:T(8,128)(2,1)S(1)}, bf16[32,2048]{1,0:T(8,128)(2,1)S(1)}, u32[]{:S(2)}, u32[]{:S(2)}) collective-permute-start(bf16[32,2048]{1,0:T(8,128)(2,1)S(1)} %get-tuple-element.47), channel_id=1, source_target_pairs={{2,0},{3,1},{0,2},{1,3},{6,4},{7,5},{4,6},{5,7},{10,8},{11,9},{8,1... | collective-permute-start | bytes 393224 | tf_op jit(solution)/shard_map/ppermute | solution.py:542
  24.4 14.3 %collective-permute-start.6 = (bf16[32,2048]{1,0:T(8,128)(2,1)S(1)}, bf16[32,2048]{1,0:T(8,128)(2,1)S(1)}, u32[]{:S(2)}, u32[]{:S(2)}) collective-permute-start(bf16[32,2048]{1,0:T(8,128)(2,1)S(1)} %get-tuple-element.48), channel_id=1, source_target_pairs={{1,0},{0,1},{3,2},{2,3},{5,4},{4,5},{7,6},{6,7},{9,8},{8,9},{11,10... | collective-permute-start | bytes 393224 | tf_op jit(solution)/shard_map/ppermute | solution.py:542
  31.2 24.9 %collective-permute-start.15 = (bf16[32,2048]{1,0:T(8,128)(2,1)S(1)}, bf16[32,2048]{1,0:T(8,128)(2,1)S(1)}, u32[]{:S(2)}, u32[]{:S(2)}) collective-permute-start(bf16[32,2048]{1,0:T(8,128)(2,1)S(1)} %get-tuple-element.38), channel_id=1, source_target_pairs={{0,0},{1,4},{2,8},{3,12},{4,1},{5,5},{6,9},{7,13},{8,2},{9,6},{10,... | collective-permute-start | bytes 393224 | tf_op jit(solution)/shard_map/ppermute | solution.py:578
  31.8 26.9 %collective-permute-start.18 = (bf16[32,2048]{1,0:T(8,128)(2,1)S(1)}, bf16[32,2048]{1,0:T(8,128)(2,1)S(1)}, u32[]{:S(2)}, u32[]{:S(2)}) collective-permute-start(bf16[32,2048]{1,0:T(8,128)(2,1)S(1)} %get-tuple-element.39), channel_id=1, source_target_pairs={{0,3},{1,7},{2,11},{3,15},{4,2},{5,6},{6,10},{7,14},{8,1},{9,5},{1... | collective-permute-start | bytes 393224 | tf_op jit(solution)/shard_map/ppermute | solution.py:578
  37.6 21.1 %collective-permute-start.17 = (bf16[32,2048]{1,0:T(8,128)(2,1)S(1)}, bf16[32,2048]{1,0:T(8,128)(2,1)S(1)}, u32[]{:S(2)}, u32[]{:S(2)}) collective-permute-start(bf16[32,2048]{1,0:T(8,128)(2,1)S(1)} %get-tuple-element.40), channel_id=1, source_target_pairs={{0,2},{1,6},{2,10},{3,14},{4,3},{5,7},{6,11},{7,15},{8,0},{9,4},{1... | collective-permute-start | bytes 393224 | tf_op jit(solution)/shard_map/ppermute | solution.py:578
  38.7 21.6 %collective-permute-start.16 = (bf16[32,2048]{1,0:T(8,128)(2,1)S(1)}, bf16[32,2048]{1,0:T(8,128)(2,1)S(1)}, u32[]{:S(2)}, u32[]{:S(2)}) collective-permute-start(bf16[32,2048]{1,0:T(8,128)(2,1)S(1)} %get-tuple-element.41), channel_id=1, source_target_pairs={{0,1},{1,5},{2,9},{3,13},{4,0},{5,4},{6,8},{7,12},{8,3},{9,7},{10,... | collective-permute-start | bytes 393224 | tf_op jit(solution)/shard_map/ppermute | solution.py:578
  49.5 14.0 %collective-permute-start.9 = (bf16[256,128]{1,0:T(8,128)(2,1)S(1)}, bf16[256,128]{1,0:T(8,128)(2,1)S(1)}, u32[]{:S(2)}, u32[]{:S(2)}) collective-permute-start(bf16[256,128]{1,0:T(8,128)(2,1)S(1)} %get-tuple-element.49), channel_id=1, source_target_pairs={{4,0},{0,4},{12,8},{8,12},{5,1},{1,5},{13,9},{9,13},{6,2},{2,6},{1... | collective-permute-start | bytes 196616 | tf_op jit(solution)/shard_map/ppermute | solution.py:545
  50.8 17.3 %copy-start = (f32[128]{0:T(128)S(1)}, f32[128]{0:T(128)}, u32[]{:S(2)}) copy-start(f32[128]{0:T(128)} %param.16) | copy-start | bytes 1540
  56.1 7.5 %collective-permute-start.11 = (bf16[256,128]{1,0:T(8,128)(2,1)S(1)}, bf16[256,128]{1,0:T(8,128)(2,1)S(1)}, u32[]{:S(2)}, u32[]{:S(2)}) collective-permute-start(bf16[256,128]{1,0:T(8,128)(2,1)S(1)} %get-tuple-element.50), channel_id=1, source_target_pairs={{12,0},{8,4},{4,8},{0,12},{13,1},{9,5},{5,9},{1,13},{14,2},{10,6},... | collective-permute-start | bytes 196616 | tf_op jit(solution)/shard_map/ppermute | solution.py:545
  58.7 4.8 %collective-permute-start.10 = (bf16[256,128]{1,0:T(8,128)(2,1)S(1)}, bf16[256,128]{1,0:T(8,128)(2,1)S(1)}, u32[]{:S(2)}, u32[]{:S(2)}) collective-permute-start(bf16[256,128]{1,0:T(8,128)(2,1)S(1)} %get-tuple-element.51), channel_id=1, source_target_pairs={{8,0},{12,4},{0,8},{4,12},{9,1},{13,5},{1,9},{5,13},{10,2},{14,6},... | collective-permute-start | bytes 196616 | tf_op jit(solution)/shard_map/ppermute | solution.py:545
  58.7 17.9 %collective-permute-start.12 = (bf16[32,2048]{1,0:T(8,128)(2,1)S(1)}, bf16[32,2048]{1,0:T(8,128)(2,1)S(1)}, u32[]{:S(2)}, u32[]{:S(2)}) collective-permute-start(bf16[32,2048]{1,0:T(8,128)(2,1)S(1)} %get-tuple-element.42), channel_id=1, source_target_pairs={{1,0},{0,1},{3,2},{2,3},{5,4},{4,5},{7,6},{6,7},{9,8},{8,9},{11,10... | collective-permute-start | bytes 393224 | tf_op jit(solution)/shard_map/ppermute | solution.py:542
  60.2 17.0 %collective-permute-start.14 = (bf16[32,2048]{1,0:T(8,128)(2,1)S(1)}, bf16[32,2048]{1,0:T(8,128)(2,1)S(1)}, u32[]{:S(2)}, u32[]{:S(2)}) collective-permute-start(bf16[32,2048]{1,0:T(8,128)(2,1)S(1)} %get-tuple-element.43), channel_id=1, source_target_pairs={{3,0},{2,1},{1,2},{0,3},{7,4},{6,5},{5,6},{4,7},{11,8},{10,9},{9,1... | collective-permute-start | bytes 393224 | tf_op jit(solution)/shard_map/ppermute | solution.py:542
  63.6 7.8 %collective-permute-start.21 = (bf16[256,128]{1,0:T(8,128)(2,1)S(1)}, bf16[256,128]{1,0:T(8,128)(2,1)S(1)}, u32[]{:S(2)}, u32[]{:S(2)}) collective-permute-start(bf16[256,128]{1,0:T(8,128)(2,1)S(1)} %convert_element_type.100), channel_id=1, source_target_pairs={{3,0},{2,1},{1,2},{0,3},{7,4},{6,5},{5,6},{4,7},{11,8},{10,9},{9,1... | collective-permute-start | bytes 196616 | tf_op jit(solution)/shard_map/ppermute | solution.py:542
  65.3 9.9 %collective-permute-start.20 = (bf16[256,128]{1,0:T(8,128)(2,1)S(1)}, bf16[256,128]{1,0:T(8,128)(2,1)S(1)}, u32[]{:S(2)}, u32[]{:S(2)}) collective-permute-start(bf16[256,128]{1,0:T(8,128)(2,1)S(1)} %convert_element_type.100), channel_id=1, source_target_pairs={{2,0},{3,1},{0,2},{1,3},{6,4},{7,5},{4,6},{5,7},{10,8},{11,9},{8,1... | collective-permute-start | bytes 196616 | tf_op jit(solution)/shard_map/ppermute | solution.py:542
  66.0 9.2 %collective-permute-start.19 = (bf16[256,128]{1,0:T(8,128)(2,1)S(1)}, bf16[256,128]{1,0:T(8,128)(2,1)S(1)}, u32[]{:S(2)}, u32[]{:S(2)}) collective-permute-start(bf16[256,128]{1,0:T(8,128)(2,1)S(1)} %convert_element_type.100), channel_id=1, source_target_pairs={{1,0},{0,1},{3,2},{2,3},{5,4},{4,5},{7,6},{6,7},{9,8},{8,9},{11,10... | collective-permute-start | bytes 196616 | tf_op jit(solution)/shard_map/ppermute | solution.py:542
  71.4 8.5 %collective-permute-start.13 = (bf16[32,2048]{1,0:T(8,128)(2,1)S(1)}, bf16[32,2048]{1,0:T(8,128)(2,1)S(1)}, u32[]{:S(2)}, u32[]{:S(2)}) collective-permute-start(bf16[32,2048]{1,0:T(8,128)(2,1)S(1)} %get-tuple-element.44), channel_id=1, source_target_pairs={{2,0},{3,1},{0,2},{1,3},{6,4},{7,5},{4,6},{5,7},{10,8},{11,9},{8,1... | collective-permute-start | bytes 393224 | tf_op jit(solution)/shard_map/ppermute | solution.py:542
  75.3 5.3 %collective-permute-start.24 = (bf16[256,128]{1,0:T(8,128)(2,1)S(1)}, bf16[256,128]{1,0:T(8,128)(2,1)S(1)}, u32[]{:S(2)}, u32[]{:S(2)}) collective-permute-start(bf16[256,128]{1,0:T(8,128)(2,1)S(1)} %add_convert_fusion.2), channel_id=1, source_target_pairs={{4,0},{0,4},{12,8},{8,12},{5,1},{1,5},{13,9},{9,13},{6,2},{2,6},{1... | collective-permute-start | bytes 196616 | tf_op jit(solution)/shard_map/ppermute | solution.py:545
  75.4 5.2 %collective-permute-start.23 = (bf16[256,128]{1,0:T(8,128)(2,1)S(1)}, bf16[256,128]{1,0:T(8,128)(2,1)S(1)}, u32[]{:S(2)}, u32[]{:S(2)}) collective-permute-start(bf16[256,128]{1,0:T(8,128)(2,1)S(1)} %add_convert_fusion.2), channel_id=1, source_target_pairs={{8,0},{12,4},{0,8},{4,12},{9,1},{13,5},{1,9},{5,13},{10,2},{14,6},... | collective-permute-start | bytes 196616 | tf_op jit(solution)/shard_map/ppermute | solution.py:545
  76.7 4.4 %collective-permute-start.22 = (bf16[256,128]{1,0:T(8,128)(2,1)S(1)}, bf16[256,128]{1,0:T(8,128)(2,1)S(1)}, u32[]{:S(2)}, u32[]{:S(2)}) collective-permute-start(bf16[256,128]{1,0:T(8,128)(2,1)S(1)} %add_convert_fusion.2), channel_id=1, source_target_pairs={{12,0},{8,4},{4,8},{0,12},{13,1},{9,5},{5,9},{1,13},{14,2},{10,6},... | collective-permute-start | bytes 196616 | tf_op jit(solution)/shard_map/ppermute | solution.py:545

commit v14 on v13

--- a/solution.py
+++ b/solution.py
@@ -416,7 +416,7 @@
 
 
 def outer_body(at_ref, labels_ref, left_ref, lab_ref, right_ref, wide_ref, grad_ref,
-               outer_ref, weight_out, rm_ref, lb_ref, acc_ref, sum_ref, turn_ref, flip_ref, part_ref):
+               outer_ref, weight_out, rm_ref, lb_ref, even_ref, odd_ref, sum_ref, turn_ref, flip_ref, part_ref):
     seqs = left_ref.shape[0]
     span = right_ref.shape[1]
     cols = span // PROJ
@@ -443,16 +443,17 @@
     sum_ref[...] = jnp.zeros_like(sum_ref)
     quarter = span // PER_TILE
 
-    def product(chain, g, add):
+    def product(chain, g, acc_ref, add):
         masked_left(left_ref, lab_ref, lb_ref, chain, g)
         for q in range(PER_TILE):
             rows = slice(q * quarter, (q + 1) * quarter)
             part = nn_dot(rm_ref[rows, slots(chain, 2, seqs)], rolled(lb_ref[...], q))
             acc_ref[rows] = acc_ref[rows] + part if add else part
 
-    def group(g):
-        product(first(g), g, False)
-        each(1, (last(g) - first(g)) // 2, lambda k: product(first(g) + 2 * k, g, True))
+    def rest(g, acc_ref):
+        each(1, (last(g) - first(g)) // 2, lambda k: product(first(g) + 2 * k, g, acc_ref, True))
+
+    def finish(g, acc_ref):
         for half in range(WIDE // LANES):
             lanes = slice(half * LANES, (half + 1) * LANES)
             for t in range(PROJ // PER_TILE):
@@ -468,7 +469,20 @@
         flat = grad_ref[g].reshape(step * cols, width)
         sum_ref[...] += nn_dot(flat.T, outer_ref[g])
 
-    each(0, groups - 1, group)
+    def turn(g, acc_ref, next_ref):
+        product(first(g + 1), g + 1, next_ref, False)
+        finish(g, acc_ref)
+        rest(g + 1, next_ref)
+
+    def two_groups(i):
+        turn(2 * i, even_ref, odd_ref)
+        turn(2 * i + 1, odd_ref, even_ref)
+
+    product(first(0), 0, even_ref, False)
+    rest(0, even_ref)
+    each(0, groups // 2 - 2, two_groups)
+    turn(groups - 2, even_ref, odd_ref)
+    finish(groups - 1, odd_ref)
     for t in range(PROJ * PROJ // LANES):
         part = slice(t * LANES, (t + 1) * LANES)
         turn_ref[part] = sum_ref[:, part].T
@@ -491,6 +505,7 @@
         scratch_shapes=[
             pltpu.VMEM((span, (CHAINS + 1) * seqs), BF16),
             pltpu.VMEM((2 * seqs, WIDE), BF16),
+            pltpu.VMEM((span, WIDE), F32),
             pltpu.VMEM((span, WIDE), F32),
             pltpu.VMEM((width, PROJ * PROJ), F32),
             pltpu.VMEM((PROJ * PROJ, width), F32),

time: 82.5 us -> 80.2 us (0.972)
  Pallas kernels: 35.9 us -> 33.3 us
    pallas_call x1, Pallas kernels: 10.7 us -> 8.4 us  [outer_call(): pl.pallas_call(outer_body, in_specs=[SMEM] * 2 + [VMEM] * 5, out_specs=[V...]
  transfers between devices with their start and end apart: 25 -> 25, of which waited for: 3 -> 3; matrix products, arithmetic and copies ran while one was open for 3% -> 3% of each run, Pallas kernels for 39% -> 37%
where the time goes in v14:
time: 80.2 us; the launch traced here: 80 us
  starting transfers between devices  38.2 us (48%)
  Pallas kernels  33.3 us (42%)
  waiting for transfers between devices  4.15 us (5%)
  other arithmetic  3.03 us (4%)
  between operations  0.88 us (1%)
    ppermute x12, starting transfers between devices, col_swap(): return lax.ppermute(value, 'col', [(t ^ k, t) for t in range(self.n_col)])  22.8 us
    pallas_call x1, Pallas kernels, outer_call(): pl.pallas_call(outer_body, in_specs=[SMEM] * 2 + [VMEM] * 5, out_specs=[V...  8.4 us
    ppermute x9, starting transfers between devices, row_swap(): return lax.ppermute(value, 'row', [(t ^ k, t) for t in range(self.n_row)])  7.91 us
    ppermute x4, starting transfers between devices, right_grad_home(): got = lax.ppermute(block, ('row', 'col'), pairs).astype(F32)[None]  7.48 us
    pallas_call x1, Pallas kernels, back_call(): pl.pallas_call(lambda *refs: back_body(*refs, seqs=seqs, n_col=n_col), in...  6.94 us
    pallas_call x1, Pallas kernels, right_grad_call(): pl.pallas_call(right_grad_body, in_specs=[SMEM] * 2 + [VMEM] * 4, out_spe...  5.91 us
    pallas_call x1, Pallas kernels, left_grad_call(): pl.pallas_call(left_grad_body, in_specs=[SMEM] * 2 + [VMEM] * 4, out_spec...  5.05 us
    pallas_call x1, Pallas kernels, project_call(): pl.pallas_call(lambda *refs: project_body(*refs, cols=cols), in_specs=[HB...  3.74 us
  transfers between devices with their start and end apart: 25, of which 3 were waited for; matrix products, arithmetic and copies ran while one was open for 3% of the time, Pallas kernels for 37%

profile of v14, /device:TPU:0, one launch (start us, length us, event | category | flops | bytes accessed | tf_op | source)
XLA Modules:
  0.0 80.0 jit_solution(13105221247044073846)
XLA Ops:
  0.6 3.7 %project.1 = (bf16[32,2048]{1,0:T(8,128)(2,1)S(1)}, bf16[32,2048]{1,0:T(8,128)(2,1)S(1)}) custom-call(bf16[32,64,256]{2,1,0:T(8,128)(2,1)} %refs_0_.1, f32[1,256]{1,0:T(1,128)} %bitcast.61, f32[1,256]{1,0:T(1,128)} %bitcast.62, bf16[32,256]{1,0:T(8,128)(2,1)} %bitcast.59, bf16[32,256]{1,0:T(8,128)(2,1)} %bitcast.60), custom_call_target="tpu_custom_call" | custom-call | tf_op jit(solution)/shard_map/project/pallas_call | solution.py:122
  4.4 5.1 %collective-permute-start.2 = (bf16[32,2048]{1,0:T(8,128)(2,1)S(1)}, bf16[32,2048]{1,0:T(8,128)(2,1)S(1)}, u32[]{:S(2)}, u32[]{:S(2)}) collective-permute-start(bf16[32,2048]{1,0:T(8,128)(2,1)S(1)} %get-tuple-element.21), channel_id=1, source_target_pairs={{3,0},{2,1},{1,2},{0,3},{7,4},{6,5},{5,6},{4,7},{11,8},{10,9},{9,1... | collective-permute-start | bytes 393224 | tf_op jit(solution)/shard_map/ppermute | solution.py:557
  9.5 0.7 collective-permute-start.5
  10.2 0.8 %collective-permute-start.4 = (bf16[32,2048]{1,0:T(8,128)(2,1)S(1)}, bf16[32,2048]{1,0:T(8,128)(2,1)S(1)}, u32[]{:S(2)}, u32[]{:S(2)}) collective-permute-start(bf16[32,2048]{1,0:T(8,128)(2,1)S(1)} %get-tuple-element.22), channel_id=1, source_target_pairs={{8,0},{12,4},{0,8},{4,12},{9,1},{13,5},{1,9},{5,13},{10,2},{14,6},... | collective-permute-start | bytes 393224 | tf_op jit(solution)/shard_map/ppermute | solution.py:560
  11.0 0.4 collective-permute-start.3
  11.8 6.9 %back.1 = (s32[1,2048]{1,0:T(1,128)S(1)}, bf16[8,2,128,128]{3,2,1,0:T(8,128)(2,1)S(1)}, bf16[8,2,64,128]{3,2,1,0:T(8,128)(2,1)S(1)}, f32[8,64,128]{2,1,0:T(8,128...) custom-call(s32[3]{0:T(128)S(1)} %add_convert_fusion.3.refs_0_.at_ref, ...), custom_call_target="tpu_custom_call" | custom-call | flops 21474836480 | bytes 8388608 | tf_op jit(solution)/shard_map/back/pallas_call | solution.py:246
  18.7 0.7 collective-permute-start
  19.6 3.8 %collective-permute-start.8 = (bf16[32,2048]{1,0:T(8,128)(2,1)S(1)}, bf16[32,2048]{1,0:T(8,128)(2,1)S(1)}, u32[]{:S(2)}, u32[]{:S(2)}) collective-permute-start(bf16[32,2048]{1,0:T(8,128)(2,1)S(1)} %get-tuple-element.46), channel_id=1, source_target_pairs={{3,0},{2,1},{1,2},{0,3},{7,4},{6,5},{5,6},{4,7},{11,8},{10,9},{9,1... | collective-permute-start | bytes 393224 | tf_op jit(solution)/shard_map/ppermute | solution.py:557
  23.4 1.0 %collective-permute-done = bf16[32,2048]{1,0:T(8,128)(2,1)S(1)} collective-permute-done((bf16[32,2048]{1,0:T(8,128)(2,1)S(1)}, bf16[32,2048]{1,0:T(8,128)(2,1)S(1)}, u32[]{:S(2)}, u32[]{:S(2)}) %collective-permute-start) | collective-permute-done | bytes 131104 | tf_op jit(solution)/shard_map/ppermute | solution.py:557
  24.4 0.8 collective-permute-start.6
  25.2 5.9 %right_grad.1 = bf16[128,2048]{1,0:T(8,128)(2,1)S(1)} custom-call(s32[3]{0:T(128)S(1)} %add_convert_fusion.3.refs_0_.at_ref, s32[256]{0:T(256)S(1)} %copy-done.1, bf16[8,2048,256]{2,1,0:T(8,128)(2,1)S(1)} %get-tuple-element.25.back_ref, bf16[128,2048]{1,0:T(8,128)(2,1)S(1)} %constant_dynamic-update-slice_fusion.left_ref, ...), custom_call_target="tpu_custom_call" | custom-call | flops 21474836480 | bytes 8388608 | tf_op jit(solution)/shard_map/right_grad/pallas_call | solution.py:347
  31.2 0.7 collective-permute-start.15
  31.8 5.7 %collective-permute-start.18 = (bf16[32,2048]{1,0:T(8,128)(2,1)S(1)}, bf16[32,2048]{1,0:T(8,128)(2,1)S(1)}, u32[]{:S(2)}, u32[]{:S(2)}) collective-permute-start(bf16[32,2048]{1,0:T(8,128)(2,1)S(1)} %get-tuple-element.39), channel_id=1, source_target_pairs={{0,3},{1,7},{2,11},{3,15},{4,2},{5,6},{6,10},{7,14},{8,1},{9,5},{1... | collective-permute-start | bytes 393224 | tf_op jit(solution)/shard_map/ppermute | solution.py:593
  37.6 1.1 %collective-permute-start.17 = (bf16[32,2048]{1,0:T(8,128)(2,1)S(1)}, bf16[32,2048]{1,0:T(8,128)(2,1)S(1)}, u32[]{:S(2)}, u32[]{:S(2)}) collective-permute-start(bf16[32,2048]{1,0:T(8,128)(2,1)S(1)} %get-tuple-element.40), channel_id=1, source_target_pairs={{0,2},{1,6},{2,10},{3,14},{4,3},{5,7},{6,11},{7,15},{8,0},{9,4},{1... | collective-permute-start | bytes 393224 | tf_op jit(solution)/shard_map/ppermute | solution.py:593
  38.7 8.4 %outer.1 = (bf16[8,512,1024]{2,1,0:T(8,128)(2,1)S(1)}, f32[1024,128]{1,0:T(8,128)S(1)}) custom-call(s32[3]{0:T(128)S(1)} %add_convert_fusion.3.refs_0_.at_ref, s32[256]{0:T(256)S(1)} %copy-done.1, bf16[128,2048]{1,0:T(8,128)(2,1)S(1)} %constant_dynamic-update-slice_fusion.left_ref, s32[1,2048]{1,0:T(1,128)S(1)} %get-tuple-element.33.lab_ref, ...), custom_call_target="tpu_custom_call" | custom-call | flops 42949672960 | bytes 8388608 | tf_op jit(solution)/shard_map/outer/pallas_call | solution.py:497
  47.2 1.5 %collective-permute-start.9 = (bf16[256,128]{1,0:T(8,128)(2,1)S(1)}, bf16[256,128]{1,0:T(8,128)(2,1)S(1)}, u32[]{:S(2)}, u32[]{:S(2)}) collective-permute-start(bf16[256,128]{1,0:T(8,128)(2,1)S(1)} %get-tuple-element.49), channel_id=1, source_target_pairs={{4,0},{0,4},{12,8},{8,12},{5,1},{1,5},{13,9},{9,13},{6,2},{2,6},{1... | collective-permute-start | bytes 196616 | tf_op jit(solution)/shard_map/ppermute | solution.py:560
  48.7 5.1 %left_grad.1 = bf16[128,2048]{1,0:T(8,128)(2,1)S(1)} custom-call(s32[3]{0:T(128)S(1)} %add_convert_fusion.3.refs_0_.at_ref, s32[256]{0:T(256)S(1)} %copy-done.1, bf16[8,2048,256]{2,1,0:T(8,128)(2,1)S(1)} %get-tuple-element.25.back_ref, s32[1,2048]{1,0:T(1,128)S(1)} %get-tuple-element.33.lab_ref, bf16[128,2048]{1,0:T(8,128)(2,1)S(1)} %pad_maximum_fusion.1.right_ref, ...), custom_call_target="tpu_custom_call" | custom-call | flops 21474836480 | bytes 8388608 | tf_op jit(solution)/shard_map/left_grad/pallas_call | solution.py:403
  53.8 2.7 %collective-permute-start.11 = (bf16[256,128]{1,0:T(8,128)(2,1)S(1)}, bf16[256,128]{1,0:T(8,128)(2,1)S(1)}, u32[]{:S(2)}, u32[]{:S(2)}) collective-permute-start(bf16[256,128]{1,0:T(8,128)(2,1)S(1)} %get-tuple-element.50), channel_id=1, source_target_pairs={{12,0},{8,4},{4,8},{0,12},{13,1},{9,5},{5,9},{1,13},{14,2},{10,6},... | collective-permute-start | bytes 196616 | tf_op jit(solution)/shard_map/ppermute | solution.py:560
  56.4 1.5 %collective-permute-start.12 = (bf16[32,2048]{1,0:T(8,128)(2,1)S(1)}, bf16[32,2048]{1,0:T(8,128)(2,1)S(1)}, u32[]{:S(2)}, u32[]{:S(2)}) collective-permute-start(bf16[32,2048]{1,0:T(8,128)(2,1)S(1)} %get-tuple-element.42), channel_id=1, source_target_pairs={{1,0},{0,1},{3,2},{2,3},{5,4},{4,5},{7,6},{6,7},{9,8},{8,9},{11,10... | collective-permute-start | bytes 393224 | tf_op jit(solution)/shard_map/ppermute | solution.py:557
  58.0 2.6 %collective-permute-start.14 = (bf16[32,2048]{1,0:T(8,128)(2,1)S(1)}, bf16[32,2048]{1,0:T(8,128)(2,1)S(1)}, u32[]{:S(2)}, u32[]{:S(2)}) collective-permute-start(bf16[32,2048]{1,0:T(8,128)(2,1)S(1)} %get-tuple-element.43), channel_id=1, source_target_pairs={{3,0},{2,1},{1,2},{0,3},{7,4},{6,5},{5,6},{4,7},{11,8},{10,9},{9,1... | collective-permute-start | bytes 393224 | tf_op jit(solution)/shard_map/ppermute | solution.py:557
  60.5 0.7 add_convert_fusion
  61.3 1.7 %collective-permute-start.21 = (bf16[256,128]{1,0:T(8,128)(2,1)S(1)}, bf16[256,128]{1,0:T(8,128)(2,1)S(1)}, u32[]{:S(2)}, u32[]{:S(2)}) collective-permute-start(bf16[256,128]{1,0:T(8,128)(2,1)S(1)} %convert_element_type.100), channel_id=1, source_target_pairs={{3,0},{2,1},{1,2},{0,3},{7,4},{6,5},{5,6},{4,7},{11,8},{10,9},{9,1... | collective-permute-start | bytes 196616 | tf_op jit(solution)/shard_map/ppermute | solution.py:557
  63.0 0.7 collective-permute-start.20
  63.7 2.0 %collective-permute-start.19 = (bf16[256,128]{1,0:T(8,128)(2,1)S(1)}, bf16[256,128]{1,0:T(8,128)(2,1)S(1)}, u32[]{:S(2)}, u32[]{:S(2)}) collective-permute-start(bf16[256,128]{1,0:T(8,128)(2,1)S(1)} %convert_element_type.100), channel_id=1, source_target_pairs={{1,0},{0,1},{3,2},{2,3},{5,4},{4,5},{7,6},{6,7},{9,8},{8,9},{11,10... | collective-permute-start | bytes 196616 | tf_op jit(solution)/shard_map/ppermute | solution.py:557
  65.8 3.3 %pair.1 = bf16[4096,128]{1,0:T(8,128)(2,1)} custom-call(bf16[8,512,1024]{2,1,0:T(8,128)(2,1)S(1)} %get-tuple-element.30.outer_ref, bf16[1024,128]{1,0:T(8,128)(2,1)S(1)} %get-tuple-element.36.w_ref, f32[1,128]{1,0:T(1,128)S(1)} %bitcast.52), custom_call_target="tpu_custom_call" | custom-call | flops 1073741824 | bytes 1048576 | tf_op jit(solution)/shard_map/pair/pallas_call | solution.py:533
  69.1 3.8 %collective-permute-start.13 = (bf16[32,2048]{1,0:T(8,128)(2,1)S(1)}, bf16[32,2048]{1,0:T(8,128)(2,1)S(1)}, u32[]{:S(2)}, u32[]{:S(2)}) collective-permute-start(bf16[32,2048]{1,0:T(8,128)(2,1)S(1)} %get-tuple-element.44), channel_id=1, source_target_pairs={{2,0},{3,1},{0,2},{1,3},{6,4},{7,5},{4,6},{5,7},{10,8},{11,9},{8,1... | collective-permute-start | bytes 393224 | tf_op jit(solution)/shard_map/ppermute | solution.py:557
  73.0 1.3 %collective-permute-start.23 = (bf16[256,128]{1,0:T(8,128)(2,1)S(1)}, bf16[256,128]{1,0:T(8,128)(2,1)S(1)}, u32[]{:S(2)}, u32[]{:S(2)}) collective-permute-start(bf16[256,128]{1,0:T(8,128)(2,1)S(1)} %add_convert_fusion.2), channel_id=1, source_target_pairs={{8,0},{12,4},{0,8},{4,12},{9,1},{13,5},{1,9},{5,13},{10,2},{14,6},... | collective-permute-start | bytes 196616 | tf_op jit(solution)/shard_map/ppermute | solution.py:560
  74.4 0.5 collective-permute-start.22
  74.9 2.7 %collective-permute-done.13 = bf16[32,2048]{1,0:T(8,128)(2,1)S(1)} collective-permute-done((bf16[32,2048]{1,0:T(8,128)(2,1)S(1)}, bf16[32,2048]{1,0:T(8,128)(2,1)S(1)}, u32[]{:S(2)}, u32[]{:S(2)}) %collective-permute-start.13) | collective-permute-done | bytes 131104 | tf_op jit(solution)/shard_map/ppermute | solution.py:557
  77.6 0.7 add_convert_fusion.1
  78.3 0.5 collective-permute-done.22
  78.8 1.3 %convert_multiply_fusion = f32[1024,128]{1,0:T(8,128)} fusion(pred[1024]{0:T(1024)(128)(4,1)S(1)} %broadcast_in_dim.105, pred[1024]{0:T(1024)(128)(4,1)S(1)} %broadcast_in_dim.100, pred[1024]{0:T(1024)(128)(4,1)S(1)} %broadcast_in_dim.95, bf16[256,128]{1,0:T(8,128)(2,1)S(1)} %add_convert_fusion.2, bf16[256,128]{1,0:T(8,128)(2,1)S(1)} %collective-permute-done.24, ...), kind=kLoop, calls=%fused_computation.2 | loop fusion | flops 655360 | bytes 789504 | tf_op jit(solution)/shard_map/div | solution.py:662
  (54 shorter events, 0.9 us)
Async XLA Ops:
  4.4 20.8 %collective-permute-start.2 = (bf16[32,2048]{1,0:T(8,128)(2,1)S(1)}, bf16[32,2048]{1,0:T(8,128)(2,1)S(1)}, u32[]{:S(2)}, u32[]{:S(2)}) collective-permute-start(bf16[32,2048]{1,0:T(8,128)(2,1)S(1)} %get-tuple-element.21), channel_id=1, source_target_pairs={{3,0},{2,1},{1,2},{0,3},{7,4},{6,5},{5,6},{4,7},{11,8},{10,9},{9,1... | collective-permute-start | bytes 393224 | tf_op jit(solution)/shard_map/ppermute | solution.py:557
  9.5 15.6 %collective-permute-start.1 = (bf16[32,2048]{1,0:T(8,128)(2,1)S(1)}, bf16[32,2048]{1,0:T(8,128)(2,1)S(1)}, u32[]{:S(2)}, u32[]{:S(2)}) collective-permute-start(bf16[32,2048]{1,0:T(8,128)(2,1)S(1)} %get-tuple-element.21), channel_id=1, source_target_pairs={{2,0},{3,1},{0,2},{1,3},{6,4},{7,5},{4,6},{5,7},{10,8},{11,9},{8,1... | collective-permute-start | bytes 393224 | tf_op jit(solution)/shard_map/ppermute | solution.py:557
  9.5 9.2 %collective-permute-start.5 = (bf16[32,2048]{1,0:T(8,128)(2,1)S(1)}, bf16[32,2048]{1,0:T(8,128)(2,1)S(1)}, u32[]{:S(2)}, u32[]{:S(2)}) collective-permute-start(bf16[32,2048]{1,0:T(8,128)(2,1)S(1)} %get-tuple-element.22), channel_id=1, source_target_pairs={{12,0},{8,4},{4,8},{0,12},{13,1},{9,5},{5,9},{1,13},{14,2},{10,6},... | collective-permute-start | bytes 393224 | tf_op jit(solution)/shard_map/ppermute | solution.py:560
  10.2 9.3 %collective-permute-start.4 = (bf16[32,2048]{1,0:T(8,128)(2,1)S(1)}, bf16[32,2048]{1,0:T(8,128)(2,1)S(1)}, u32[]{:S(2)}, u32[]{:S(2)}) collective-permute-start(bf16[32,2048]{1,0:T(8,128)(2,1)S(1)} %get-tuple-element.22), channel_id=1, source_target_pairs={{8,0},{12,4},{0,8},{4,12},{9,1},{13,5},{1,9},{5,13},{10,2},{14,6},... | collective-permute-start | bytes 393224 | tf_op jit(solution)/shard_map/ppermute | solution.py:560
  11.0 8.4 %collective-permute-start.3 = (bf16[32,2048]{1,0:T(8,128)(2,1)S(1)}, bf16[32,2048]{1,0:T(8,128)(2,1)S(1)}, u32[]{:S(2)}, u32[]{:S(2)}) collective-permute-start(bf16[32,2048]{1,0:T(8,128)(2,1)S(1)} %get-tuple-element.22), channel_id=1, source_target_pairs={{4,0},{0,4},{12,8},{8,12},{5,1},{1,5},{13,9},{9,13},{6,2},{2,6},{1... | collective-permute-start | bytes 393224 | tf_op jit(solution)/shard_map/ppermute | solution.py:560
  11.8 13.4 %copy-start.1 = (s32[256]{0:T(256)S(1)}, s32[256]{0:T(256)}, u32[]{:S(2)}) copy-start(s32[256]{0:T(256)} %labels_ref.5) | copy-start | bytes 3076
  18.7 5.6 %collective-permute-start = (bf16[32,2048]{1,0:T(8,128)(2,1)S(1)}, bf16[32,2048]{1,0:T(8,128)(2,1)S(1)}, u32[]{:S(2)}, u32[]{:S(2)}) collective-permute-start(bf16[32,2048]{1,0:T(8,128)(2,1)S(1)} %get-tuple-element.21), channel_id=1, source_target_pairs={{1,0},{0,1},{3,2},{2,3},{5,4},{4,5},{7,6},{6,7},{9,8},{8,9},{11,10... | collective-permute-start | bytes 393224 | tf_op jit(solution)/shard_map/ppermute | solution.py:557
  19.6 18.0 %collective-permute-start.8 = (bf16[32,2048]{1,0:T(8,128)(2,1)S(1)}, bf16[32,2048]{1,0:T(8,128)(2,1)S(1)}, u32[]{:S(2)}, u32[]{:S(2)}) collective-permute-start(bf16[32,2048]{1,0:T(8,128)(2,1)S(1)} %get-tuple-element.46), channel_id=1, source_target_pairs={{3,0},{2,1},{1,2},{0,3},{7,4},{6,5},{5,6},{4,7},{11,8},{10,9},{9,1... | collective-permute-start | bytes 393224 | tf_op jit(solution)/shard_map/ppermute | solution.py:557
  23.4 15.3 %collective-permute-start.7 = (bf16[32,2048]{1,0:T(8,128)(2,1)S(1)}, bf16[32,2048]{1,0:T(8,128)(2,1)S(1)}, u32[]{:S(2)}, u32[]{:S(2)}) collective-permute-start(bf16[32,2048]{1,0:T(8,128)(2,1)S(1)} %get-tuple-element.47), channel_id=1, source_target_pairs={{2,0},{3,1},{0,2},{1,3},{6,4},{7,5},{4,6},{5,7},{10,8},{11,9},{8,1... | collective-permute-start | bytes 393224 | tf_op jit(solution)/shard_map/ppermute | solution.py:557
  24.4 14.3 %collective-permute-start.6 = (bf16[32,2048]{1,0:T(8,128)(2,1)S(1)}, bf16[32,2048]{1,0:T(8,128)(2,1)S(1)}, u32[]{:S(2)}, u32[]{:S(2)}) collective-permute-start(bf16[32,2048]{1,0:T(8,128)(2,1)S(1)} %get-tuple-element.48), channel_id=1, source_target_pairs={{1,0},{0,1},{3,2},{2,3},{5,4},{4,5},{7,6},{6,7},{9,8},{8,9},{11,10... | collective-permute-start | bytes 393224 | tf_op jit(solution)/shard_map/ppermute | solution.py:557
  31.2 22.6 %collective-permute-start.15 = (bf16[32,2048]{1,0:T(8,128)(2,1)S(1)}, bf16[32,2048]{1,0:T(8,128)(2,1)S(1)}, u32[]{:S(2)}, u32[]{:S(2)}) collective-permute-start(bf16[32,2048]{1,0:T(8,128)(2,1)S(1)} %get-tuple-element.38), channel_id=1, source_target_pairs={{0,0},{1,4},{2,8},{3,12},{4,1},{5,5},{6,9},{7,13},{8,2},{9,6},{10,... | collective-permute-start | bytes 393224 | tf_op jit(solution)/shard_map/ppermute | solution.py:593
  31.8 24.6 %collective-permute-start.18 = (bf16[32,2048]{1,0:T(8,128)(2,1)S(1)}, bf16[32,2048]{1,0:T(8,128)(2,1)S(1)}, u32[]{:S(2)}, u32[]{:S(2)}) collective-permute-start(bf16[32,2048]{1,0:T(8,128)(2,1)S(1)} %get-tuple-element.39), channel_id=1, source_target_pairs={{0,3},{1,7},{2,11},{3,15},{4,2},{5,6},{6,10},{7,14},{8,1},{9,5},{1... | collective-permute-start | bytes 393224 | tf_op jit(solution)/shard_map/ppermute | solution.py:593
  37.6 18.8 %collective-permute-start.17 = (bf16[32,2048]{1,0:T(8,128)(2,1)S(1)}, bf16[32,2048]{1,0:T(8,128)(2,1)S(1)}, u32[]{:S(2)}, u32[]{:S(2)}) collective-permute-start(bf16[32,2048]{1,0:T(8,128)(2,1)S(1)} %get-tuple-element.40), channel_id=1, source_target_pairs={{0,2},{1,6},{2,10},{3,14},{4,3},{5,7},{6,11},{7,15},{8,0},{9,4},{1... | collective-permute-start | bytes 393224 | tf_op jit(solution)/shard_map/ppermute | solution.py:593
  38.7 19.3 %collective-permute-start.16 = (bf16[32,2048]{1,0:T(8,128)(2,1)S(1)}, bf16[32,2048]{1,0:T(8,128)(2,1)S(1)}, u32[]{:S(2)}, u32[]{:S(2)}) collective-permute-start(bf16[32,2048]{1,0:T(8,128)(2,1)S(1)} %get-tuple-element.41), channel_id=1, source_target_pairs={{0,1},{1,5},{2,9},{3,13},{4,0},{5,4},{6,8},{7,12},{8,3},{9,7},{10,... | collective-permute-start | bytes 393224 | tf_op jit(solution)/shard_map/ppermute | solution.py:593
  47.2 14.1 %collective-permute-start.9 = (bf16[256,128]{1,0:T(8,128)(2,1)S(1)}, bf16[256,128]{1,0:T(8,128)(2,1)S(1)}, u32[]{:S(2)}, u32[]{:S(2)}) collective-permute-start(bf16[256,128]{1,0:T(8,128)(2,1)S(1)} %get-tuple-element.49), channel_id=1, source_target_pairs={{4,0},{0,4},{12,8},{8,12},{5,1},{1,5},{13,9},{9,13},{6,2},{2,6},{1... | collective-permute-start | bytes 196616 | tf_op jit(solution)/shard_map/ppermute | solution.py:560
  48.7 17.1 %copy-start = (f32[128]{0:T(128)S(1)}, f32[128]{0:T(128)}, u32[]{:S(2)}) copy-start(f32[128]{0:T(128)} %param.16) | copy-start | bytes 1540
  53.8 7.5 %collective-permute-start.11 = (bf16[256,128]{1,0:T(8,128)(2,1)S(1)}, bf16[256,128]{1,0:T(8,128)(2,1)S(1)}, u32[]{:S(2)}, u32[]{:S(2)}) collective-permute-start(bf16[256,128]{1,0:T(8,128)(2,1)S(1)} %get-tuple-element.50), channel_id=1, source_target_pairs={{12,0},{8,4},{4,8},{0,12},{13,1},{9,5},{5,9},{1,13},{14,2},{10,6},... | collective-permute-start | bytes 196616 | tf_op jit(solution)/shard_map/ppermute | solution.py:560
  56.4 4.8 %collective-permute-start.10 = (bf16[256,128]{1,0:T(8,128)(2,1)S(1)}, bf16[256,128]{1,0:T(8,128)(2,1)S(1)}, u32[]{:S(2)}, u32[]{:S(2)}) collective-permute-start(bf16[256,128]{1,0:T(8,128)(2,1)S(1)} %get-tuple-element.51), channel_id=1, source_target_pairs={{8,0},{12,4},{0,8},{4,12},{9,1},{13,5},{1,9},{5,13},{10,2},{14,6},... | collective-permute-start | bytes 196616 | tf_op jit(solution)/shard_map/ppermute | solution.py:560
  56.4 17.9 %collective-permute-start.12 = (bf16[32,2048]{1,0:T(8,128)(2,1)S(1)}, bf16[32,2048]{1,0:T(8,128)(2,1)S(1)}, u32[]{:S(2)}, u32[]{:S(2)}) collective-permute-start(bf16[32,2048]{1,0:T(8,128)(2,1)S(1)} %get-tuple-element.42), channel_id=1, source_target_pairs={{1,0},{0,1},{3,2},{2,3},{5,4},{4,5},{7,6},{6,7},{9,8},{8,9},{11,10... | collective-permute-start | bytes 393224 | tf_op jit(solution)/shard_map/ppermute | solution.py:557
  58.0 16.9 %collective-permute-start.14 = (bf16[32,2048]{1,0:T(8,128)(2,1)S(1)}, bf16[32,2048]{1,0:T(8,128)(2,1)S(1)}, u32[]{:S(2)}, u32[]{:S(2)}) collective-permute-start(bf16[32,2048]{1,0:T(8,128)(2,1)S(1)} %get-tuple-element.43), channel_id=1, source_target_pairs={{3,0},{2,1},{1,2},{0,3},{7,4},{6,5},{5,6},{4,7},{11,8},{10,9},{9,1... | collective-permute-start | bytes 393224 | tf_op jit(solution)/shard_map/ppermute | solution.py:557
  61.3 7.8 %collective-permute-start.21 = (bf16[256,128]{1,0:T(8,128)(2,1)S(1)}, bf16[256,128]{1,0:T(8,128)(2,1)S(1)}, u32[]{:S(2)}, u32[]{:S(2)}) collective-permute-start(bf16[256,128]{1,0:T(8,128)(2,1)S(1)} %convert_element_type.100), channel_id=1, source_target_pairs={{3,0},{2,1},{1,2},{0,3},{7,4},{6,5},{5,6},{4,7},{11,8},{10,9},{9,1... | collective-permute-start | bytes 196616 | tf_op jit(solution)/shard_map/ppermute | solution.py:557
  63.0 9.9 %collective-permute-start.20 = (bf16[256,128]{1,0:T(8,128)(2,1)S(1)}, bf16[256,128]{1,0:T(8,128)(2,1)S(1)}, u32[]{:S(2)}, u32[]{:S(2)}) collective-permute-start(bf16[256,128]{1,0:T(8,128)(2,1)S(1)} %convert_element_type.100), channel_id=1, source_target_pairs={{2,0},{3,1},{0,2},{1,3},{6,4},{7,5},{4,6},{5,7},{10,8},{11,9},{8,1... | collective-permute-start | bytes 196616 | tf_op jit(solution)/shard_map/ppermute | solution.py:557
  63.7 9.2 %collective-permute-start.19 = (bf16[256,128]{1,0:T(8,128)(2,1)S(1)}, bf16[256,128]{1,0:T(8,128)(2,1)S(1)}, u32[]{:S(2)}, u32[]{:S(2)}) collective-permute-start(bf16[256,128]{1,0:T(8,128)(2,1)S(1)} %convert_element_type.100), channel_id=1, source_target_pairs={{1,0},{0,1},{3,2},{2,3},{5,4},{4,5},{7,6},{6,7},{9,8},{8,9},{11,10... | collective-permute-start | bytes 196616 | tf_op jit(solution)/shard_map/ppermute | solution.py:557
  69.1 8.5 %collective-permute-start.13 = (bf16[32,2048]{1,0:T(8,128)(2,1)S(1)}, bf16[32,2048]{1,0:T(8,128)(2,1)S(1)}, u32[]{:S(2)}, u32[]{:S(2)}) collective-permute-start(bf16[32,2048]{1,0:T(8,128)(2,1)S(1)} %get-tuple-element.44), channel_id=1, source_target_pairs={{2,0},{3,1},{0,2},{1,3},{6,4},{7,5},{4,6},{5,7},{10,8},{11,9},{8,1... | collective-permute-start | bytes 393224 | tf_op jit(solution)/shard_map/ppermute | solution.py:557
  73.0 5.3 %collective-permute-start.24 = (bf16[256,128]{1,0:T(8,128)(2,1)S(1)}, bf16[256,128]{1,0:T(8,128)(2,1)S(1)}, u32[]{:S(2)}, u32[]{:S(2)}) collective-permute-start(bf16[256,128]{1,0:T(8,128)(2,1)S(1)} %add_convert_fusion.2), channel_id=1, source_target_pairs={{4,0},{0,4},{12,8},{8,12},{5,1},{1,5},{13,9},{9,13},{6,2},{2,6},{1... | collective-permute-start | bytes 196616 | tf_op jit(solution)/shard_map/ppermute | solution.py:560
  73.0 5.3 %collective-permute-start.23 = (bf16[256,128]{1,0:T(8,128)(2,1)S(1)}, bf16[256,128]{1,0:T(8,128)(2,1)S(1)}, u32[]{:S(2)}, u32[]{:S(2)}) collective-permute-start(bf16[256,128]{1,0:T(8,128)(2,1)S(1)} %add_convert_fusion.2), channel_id=1, source_target_pairs={{8,0},{12,4},{0,8},{4,12},{9,1},{13,5},{1,9},{5,13},{10,2},{14,6},... | collective-permute-start | bytes 196616 | tf_op jit(solution)/shard_map/ppermute | solution.py:560
  74.4 4.4 %collective-permute-start.22 = (bf16[256,128]{1,0:T(8,128)(2,1)S(1)}, bf16[256,128]{1,0:T(8,128)(2,1)S(1)}, u32[]{:S(2)}, u32[]{:S(2)}) collective-permute-start(bf16[256,128]{1,0:T(8,128)(2,1)S(1)} %add_convert_fusion.2), channel_id=1, source_target_pairs={{12,0},{8,4},{4,8},{0,12},{13,1},{9,5},{5,9},{1,13},{14,2},{10,6},... | collective-permute-start | bytes 196616 | tf_op jit(solution)/shard_map/ppermute | solution.py:560

commit v15 on v14

--- a/solution.py
+++ b/solution.py
@@ -1,3 +1,5 @@
+import functools
+
 import jax
 import jax.numpy as jnp
 from jax import lax
@@ -212,8 +214,7 @@
           groups * step, cols, seqs, n_col)
     halves = step // PER_TILE
 
-    def group(g, carry):
-        grad_of(g).wait()
+    def group(g):
         blocks = [
             jnp.concatenate([grad_ref[g, half * PER_TILE + p] for half in range(halves)], axis=0)
             for p in range(PER_TILE)
@@ -233,9 +234,14 @@
                         e = u * (WIDE // PROJ) + t * PER_TILE + q
                         at = (g, slice(e * cols, (e + 1) * cols))
                         back_ref[at + (slice(half * LANES, (half + 1) * LANES),)] = part
-        return carry
-
-    lax.fori_loop(0, groups, group, 0)
+
+    def two_groups(i):
+        grad_of(2 * i).wait()
+        grad_of(2 * i + 1).wait()
+        group(2 * i)
+        group(2 * i + 1)
+
+    each(0, groups // 2 - 1, two_groups)
 
 
 def back_call(at, labels, counts, w, grad, seqs, n_col):
@@ -380,20 +386,22 @@
     each(first(0), last(groups - 1), build)
     rm_ref[slots(last(groups - 1) + 1, 1, seqs)] = jnp.zeros((seqs, span), BF16)
 
-    def group(g):
+    def two_chains(g, k, total):
         lab = lab_ref[:, lanes_of(g)]
-
-        def two_chains(k, total):
-            chain = first(g) + 2 * k
-            part = nn_dot(rm_ref[slots(chain, 2, seqs)], back_ref[g])
-            keep0, keep1 = lab == chain, lab == chain + 1
-            return total + jnp.where(keep0, part[:seqs], 0.0) + jnp.where(keep1, part[seqs:], 0.0)
-
-        passes = (last(g) - first(g)) // 2 + 1
-        total = lax.fori_loop(0, passes, two_chains, jnp.zeros((seqs, WIDE), F32))
-        left_out[:, lanes_of(g)] = total.astype(BF16)
-
-    each(0, groups - 1, group)
+        chain = first(g) + 2 * k
+        part = nn_dot(rm_ref[slots(chain, 2, seqs)], back_ref[g])
+        keep0, keep1 = lab == chain, lab == chain + 1
+        part = jnp.where(keep0, part[:seqs], 0.0) + jnp.where(keep1, part[seqs:], 0.0)
+        return part if total is None else total + part
+
+    def two_groups(i):
+        totals = [two_chains(g, 0, None) for g in (2 * i, 2 * i + 1)]
+        for g, total in zip((2 * i, 2 * i + 1), totals):
+            more = functools.partial(two_chains, g)
+            total = lax.fori_loop(1, (last(g) - first(g)) // 2 + 1, more, total)
+            left_out[:, lanes_of(g)] = total.astype(BF16)
+
+    each(0, groups // 2 - 1, two_groups)
 
 
 def left_grad_call(at, labels, back, lab, right, tall):

time: 80.2 us -> 78.7 us (0.981)
  Pallas kernels: 33.3 us -> 31.9 us
  transfers between devices with their start and end apart: 25 -> 25, of which waited for: 3 -> 3; matrix products, arithmetic and copies ran while one was open for 3% -> 3% of each run, Pallas kernels for 37% -> 36%
where the time goes in v15:
time: 78.7 us; the launch traced here: 78.6 us
  starting transfers between devices  38.2 us (49%)
  Pallas kernels  31.9 us (41%)
  waiting for transfers between devices  4.13 us (5%)
  other arithmetic  3.03 us (4%)
  between operations  0.88 us (1%)
    ppermute x12, starting transfers between devices, col_swap(): return lax.ppermute(value, 'col', [(t ^ k, t) for t in range(self.n_col)])  22.8 us
    pallas_call x1, Pallas kernels, outer_call(): pl.pallas_call(outer_body, in_specs=[SMEM] * 2 + [VMEM] * 5, out_specs=[V...  8.4 us
    ppermute x9, starting transfers between devices, row_swap(): return lax.ppermute(value, 'row', [(t ^ k, t) for t in range(self.n_row)])  7.91 us
    ppermute x4, starting transfers between devices, right_grad_home(): got = lax.ppermute(block, ('row', 'col'), pairs).astype(F32)[None]  7.47 us
    pallas_call x1, Pallas kernels, back_call(): pl.pallas_call(lambda *refs: back_body(*refs, seqs=seqs, n_col=n_col), in...  6.21 us
    pallas_call x1, Pallas kernels, right_grad_call(): pl.pallas_call(right_grad_body, in_specs=[SMEM] * 2 + [VMEM] * 4, out_spe...  5.91 us
    pallas_call x1, Pallas kernels, left_grad_call(): pl.pallas_call(left_grad_body, in_specs=[SMEM] * 2 + [VMEM] * 4, out_spec...  4.29 us
    pallas_call x1, Pallas kernels, project_call(): pl.pallas_call(lambda *refs: project_body(*refs, cols=cols), in_specs=[HB...  3.74 us
  transfers between devices with their start and end apart: 25, of which 3 were waited for; matrix products, arithmetic and copies ran while one was open for 3% of the time, Pallas kernels for 36%

profile of v15, /device:TPU:0, one launch (start us, length us, event | category | flops | bytes accessed | tf_op | source)
XLA Modules:
  0.0 78.6 jit_solution(15895105311295961172)
XLA Ops:
  0.6 3.7 %project.1 = (bf16[32,2048]{1,0:T(8,128)(2,1)S(1)}, bf16[32,2048]{1,0:T(8,128)(2,1)S(1)}) custom-call(bf16[32,64,256]{2,1,0:T(8,128)(2,1)} %refs_0_.1, f32[1,256]{1,0:T(1,128)} %bitcast.61, f32[1,256]{1,0:T(1,128)} %bitcast.62, bf16[32,256]{1,0:T(8,128)(2,1)} %bitcast.59, bf16[32,256]{1,0:T(8,128)(2,1)} %bitcast.60), custom_call_target="tpu_custom_call" | custom-call | tf_op jit(solution)/shard_map/project/pallas_call | solution.py:124
  4.4 5.1 %collective-permute-start.2 = (bf16[32,2048]{1,0:T(8,128)(2,1)S(1)}, bf16[32,2048]{1,0:T(8,128)(2,1)S(1)}, u32[]{:S(2)}, u32[]{:S(2)}) collective-permute-start(bf16[32,2048]{1,0:T(8,128)(2,1)S(1)} %get-tuple-element.21), channel_id=1, source_target_pairs={{3,0},{2,1},{1,2},{0,3},{7,4},{6,5},{5,6},{4,7},{11,8},{10,9},{9,1... | collective-permute-start | bytes 393224 | tf_op jit(solution)/shard_map/ppermute | solution.py:565
  9.5 0.7 collective-permute-start.5
  10.2 0.8 %collective-permute-start.4 = (bf16[32,2048]{1,0:T(8,128)(2,1)S(1)}, bf16[32,2048]{1,0:T(8,128)(2,1)S(1)}, u32[]{:S(2)}, u32[]{:S(2)}) collective-permute-start(bf16[32,2048]{1,0:T(8,128)(2,1)S(1)} %get-tuple-element.22), channel_id=1, source_target_pairs={{8,0},{12,4},{0,8},{4,12},{9,1},{13,5},{1,9},{5,13},{10,2},{14,6},... | collective-permute-start | bytes 393224 | tf_op jit(solution)/shard_map/ppermute | solution.py:568
  11.0 0.4 collective-permute-start.3
  11.8 6.2 %back.1 = (s32[1,2048]{1,0:T(1,128)S(1)}, bf16[8,2,128,128]{3,2,1,0:T(8,128)(2,1)S(1)}, bf16[8,2,64,128]{3,2,1,0:T(8,128)(2,1)S(1)}, f32[8,64,128]{2,1,0:T(8,128...) custom-call(s32[3]{0:T(128)S(1)} %add_convert_fusion.3.refs_0_.at_ref, ...), custom_call_target="tpu_custom_call" | custom-call | flops 21474836480 | bytes 8388608 | tf_op jit(solution)/shard_map/back/pallas_call | solution.py:252
  18.0 0.7 collective-permute-start
  18.8 3.8 %collective-permute-start.8 = (bf16[32,2048]{1,0:T(8,128)(2,1)S(1)}, bf16[32,2048]{1,0:T(8,128)(2,1)S(1)}, u32[]{:S(2)}, u32[]{:S(2)}) collective-permute-start(bf16[32,2048]{1,0:T(8,128)(2,1)S(1)} %get-tuple-element.46), channel_id=1, source_target_pairs={{3,0},{2,1},{1,2},{0,3},{7,4},{6,5},{5,6},{4,7},{11,8},{10,9},{9,1... | collective-permute-start | bytes 393224 | tf_op jit(solution)/shard_map/ppermute | solution.py:565
  22.7 1.0 %collective-permute-done = bf16[32,2048]{1,0:T(8,128)(2,1)S(1)} collective-permute-done((bf16[32,2048]{1,0:T(8,128)(2,1)S(1)}, bf16[32,2048]{1,0:T(8,128)(2,1)S(1)}, u32[]{:S(2)}, u32[]{:S(2)}) %collective-permute-start) | collective-permute-done | bytes 131104 | tf_op jit(solution)/shard_map/ppermute | solution.py:565
  23.6 0.8 collective-permute-start.6
  24.5 5.9 %right_grad.1 = bf16[128,2048]{1,0:T(8,128)(2,1)S(1)} custom-call(s32[3]{0:T(128)S(1)} %add_convert_fusion.3.refs_0_.at_ref, s32[256]{0:T(256)S(1)} %copy-done.1, bf16[8,2048,256]{2,1,0:T(8,128)(2,1)S(1)} %get-tuple-element.25.back_ref, bf16[128,2048]{1,0:T(8,128)(2,1)S(1)} %constant_dynamic-update-slice_fusion.left_ref, ...), custom_call_target="tpu_custom_call" | custom-call | flops 21474836480 | bytes 8388608 | tf_op jit(solution)/shard_map/right_grad/pallas_call | solution.py:353
  30.5 0.7 collective-permute-start.15
  31.1 5.7 %collective-permute-start.18 = (bf16[32,2048]{1,0:T(8,128)(2,1)S(1)}, bf16[32,2048]{1,0:T(8,128)(2,1)S(1)}, u32[]{:S(2)}, u32[]{:S(2)}) collective-permute-start(bf16[32,2048]{1,0:T(8,128)(2,1)S(1)} %get-tuple-element.39), channel_id=1, source_target_pairs={{0,3},{1,7},{2,11},{3,15},{4,2},{5,6},{6,10},{7,14},{8,1},{9,5},{1... | collective-permute-start | bytes 393224 | tf_op jit(solution)/shard_map/ppermute | solution.py:601
  36.9 1.1 %collective-permute-start.17 = (bf16[32,2048]{1,0:T(8,128)(2,1)S(1)}, bf16[32,2048]{1,0:T(8,128)(2,1)S(1)}, u32[]{:S(2)}, u32[]{:S(2)}) collective-permute-start(bf16[32,2048]{1,0:T(8,128)(2,1)S(1)} %get-tuple-element.40), channel_id=1, source_target_pairs={{0,2},{1,6},{2,10},{3,14},{4,3},{5,7},{6,11},{7,15},{8,0},{9,4},{1... | collective-permute-start | bytes 393224 | tf_op jit(solution)/shard_map/ppermute | solution.py:601
  38.0 8.4 %outer.1 = (bf16[8,512,1024]{2,1,0:T(8,128)(2,1)S(1)}, f32[1024,128]{1,0:T(8,128)S(1)}) custom-call(s32[3]{0:T(128)S(1)} %add_convert_fusion.3.refs_0_.at_ref, s32[256]{0:T(256)S(1)} %copy-done.1, bf16[128,2048]{1,0:T(8,128)(2,1)S(1)} %constant_dynamic-update-slice_fusion.left_ref, s32[1,2048]{1,0:T(1,128)S(1)} %get-tuple-element.33.lab_ref, ...), custom_call_target="tpu_custom_call" | custom-call | flops 42949672960 | bytes 8388608 | tf_op jit(solution)/shard_map/outer/pallas_call | solution.py:505
  46.5 1.5 %collective-permute-start.9 = (bf16[256,128]{1,0:T(8,128)(2,1)S(1)}, bf16[256,128]{1,0:T(8,128)(2,1)S(1)}, u32[]{:S(2)}, u32[]{:S(2)}) collective-permute-start(bf16[256,128]{1,0:T(8,128)(2,1)S(1)} %get-tuple-element.49), channel_id=1, source_target_pairs={{4,0},{0,4},{12,8},{8,12},{5,1},{1,5},{13,9},{9,13},{6,2},{2,6},{1... | collective-permute-start | bytes 196616 | tf_op jit(solution)/shard_map/ppermute | solution.py:568
  47.9 4.3 %left_grad.1 = bf16[128,2048]{1,0:T(8,128)(2,1)S(1)} custom-call(s32[3]{0:T(128)S(1)} %add_convert_fusion.3.refs_0_.at_ref, s32[256]{0:T(256)S(1)} %copy-done.1, bf16[8,2048,256]{2,1,0:T(8,128)(2,1)S(1)} %get-tuple-element.25.back_ref, s32[1,2048]{1,0:T(1,128)S(1)} %get-tuple-element.33.lab_ref, bf16[128,2048]{1,0:T(8,128)(2,1)S(1)} %pad_maximum_fusion.1.right_ref, ...), custom_call_target="tpu_custom_call" | custom-call | flops 21474836480 | bytes 8388608 | tf_op jit(solution)/shard_map/left_grad/pallas_call | solution.py:411
  52.3 2.7 %collective-permute-start.11 = (bf16[256,128]{1,0:T(8,128)(2,1)S(1)}, bf16[256,128]{1,0:T(8,128)(2,1)S(1)}, u32[]{:S(2)}, u32[]{:S(2)}) collective-permute-start(bf16[256,128]{1,0:T(8,128)(2,1)S(1)} %get-tuple-element.50), channel_id=1, source_target_pairs={{12,0},{8,4},{4,8},{0,12},{13,1},{9,5},{5,9},{1,13},{14,2},{10,6},... | collective-permute-start | bytes 196616 | tf_op jit(solution)/shard_map/ppermute | solution.py:568
  55.0 1.5 %collective-permute-start.12 = (bf16[32,2048]{1,0:T(8,128)(2,1)S(1)}, bf16[32,2048]{1,0:T(8,128)(2,1)S(1)}, u32[]{:S(2)}, u32[]{:S(2)}) collective-permute-start(bf16[32,2048]{1,0:T(8,128)(2,1)S(1)} %get-tuple-element.42), channel_id=1, source_target_pairs={{1,0},{0,1},{3,2},{2,3},{5,4},{4,5},{7,6},{6,7},{9,8},{8,9},{11,10... | collective-permute-start | bytes 393224 | tf_op jit(solution)/shard_map/ppermute | solution.py:565
  56.5 2.6 %collective-permute-start.14 = (bf16[32,2048]{1,0:T(8,128)(2,1)S(1)}, bf16[32,2048]{1,0:T(8,128)(2,1)S(1)}, u32[]{:S(2)}, u32[]{:S(2)}) collective-permute-start(bf16[32,2048]{1,0:T(8,128)(2,1)S(1)} %get-tuple-element.43), channel_id=1, source_target_pairs={{3,0},{2,1},{1,2},{0,3},{7,4},{6,5},{5,6},{4,7},{11,8},{10,9},{9,1... | collective-permute-start | bytes 393224 | tf_op jit(solution)/shard_map/ppermute | solution.py:565
  59.1 0.7 add_convert_fusion
  59.9 1.7 %collective-permute-start.21 = (bf16[256,128]{1,0:T(8,128)(2,1)S(1)}, bf16[256,128]{1,0:T(8,128)(2,1)S(1)}, u32[]{:S(2)}, u32[]{:S(2)}) collective-permute-start(bf16[256,128]{1,0:T(8,128)(2,1)S(1)} %convert_element_type.100), channel_id=1, source_target_pairs={{3,0},{2,1},{1,2},{0,3},{7,4},{6,5},{5,6},{4,7},{11,8},{10,9},{9,1... | collective-permute-start | bytes 196616 | tf_op jit(solution)/shard_map/ppermute | solution.py:565
  61.5 0.7 collective-permute-start.20
  62.3 2.1 %collective-permute-start.19 = (bf16[256,128]{1,0:T(8,128)(2,1)S(1)}, bf16[256,128]{1,0:T(8,128)(2,1)S(1)}, u32[]{:S(2)}, u32[]{:S(2)}) collective-permute-start(bf16[256,128]{1,0:T(8,128)(2,1)S(1)} %convert_element_type.100), channel_id=1, source_target_pairs={{1,0},{0,1},{3,2},{2,3},{5,4},{4,5},{7,6},{6,7},{9,8},{8,9},{11,10... | collective-permute-start | bytes 196616 | tf_op jit(solution)/shard_map/ppermute | solution.py:565
  64.3 3.3 %pair.1 = bf16[4096,128]{1,0:T(8,128)(2,1)} custom-call(bf16[8,512,1024]{2,1,0:T(8,128)(2,1)S(1)} %get-tuple-element.30.outer_ref, bf16[1024,128]{1,0:T(8,128)(2,1)S(1)} %get-tuple-element.36.w_ref, f32[1,128]{1,0:T(1,128)S(1)} %bitcast.52), custom_call_target="tpu_custom_call" | custom-call | flops 1073741824 | bytes 1048576 | tf_op jit(solution)/shard_map/pair/pallas_call | solution.py:541
  67.6 3.8 %collective-permute-start.13 = (bf16[32,2048]{1,0:T(8,128)(2,1)S(1)}, bf16[32,2048]{1,0:T(8,128)(2,1)S(1)}, u32[]{:S(2)}, u32[]{:S(2)}) collective-permute-start(bf16[32,2048]{1,0:T(8,128)(2,1)S(1)} %get-tuple-element.44), channel_id=1, source_target_pairs={{2,0},{3,1},{0,2},{1,3},{6,4},{7,5},{4,6},{5,7},{10,8},{11,9},{8,1... | collective-permute-start | bytes 393224 | tf_op jit(solution)/shard_map/ppermute | solution.py:565
  71.6 1.3 %collective-permute-start.23 = (bf16[256,128]{1,0:T(8,128)(2,1)S(1)}, bf16[256,128]{1,0:T(8,128)(2,1)S(1)}, u32[]{:S(2)}, u32[]{:S(2)}) collective-permute-start(bf16[256,128]{1,0:T(8,128)(2,1)S(1)} %add_convert_fusion.2), channel_id=1, source_target_pairs={{8,0},{12,4},{0,8},{4,12},{9,1},{13,5},{1,9},{5,13},{10,2},{14,6},... | collective-permute-start | bytes 196616 | tf_op jit(solution)/shard_map/ppermute | solution.py:568
  72.9 0.5 collective-permute-start.22
  73.4 2.7 %collective-permute-done.13 = bf16[32,2048]{1,0:T(8,128)(2,1)S(1)} collective-permute-done((bf16[32,2048]{1,0:T(8,128)(2,1)S(1)}, bf16[32,2048]{1,0:T(8,128)(2,1)S(1)}, u32[]{:S(2)}, u32[]{:S(2)}) %collective-permute-start.13) | collective-permute-done | bytes 131104 | tf_op jit(solution)/shard_map/ppermute | solution.py:565
  76.1 0.7 add_convert_fusion.1
  76.8 0.5 collective-permute-done.22
  77.3 1.3 %convert_multiply_fusion = f32[1024,128]{1,0:T(8,128)} fusion(pred[1024]{0:T(1024)(128)(4,1)S(1)} %broadcast_in_dim.105, pred[1024]{0:T(1024)(128)(4,1)S(1)} %broadcast_in_dim.100, pred[1024]{0:T(1024)(128)(4,1)S(1)} %broadcast_in_dim.95, bf16[256,128]{1,0:T(8,128)(2,1)S(1)} %add_convert_fusion.2, bf16[256,128]{1,0:T(8,128)(2,1)S(1)} %collective-permute-done.24, ...), kind=kLoop, calls=%fused_computation.2 | loop fusion | flops 655360 | bytes 789504 | tf_op jit(solution)/shard_map/div | solution.py:670
  (54 shorter events, 0.9 us)
Async XLA Ops:
  4.4 20.1 %collective-permute-start.2 = (bf16[32,2048]{1,0:T(8,128)(2,1)S(1)}, bf16[32,2048]{1,0:T(8,128)(2,1)S(1)}, u32[]{:S(2)}, u32[]{:S(2)}) collective-permute-start(bf16[32,2048]{1,0:T(8,128)(2,1)S(1)} %get-tuple-element.21), channel_id=1, source_target_pairs={{3,0},{2,1},{1,2},{0,3},{7,4},{6,5},{5,6},{4,7},{11,8},{10,9},{9,1... | collective-permute-start | bytes 393224 | tf_op jit(solution)/shard_map/ppermute | solution.py:565
  9.5 14.9 %collective-permute-start.1 = (bf16[32,2048]{1,0:T(8,128)(2,1)S(1)}, bf16[32,2048]{1,0:T(8,128)(2,1)S(1)}, u32[]{:S(2)}, u32[]{:S(2)}) collective-permute-start(bf16[32,2048]{1,0:T(8,128)(2,1)S(1)} %get-tuple-element.21), channel_id=1, source_target_pairs={{2,0},{3,1},{0,2},{1,3},{6,4},{7,5},{4,6},{5,7},{10,8},{11,9},{8,1... | collective-permute-start | bytes 393224 | tf_op jit(solution)/shard_map/ppermute | solution.py:565
  9.5 8.5 %collective-permute-start.5 = (bf16[32,2048]{1,0:T(8,128)(2,1)S(1)}, bf16[32,2048]{1,0:T(8,128)(2,1)S(1)}, u32[]{:S(2)}, u32[]{:S(2)}) collective-permute-start(bf16[32,2048]{1,0:T(8,128)(2,1)S(1)} %get-tuple-element.22), channel_id=1, source_target_pairs={{12,0},{8,4},{4,8},{0,12},{13,1},{9,5},{5,9},{1,13},{14,2},{10,6},... | collective-permute-start | bytes 393224 | tf_op jit(solution)/shard_map/ppermute | solution.py:568
  10.2 8.5 %collective-permute-start.4 = (bf16[32,2048]{1,0:T(8,128)(2,1)S(1)}, bf16[32,2048]{1,0:T(8,128)(2,1)S(1)}, u32[]{:S(2)}, u32[]{:S(2)}) collective-permute-start(bf16[32,2048]{1,0:T(8,128)(2,1)S(1)} %get-tuple-element.22), channel_id=1, source_target_pairs={{8,0},{12,4},{0,8},{4,12},{9,1},{13,5},{1,9},{5,13},{10,2},{14,6},... | collective-permute-start | bytes 393224 | tf_op jit(solution)/shard_map/ppermute | solution.py:568
  11.0 7.7 %collective-permute-start.3 = (bf16[32,2048]{1,0:T(8,128)(2,1)S(1)}, bf16[32,2048]{1,0:T(8,128)(2,1)S(1)}, u32[]{:S(2)}, u32[]{:S(2)}) collective-permute-start(bf16[32,2048]{1,0:T(8,128)(2,1)S(1)} %get-tuple-element.22), channel_id=1, source_target_pairs={{4,0},{0,4},{12,8},{8,12},{5,1},{1,5},{13,9},{9,13},{6,2},{2,6},{1... | collective-permute-start | bytes 393224 | tf_op jit(solution)/shard_map/ppermute | solution.py:568
  11.8 12.7 %copy-start.1 = (s32[256]{0:T(256)S(1)}, s32[256]{0:T(256)}, u32[]{:S(2)}) copy-start(s32[256]{0:T(256)} %labels_ref.5) | copy-start | bytes 3076
  18.0 5.6 %collective-permute-start = (bf16[32,2048]{1,0:T(8,128)(2,1)S(1)}, bf16[32,2048]{1,0:T(8,128)(2,1)S(1)}, u32[]{:S(2)}, u32[]{:S(2)}) collective-permute-start(bf16[32,2048]{1,0:T(8,128)(2,1)S(1)} %get-tuple-element.21), channel_id=1, source_target_pairs={{1,0},{0,1},{3,2},{2,3},{5,4},{4,5},{7,6},{6,7},{9,8},{8,9},{11,10... | collective-permute-start | bytes 393224 | tf_op jit(solution)/shard_map/ppermute | solution.py:565
  18.8 18.0 %collective-permute-start.8 = (bf16[32,2048]{1,0:T(8,128)(2,1)S(1)}, bf16[32,2048]{1,0:T(8,128)(2,1)S(1)}, u32[]{:S(2)}, u32[]{:S(2)}) collective-permute-start(bf16[32,2048]{1,0:T(8,128)(2,1)S(1)} %get-tuple-element.46), channel_id=1, source_target_pairs={{3,0},{2,1},{1,2},{0,3},{7,4},{6,5},{5,6},{4,7},{11,8},{10,9},{9,1... | collective-permute-start | bytes 393224 | tf_op jit(solution)/shard_map/ppermute | solution.py:565
  22.7 15.3 %collective-permute-start.7 = (bf16[32,2048]{1,0:T(8,128)(2,1)S(1)}, bf16[32,2048]{1,0:T(8,128)(2,1)S(1)}, u32[]{:S(2)}, u32[]{:S(2)}) collective-permute-start(bf16[32,2048]{1,0:T(8,128)(2,1)S(1)} %get-tuple-element.47), channel_id=1, source_target_pairs={{2,0},{3,1},{0,2},{1,3},{6,4},{7,5},{4,6},{5,7},{10,8},{11,9},{8,1... | collective-permute-start | bytes 393224 | tf_op jit(solution)/shard_map/ppermute | solution.py:565
  23.6 14.3 %collective-permute-start.6 = (bf16[32,2048]{1,0:T(8,128)(2,1)S(1)}, bf16[32,2048]{1,0:T(8,128)(2,1)S(1)}, u32[]{:S(2)}, u32[]{:S(2)}) collective-permute-start(bf16[32,2048]{1,0:T(8,128)(2,1)S(1)} %get-tuple-element.48), channel_id=1, source_target_pairs={{1,0},{0,1},{3,2},{2,3},{5,4},{4,5},{7,6},{6,7},{9,8},{8,9},{11,10... | collective-permute-start | bytes 393224 | tf_op jit(solution)/shard_map/ppermute | solution.py:565
  30.5 21.8 %collective-permute-start.15 = (bf16[32,2048]{1,0:T(8,128)(2,1)S(1)}, bf16[32,2048]{1,0:T(8,128)(2,1)S(1)}, u32[]{:S(2)}, u32[]{:S(2)}) collective-permute-start(bf16[32,2048]{1,0:T(8,128)(2,1)S(1)} %get-tuple-element.38), channel_id=1, source_target_pairs={{0,0},{1,4},{2,8},{3,12},{4,1},{5,5},{6,9},{7,13},{8,2},{9,6},{10,... | collective-permute-start | bytes 393224 | tf_op jit(solution)/shard_map/ppermute | solution.py:601
  31.1 23.8 %collective-permute-start.18 = (bf16[32,2048]{1,0:T(8,128)(2,1)S(1)}, bf16[32,2048]{1,0:T(8,128)(2,1)S(1)}, u32[]{:S(2)}, u32[]{:S(2)}) collective-permute-start(bf16[32,2048]{1,0:T(8,128)(2,1)S(1)} %get-tuple-element.39), channel_id=1, source_target_pairs={{0,3},{1,7},{2,11},{3,15},{4,2},{5,6},{6,10},{7,14},{8,1},{9,5},{1... | collective-permute-start | bytes 393224 | tf_op jit(solution)/shard_map/ppermute | solution.py:601
  36.9 18.1 %collective-permute-start.17 = (bf16[32,2048]{1,0:T(8,128)(2,1)S(1)}, bf16[32,2048]{1,0:T(8,128)(2,1)S(1)}, u32[]{:S(2)}, u32[]{:S(2)}) collective-permute-start(bf16[32,2048]{1,0:T(8,128)(2,1)S(1)} %get-tuple-element.40), channel_id=1, source_target_pairs={{0,2},{1,6},{2,10},{3,14},{4,3},{5,7},{6,11},{7,15},{8,0},{9,4},{1... | collective-permute-start | bytes 393224 | tf_op jit(solution)/shard_map/ppermute | solution.py:601
  37.9 18.5 %collective-permute-start.16 = (bf16[32,2048]{1,0:T(8,128)(2,1)S(1)}, bf16[32,2048]{1,0:T(8,128)(2,1)S(1)}, u32[]{:S(2)}, u32[]{:S(2)}) collective-permute-start(bf16[32,2048]{1,0:T(8,128)(2,1)S(1)} %get-tuple-element.41), channel_id=1, source_target_pairs={{0,1},{1,5},{2,9},{3,13},{4,0},{5,4},{6,8},{7,12},{8,3},{9,7},{10,... | collective-permute-start | bytes 393224 | tf_op jit(solution)/shard_map/ppermute | solution.py:601
  46.5 13.3 %collective-permute-start.9 = (bf16[256,128]{1,0:T(8,128)(2,1)S(1)}, bf16[256,128]{1,0:T(8,128)(2,1)S(1)}, u32[]{:S(2)}, u32[]{:S(2)}) collective-permute-start(bf16[256,128]{1,0:T(8,128)(2,1)S(1)} %get-tuple-element.49), channel_id=1, source_target_pairs={{4,0},{0,4},{12,8},{8,12},{5,1},{1,5},{13,9},{9,13},{6,2},{2,6},{1... | collective-permute-start | bytes 196616 | tf_op jit(solution)/shard_map/ppermute | solution.py:568
  47.9 16.4 %copy-start = (f32[128]{0:T(128)S(1)}, f32[128]{0:T(128)}, u32[]{:S(2)}) copy-start(f32[128]{0:T(128)} %param.16) | copy-start | bytes 1540
  52.3 7.5 %collective-permute-start.11 = (bf16[256,128]{1,0:T(8,128)(2,1)S(1)}, bf16[256,128]{1,0:T(8,128)(2,1)S(1)}, u32[]{:S(2)}, u32[]{:S(2)}) collective-permute-start(bf16[256,128]{1,0:T(8,128)(2,1)S(1)} %get-tuple-element.50), channel_id=1, source_target_pairs={{12,0},{8,4},{4,8},{0,12},{13,1},{9,5},{5,9},{1,13},{14,2},{10,6},... | collective-permute-start | bytes 196616 | tf_op jit(solution)/shard_map/ppermute | solution.py:568
  54.9 4.8 %collective-permute-start.10 = (bf16[256,128]{1,0:T(8,128)(2,1)S(1)}, bf16[256,128]{1,0:T(8,128)(2,1)S(1)}, u32[]{:S(2)}, u32[]{:S(2)}) collective-permute-start(bf16[256,128]{1,0:T(8,128)(2,1)S(1)} %get-tuple-element.51), channel_id=1, source_target_pairs={{8,0},{12,4},{0,8},{4,12},{9,1},{13,5},{1,9},{5,13},{10,2},{14,6},... | collective-permute-start | bytes 196616 | tf_op jit(solution)/shard_map/ppermute | solution.py:568
  55.0 17.9 %collective-permute-start.12 = (bf16[32,2048]{1,0:T(8,128)(2,1)S(1)}, bf16[32,2048]{1,0:T(8,128)(2,1)S(1)}, u32[]{:S(2)}, u32[]{:S(2)}) collective-permute-start(bf16[32,2048]{1,0:T(8,128)(2,1)S(1)} %get-tuple-element.42), channel_id=1, source_target_pairs={{1,0},{0,1},{3,2},{2,3},{5,4},{4,5},{7,6},{6,7},{9,8},{8,9},{11,10... | collective-permute-start | bytes 393224 | tf_op jit(solution)/shard_map/ppermute | solution.py:565
  56.5 17.0 %collective-permute-start.14 = (bf16[32,2048]{1,0:T(8,128)(2,1)S(1)}, bf16[32,2048]{1,0:T(8,128)(2,1)S(1)}, u32[]{:S(2)}, u32[]{:S(2)}) collective-permute-start(bf16[32,2048]{1,0:T(8,128)(2,1)S(1)} %get-tuple-element.43), channel_id=1, source_target_pairs={{3,0},{2,1},{1,2},{0,3},{7,4},{6,5},{5,6},{4,7},{11,8},{10,9},{9,1... | collective-permute-start | bytes 393224 | tf_op jit(solution)/shard_map/ppermute | solution.py:565
  59.9 7.8 %collective-permute-start.21 = (bf16[256,128]{1,0:T(8,128)(2,1)S(1)}, bf16[256,128]{1,0:T(8,128)(2,1)S(1)}, u32[]{:S(2)}, u32[]{:S(2)}) collective-permute-start(bf16[256,128]{1,0:T(8,128)(2,1)S(1)} %convert_element_type.100), channel_id=1, source_target_pairs={{3,0},{2,1},{1,2},{0,3},{7,4},{6,5},{5,6},{4,7},{11,8},{10,9},{9,1... | collective-permute-start | bytes 196616 | tf_op jit(solution)/shard_map/ppermute | solution.py:565
  61.5 9.9 %collective-permute-start.20 = (bf16[256,128]{1,0:T(8,128)(2,1)S(1)}, bf16[256,128]{1,0:T(8,128)(2,1)S(1)}, u32[]{:S(2)}, u32[]{:S(2)}) collective-permute-start(bf16[256,128]{1,0:T(8,128)(2,1)S(1)} %convert_element_type.100), channel_id=1, source_target_pairs={{2,0},{3,1},{0,2},{1,3},{6,4},{7,5},{4,6},{5,7},{10,8},{11,9},{8,1... | collective-permute-start | bytes 196616 | tf_op jit(solution)/shard_map/ppermute | solution.py:565
  62.3 9.2 %collective-permute-start.19 = (bf16[256,128]{1,0:T(8,128)(2,1)S(1)}, bf16[256,128]{1,0:T(8,128)(2,1)S(1)}, u32[]{:S(2)}, u32[]{:S(2)}) collective-permute-start(bf16[256,128]{1,0:T(8,128)(2,1)S(1)} %convert_element_type.100), channel_id=1, source_target_pairs={{1,0},{0,1},{3,2},{2,3},{5,4},{4,5},{7,6},{6,7},{9,8},{8,9},{11,10... | collective-permute-start | bytes 196616 | tf_op jit(solution)/shard_map/ppermute | solution.py:565
  67.6 8.5 %collective-permute-start.13 = (bf16[32,2048]{1,0:T(8,128)(2,1)S(1)}, bf16[32,2048]{1,0:T(8,128)(2,1)S(1)}, u32[]{:S(2)}, u32[]{:S(2)}) collective-permute-start(bf16[32,2048]{1,0:T(8,128)(2,1)S(1)} %get-tuple-element.44), channel_id=1, source_target_pairs={{2,0},{3,1},{0,2},{1,3},{6,4},{7,5},{4,6},{5,7},{10,8},{11,9},{8,1... | collective-permute-start | bytes 393224 | tf_op jit(solution)/shard_map/ppermute | solution.py:565
  71.5 5.3 %collective-permute-start.24 = (bf16[256,128]{1,0:T(8,128)(2,1)S(1)}, bf16[256,128]{1,0:T(8,128)(2,1)S(1)}, u32[]{:S(2)}, u32[]{:S(2)}) collective-permute-start(bf16[256,128]{1,0:T(8,128)(2,1)S(1)} %add_convert_fusion.2), channel_id=1, source_target_pairs={{4,0},{0,4},{12,8},{8,12},{5,1},{1,5},{13,9},{9,13},{6,2},{2,6},{1... | collective-permute-start | bytes 196616 | tf_op jit(solution)/shard_map/ppermute | solution.py:568
  71.6 5.2 %collective-permute-start.23 = (bf16[256,128]{1,0:T(8,128)(2,1)S(1)}, bf16[256,128]{1,0:T(8,128)(2,1)S(1)}, u32[]{:S(2)}, u32[]{:S(2)}) collective-permute-start(bf16[256,128]{1,0:T(8,128)(2,1)S(1)} %add_convert_fusion.2), channel_id=1, source_target_pairs={{8,0},{12,4},{0,8},{4,12},{9,1},{13,5},{1,9},{5,13},{10,2},{14,6},... | collective-permute-start | bytes 196616 | tf_op jit(solution)/shard_map/ppermute | solution.py:568
  72.9 4.4 %collective-permute-start.22 = (bf16[256,128]{1,0:T(8,128)(2,1)S(1)}, bf16[256,128]{1,0:T(8,128)(2,1)S(1)}, u32[]{:S(2)}, u32[]{:S(2)}) collective-permute-start(bf16[256,128]{1,0:T(8,128)(2,1)S(1)} %add_convert_fusion.2), channel_id=1, source_target_pairs={{12,0},{8,4},{4,8},{0,12},{13,1},{9,5},{5,9},{1,13},{14,2},{10,6},... | collective-permute-start | bytes 196616 | tf_op jit(solution)/shard_map/ppermute | solution.py:568

commit v16 on v15

--- a/solution.py
+++ b/solution.py
@@ -309,7 +309,7 @@
 
 
 def right_grad_body(at_ref, labels_ref, back_ref, left_ref, lab_ref, wide_ref,
-                    right_out, q_ref, lb_ref, flip_ref, turn_ref):
+                    right_out, q_ref, lb_ref, next_ref, flip_ref, turn_ref):
     seqs = left_ref.shape[0]
     groups, span, _ = back_ref.shape
     cols = span // PROJ
@@ -321,15 +321,33 @@
 
     each(first(0), last(groups - 1) + 1, clear)
 
-    def group(g):
-        def two_chains(k):
-            chain = first(g) + 2 * k
+    def two_chains(g, k):
+        chain = first(g) + 2 * k
+        masked_left(left_ref, lab_ref, lb_ref, chain, g)
+        q_ref[:, slots(chain, 2, seqs)] += nt_dot(back_ref[g], lb_ref[...])
+
+    def two_groups(i):
+        g = 2 * i
+        chain = first(g)
+        same = first(g + 1) == chain
+
+        @pl.when(same)
+        def _():
             masked_left(left_ref, lab_ref, lb_ref, chain, g)
-            q_ref[:, slots(chain, 2, seqs)] += nt_dot(back_ref[g], lb_ref[...])
-
-        each(0, (last(g) - first(g)) // 2, two_chains)
-
-    each(0, groups - 1, group)
+            masked_left(left_ref, lab_ref, next_ref, chain, g + 1)
+            q_ref[:, slots(chain, 2, seqs)] += nt_dot(back_ref[g], lb_ref[...]) + nt_dot(
+                back_ref[g + 1], next_ref[...]
+            )
+
+        @pl.when(jnp.logical_not(same))
+        def _():
+            two_chains(g, 0)
+            two_chains(g + 1, 0)
+
+        each(1, (last(g) - first(g)) // 2, lambda k: two_chains(g, k))
+        each(1, (last(g + 1) - first(g + 1)) // 2, lambda k: two_chains(g + 1, k))
+
+    each(0, groups // 2 - 1, two_groups)
 
     def combine(chain, start):
         for e in range(PROJ):
@@ -357,6 +375,7 @@
         out_shape=jax.ShapeDtypeStruct((seqs, span), BF16),
         scratch_shapes=[
             pltpu.VMEM((span, (CHAINS + 1) * seqs), F32),
+            pltpu.VMEM((2 * seqs, WIDE), BF16),
             pltpu.VMEM((2 * seqs, WIDE), BF16),
             pltpu.VMEM((span, seqs), F32),
             pltpu.VMEM((span, seqs), F32),

time: 78.7 us -> 78.2 us (level)
  transfers between devices with their start and end apart: 25 -> 25, of which waited for: 3 -> 3; matrix products, arithmetic and copies ran while one was open for 3% -> 3% of each run, Pallas kernels for 36% -> 35%
where the time goes in v16:
time: 78.2 us; the launch traced here: 78 us
  starting transfers between devices  38.2 us (49%)
  Pallas kernels  31.3 us (40%)
  waiting for transfers between devices  4.12 us (5%)
  other arithmetic  3.03 us (4%)
  between operations  0.88 us (1%)
    ppermute x12, starting transfers between devices, col_swap(): return lax.ppermute(value, 'col', [(t ^ k, t) for t in range(self.n_col)])  22.8 us
    pallas_call x1, Pallas kernels, outer_call(): pl.pallas_call(outer_body, in_specs=[SMEM] * 2 + [VMEM] * 5, out_specs=[V...  8.39 us
    ppermute x9, starting transfers between devices, row_swap(): return lax.ppermute(value, 'row', [(t ^ k, t) for t in range(self.n_row)])  8.17 us
    ppermute x4, starting transfers between devices, right_grad_home(): got = lax.ppermute(block, ('row', 'col'), pairs).astype(F32)[None]  7.21 us
    pallas_call x1, Pallas kernels, back_call(): pl.pallas_call(lambda *refs: back_body(*refs, seqs=seqs, n_col=n_col), in...  6.21 us
    pallas_call x1, Pallas kernels, right_grad_call(): pl.pallas_call(right_grad_body, in_specs=[SMEM] * 2 + [VMEM] * 4, out_spe...  5.36 us
    pallas_call x1, Pallas kernels, left_grad_call(): pl.pallas_call(left_grad_body, in_specs=[SMEM] * 2 + [VMEM] * 4, out_spec...  4.29 us
    pallas_call x1, Pallas kernels, project_call(): pl.pallas_call(lambda *refs: project_body(*refs, cols=cols), in_specs=[HB...  3.74 us
  transfers between devices with their start and end apart: 25, of which 3 were waited for; matrix products, arithmetic and copies ran while one was open for 3% of the time, Pallas kernels for 35%

profile of v16, /device:TPU:0, one launch (start us, length us, event | category | flops | bytes accessed | tf_op | source)
XLA Modules:
  0.0 78.0 jit_solution(679624572804754095)
XLA Ops:
  0.6 3.7 %project.1 = (bf16[32,2048]{1,0:T(8,128)(2,1)S(1)}, bf16[32,2048]{1,0:T(8,128)(2,1)S(1)}) custom-call(bf16[32,64,256]{2,1,0:T(8,128)(2,1)} %refs_0_.1, f32[1,256]{1,0:T(1,128)} %bitcast.61, f32[1,256]{1,0:T(1,128)} %bitcast.62, bf16[32,256]{1,0:T(8,128)(2,1)} %bitcast.59, bf16[32,256]{1,0:T(8,128)(2,1)} %bitcast.60), custom_call_target="tpu_custom_call" | custom-call | tf_op jit(solution)/shard_map/project/pallas_call | solution.py:124
  4.4 5.1 %collective-permute-start.2 = (bf16[32,2048]{1,0:T(8,128)(2,1)S(1)}, bf16[32,2048]{1,0:T(8,128)(2,1)S(1)}, u32[]{:S(2)}, u32[]{:S(2)}) collective-permute-start(bf16[32,2048]{1,0:T(8,128)(2,1)S(1)} %get-tuple-element.21), channel_id=1, source_target_pairs={{3,0},{2,1},{1,2},{0,3},{7,4},{6,5},{5,6},{4,7},{11,8},{10,9},{9,1... | collective-permute-start | bytes 393224 | tf_op jit(solution)/shard_map/ppermute | solution.py:584
  9.5 0.7 collective-permute-start.5
  10.2 0.8 %collective-permute-start.4 = (bf16[32,2048]{1,0:T(8,128)(2,1)S(1)}, bf16[32,2048]{1,0:T(8,128)(2,1)S(1)}, u32[]{:S(2)}, u32[]{:S(2)}) collective-permute-start(bf16[32,2048]{1,0:T(8,128)(2,1)S(1)} %get-tuple-element.22), channel_id=1, source_target_pairs={{8,0},{12,4},{0,8},{4,12},{9,1},{13,5},{1,9},{5,13},{10,2},{14,6},... | collective-permute-start | bytes 393224 | tf_op jit(solution)/shard_map/ppermute | solution.py:587
  11.0 0.4 collective-permute-start.3
  11.8 6.2 %back.1 = (s32[1,2048]{1,0:T(1,128)S(1)}, bf16[8,2,128,128]{3,2,1,0:T(8,128)(2,1)S(1)}, bf16[8,2,64,128]{3,2,1,0:T(8,128)(2,1)S(1)}, f32[8,64,128]{2,1,0:T(8,128...) custom-call(s32[3]{0:T(128)S(1)} %add_convert_fusion.3.refs_0_.at_ref, ...), custom_call_target="tpu_custom_call" | custom-call | flops 21474836480 | bytes 8388608 | tf_op jit(solution)/shard_map/back/pallas_call | solution.py:252
  18.0 0.7 collective-permute-start
  18.8 3.8 %collective-permute-start.8 = (bf16[32,2048]{1,0:T(8,128)(2,1)S(1)}, bf16[32,2048]{1,0:T(8,128)(2,1)S(1)}, u32[]{:S(2)}, u32[]{:S(2)}) collective-permute-start(bf16[32,2048]{1,0:T(8,128)(2,1)S(1)} %get-tuple-element.46), channel_id=1, source_target_pairs={{3,0},{2,1},{1,2},{0,3},{7,4},{6,5},{5,6},{4,7},{11,8},{10,9},{9,1... | collective-permute-start | bytes 393224 | tf_op jit(solution)/shard_map/ppermute | solution.py:584
  22.7 1.0 %collective-permute-done = bf16[32,2048]{1,0:T(8,128)(2,1)S(1)} collective-permute-done((bf16[32,2048]{1,0:T(8,128)(2,1)S(1)}, bf16[32,2048]{1,0:T(8,128)(2,1)S(1)}, u32[]{:S(2)}, u32[]{:S(2)}) %collective-permute-start) | collective-permute-done | bytes 131104 | tf_op jit(solution)/shard_map/ppermute | solution.py:584
  23.6 0.8 %collective-permute-start.6 = (bf16[32,2048]{1,0:T(8,128)(2,1)S(1)}, bf16[32,2048]{1,0:T(8,128)(2,1)S(1)}, u32[]{:S(2)}, u32[]{:S(2)}) collective-permute-start(bf16[32,2048]{1,0:T(8,128)(2,1)S(1)} %get-tuple-element.48), channel_id=1, source_target_pairs={{1,0},{0,1},{3,2},{2,3},{5,4},{4,5},{7,6},{6,7},{9,8},{8,9},{11,10... | collective-permute-start | bytes 393224 | tf_op jit(solution)/shard_map/ppermute | solution.py:584
  24.5 5.4 %right_grad.1 = bf16[128,2048]{1,0:T(8,128)(2,1)S(1)} custom-call(s32[3]{0:T(128)S(1)} %add_convert_fusion.3.refs_0_.at_ref, s32[256]{0:T(256)S(1)} %copy-done.1, bf16[8,2048,256]{2,1,0:T(8,128)(2,1)S(1)} %get-tuple-element.25.back_ref, bf16[128,2048]{1,0:T(8,128)(2,1)S(1)} %constant_dynamic-update-slice_fusion.left_ref, ...), custom_call_target="tpu_custom_call" | custom-call | flops 21474836480 | bytes 8388608 | tf_op jit(solution)/shard_map/right_grad/pallas_call | solution.py:371
  29.9 0.7 collective-permute-start.15
  30.6 5.7 %collective-permute-start.18 = (bf16[32,2048]{1,0:T(8,128)(2,1)S(1)}, bf16[32,2048]{1,0:T(8,128)(2,1)S(1)}, u32[]{:S(2)}, u32[]{:S(2)}) collective-permute-start(bf16[32,2048]{1,0:T(8,128)(2,1)S(1)} %get-tuple-element.39), channel_id=1, source_target_pairs={{0,3},{1,7},{2,11},{3,15},{4,2},{5,6},{6,10},{7,14},{8,1},{9,5},{1... | collective-permute-start | bytes 393224 | tf_op jit(solution)/shard_map/ppermute | solution.py:620
  36.3 0.8 %collective-permute-start.17 = (bf16[32,2048]{1,0:T(8,128)(2,1)S(1)}, bf16[32,2048]{1,0:T(8,128)(2,1)S(1)}, u32[]{:S(2)}, u32[]{:S(2)}) collective-permute-start(bf16[32,2048]{1,0:T(8,128)(2,1)S(1)} %get-tuple-element.40), channel_id=1, source_target_pairs={{0,2},{1,6},{2,10},{3,14},{4,3},{5,7},{6,11},{7,15},{8,0},{9,4},{1... | collective-permute-start | bytes 393224 | tf_op jit(solution)/shard_map/ppermute | solution.py:620
  37.2 8.4 %outer.1 = (bf16[8,512,1024]{2,1,0:T(8,128)(2,1)S(1)}, f32[1024,128]{1,0:T(8,128)S(1)}) custom-call(s32[3]{0:T(128)S(1)} %add_convert_fusion.3.refs_0_.at_ref, s32[256]{0:T(256)S(1)} %copy-done.1, bf16[128,2048]{1,0:T(8,128)(2,1)S(1)} %constant_dynamic-update-slice_fusion.left_ref, s32[1,2048]{1,0:T(1,128)S(1)} %get-tuple-element.33.lab_ref, ...), custom_call_target="tpu_custom_call" | custom-call | flops 42949672960 | bytes 8388608 | tf_op jit(solution)/shard_map/outer/pallas_call | solution.py:524
  45.7 1.5 %collective-permute-start.9 = (bf16[256,128]{1,0:T(8,128)(2,1)S(1)}, bf16[256,128]{1,0:T(8,128)(2,1)S(1)}, u32[]{:S(2)}, u32[]{:S(2)}) collective-permute-start(bf16[256,128]{1,0:T(8,128)(2,1)S(1)} %get-tuple-element.49), channel_id=1, source_target_pairs={{4,0},{0,4},{12,8},{8,12},{5,1},{1,5},{13,9},{9,13},{6,2},{2,6},{1... | collective-permute-start | bytes 196616 | tf_op jit(solution)/shard_map/ppermute | solution.py:587
  47.1 4.3 %left_grad.1 = bf16[128,2048]{1,0:T(8,128)(2,1)S(1)} custom-call(s32[3]{0:T(128)S(1)} %add_convert_fusion.3.refs_0_.at_ref, s32[256]{0:T(256)S(1)} %copy-done.1, bf16[8,2048,256]{2,1,0:T(8,128)(2,1)S(1)} %get-tuple-element.25.back_ref, s32[1,2048]{1,0:T(1,128)S(1)} %get-tuple-element.33.lab_ref, bf16[128,2048]{1,0:T(8,128)(2,1)S(1)} %pad_maximum_fusion.1.right_ref, ...), custom_call_target="tpu_custom_call" | custom-call | flops 21474836480 | bytes 8388608 | tf_op jit(solution)/shard_map/left_grad/pallas_call | solution.py:430
  51.5 2.9 %collective-permute-start.11 = (bf16[256,128]{1,0:T(8,128)(2,1)S(1)}, bf16[256,128]{1,0:T(8,128)(2,1)S(1)}, u32[]{:S(2)}, u32[]{:S(2)}) collective-permute-start(bf16[256,128]{1,0:T(8,128)(2,1)S(1)} %get-tuple-element.50), channel_id=1, source_target_pairs={{12,0},{8,4},{4,8},{0,12},{13,1},{9,5},{5,9},{1,13},{14,2},{10,6},... | collective-permute-start | bytes 196616 | tf_op jit(solution)/shard_map/ppermute | solution.py:587
  54.4 1.5 %collective-permute-start.12 = (bf16[32,2048]{1,0:T(8,128)(2,1)S(1)}, bf16[32,2048]{1,0:T(8,128)(2,1)S(1)}, u32[]{:S(2)}, u32[]{:S(2)}) collective-permute-start(bf16[32,2048]{1,0:T(8,128)(2,1)S(1)} %get-tuple-element.42), channel_id=1, source_target_pairs={{1,0},{0,1},{3,2},{2,3},{5,4},{4,5},{7,6},{6,7},{9,8},{8,9},{11,10... | collective-permute-start | bytes 393224 | tf_op jit(solution)/shard_map/ppermute | solution.py:584
  55.9 2.6 %collective-permute-start.14 = (bf16[32,2048]{1,0:T(8,128)(2,1)S(1)}, bf16[32,2048]{1,0:T(8,128)(2,1)S(1)}, u32[]{:S(2)}, u32[]{:S(2)}) collective-permute-start(bf16[32,2048]{1,0:T(8,128)(2,1)S(1)} %get-tuple-element.43), channel_id=1, source_target_pairs={{3,0},{2,1},{1,2},{0,3},{7,4},{6,5},{5,6},{4,7},{11,8},{10,9},{9,1... | collective-permute-start | bytes 393224 | tf_op jit(solution)/shard_map/ppermute | solution.py:584
  58.5 0.7 add_convert_fusion
  59.3 1.7 %collective-permute-start.21 = (bf16[256,128]{1,0:T(8,128)(2,1)S(1)}, bf16[256,128]{1,0:T(8,128)(2,1)S(1)}, u32[]{:S(2)}, u32[]{:S(2)}) collective-permute-start(bf16[256,128]{1,0:T(8,128)(2,1)S(1)} %convert_element_type.100), channel_id=1, source_target_pairs={{3,0},{2,1},{1,2},{0,3},{7,4},{6,5},{5,6},{4,7},{11,8},{10,9},{9,1... | collective-permute-start | bytes 196616 | tf_op jit(solution)/shard_map/ppermute | solution.py:584
  61.0 0.7 collective-permute-start.20
  61.7 2.1 %collective-permute-start.19 = (bf16[256,128]{1,0:T(8,128)(2,1)S(1)}, bf16[256,128]{1,0:T(8,128)(2,1)S(1)}, u32[]{:S(2)}, u32[]{:S(2)}) collective-permute-start(bf16[256,128]{1,0:T(8,128)(2,1)S(1)} %convert_element_type.100), channel_id=1, source_target_pairs={{1,0},{0,1},{3,2},{2,3},{5,4},{4,5},{7,6},{6,7},{9,8},{8,9},{11,10... | collective-permute-start | bytes 196616 | tf_op jit(solution)/shard_map/ppermute | solution.py:584
  63.8 3.3 %pair.1 = bf16[4096,128]{1,0:T(8,128)(2,1)} custom-call(bf16[8,512,1024]{2,1,0:T(8,128)(2,1)S(1)} %get-tuple-element.30.outer_ref, bf16[1024,128]{1,0:T(8,128)(2,1)S(1)} %get-tuple-element.36.w_ref, f32[1,128]{1,0:T(1,128)S(1)} %bitcast.52), custom_call_target="tpu_custom_call" | custom-call | flops 1073741824 | bytes 1048576 | tf_op jit(solution)/shard_map/pair/pallas_call | solution.py:560
  67.1 3.8 %collective-permute-start.13 = (bf16[32,2048]{1,0:T(8,128)(2,1)S(1)}, bf16[32,2048]{1,0:T(8,128)(2,1)S(1)}, u32[]{:S(2)}, u32[]{:S(2)}) collective-permute-start(bf16[32,2048]{1,0:T(8,128)(2,1)S(1)} %get-tuple-element.44), channel_id=1, source_target_pairs={{2,0},{3,1},{0,2},{1,3},{6,4},{7,5},{4,6},{5,7},{10,8},{11,9},{8,1... | collective-permute-start | bytes 393224 | tf_op jit(solution)/shard_map/ppermute | solution.py:584
  71.0 1.3 %collective-permute-start.23 = (bf16[256,128]{1,0:T(8,128)(2,1)S(1)}, bf16[256,128]{1,0:T(8,128)(2,1)S(1)}, u32[]{:S(2)}, u32[]{:S(2)}) collective-permute-start(bf16[256,128]{1,0:T(8,128)(2,1)S(1)} %add_convert_fusion.2), channel_id=1, source_target_pairs={{8,0},{12,4},{0,8},{4,12},{9,1},{13,5},{1,9},{5,13},{10,2},{14,6},... | collective-permute-start | bytes 196616 | tf_op jit(solution)/shard_map/ppermute | solution.py:587
  72.4 0.5 collective-permute-start.22
  72.9 2.6 %collective-permute-done.13 = bf16[32,2048]{1,0:T(8,128)(2,1)S(1)} collective-permute-done((bf16[32,2048]{1,0:T(8,128)(2,1)S(1)}, bf16[32,2048]{1,0:T(8,128)(2,1)S(1)}, u32[]{:S(2)}, u32[]{:S(2)}) %collective-permute-start.13) | collective-permute-done | bytes 131104 | tf_op jit(solution)/shard_map/ppermute | solution.py:584
  75.5 0.7 add_convert_fusion.1
  76.3 0.5 collective-permute-done.22
  76.7 1.3 %convert_multiply_fusion = f32[1024,128]{1,0:T(8,128)} fusion(pred[1024]{0:T(1024)(128)(4,1)S(1)} %broadcast_in_dim.105, pred[1024]{0:T(1024)(128)(4,1)S(1)} %broadcast_in_dim.100, pred[1024]{0:T(1024)(128)(4,1)S(1)} %broadcast_in_dim.95, bf16[256,128]{1,0:T(8,128)(2,1)S(1)} %add_convert_fusion.2, bf16[256,128]{1,0:T(8,128)(2,1)S(1)} %collective-permute-done.24, ...), kind=kLoop, calls=%fused_computation.2 | loop fusion | flops 655360 | bytes 789504 | tf_op jit(solution)/shard_map/div | solution.py:689
  (54 shorter events, 0.9 us)
Async XLA Ops:
  4.4 20.1 %collective-permute-start.2 = (bf16[32,2048]{1,0:T(8,128)(2,1)S(1)}, bf16[32,2048]{1,0:T(8,128)(2,1)S(1)}, u32[]{:S(2)}, u32[]{:S(2)}) collective-permute-start(bf16[32,2048]{1,0:T(8,128)(2,1)S(1)} %get-tuple-element.21), channel_id=1, source_target_pairs={{3,0},{2,1},{1,2},{0,3},{7,4},{6,5},{5,6},{4,7},{11,8},{10,9},{9,1... | collective-permute-start | bytes 393224 | tf_op jit(solution)/shard_map/ppermute | solution.py:584
  9.5 14.9 %collective-permute-start.1 = (bf16[32,2048]{1,0:T(8,128)(2,1)S(1)}, bf16[32,2048]{1,0:T(8,128)(2,1)S(1)}, u32[]{:S(2)}, u32[]{:S(2)}) collective-permute-start(bf16[32,2048]{1,0:T(8,128)(2,1)S(1)} %get-tuple-element.21), channel_id=1, source_target_pairs={{2,0},{3,1},{0,2},{1,3},{6,4},{7,5},{4,6},{5,7},{10,8},{11,9},{8,1... | collective-permute-start | bytes 393224 | tf_op jit(solution)/shard_map/ppermute | solution.py:584
  9.5 8.5 %collective-permute-start.5 = (bf16[32,2048]{1,0:T(8,128)(2,1)S(1)}, bf16[32,2048]{1,0:T(8,128)(2,1)S(1)}, u32[]{:S(2)}, u32[]{:S(2)}) collective-permute-start(bf16[32,2048]{1,0:T(8,128)(2,1)S(1)} %get-tuple-element.22), channel_id=1, source_target_pairs={{12,0},{8,4},{4,8},{0,12},{13,1},{9,5},{5,9},{1,13},{14,2},{10,6},... | collective-permute-start | bytes 393224 | tf_op jit(solution)/shard_map/ppermute | solution.py:587
  10.2 8.5 %collective-permute-start.4 = (bf16[32,2048]{1,0:T(8,128)(2,1)S(1)}, bf16[32,2048]{1,0:T(8,128)(2,1)S(1)}, u32[]{:S(2)}, u32[]{:S(2)}) collective-permute-start(bf16[32,2048]{1,0:T(8,128)(2,1)S(1)} %get-tuple-element.22), channel_id=1, source_target_pairs={{8,0},{12,4},{0,8},{4,12},{9,1},{13,5},{1,9},{5,13},{10,2},{14,6},... | collective-permute-start | bytes 393224 | tf_op jit(solution)/shard_map/ppermute | solution.py:587
  11.0 7.7 %collective-permute-start.3 = (bf16[32,2048]{1,0:T(8,128)(2,1)S(1)}, bf16[32,2048]{1,0:T(8,128)(2,1)S(1)}, u32[]{:S(2)}, u32[]{:S(2)}) collective-permute-start(bf16[32,2048]{1,0:T(8,128)(2,1)S(1)} %get-tuple-element.22), channel_id=1, source_target_pairs={{4,0},{0,4},{12,8},{8,12},{5,1},{1,5},{13,9},{9,13},{6,2},{2,6},{1... | collective-permute-start | bytes 393224 | tf_op jit(solution)/shard_map/ppermute | solution.py:587
  11.8 12.7 %copy-start.1 = (s32[256]{0:T(256)S(1)}, s32[256]{0:T(256)}, u32[]{:S(2)}) copy-start(s32[256]{0:T(256)} %labels_ref.5) | copy-start | bytes 3076
  18.0 5.6 %collective-permute-start = (bf16[32,2048]{1,0:T(8,128)(2,1)S(1)}, bf16[32,2048]{1,0:T(8,128)(2,1)S(1)}, u32[]{:S(2)}, u32[]{:S(2)}) collective-permute-start(bf16[32,2048]{1,0:T(8,128)(2,1)S(1)} %get-tuple-element.21), channel_id=1, source_target_pairs={{1,0},{0,1},{3,2},{2,3},{5,4},{4,5},{7,6},{6,7},{9,8},{8,9},{11,10... | collective-permute-start | bytes 393224 | tf_op jit(solution)/shard_map/ppermute | solution.py:584
  18.8 17.5 %collective-permute-start.8 = (bf16[32,2048]{1,0:T(8,128)(2,1)S(1)}, bf16[32,2048]{1,0:T(8,128)(2,1)S(1)}, u32[]{:S(2)}, u32[]{:S(2)}) collective-permute-start(bf16[32,2048]{1,0:T(8,128)(2,1)S(1)} %get-tuple-element.46), channel_id=1, source_target_pairs={{3,0},{2,1},{1,2},{0,3},{7,4},{6,5},{5,6},{4,7},{11,8},{10,9},{9,1... | collective-permute-start | bytes 393224 | tf_op jit(solution)/shard_map/ppermute | solution.py:584
  22.7 14.5 %collective-permute-start.7 = (bf16[32,2048]{1,0:T(8,128)(2,1)S(1)}, bf16[32,2048]{1,0:T(8,128)(2,1)S(1)}, u32[]{:S(2)}, u32[]{:S(2)}) collective-permute-start(bf16[32,2048]{1,0:T(8,128)(2,1)S(1)} %get-tuple-element.47), channel_id=1, source_target_pairs={{2,0},{3,1},{0,2},{1,3},{6,4},{7,5},{4,6},{5,7},{10,8},{11,9},{8,1... | collective-permute-start | bytes 393224 | tf_op jit(solution)/shard_map/ppermute | solution.py:584
  23.6 13.5 %collective-permute-start.6 = (bf16[32,2048]{1,0:T(8,128)(2,1)S(1)}, bf16[32,2048]{1,0:T(8,128)(2,1)S(1)}, u32[]{:S(2)}, u32[]{:S(2)}) collective-permute-start(bf16[32,2048]{1,0:T(8,128)(2,1)S(1)} %get-tuple-element.48), channel_id=1, source_target_pairs={{1,0},{0,1},{3,2},{2,3},{5,4},{4,5},{7,6},{6,7},{9,8},{8,9},{11,10... | collective-permute-start | bytes 393224 | tf_op jit(solution)/shard_map/ppermute | solution.py:584
  29.9 21.6 %collective-permute-start.15 = (bf16[32,2048]{1,0:T(8,128)(2,1)S(1)}, bf16[32,2048]{1,0:T(8,128)(2,1)S(1)}, u32[]{:S(2)}, u32[]{:S(2)}) collective-permute-start(bf16[32,2048]{1,0:T(8,128)(2,1)S(1)} %get-tuple-element.38), channel_id=1, source_target_pairs={{0,0},{1,4},{2,8},{3,12},{4,1},{5,5},{6,9},{7,13},{8,2},{9,6},{10,... | collective-permute-start | bytes 393224 | tf_op jit(solution)/shard_map/ppermute | solution.py:620
  30.6 23.8 %collective-permute-start.18 = (bf16[32,2048]{1,0:T(8,128)(2,1)S(1)}, bf16[32,2048]{1,0:T(8,128)(2,1)S(1)}, u32[]{:S(2)}, u32[]{:S(2)}) collective-permute-start(bf16[32,2048]{1,0:T(8,128)(2,1)S(1)} %get-tuple-element.39), channel_id=1, source_target_pairs={{0,3},{1,7},{2,11},{3,15},{4,2},{5,6},{6,10},{7,14},{8,1},{9,5},{1... | collective-permute-start | bytes 393224 | tf_op jit(solution)/shard_map/ppermute | solution.py:620
  36.3 18.1 %collective-permute-start.17 = (bf16[32,2048]{1,0:T(8,128)(2,1)S(1)}, bf16[32,2048]{1,0:T(8,128)(2,1)S(1)}, u32[]{:S(2)}, u32[]{:S(2)}) collective-permute-start(bf16[32,2048]{1,0:T(8,128)(2,1)S(1)} %get-tuple-element.40), channel_id=1, source_target_pairs={{0,2},{1,6},{2,10},{3,14},{4,3},{5,7},{6,11},{7,15},{8,0},{9,4},{1... | collective-permute-start | bytes 393224 | tf_op jit(solution)/shard_map/ppermute | solution.py:620
  37.1 18.8 %collective-permute-start.16 = (bf16[32,2048]{1,0:T(8,128)(2,1)S(1)}, bf16[32,2048]{1,0:T(8,128)(2,1)S(1)}, u32[]{:S(2)}, u32[]{:S(2)}) collective-permute-start(bf16[32,2048]{1,0:T(8,128)(2,1)S(1)} %get-tuple-element.41), channel_id=1, source_target_pairs={{0,1},{1,5},{2,9},{3,13},{4,0},{5,4},{6,8},{7,12},{8,3},{9,7},{10,... | collective-permute-start | bytes 393224 | tf_op jit(solution)/shard_map/ppermute | solution.py:620
  45.7 13.6 %collective-permute-start.9 = (bf16[256,128]{1,0:T(8,128)(2,1)S(1)}, bf16[256,128]{1,0:T(8,128)(2,1)S(1)}, u32[]{:S(2)}, u32[]{:S(2)}) collective-permute-start(bf16[256,128]{1,0:T(8,128)(2,1)S(1)} %get-tuple-element.49), channel_id=1, source_target_pairs={{4,0},{0,4},{12,8},{8,12},{5,1},{1,5},{13,9},{9,13},{6,2},{2,6},{1... | collective-permute-start | bytes 196616 | tf_op jit(solution)/shard_map/ppermute | solution.py:587
  47.1 16.6 %copy-start = (f32[128]{0:T(128)S(1)}, f32[128]{0:T(128)}, u32[]{:S(2)}) copy-start(f32[128]{0:T(128)} %param.16) | copy-start | bytes 1540
  51.5 7.8 %collective-permute-start.11 = (bf16[256,128]{1,0:T(8,128)(2,1)S(1)}, bf16[256,128]{1,0:T(8,128)(2,1)S(1)}, u32[]{:S(2)}, u32[]{:S(2)}) collective-permute-start(bf16[256,128]{1,0:T(8,128)(2,1)S(1)} %get-tuple-element.50), channel_id=1, source_target_pairs={{12,0},{8,4},{4,8},{0,12},{13,1},{9,5},{5,9},{1,13},{14,2},{10,6},... | collective-permute-start | bytes 196616 | tf_op jit(solution)/shard_map/ppermute | solution.py:587
  54.4 4.8 %collective-permute-start.10 = (bf16[256,128]{1,0:T(8,128)(2,1)S(1)}, bf16[256,128]{1,0:T(8,128)(2,1)S(1)}, u32[]{:S(2)}, u32[]{:S(2)}) collective-permute-start(bf16[256,128]{1,0:T(8,128)(2,1)S(1)} %get-tuple-element.51), channel_id=1, source_target_pairs={{8,0},{12,4},{0,8},{4,12},{9,1},{13,5},{1,9},{5,13},{10,2},{14,6},... | collective-permute-start | bytes 196616 | tf_op jit(solution)/shard_map/ppermute | solution.py:587
  54.4 17.9 %collective-permute-start.12 = (bf16[32,2048]{1,0:T(8,128)(2,1)S(1)}, bf16[32,2048]{1,0:T(8,128)(2,1)S(1)}, u32[]{:S(2)}, u32[]{:S(2)}) collective-permute-start(bf16[32,2048]{1,0:T(8,128)(2,1)S(1)} %get-tuple-element.42), channel_id=1, source_target_pairs={{1,0},{0,1},{3,2},{2,3},{5,4},{4,5},{7,6},{6,7},{9,8},{8,9},{11,10... | collective-permute-start | bytes 393224 | tf_op jit(solution)/shard_map/ppermute | solution.py:584
  55.9 17.0 %collective-permute-start.14 = (bf16[32,2048]{1,0:T(8,128)(2,1)S(1)}, bf16[32,2048]{1,0:T(8,128)(2,1)S(1)}, u32[]{:S(2)}, u32[]{:S(2)}) collective-permute-start(bf16[32,2048]{1,0:T(8,128)(2,1)S(1)} %get-tuple-element.43), channel_id=1, source_target_pairs={{3,0},{2,1},{1,2},{0,3},{7,4},{6,5},{5,6},{4,7},{11,8},{10,9},{9,1... | collective-permute-start | bytes 393224 | tf_op jit(solution)/shard_map/ppermute | solution.py:584
  59.3 7.8 %collective-permute-start.21 = (bf16[256,128]{1,0:T(8,128)(2,1)S(1)}, bf16[256,128]{1,0:T(8,128)(2,1)S(1)}, u32[]{:S(2)}, u32[]{:S(2)}) collective-permute-start(bf16[256,128]{1,0:T(8,128)(2,1)S(1)} %convert_element_type.100), channel_id=1, source_target_pairs={{3,0},{2,1},{1,2},{0,3},{7,4},{6,5},{5,6},{4,7},{11,8},{10,9},{9,1... | collective-permute-start | bytes 196616 | tf_op jit(solution)/shard_map/ppermute | solution.py:584
  61.0 9.9 %collective-permute-start.20 = (bf16[256,128]{1,0:T(8,128)(2,1)S(1)}, bf16[256,128]{1,0:T(8,128)(2,1)S(1)}, u32[]{:S(2)}, u32[]{:S(2)}) collective-permute-start(bf16[256,128]{1,0:T(8,128)(2,1)S(1)} %convert_element_type.100), channel_id=1, source_target_pairs={{2,0},{3,1},{0,2},{1,3},{6,4},{7,5},{4,6},{5,7},{10,8},{11,9},{8,1... | collective-permute-start | bytes 196616 | tf_op jit(solution)/shard_map/ppermute | solution.py:584
  61.7 9.2 %collective-permute-start.19 = (bf16[256,128]{1,0:T(8,128)(2,1)S(1)}, bf16[256,128]{1,0:T(8,128)(2,1)S(1)}, u32[]{:S(2)}, u32[]{:S(2)}) collective-permute-start(bf16[256,128]{1,0:T(8,128)(2,1)S(1)} %convert_element_type.100), channel_id=1, source_target_pairs={{1,0},{0,1},{3,2},{2,3},{5,4},{4,5},{7,6},{6,7},{9,8},{8,9},{11,10... | collective-permute-start | bytes 196616 | tf_op jit(solution)/shard_map/ppermute | solution.py:584
  67.1 8.5 %collective-permute-start.13 = (bf16[32,2048]{1,0:T(8,128)(2,1)S(1)}, bf16[32,2048]{1,0:T(8,128)(2,1)S(1)}, u32[]{:S(2)}, u32[]{:S(2)}) collective-permute-start(bf16[32,2048]{1,0:T(8,128)(2,1)S(1)} %get-tuple-element.44), channel_id=1, source_target_pairs={{2,0},{3,1},{0,2},{1,3},{6,4},{7,5},{4,6},{5,7},{10,8},{11,9},{8,1... | collective-permute-start | bytes 393224 | tf_op jit(solution)/shard_map/ppermute | solution.py:584
  71.0 5.3 %collective-permute-start.24 = (bf16[256,128]{1,0:T(8,128)(2,1)S(1)}, bf16[256,128]{1,0:T(8,128)(2,1)S(1)}, u32[]{:S(2)}, u32[]{:S(2)}) collective-permute-start(bf16[256,128]{1,0:T(8,128)(2,1)S(1)} %add_convert_fusion.2), channel_id=1, source_target_pairs={{4,0},{0,4},{12,8},{8,12},{5,1},{1,5},{13,9},{9,13},{6,2},{2,6},{1... | collective-permute-start | bytes 196616 | tf_op jit(solution)/shard_map/ppermute | solution.py:587
  71.0 5.2 %collective-permute-start.23 = (bf16[256,128]{1,0:T(8,128)(2,1)S(1)}, bf16[256,128]{1,0:T(8,128)(2,1)S(1)}, u32[]{:S(2)}, u32[]{:S(2)}) collective-permute-start(bf16[256,128]{1,0:T(8,128)(2,1)S(1)} %add_convert_fusion.2), channel_id=1, source_target_pairs={{8,0},{12,4},{0,8},{4,12},{9,1},{13,5},{1,9},{5,13},{10,2},{14,6},... | collective-permute-start | bytes 196616 | tf_op jit(solution)/shard_map/ppermute | solution.py:587
  72.4 4.4 %collective-permute-start.22 = (bf16[256,128]{1,0:T(8,128)(2,1)S(1)}, bf16[256,128]{1,0:T(8,128)(2,1)S(1)}, u32[]{:S(2)}, u32[]{:S(2)}) collective-permute-start(bf16[256,128]{1,0:T(8,128)(2,1)S(1)} %add_convert_fusion.2), channel_id=1, source_target_pairs={{12,0},{8,4},{4,8},{0,12},{13,1},{9,5},{5,9},{1,13},{14,2},{10,6},... | collective-permute-start | bytes 196616 | tf_op jit(solution)/shard_map/ppermute | solution.py:587

commit v17 on v15

--- a/solution.py
+++ b/solution.py
@@ -235,13 +235,13 @@
                         at = (g, slice(e * cols, (e + 1) * cols))
                         back_ref[at + (slice(half * LANES, (half + 1) * LANES),)] = part
 
-    def two_groups(i):
-        grad_of(2 * i).wait()
-        grad_of(2 * i + 1).wait()
-        group(2 * i)
-        group(2 * i + 1)
-
-    each(0, groups // 2 - 1, two_groups)
+    def four_groups(i):
+        for g in range(4):
+            grad_of(4 * i + g).wait()
+        for g in range(4):
+            group(4 * i + g)
+
+    each(0, groups // 4 - 1, four_groups)
 
 
 def back_call(at, labels, counts, w, grad, seqs, n_col):
@@ -394,14 +394,15 @@
         part = jnp.where(keep0, part[:seqs], 0.0) + jnp.where(keep1, part[seqs:], 0.0)
         return part if total is None else total + part
 
-    def two_groups(i):
-        totals = [two_chains(g, 0, None) for g in (2 * i, 2 * i + 1)]
-        for g, total in zip((2 * i, 2 * i + 1), totals):
+    def four_groups(i):
+        some = [4 * i + g for g in range(4)]
+        totals = [two_chains(g, 0, None) for g in some]
+        for g, total in zip(some, totals):
             more = functools.partial(two_chains, g)
             total = lax.fori_loop(1, (last(g) - first(g)) // 2 + 1, more, total)
             left_out[:, lanes_of(g)] = total.astype(BF16)
 
-    each(0, groups // 2 - 1, two_groups)
+    each(0, groups // 4 - 1, four_groups)
 
 
 def left_grad_call(at, labels, back, lab, right, tall):

time: 78.7 us -> 78.1 us (level)
  transfers between devices with their start and end apart: 25 -> 25, of which waited for: 3 -> 3; matrix products, arithmetic and copies ran while one was open for 3% -> 3% of each run, Pallas kernels for 36% -> 35%
where the time goes in v17:
time: 78.1 us; the launch traced here: 77.9 us
  starting transfers between devices  38.1 us (49%)
  Pallas kernels  31.2 us (40%)
  waiting for transfers between devices  4.25 us (5%)
  other arithmetic  3.03 us (4%)
  between operations  0.88 us (1%)
    ppermute x12, starting transfers between devices, col_swap(): return lax.ppermute(value, 'col', [(t ^ k, t) for t in range(self.n_col)])  22.7 us
    pallas_call x1, Pallas kernels, outer_call(): pl.pallas_call(outer_body, in_specs=[SMEM] * 2 + [VMEM] * 5, out_specs=[V...  8.39 us
    ppermute x9, starting transfers between devices, row_swap(): return lax.ppermute(value, 'row', [(t ^ k, t) for t in range(self.n_row)])  7.91 us
    ppermute x4, starting transfers between devices, right_grad_home(): got = lax.ppermute(block, ('row', 'col'), pairs).astype(F32)[None]  7.46 us
    pallas_call x1, Pallas kernels, right_grad_call(): pl.pallas_call(right_grad_body, in_specs=[SMEM] * 2 + [VMEM] * 4, out_spe...  5.91 us
    pallas_call x1, Pallas kernels, back_call(): pl.pallas_call(lambda *refs: back_body(*refs, seqs=seqs, n_col=n_col), in...  5.88 us
    pallas_call x1, Pallas kernels, left_grad_call(): pl.pallas_call(left_grad_body, in_specs=[SMEM] * 2 + [VMEM] * 4, out_spec...  3.98 us
    ppermute x12, waiting for transfers between devices, col_swap(): return lax.ppermute(value, 'col', [(t ^ k, t) for t in range(self.n_col)])  3.75 us
  transfers between devices with their start and end apart: 25, of which 3 were waited for; matrix products, arithmetic and copies ran while one was open for 3% of the time, Pallas kernels for 35%

profile of v17, /device:TPU:0, one launch (start us, length us, event | category | flops | bytes accessed | tf_op | source)
XLA Modules:
  0.0 77.9 jit_solution(13739674274416582003)
XLA Ops:
  0.6 3.7 %project.1 = (bf16[32,2048]{1,0:T(8,128)(2,1)S(1)}, bf16[32,2048]{1,0:T(8,128)(2,1)S(1)}) custom-call(bf16[32,64,256]{2,1,0:T(8,128)(2,1)} %refs_0_.1, f32[1,256]{1,0:T(1,128)} %bitcast.61, f32[1,256]{1,0:T(1,128)} %bitcast.62, bf16[32,256]{1,0:T(8,128)(2,1)} %bitcast.59, bf16[32,256]{1,0:T(8,128)(2,1)} %bitcast.60), custom_call_target="tpu_custom_call" | custom-call | tf_op jit(solution)/shard_map/project/pallas_call | solution.py:124
  4.4 5.1 %collective-permute-start.2 = (bf16[32,2048]{1,0:T(8,128)(2,1)S(1)}, bf16[32,2048]{1,0:T(8,128)(2,1)S(1)}, u32[]{:S(2)}, u32[]{:S(2)}) collective-permute-start(bf16[32,2048]{1,0:T(8,128)(2,1)S(1)} %get-tuple-element.21), channel_id=1, source_target_pairs={{3,0},{2,1},{1,2},{0,3},{7,4},{6,5},{5,6},{4,7},{11,8},{10,9},{9,1... | collective-permute-start | bytes 393224 | tf_op jit(solution)/shard_map/ppermute | solution.py:566
  9.5 0.7 collective-permute-start.5
  10.2 0.8 %collective-permute-start.4 = (bf16[32,2048]{1,0:T(8,128)(2,1)S(1)}, bf16[32,2048]{1,0:T(8,128)(2,1)S(1)}, u32[]{:S(2)}, u32[]{:S(2)}) collective-permute-start(bf16[32,2048]{1,0:T(8,128)(2,1)S(1)} %get-tuple-element.22), channel_id=1, source_target_pairs={{8,0},{12,4},{0,8},{4,12},{9,1},{13,5},{1,9},{5,13},{10,2},{14,6},... | collective-permute-start | bytes 393224 | tf_op jit(solution)/shard_map/ppermute | solution.py:569
  11.0 0.4 collective-permute-start.3
  11.8 5.9 %back.1 = (s32[1,2048]{1,0:T(1,128)S(1)}, bf16[8,2,128,128]{3,2,1,0:T(8,128)(2,1)S(1)}, bf16[8,2,64,128]{3,2,1,0:T(8,128)(2,1)S(1)}, f32[8,64,128]{2,1,0:T(8,128...) custom-call(s32[3]{0:T(128)S(1)} %add_convert_fusion.3.refs_0_.at_ref, ...), custom_call_target="tpu_custom_call" | custom-call | flops 21474836480 | bytes 8388608 | tf_op jit(solution)/shard_map/back/pallas_call | solution.py:252
  17.7 0.7 collective-permute-start
  18.5 3.8 %collective-permute-start.8 = (bf16[32,2048]{1,0:T(8,128)(2,1)S(1)}, bf16[32,2048]{1,0:T(8,128)(2,1)S(1)}, u32[]{:S(2)}, u32[]{:S(2)}) collective-permute-start(bf16[32,2048]{1,0:T(8,128)(2,1)S(1)} %get-tuple-element.46), channel_id=1, source_target_pairs={{3,0},{2,1},{1,2},{0,3},{7,4},{6,5},{5,6},{4,7},{11,8},{10,9},{9,1... | collective-permute-start | bytes 393224 | tf_op jit(solution)/shard_map/ppermute | solution.py:566
  22.3 1.1 %collective-permute-done = bf16[32,2048]{1,0:T(8,128)(2,1)S(1)} collective-permute-done((bf16[32,2048]{1,0:T(8,128)(2,1)S(1)}, bf16[32,2048]{1,0:T(8,128)(2,1)S(1)}, u32[]{:S(2)}, u32[]{:S(2)}) %collective-permute-start) | collective-permute-done | bytes 131104 | tf_op jit(solution)/shard_map/ppermute | solution.py:566
  23.4 0.7 collective-permute-start.6
  24.2 5.9 %right_grad.1 = bf16[128,2048]{1,0:T(8,128)(2,1)S(1)} custom-call(s32[3]{0:T(128)S(1)} %add_convert_fusion.3.refs_0_.at_ref, s32[256]{0:T(256)S(1)} %copy-done.1, bf16[8,2048,256]{2,1,0:T(8,128)(2,1)S(1)} %get-tuple-element.25.back_ref, bf16[128,2048]{1,0:T(8,128)(2,1)S(1)} %constant_dynamic-update-slice_fusion.left_ref, ...), custom_call_target="tpu_custom_call" | custom-call | flops 21474836480 | bytes 8388608 | tf_op jit(solution)/shard_map/right_grad/pallas_call | solution.py:353
  30.1 0.7 collective-permute-start.15
  30.8 5.7 %collective-permute-start.18 = (bf16[32,2048]{1,0:T(8,128)(2,1)S(1)}, bf16[32,2048]{1,0:T(8,128)(2,1)S(1)}, u32[]{:S(2)}, u32[]{:S(2)}) collective-permute-start(bf16[32,2048]{1,0:T(8,128)(2,1)S(1)} %get-tuple-element.39), channel_id=1, source_target_pairs={{0,3},{1,7},{2,11},{3,15},{4,2},{5,6},{6,10},{7,14},{8,1},{9,5},{1... | collective-permute-start | bytes 393224 | tf_op jit(solution)/shard_map/ppermute | solution.py:602
  36.5 1.1 %collective-permute-start.17 = (bf16[32,2048]{1,0:T(8,128)(2,1)S(1)}, bf16[32,2048]{1,0:T(8,128)(2,1)S(1)}, u32[]{:S(2)}, u32[]{:S(2)}) collective-permute-start(bf16[32,2048]{1,0:T(8,128)(2,1)S(1)} %get-tuple-element.40), channel_id=1, source_target_pairs={{0,2},{1,6},{2,10},{3,14},{4,3},{5,7},{6,11},{7,15},{8,0},{9,4},{1... | collective-permute-start | bytes 393224 | tf_op jit(solution)/shard_map/ppermute | solution.py:602
  37.7 8.4 %outer.1 = (bf16[8,512,1024]{2,1,0:T(8,128)(2,1)S(1)}, f32[1024,128]{1,0:T(8,128)S(1)}) custom-call(s32[3]{0:T(128)S(1)} %add_convert_fusion.3.refs_0_.at_ref, s32[256]{0:T(256)S(1)} %copy-done.1, bf16[128,2048]{1,0:T(8,128)(2,1)S(1)} %constant_dynamic-update-slice_fusion.left_ref, s32[1,2048]{1,0:T(1,128)S(1)} %get-tuple-element.33.lab_ref, ...), custom_call_target="tpu_custom_call" | custom-call | flops 42949672960 | bytes 8388608 | tf_op jit(solution)/shard_map/outer/pallas_call | solution.py:506
  46.1 1.5 %collective-permute-start.9 = (bf16[256,128]{1,0:T(8,128)(2,1)S(1)}, bf16[256,128]{1,0:T(8,128)(2,1)S(1)}, u32[]{:S(2)}, u32[]{:S(2)}) collective-permute-start(bf16[256,128]{1,0:T(8,128)(2,1)S(1)} %get-tuple-element.49), channel_id=1, source_target_pairs={{4,0},{0,4},{12,8},{8,12},{5,1},{1,5},{13,9},{9,13},{6,2},{2,6},{1... | collective-permute-start | bytes 196616 | tf_op jit(solution)/shard_map/ppermute | solution.py:569
  47.6 4.0 %left_grad.1 = bf16[128,2048]{1,0:T(8,128)(2,1)S(1)} custom-call(s32[3]{0:T(128)S(1)} %add_convert_fusion.3.refs_0_.at_ref, s32[256]{0:T(256)S(1)} %copy-done.1, bf16[8,2048,256]{2,1,0:T(8,128)(2,1)S(1)} %get-tuple-element.25.back_ref, s32[1,2048]{1,0:T(1,128)S(1)} %get-tuple-element.33.lab_ref, bf16[128,2048]{1,0:T(8,128)(2,1)S(1)} %pad_maximum_fusion.1.right_ref, ...), custom_call_target="tpu_custom_call" | custom-call | flops 21474836480 | bytes 8388608 | tf_op jit(solution)/shard_map/left_grad/pallas_call | solution.py:412
  51.6 2.7 %collective-permute-start.11 = (bf16[256,128]{1,0:T(8,128)(2,1)S(1)}, bf16[256,128]{1,0:T(8,128)(2,1)S(1)}, u32[]{:S(2)}, u32[]{:S(2)}) collective-permute-start(bf16[256,128]{1,0:T(8,128)(2,1)S(1)} %get-tuple-element.50), channel_id=1, source_target_pairs={{12,0},{8,4},{4,8},{0,12},{13,1},{9,5},{5,9},{1,13},{14,2},{10,6},... | collective-permute-start | bytes 196616 | tf_op jit(solution)/shard_map/ppermute | solution.py:569
  54.3 1.5 %collective-permute-start.12 = (bf16[32,2048]{1,0:T(8,128)(2,1)S(1)}, bf16[32,2048]{1,0:T(8,128)(2,1)S(1)}, u32[]{:S(2)}, u32[]{:S(2)}) collective-permute-start(bf16[32,2048]{1,0:T(8,128)(2,1)S(1)} %get-tuple-element.42), channel_id=1, source_target_pairs={{1,0},{0,1},{3,2},{2,3},{5,4},{4,5},{7,6},{6,7},{9,8},{8,9},{11,10... | collective-permute-start | bytes 393224 | tf_op jit(solution)/shard_map/ppermute | solution.py:566
  55.8 2.6 %collective-permute-start.14 = (bf16[32,2048]{1,0:T(8,128)(2,1)S(1)}, bf16[32,2048]{1,0:T(8,128)(2,1)S(1)}, u32[]{:S(2)}, u32[]{:S(2)}) collective-permute-start(bf16[32,2048]{1,0:T(8,128)(2,1)S(1)} %get-tuple-element.43), channel_id=1, source_target_pairs={{3,0},{2,1},{1,2},{0,3},{7,4},{6,5},{5,6},{4,7},{11,8},{10,9},{9,1... | collective-permute-start | bytes 393224 | tf_op jit(solution)/shard_map/ppermute | solution.py:566
  58.4 0.7 add_convert_fusion
  59.2 1.7 %collective-permute-start.21 = (bf16[256,128]{1,0:T(8,128)(2,1)S(1)}, bf16[256,128]{1,0:T(8,128)(2,1)S(1)}, u32[]{:S(2)}, u32[]{:S(2)}) collective-permute-start(bf16[256,128]{1,0:T(8,128)(2,1)S(1)} %convert_element_type.100), channel_id=1, source_target_pairs={{3,0},{2,1},{1,2},{0,3},{7,4},{6,5},{5,6},{4,7},{11,8},{10,9},{9,1... | collective-permute-start | bytes 196616 | tf_op jit(solution)/shard_map/ppermute | solution.py:566
  60.9 0.7 collective-permute-start.20
  61.6 2.1 %collective-permute-start.19 = (bf16[256,128]{1,0:T(8,128)(2,1)S(1)}, bf16[256,128]{1,0:T(8,128)(2,1)S(1)}, u32[]{:S(2)}, u32[]{:S(2)}) collective-permute-start(bf16[256,128]{1,0:T(8,128)(2,1)S(1)} %convert_element_type.100), channel_id=1, source_target_pairs={{1,0},{0,1},{3,2},{2,3},{5,4},{4,5},{7,6},{6,7},{9,8},{8,9},{11,10... | collective-permute-start | bytes 196616 | tf_op jit(solution)/shard_map/ppermute | solution.py:566
  63.7 3.3 %pair.1 = bf16[4096,128]{1,0:T(8,128)(2,1)} custom-call(bf16[8,512,1024]{2,1,0:T(8,128)(2,1)S(1)} %get-tuple-element.30.outer_ref, bf16[1024,128]{1,0:T(8,128)(2,1)S(1)} %get-tuple-element.36.w_ref, f32[1,128]{1,0:T(1,128)S(1)} %bitcast.52), custom_call_target="tpu_custom_call" | custom-call | flops 1073741824 | bytes 1048576 | tf_op jit(solution)/shard_map/pair/pallas_call | solution.py:542
  67.0 3.8 %collective-permute-start.13 = (bf16[32,2048]{1,0:T(8,128)(2,1)S(1)}, bf16[32,2048]{1,0:T(8,128)(2,1)S(1)}, u32[]{:S(2)}, u32[]{:S(2)}) collective-permute-start(bf16[32,2048]{1,0:T(8,128)(2,1)S(1)} %get-tuple-element.44), channel_id=1, source_target_pairs={{2,0},{3,1},{0,2},{1,3},{6,4},{7,5},{4,6},{5,7},{10,8},{11,9},{8,1... | collective-permute-start | bytes 393224 | tf_op jit(solution)/shard_map/ppermute | solution.py:566
  70.9 1.3 %collective-permute-start.23 = (bf16[256,128]{1,0:T(8,128)(2,1)S(1)}, bf16[256,128]{1,0:T(8,128)(2,1)S(1)}, u32[]{:S(2)}, u32[]{:S(2)}) collective-permute-start(bf16[256,128]{1,0:T(8,128)(2,1)S(1)} %add_convert_fusion.2), channel_id=1, source_target_pairs={{8,0},{12,4},{0,8},{4,12},{9,1},{13,5},{1,9},{5,13},{10,2},{14,6},... | collective-permute-start | bytes 196616 | tf_op jit(solution)/shard_map/ppermute | solution.py:569
  72.3 0.5 collective-permute-start.22
  72.8 2.7 %collective-permute-done.13 = bf16[32,2048]{1,0:T(8,128)(2,1)S(1)} collective-permute-done((bf16[32,2048]{1,0:T(8,128)(2,1)S(1)}, bf16[32,2048]{1,0:T(8,128)(2,1)S(1)}, u32[]{:S(2)}, u32[]{:S(2)}) %collective-permute-start.13) | collective-permute-done | bytes 131104 | tf_op jit(solution)/shard_map/ppermute | solution.py:566
  75.4 0.7 add_convert_fusion.1
  76.2 0.5 collective-permute-done.22
  76.6 1.3 %convert_multiply_fusion = f32[1024,128]{1,0:T(8,128)} fusion(pred[1024]{0:T(1024)(128)(4,1)S(1)} %broadcast_in_dim.105, pred[1024]{0:T(1024)(128)(4,1)S(1)} %broadcast_in_dim.100, pred[1024]{0:T(1024)(128)(4,1)S(1)} %broadcast_in_dim.95, bf16[256,128]{1,0:T(8,128)(2,1)S(1)} %add_convert_fusion.2, bf16[256,128]{1,0:T(8,128)(2,1)S(1)} %collective-permute-done.24, ...), kind=kLoop, calls=%fused_computation.2 | loop fusion | flops 655360 | bytes 789504 | tf_op jit(solution)/shard_map/div | solution.py:671
  (54 shorter events, 0.9 us)
Async XLA Ops:
  4.4 19.7 %collective-permute-start.2 = (bf16[32,2048]{1,0:T(8,128)(2,1)S(1)}, bf16[32,2048]{1,0:T(8,128)(2,1)S(1)}, u32[]{:S(2)}, u32[]{:S(2)}) collective-permute-start(bf16[32,2048]{1,0:T(8,128)(2,1)S(1)} %get-tuple-element.21), channel_id=1, source_target_pairs={{3,0},{2,1},{1,2},{0,3},{7,4},{6,5},{5,6},{4,7},{11,8},{10,9},{9,1... | collective-permute-start | bytes 393224 | tf_op jit(solution)/shard_map/ppermute | solution.py:566
  9.5 14.6 %collective-permute-start.1 = (bf16[32,2048]{1,0:T(8,128)(2,1)S(1)}, bf16[32,2048]{1,0:T(8,128)(2,1)S(1)}, u32[]{:S(2)}, u32[]{:S(2)}) collective-permute-start(bf16[32,2048]{1,0:T(8,128)(2,1)S(1)} %get-tuple-element.21), channel_id=1, source_target_pairs={{2,0},{3,1},{0,2},{1,3},{6,4},{7,5},{4,6},{5,7},{10,8},{11,9},{8,1... | collective-permute-start | bytes 393224 | tf_op jit(solution)/shard_map/ppermute | solution.py:566
  9.5 8.2 %collective-permute-start.5 = (bf16[32,2048]{1,0:T(8,128)(2,1)S(1)}, bf16[32,2048]{1,0:T(8,128)(2,1)S(1)}, u32[]{:S(2)}, u32[]{:S(2)}) collective-permute-start(bf16[32,2048]{1,0:T(8,128)(2,1)S(1)} %get-tuple-element.22), channel_id=1, source_target_pairs={{12,0},{8,4},{4,8},{0,12},{13,1},{9,5},{5,9},{1,13},{14,2},{10,6},... | collective-permute-start | bytes 393224 | tf_op jit(solution)/shard_map/ppermute | solution.py:569
  10.2 8.2 %collective-permute-start.4 = (bf16[32,2048]{1,0:T(8,128)(2,1)S(1)}, bf16[32,2048]{1,0:T(8,128)(2,1)S(1)}, u32[]{:S(2)}, u32[]{:S(2)}) collective-permute-start(bf16[32,2048]{1,0:T(8,128)(2,1)S(1)} %get-tuple-element.22), channel_id=1, source_target_pairs={{8,0},{12,4},{0,8},{4,12},{9,1},{13,5},{1,9},{5,13},{10,2},{14,6},... | collective-permute-start | bytes 393224 | tf_op jit(solution)/shard_map/ppermute | solution.py:569
  11.0 7.4 %collective-permute-start.3 = (bf16[32,2048]{1,0:T(8,128)(2,1)S(1)}, bf16[32,2048]{1,0:T(8,128)(2,1)S(1)}, u32[]{:S(2)}, u32[]{:S(2)}) collective-permute-start(bf16[32,2048]{1,0:T(8,128)(2,1)S(1)} %get-tuple-element.22), channel_id=1, source_target_pairs={{4,0},{0,4},{12,8},{8,12},{5,1},{1,5},{13,9},{9,13},{6,2},{2,6},{1... | collective-permute-start | bytes 393224 | tf_op jit(solution)/shard_map/ppermute | solution.py:569
  11.8 12.4 %copy-start.1 = (s32[256]{0:T(256)S(1)}, s32[256]{0:T(256)}, u32[]{:S(2)}) copy-start(s32[256]{0:T(256)} %labels_ref.5) | copy-start | bytes 3076
  17.7 5.7 %collective-permute-start = (bf16[32,2048]{1,0:T(8,128)(2,1)S(1)}, bf16[32,2048]{1,0:T(8,128)(2,1)S(1)}, u32[]{:S(2)}, u32[]{:S(2)}) collective-permute-start(bf16[32,2048]{1,0:T(8,128)(2,1)S(1)} %get-tuple-element.21), channel_id=1, source_target_pairs={{1,0},{0,1},{3,2},{2,3},{5,4},{4,5},{7,6},{6,7},{9,8},{8,9},{11,10... | collective-permute-start | bytes 393224 | tf_op jit(solution)/shard_map/ppermute | solution.py:566
  18.5 18.0 %collective-permute-start.8 = (bf16[32,2048]{1,0:T(8,128)(2,1)S(1)}, bf16[32,2048]{1,0:T(8,128)(2,1)S(1)}, u32[]{:S(2)}, u32[]{:S(2)}) collective-permute-start(bf16[32,2048]{1,0:T(8,128)(2,1)S(1)} %get-tuple-element.46), channel_id=1, source_target_pairs={{3,0},{2,1},{1,2},{0,3},{7,4},{6,5},{5,6},{4,7},{11,8},{10,9},{9,1... | collective-permute-start | bytes 393224 | tf_op jit(solution)/shard_map/ppermute | solution.py:566
  22.3 15.3 %collective-permute-start.7 = (bf16[32,2048]{1,0:T(8,128)(2,1)S(1)}, bf16[32,2048]{1,0:T(8,128)(2,1)S(1)}, u32[]{:S(2)}, u32[]{:S(2)}) collective-permute-start(bf16[32,2048]{1,0:T(8,128)(2,1)S(1)} %get-tuple-element.47), channel_id=1, source_target_pairs={{2,0},{3,1},{0,2},{1,3},{6,4},{7,5},{4,6},{5,7},{10,8},{11,9},{8,1... | collective-permute-start | bytes 393224 | tf_op jit(solution)/shard_map/ppermute | solution.py:566
  23.4 14.2 %collective-permute-start.6 = (bf16[32,2048]{1,0:T(8,128)(2,1)S(1)}, bf16[32,2048]{1,0:T(8,128)(2,1)S(1)}, u32[]{:S(2)}, u32[]{:S(2)}) collective-permute-start(bf16[32,2048]{1,0:T(8,128)(2,1)S(1)} %get-tuple-element.48), channel_id=1, source_target_pairs={{1,0},{0,1},{3,2},{2,3},{5,4},{4,5},{7,6},{6,7},{9,8},{8,9},{11,10... | collective-permute-start | bytes 393224 | tf_op jit(solution)/shard_map/ppermute | solution.py:566
  30.1 21.5 %collective-permute-start.15 = (bf16[32,2048]{1,0:T(8,128)(2,1)S(1)}, bf16[32,2048]{1,0:T(8,128)(2,1)S(1)}, u32[]{:S(2)}, u32[]{:S(2)}) collective-permute-start(bf16[32,2048]{1,0:T(8,128)(2,1)S(1)} %get-tuple-element.38), channel_id=1, source_target_pairs={{0,0},{1,4},{2,8},{3,12},{4,1},{5,5},{6,9},{7,13},{8,2},{9,6},{10,... | collective-permute-start | bytes 393224 | tf_op jit(solution)/shard_map/ppermute | solution.py:602
  30.8 23.5 %collective-permute-start.18 = (bf16[32,2048]{1,0:T(8,128)(2,1)S(1)}, bf16[32,2048]{1,0:T(8,128)(2,1)S(1)}, u32[]{:S(2)}, u32[]{:S(2)}) collective-permute-start(bf16[32,2048]{1,0:T(8,128)(2,1)S(1)} %get-tuple-element.39), channel_id=1, source_target_pairs={{0,3},{1,7},{2,11},{3,15},{4,2},{5,6},{6,10},{7,14},{8,1},{9,5},{1... | collective-permute-start | bytes 393224 | tf_op jit(solution)/shard_map/ppermute | solution.py:602
  36.5 17.8 %collective-permute-start.17 = (bf16[32,2048]{1,0:T(8,128)(2,1)S(1)}, bf16[32,2048]{1,0:T(8,128)(2,1)S(1)}, u32[]{:S(2)}, u32[]{:S(2)}) collective-permute-start(bf16[32,2048]{1,0:T(8,128)(2,1)S(1)} %get-tuple-element.40), channel_id=1, source_target_pairs={{0,2},{1,6},{2,10},{3,14},{4,3},{5,7},{6,11},{7,15},{8,0},{9,4},{1... | collective-permute-start | bytes 393224 | tf_op jit(solution)/shard_map/ppermute | solution.py:602
  37.6 18.2 %collective-permute-start.16 = (bf16[32,2048]{1,0:T(8,128)(2,1)S(1)}, bf16[32,2048]{1,0:T(8,128)(2,1)S(1)}, u32[]{:S(2)}, u32[]{:S(2)}) collective-permute-start(bf16[32,2048]{1,0:T(8,128)(2,1)S(1)} %get-tuple-element.41), channel_id=1, source_target_pairs={{0,1},{1,5},{2,9},{3,13},{4,0},{5,4},{6,8},{7,12},{8,3},{9,7},{10,... | collective-permute-start | bytes 393224 | tf_op jit(solution)/shard_map/ppermute | solution.py:602
  46.1 13.0 %collective-permute-start.9 = (bf16[256,128]{1,0:T(8,128)(2,1)S(1)}, bf16[256,128]{1,0:T(8,128)(2,1)S(1)}, u32[]{:S(2)}, u32[]{:S(2)}) collective-permute-start(bf16[256,128]{1,0:T(8,128)(2,1)S(1)} %get-tuple-element.49), channel_id=1, source_target_pairs={{4,0},{0,4},{12,8},{8,12},{5,1},{1,5},{13,9},{9,13},{6,2},{2,6},{1... | collective-permute-start | bytes 196616 | tf_op jit(solution)/shard_map/ppermute | solution.py:569
  47.6 16.1 %copy-start = (f32[128]{0:T(128)S(1)}, f32[128]{0:T(128)}, u32[]{:S(2)}) copy-start(f32[128]{0:T(128)} %param.16) | copy-start | bytes 1540
  51.6 7.5 %collective-permute-start.11 = (bf16[256,128]{1,0:T(8,128)(2,1)S(1)}, bf16[256,128]{1,0:T(8,128)(2,1)S(1)}, u32[]{:S(2)}, u32[]{:S(2)}) collective-permute-start(bf16[256,128]{1,0:T(8,128)(2,1)S(1)} %get-tuple-element.50), channel_id=1, source_target_pairs={{12,0},{8,4},{4,8},{0,12},{13,1},{9,5},{5,9},{1,13},{14,2},{10,6},... | collective-permute-start | bytes 196616 | tf_op jit(solution)/shard_map/ppermute | solution.py:569
  54.3 4.8 %collective-permute-start.10 = (bf16[256,128]{1,0:T(8,128)(2,1)S(1)}, bf16[256,128]{1,0:T(8,128)(2,1)S(1)}, u32[]{:S(2)}, u32[]{:S(2)}) collective-permute-start(bf16[256,128]{1,0:T(8,128)(2,1)S(1)} %get-tuple-element.51), channel_id=1, source_target_pairs={{8,0},{12,4},{0,8},{4,12},{9,1},{13,5},{1,9},{5,13},{10,2},{14,6},... | collective-permute-start | bytes 196616 | tf_op jit(solution)/shard_map/ppermute | solution.py:569
  54.3 17.9 %collective-permute-start.12 = (bf16[32,2048]{1,0:T(8,128)(2,1)S(1)}, bf16[32,2048]{1,0:T(8,128)(2,1)S(1)}, u32[]{:S(2)}, u32[]{:S(2)}) collective-permute-start(bf16[32,2048]{1,0:T(8,128)(2,1)S(1)} %get-tuple-element.42), channel_id=1, source_target_pairs={{1,0},{0,1},{3,2},{2,3},{5,4},{4,5},{7,6},{6,7},{9,8},{8,9},{11,10... | collective-permute-start | bytes 393224 | tf_op jit(solution)/shard_map/ppermute | solution.py:566
  55.8 17.0 %collective-permute-start.14 = (bf16[32,2048]{1,0:T(8,128)(2,1)S(1)}, bf16[32,2048]{1,0:T(8,128)(2,1)S(1)}, u32[]{:S(2)}, u32[]{:S(2)}) collective-permute-start(bf16[32,2048]{1,0:T(8,128)(2,1)S(1)} %get-tuple-element.43), channel_id=1, source_target_pairs={{3,0},{2,1},{1,2},{0,3},{7,4},{6,5},{5,6},{4,7},{11,8},{10,9},{9,1... | collective-permute-start | bytes 393224 | tf_op jit(solution)/shard_map/ppermute | solution.py:566
  59.2 7.8 %collective-permute-start.21 = (bf16[256,128]{1,0:T(8,128)(2,1)S(1)}, bf16[256,128]{1,0:T(8,128)(2,1)S(1)}, u32[]{:S(2)}, u32[]{:S(2)}) collective-permute-start(bf16[256,128]{1,0:T(8,128)(2,1)S(1)} %convert_element_type.100), channel_id=1, source_target_pairs={{3,0},{2,1},{1,2},{0,3},{7,4},{6,5},{5,6},{4,7},{11,8},{10,9},{9,1... | collective-permute-start | bytes 196616 | tf_op jit(solution)/shard_map/ppermute | solution.py:566
  60.9 9.9 %collective-permute-start.20 = (bf16[256,128]{1,0:T(8,128)(2,1)S(1)}, bf16[256,128]{1,0:T(8,128)(2,1)S(1)}, u32[]{:S(2)}, u32[]{:S(2)}) collective-permute-start(bf16[256,128]{1,0:T(8,128)(2,1)S(1)} %convert_element_type.100), channel_id=1, source_target_pairs={{2,0},{3,1},{0,2},{1,3},{6,4},{7,5},{4,6},{5,7},{10,8},{11,9},{8,1... | collective-permute-start | bytes 196616 | tf_op jit(solution)/shard_map/ppermute | solution.py:566
  61.6 9.2 %collective-permute-start.19 = (bf16[256,128]{1,0:T(8,128)(2,1)S(1)}, bf16[256,128]{1,0:T(8,128)(2,1)S(1)}, u32[]{:S(2)}, u32[]{:S(2)}) collective-permute-start(bf16[256,128]{1,0:T(8,128)(2,1)S(1)} %convert_element_type.100), channel_id=1, source_target_pairs={{1,0},{0,1},{3,2},{2,3},{5,4},{4,5},{7,6},{6,7},{9,8},{8,9},{11,10... | collective-permute-start | bytes 196616 | tf_op jit(solution)/shard_map/ppermute | solution.py:566
  67.0 8.5 %collective-permute-start.13 = (bf16[32,2048]{1,0:T(8,128)(2,1)S(1)}, bf16[32,2048]{1,0:T(8,128)(2,1)S(1)}, u32[]{:S(2)}, u32[]{:S(2)}) collective-permute-start(bf16[32,2048]{1,0:T(8,128)(2,1)S(1)} %get-tuple-element.44), channel_id=1, source_target_pairs={{2,0},{3,1},{0,2},{1,3},{6,4},{7,5},{4,6},{5,7},{10,8},{11,9},{8,1... | collective-permute-start | bytes 393224 | tf_op jit(solution)/shard_map/ppermute | solution.py:566
  70.9 5.3 %collective-permute-start.24 = (bf16[256,128]{1,0:T(8,128)(2,1)S(1)}, bf16[256,128]{1,0:T(8,128)(2,1)S(1)}, u32[]{:S(2)}, u32[]{:S(2)}) collective-permute-start(bf16[256,128]{1,0:T(8,128)(2,1)S(1)} %add_convert_fusion.2), channel_id=1, source_target_pairs={{4,0},{0,4},{12,8},{8,12},{5,1},{1,5},{13,9},{9,13},{6,2},{2,6},{1... | collective-permute-start | bytes 196616 | tf_op jit(solution)/shard_map/ppermute | solution.py:569
  70.9 5.2 %collective-permute-start.23 = (bf16[256,128]{1,0:T(8,128)(2,1)S(1)}, bf16[256,128]{1,0:T(8,128)(2,1)S(1)}, u32[]{:S(2)}, u32[]{:S(2)}) collective-permute-start(bf16[256,128]{1,0:T(8,128)(2,1)S(1)} %add_convert_fusion.2), channel_id=1, source_target_pairs={{8,0},{12,4},{0,8},{4,12},{9,1},{13,5},{1,9},{5,13},{10,2},{14,6},... | collective-permute-start | bytes 196616 | tf_op jit(solution)/shard_map/ppermute | solution.py:569
  72.3 4.4 %collective-permute-start.22 = (bf16[256,128]{1,0:T(8,128)(2,1)S(1)}, bf16[256,128]{1,0:T(8,128)(2,1)S(1)}, u32[]{:S(2)}, u32[]{:S(2)}) collective-permute-start(bf16[256,128]{1,0:T(8,128)(2,1)S(1)} %add_convert_fusion.2), channel_id=1, source_target_pairs={{12,0},{8,4},{4,8},{0,12},{13,1},{9,5},{5,9},{1,13},{14,2},{10,6},... | collective-permute-start | bytes 196616 | tf_op jit(solution)/shard_map/ppermute | solution.py:569
